TPU v7x, 256 devices: a whole 4x4x8 slice. The times are simulated.
256 devices in a mesh: tm: 32 (over x_hi, z, core), space: 8 (over y, x_lo).
Axes of the slice: x: 4 (x_hi: 2, x_lo: 2; x = x_hi * 2 + x_lo), y: 4, z: 8, core: 2. Of those that a mesh axis runs over, the one named last changes fastest.
Arguments:
- state: bfloat16 [32, 128, 64, 128], P('tm', 'space'), may hold values from -4 to 4
- initial: bfloat16 [128, 64, 128], P('space'), may hold values from -4 to 4
- forcing: bfloat16 [32, 128, 64, 128], P('tm', 'space'), may hold values from -5 to 5
- kappa: bfloat16 [128, 64, 128], P('space'), may hold values from 0.5 to 2
- reaction: bfloat16 [128, 64, 128], P('space'), may hold values from 0.019897461 to 0.19921875
Outputs:
- updated: bfloat16 [32, 128, 64, 128], P('tm', 'space')
All inputs are finite; a program needn't handle non-finite values.
Results may differ from a plain program's by a relative error of at most 0.006.
The roundings to bfloat16 on the way count: a program that leaves them out, or rounds other values in their place, can miss the bound.
Values may be sent and summed in bfloat16 or wider, within the bound.
No kernel may reach another device: no remote copies, remote signals or barrier semaphores. Data moves between devices by JAX's collectives and lax.ppermute only.
A program may use at most 64 MiB of HBM per device.

v0:
```python
import math

import jax
import jax.numpy as jnp
from jax import lax
from jax.sharding import Mesh
from jax.sharding import PartitionSpec as P

SWEEPS = 6
TM = ("tm_0", "tm_1", "tm_2")


alpha_ratio = 0.25
near_weight = 0.5
far_weight = 1.0
centre_weight = 6.0 * (near_weight + far_weight)
highest = lax.Precision.HIGHEST


def passed_along(value, axis, steps):
    count = lax.axis_size(axis)
    initial, last = (max(0, -steps), min(count, count - steps))
    return lax.ppermute(value, axis, [(source, source + steps) for source in range(initial, last)])


def with_halo(block, sides, width):
    for axis, dim in sides:
        count = lax.axis_size(axis)
        forward = [(i, i + 1) for i in range(count - 1)]
        backward = [(target, source) for source, target in forward]
        low = lax.ppermute(
            lax.slice_in_dim(block, block.shape[dim] - width, None, axis=dim), axis, forward
        )
        high = lax.ppermute(lax.slice_in_dim(block, 0, width, axis=dim), axis, backward)
        block = jnp.concatenate([low, block, high], axis=dim)
    return block


def split_up(x, dim, count):
    dims = x.shape
    tiles = x.reshape(*dims[:dim], count, dims[dim] // count, *dims[dim + 1 :])
    return jnp.moveaxis(tiles, dim, 0)


def in_order(tiles, dim):
    tiles = jnp.moveaxis(tiles, 0, dim)
    dims = tiles.shape
    return tiles.reshape(*dims[:dim], dims[dim] * dims[dim + 1], *dims[dim + 2 :])


def moved_by_axis(tiles, axes, turns):
    inside = tiles.shape[1:]
    result = tiles.reshape(*(lax.axis_size(a) for a in axes), *inside)
    for k in turns:
        result = lax.all_to_all(result, axes[k], k, k, tiled=True)
    return result.reshape(-1, *inside)


def two_step_exchange(x, groups, turns, split_dim, concat_dim):
    count = lax.axis_size(groups[0]) * lax.axis_size(groups[1])
    tiles = split_up(x, split_dim, count)
    return in_order(moved_by_axis(tiles, groups, turns), concat_dim)


def shifted(values, axis_number, offset):
    extent = values.shape[axis_number]
    widths = [(0, 0)] * values.ndim
    widths[axis_number] = (2, 2)
    padded = jnp.pad(values, widths)
    return lax.slice_in_dim(padded, 2 + offset, 2 + offset + extent, axis=axis_number)


def stencil(source, offset, start, extent):
    axis_first = source.ndim - 3

    def planes_at(displacement):
        lower = offset + start + displacement
        return lax.slice_in_dim(source, lower, lower + extent, axis=axis_first)

    centre = planes_at(0)
    near_sum = planes_at(1) + planes_at(-1)
    far_sum = planes_at(2) + planes_at(-2)
    for axis_number in (axis_first + 1, axis_first + 2):
        near_sum = near_sum + shifted(centre, axis_number, 1) + shifted(centre, axis_number, -1)
        far_sum = far_sum + shifted(centre, axis_number, 2) + shifted(centre, axis_number, -2)
    return (centre, near_sum, far_sum)


def residual_of(centre, near_sum, far_sum, before, source_term, kappa_part, reaction_part):
    return (
        source_term
        - centre
        + before
        - kappa_part * (centre_weight * centre - near_weight * near_sum - far_weight * far_sum)
        - reaction_part * centre * centre * centre
    )


def tables(length):
    counter = jnp.arange(length, dtype=jnp.int32)
    product = counter[:, None] * counter[None, :] % length
    angles = product.astype(jnp.float32) * (2.0 * math.pi / length)
    scaling = jnp.exp(counter.astype(jnp.float32) * (math.log(alpha_ratio) / length))
    forward_cos = jnp.cos(angles) * scaling[None, :]
    forward_sin = -jnp.sin(angles) * scaling[None, :]
    unscale = 1.0 / (scaling * length)
    inverse_cos = jnp.cos(angles) * unscale[:, None]
    inverse_sin = -jnp.sin(angles) * unscale[:, None]
    return (forward_cos, forward_sin, inverse_cos, inverse_sin)


def mode_shift(index_values, length):
    phases = index_values * (2.0 * math.pi / length)
    factor = math.exp(math.log(alpha_ratio) / length)
    return (1.0 - factor * jnp.cos(phases), factor * jnp.sin(phases))


def sweep_weights():
    return [
        1.0 / (1.0 + 0.4 * math.cos(math.pi * (2 * rounds + 1) / (2 * SWEEPS)))
        for rounds in range(SWEEPS)
    ]


def divided(error_real, error_imag, base_part, shift_real, shift_imag):
    diag_real = shift_real + base_part
    magnitude = diag_real * diag_real + shift_imag * shift_imag
    return jnp.stack(
        [
            (error_real * diag_real + error_imag * shift_imag) / magnitude,
            (error_imag * diag_real - error_real * shift_imag) / magnitude,
        ]
    )


def update(
    centre, near_sum, far_sum, target, kappa_part, base_part, shift_real, shift_imag, weight
):
    applied = base_part * centre - kappa_part * (near_weight * near_sum + far_weight * far_sum)
    image_real = shift_real * centre[0] - shift_imag * centre[1] + applied[0]
    image_imag = shift_real * centre[1] + shift_imag * centre[0] + applied[1]
    error_real = target[0] - image_real
    error_imag = target[1] - image_imag
    return centre + weight * divided(error_real, error_imag, base_part, shift_real, shift_imag)


def on_device(state, initial, forcing, kappa, reaction):
    local_steps, width_x, rows_y, depth_z = state.shape
    members = lax.axis_size(TM)
    length = local_steps * members
    position = lax.axis_index(TM)
    slab_index = lax.axis_index("space")
    columns = rows_y * depth_z
    kappa_full = kappa.astype(jnp.float32)
    reaction_full = reaction.astype(jnp.float32)
    start_state = initial.astype(jnp.float32)
    before = passed_along(state[local_steps - 1], TM, 1)
    opening = jnp.where(position == 0, initial, before)
    previous = jnp.concatenate([opening[None], state[:-1]], axis=0)
    forward_cos, forward_sin, inverse_cos, inverse_sin = tables(length)
    padded = with_halo(state, (("space", 1),), 2)
    residual_centre, residual_near_sum, residual_far_sum = stencil(
        padded.astype(jnp.float32), 2, 0, width_x
    )
    result = residual_of(
        residual_centre,
        residual_near_sum,
        residual_far_sum,
        previous.astype(jnp.float32),
        forcing.astype(jnp.float32),
        kappa_full,
        reaction_full,
    )
    residual = result.astype(jnp.bfloat16).reshape(local_steps, width_x, columns)
    cells = two_step_exchange(residual, (("tm_0", "tm_1"), "tm_2"), (1, 0), 2, 0)
    share = cells.shape[2]
    flat_cells = cells.reshape(length, width_x * share).astype(jnp.float32)
    spectrum = jnp.stack(
        [
            jnp.dot(forward_cos, flat_cells, precision=highest),
            jnp.dot(forward_sin, flat_cells, precision=highest),
        ]
    )
    spectrum = spectrum.astype(jnp.bfloat16).reshape(2, length, width_x, share)
    modes = lax.all_to_all(spectrum, TM, split_axis=1, concat_axis=3, tiled=True)
    target = modes.astype(jnp.float32).reshape(2, local_steps, width_x, rows_y, depth_z)
    index_values = (position * local_steps + jnp.arange(local_steps, dtype=jnp.int32)).astype(
        jnp.float32
    )
    shift_real, shift_imag = mode_shift(index_values, length)
    shift_real = shift_real.reshape(local_steps, 1, 1, 1)
    shift_imag = shift_imag.reshape(local_steps, 1, 1, 1)
    sigma_rate = 3.0 * reaction_full * start_state * start_state
    base_rate = kappa_full * centre_weight + sigma_rate
    weights = sweep_weights()
    iterate = divided(target[0], target[1], base_rate, shift_real, shift_imag)
    stacked = jnp.concatenate(
        [
            target.reshape(2 * local_steps, width_x, rows_y, depth_z),
            kappa_full[None],
            sigma_rate[None],
        ],
        axis=0,
    )
    rim_data = with_halo(stacked, (("space", 1),), 2)
    wide_target = rim_data[: 2 * local_steps].reshape(2, local_steps, width_x + 4, rows_y, depth_z)
    wide_kappa = rim_data[2 * local_steps]
    wide_base = wide_kappa * centre_weight + rim_data[2 * local_steps + 1]
    global_x = slab_index * width_x + jnp.arange(width_x + 4, dtype=jnp.int32) - 2
    inside_mask = ((global_x >= 0) & (global_x < width_x * lax.axis_size("space"))).astype(
        jnp.float32
    )
    inside_mask = inside_mask[:, None, None]
    for pair_index in range(len(weights) // 2):
        padded_iterate = with_halo(iterate, (("space", 2),), 4)
        centre, near_sum, far_sum = stencil(padded_iterate, 4, -2, width_x + 4)
        widened = (
            update(
                centre,
                near_sum,
                far_sum,
                wide_target,
                wide_kappa,
                wide_base,
                shift_real,
                shift_imag,
                weights[2 * pair_index],
            )
            * inside_mask
        )
        centre, near_sum, far_sum = stencil(widened, 2, 0, width_x)
        iterate = update(
            centre,
            near_sum,
            far_sum,
            target,
            kappa_full,
            base_rate,
            shift_real,
            shift_imag,
            weights[2 * pair_index + 1],
        )
    solved = iterate.astype(jnp.bfloat16).reshape(2, local_steps, width_x, columns)
    gathered = two_step_exchange(solved, (("tm_0", "tm_1"), "tm_2"), (1, 0), 3, 1)
    real_part = gathered[0].reshape(length, width_x * share).astype(jnp.float32)
    imag_part = gathered[1].reshape(length, width_x * share).astype(jnp.float32)
    correction = (
        jnp.dot(inverse_cos, real_part, precision=highest)
        + jnp.dot(inverse_sin, imag_part, precision=highest)
    ).astype(jnp.bfloat16)
    correction = correction.reshape(length, width_x, share)
    returned = two_step_exchange(correction, (("tm_0", "tm_1"), "tm_2"), (1, 0), 0, 2)
    return (state.astype(jnp.float32) + returned.reshape(state.shape).astype(jnp.float32)).astype(
        jnp.bfloat16
    )


def solution(mesh):
    torus = Mesh(
        mesh.devices.reshape(2, 8, 2, mesh.shape["space"]), ("tm_0", "tm_1", "tm_2", "space")
    )
    in_specs = (
        P(TM, "space", None, None),
        P("space", None, None),
        P(TM, "space", None, None),
        P("space", None, None),
        P("space", None, None),
    )
    out_specs = P(TM, "space", None, None)
    return jax.shard_map(
        on_device, mesh=torus, in_specs=in_specs, out_specs=out_specs, check_vma=False
    )
```

profile of v0, /device:TPU:16, one launch (start us, length us, event | category | flops | bytes accessed | tf_op | source)
XLA Modules:
  0.0 197.3 jit_solution(9111580689632707195)
XLA Ops:
  0.0 1.9 collective-permute-start.2
  1.9 0.8 fusion.184
  2.7 3.4 %collective-permute-start = (bf16[1,2,64,128]{3,2,1,0:T(8,128)(2,1)S(1)}, bf16[1,2,64,128]{3,2,1,0:T(8,128)(2,1)S(1)}, u32[]{:S(2)}, u32[]{:S(2)}) collective-permute-start(bf16[1,2,64,128]{3,2,1,0:T(8,128)(2,1)S(1)} %get-tuple-element.41), channel_id=1, source_target_pairs={{0,1},{1,2},{2,3},{3,4},{4,5},{5,6},{6,7},{8,9},{9,10},{10,11},{11... | collective-permute-start | bytes 98312 | tf_op jit(solution)/shard_map/ppermute | solution.py:31
  6.1 3.3 %collective-permute-start.1 = (bf16[1,2,64,128]{3,2,1,0:T(8,128)(2,1)S(1)}, bf16[1,2,64,128]{3,2,1,0:T(8,128)(2,1)S(1)}, u32[]{:S(2)}, u32[]{:S(2)}) collective-permute-start(bf16[1,2,64,128]{3,2,1,0:T(8,128)(2,1)S(1)} %get-tuple-element.42), channel_id=1, source_target_pairs={{1,0},{2,1},{3,2},{4,3},{5,4},{6,5},{7,6},{9,8},{10,9},{11,10},{12... | collective-permute-start | bytes 98312 | tf_op jit(solution)/shard_map/ppermute | solution.py:34
  9.5 3.9 %collective-permute-done.1 = bf16[1,2,64,128]{3,2,1,0:T(8,128)(2,1)S(1)} collective-permute-done((bf16[1,2,64,128]{3,2,1,0:T(8,128)(2,1)S(1)}, bf16[1,2,64,128]{3,2,1,0:T(8,128)(2,1)S(1)}, u32[]{:S(2)}, u32[]{:S(2)}) %collective-permute-start.1) | collective-permute-done | bytes 32800 | tf_op jit(solution)/shard_map/ppermute | solution.py:34
  13.3 1.0 maximum_convert_fusion
  14.4 0.8 fusion.107
  15.5 3.9 %all_to_all.39 = bf16[16,2,1,16,256]{4,3,0,2,1:T(8,128)(2,1)S(1)} all-to-all(bf16[16,2,1,16,256]{4,3,0,2,1:T(8,128)(2,1)S(1)} %copy.36), channel_id=1, replica_groups=mesh['tm_0'=2,'tm_1'=8,'tm_2'=2,'space'=8] {'tm_2'}, dimensions={1} | all-to-all | bytes 524288 | tf_op jit(solution)/shard_map/all_to_all | solution.py:55
  19.5 0.7 copy.37
  20.2 9.7 %all-to-all-start.1 = ((bf16[16,2,1,16,256]{4,3,1,2,0:T(8,128)(2,1)}), bf16[16,2,1,16,256]{4,3,1,2,0:T(8,128)(2,1)S(1)}, u32[]{:S(2)}, u32[]{:S(2)}) async-start(bf16[16,2,1,16,256]{4,3,1,2,0:T(8,128)(2,1)} %copy.37), calls=%async_computation.1 | async-start | bytes 524288 | tf_op jit(solution)/shard_map/all_to_all | solution.py:55
  29.9 12.0 %all-to-all-done.1 = bf16[16,2,1,16,256]{4,3,1,2,0:T(8,128)(2,1)S(1)} async-done(((bf16[16,2,1,16,256]{4,3,1,2,0:T(8,128)(2,1)}), bf16[16,2,1,16,256]{4,3,1,2,0:T(8,128)(2,1)S(1)}, u32[]{:S(2)}, u32[]{:S(2)}) %all-to-all-start.1) | async-done | bytes 262176 | tf_op jit(solution)/shard_map/all_to_all | solution.py:55
  41.9 0.4 fusion.43
  42.4 0.4 fusion.44
  42.9 1.1 copy.40
  44.0 4.7 %all-to-all-start.2 = ((bf16[2,32,16,256]{3,2,0,1:T(8,128)(2,1)}), bf16[2,32,16,256]{3,2,0,1:T(8,128)(2,1)S(1)}, u32[]{:S(2)}, u32[]{:S(2)}) async-start(bf16[2,32,16,256]{3,2,0,1:T(8,128)(2,1)} %copy.40), calls=%async_computation.2 | async-start | bytes 1048576 | tf_op jit(solution)/shard_map/all_to_all | solution.py:185
  49.0 19.6 %all-to-all-done.2 = bf16[2,32,16,256]{3,2,0,1:T(8,128)(2,1)S(1)} async-done(((bf16[2,32,16,256]{3,2,0,1:T(8,128)(2,1)}), bf16[2,32,16,256]{3,2,0,1:T(8,128)(2,1)S(1)}, u32[]{:S(2)}, u32[]{:S(2)}) %all-to-all-start.2) | async-done | bytes 524320 | tf_op jit(solution)/shard_map/all_to_all | solution.py:185
  68.9 1.6 copy.43
  70.5 0.3 copy.41
  70.8 0.3 copy.42
  71.2 1.3 reshape.980
  72.5 1.3 divide_bitcast_fusion.13
  73.8 3.8 %collective-permute-start.5 = (f32[4,2,64,128]{3,2,1,0:T(8,128)S(1)}, f32[4,2,64,128]{3,2,1,0:T(8,128)S(1)}, u32[]{:S(2)}, u32[]{:S(2)}) collective-permute-start(f32[4,2,64,128]{3,2,1,0:T(8,128)S(1)} %get-tuple-element.26), channel_id=1, source_target_pairs={{0,1},{1,2},{2,3},{3,4},{4,5},{5,6},{6,7},{8,9},{9,10},{10,11},{11... | collective-permute-start | bytes 786440 | tf_op jit(solution)/shard_map/ppermute | solution.py:31
  77.6 3.0 %collective-permute-start.6 = (f32[4,2,64,128]{3,2,1,0:T(8,128)S(1)}, f32[4,2,64,128]{3,2,1,0:T(8,128)S(1)}, u32[]{:S(2)}, u32[]{:S(2)}) collective-permute-start(f32[4,2,64,128]{3,2,1,0:T(8,128)S(1)} %get-tuple-element.27), channel_id=1, source_target_pairs={{1,0},{2,1},{3,2},{4,3},{5,4},{6,5},{7,6},{9,8},{10,9},{11,10},{12... | collective-permute-start | bytes 786440 | tf_op jit(solution)/shard_map/ppermute | solution.py:34
  80.8 2.9 %collective-permute-start.3 = (f32[2,1,4,64,128]{4,3,2,1,0:T(8,128)S(1)}, f32[2,1,4,64,128]{4,3,2,1,0:T(8,128)S(1)}, u32[]{:S(2)}, u32[]{:S(2)}) collective-permute-start(f32[2,1,4,64,128]{4,3,2,1,0:T(8,128)S(1)} %get-tuple-element.32), channel_id=1, source_target_pairs={{0,1},{1,2},{2,3},{3,4},{4,5},{5,6},{6,7},{8,9},{9,10},{10,11},{11... | collective-permute-start | bytes 786440 | tf_op jit(solution)/shard_map/ppermute | solution.py:31
  83.7 3.9 %collective-permute-start.4 = (f32[2,1,4,64,128]{4,3,2,1,0:T(8,128)S(1)}, f32[2,1,4,64,128]{4,3,2,1,0:T(8,128)S(1)}, u32[]{:S(2)}, u32[]{:S(2)}) collective-permute-start(f32[2,1,4,64,128]{4,3,2,1,0:T(8,128)S(1)} %get-tuple-element.33), channel_id=1, source_target_pairs={{1,0},{2,1},{3,2},{4,3},{5,4},{6,5},{7,6},{9,8},{10,9},{11,10},{12... | collective-permute-start | bytes 786440 | tf_op jit(solution)/shard_map/ppermute | solution.py:34
  87.6 3.7 %collective-permute-done.6 = f32[4,2,64,128]{3,2,1,0:T(8,128)S(1)} collective-permute-done((f32[4,2,64,128]{3,2,1,0:T(8,128)S(1)}, f32[4,2,64,128]{3,2,1,0:T(8,128)S(1)}, u32[]{:S(2)}, u32[]{:S(2)}) %collective-permute-start.6) | collective-permute-done | bytes 262176 | tf_op jit(solution)/shard_map/ppermute | solution.py:34
  91.2 0.3 pad_maximum_fusion
  91.7 5.4 %collective-permute-done.3 = f32[2,1,4,64,128]{4,3,2,1,0:T(8,128)S(1)} collective-permute-done((f32[2,1,4,64,128]{4,3,2,1,0:T(8,128)S(1)}, f32[2,1,4,64,128]{4,3,2,1,0:T(8,128)S(1)}, u32[]{:S(2)}, u32[]{:S(2)}) %collective-permute-start.3) | collective-permute-done | bytes 262176 | tf_op jit(solution)/shard_map/ppermute | solution.py:31
  97.0 2.9 %collective-permute-done.4 = f32[2,1,4,64,128]{4,3,2,1,0:T(8,128)S(1)} collective-permute-done((f32[2,1,4,64,128]{4,3,2,1,0:T(8,128)S(1)}, f32[2,1,4,64,128]{4,3,2,1,0:T(8,128)S(1)}, u32[]{:S(2)}, u32[]{:S(2)}) %collective-permute-start.4) | collective-permute-done | bytes 262176 | tf_op jit(solution)/shard_map/ppermute | solution.py:34
  100.3 1.8 fusion.8
  102.1 0.6 divide_bitcast_fusion.5
  102.7 0.2 divide_bitcast_fusion.4
  103.3 1.2 fusion.52
  104.5 0.4 divide_bitcast_fusion.11
  105.3 2.2 %collective-permute-start.7 = (f32[2,1,4,64,128]{4,3,2,1,0:T(8,128)S(1)}, f32[2,1,4,64,128]{4,3,2,1,0:T(8,128)S(1)}, u32[]{:S(2)}, u32[]{:S(2)}) collective-permute-start(f32[2,1,4,64,128]{4,3,2,1,0:T(8,128)S(1)} %get-tuple-element.30), channel_id=1, source_target_pairs={{0,1},{1,2},{2,3},{3,4},{4,5},{5,6},{6,7},{8,9},{9,10},{10,11},{11... | collective-permute-start | bytes 786440 | tf_op jit(solution)/shard_map/ppermute | solution.py:31
  107.5 4.7 %collective-permute-start.8 = (f32[2,1,4,64,128]{4,3,2,1,0:T(8,128)S(1)}, f32[2,1,4,64,128]{4,3,2,1,0:T(8,128)S(1)}, u32[]{:S(2)}, u32[]{:S(2)}) collective-permute-start(f32[2,1,4,64,128]{4,3,2,1,0:T(8,128)S(1)} %get-tuple-element.31), channel_id=1, source_target_pairs={{1,0},{2,1},{3,2},{4,3},{5,4},{6,5},{7,6},{9,8},{10,9},{11,10},{12... | collective-permute-start | bytes 786440 | tf_op jit(solution)/shard_map/ppermute | solution.py:34
  112.3 4.5 %collective-permute-done.7 = f32[2,1,4,64,128]{4,3,2,1,0:T(8,128)S(1)} collective-permute-done((f32[2,1,4,64,128]{4,3,2,1,0:T(8,128)S(1)}, f32[2,1,4,64,128]{4,3,2,1,0:T(8,128)S(1)}, u32[]{:S(2)}, u32[]{:S(2)}) %collective-permute-start.7) | collective-permute-done | bytes 262176 | tf_op jit(solution)/shard_map/ppermute | solution.py:31
  116.7 1.5 collective-permute-done.8
  118.6 1.8 fusion.20
  120.4 0.6 divide_bitcast_fusion.3
  121.5 1.2 fusion.64
  122.7 0.4 divide_bitcast_fusion.9
  123.6 4.5 %collective-permute-start.10 = (f32[2,1,4,64,128]{4,3,2,1,0:T(8,128)S(1)}, f32[2,1,4,64,128]{4,3,2,1,0:T(8,128)S(1)}, u32[]{:S(2)}, u32[]{:S(2)}) collective-permute-start(f32[2,1,4,64,128]{4,3,2,1,0:T(8,128)S(1)} %get-tuple-element.29), channel_id=1, source_target_pairs={{1,0},{2,1},{3,2},{4,3},{5,4},{6,5},{7,6},{9,8},{10,9},{11,10},{12... | collective-permute-start | bytes 786440 | tf_op jit(solution)/shard_map/ppermute | solution.py:34
  128.1 1.9 collective-permute-start.9
  130.0 4.5 %collective-permute-done.10 = f32[2,1,4,64,128]{4,3,2,1,0:T(8,128)S(1)} collective-permute-done((f32[2,1,4,64,128]{4,3,2,1,0:T(8,128)S(1)}, f32[2,1,4,64,128]{4,3,2,1,0:T(8,128)S(1)}, u32[]{:S(2)}, u32[]{:S(2)}) %collective-permute-start.10) | collective-permute-done | bytes 262176 | tf_op jit(solution)/shard_map/ppermute | solution.py:34
  134.6 4.2 %collective-permute-done.9 = f32[2,1,4,64,128]{4,3,2,1,0:T(8,128)S(1)} collective-permute-done((f32[2,1,4,64,128]{4,3,2,1,0:T(8,128)S(1)}, f32[2,1,4,64,128]{4,3,2,1,0:T(8,128)S(1)}, u32[]{:S(2)}, u32[]{:S(2)}) %collective-permute-start.9) | collective-permute-done | bytes 262176 | tf_op jit(solution)/shard_map/ppermute | solution.py:31
  139.0 1.8 fusion.32
  140.9 0.6 divide_bitcast_fusion.1
  141.5 0.2 divide_bitcast_fusion
  141.7 0.2 fusion.42
  142.0 1.2 fusion.76
  143.2 0.5 divide_bitcast_fusion.7
  144.3 0.3 copy.44
  144.6 4.2 %all_to_all.40 = bf16[16,2,2,1,16,256]{5,4,0,2,3,1:T(8,128)(2,1)S(1)} all-to-all(bf16[16,2,2,1,16,256]{5,4,0,2,3,1:T(8,128)(2,1)S(1)} %copy.45), channel_id=1, replica_groups=mesh['tm_0'=2,'tm_1'=8,'tm_2'=2,'space'=8] {'tm_2'}, dimensions={1} | all-to-all | bytes 1048576 | tf_op jit(solution)/shard_map/all_to_all | solution.py:55
  148.8 0.9 copy.46
  149.6 6.9 %all-to-all-start.4 = ((bf16[16,2,2,1,16,256]{5,4,1,2,3,0:T(8,128)(2,1)}), bf16[16,2,2,1,16,256]{5,4,1,2,3,0:T(8,128)(2,1)S(1)}, u32[]{:S(2)}, u32[]{:S(2)}) async-start(bf16[16,2,2,1,16,256]{5,4,1,2,3,0:T(8,128)(2,1)} %copy.46), calls=%async_computation.4 | async-start | bytes 1048576 | tf_op jit(solution)/shard_map/all_to_all | solution.py:55
  156.5 17.2 %all-to-all-done.4 = bf16[16,2,2,1,16,256]{5,4,1,2,3,0:T(8,128)(2,1)S(1)} async-done(((bf16[16,2,2,1,16,256]{5,4,1,2,3,0:T(8,128)(2,1)}), bf16[16,2,2,1,16,256]{5,4,1,2,3,0:T(8,128)(2,1)S(1)}, u32[]{:S(2)}, u32[]{:S(2)}) %all-to-all-start.4) | async-done | bytes 524320 | tf_op jit(solution)/shard_map/all_to_all | solution.py:55
  174.1 0.4 fusion.137
  174.5 0.4 fusion
  175.0 3.9 %all_to_all.41 = bf16[16,2,1,16,256]{4,3,0,2,1:T(8,128)(2,1)S(1)} all-to-all(bf16[16,2,1,16,256]{4,3,0,2,1:T(8,128)(2,1)S(1)} %copy.48), channel_id=1, replica_groups=mesh['tm_0'=2,'tm_1'=8,'tm_2'=2,'space'=8] {'tm_2'}, dimensions={1} | all-to-all | bytes 524288 | tf_op jit(solution)/shard_map/all_to_all | solution.py:55
  179.0 16.6 %all_to_all.42 = bf16[16,2,1,16,256]{4,3,1,2,0:T(8,128)(2,1)S(1)} all-to-all(bf16[16,2,1,16,256]{4,3,1,2,0:T(8,128)(2,1)S(1)} %copy.49), channel_id=1, replica_groups=mesh['tm_0'=2,'tm_1'=8,'tm_2'=2,'space'=8] {'tm_0','tm_1'}, dimensions={0} | all-to-all | bytes 524288 | tf_op jit(solution)/shard_map/all_to_all | solution.py:55
  195.6 0.3 copy.50
  196.0 0.5 copy-done.1
  196.5 0.8 add_convert_fusion
  (61 shorter events, 4.9 us)
Async XLA Ops:
  0.0 14.4 %copy-start.3 = (bf16[16,64,128]{2,1,0:T(8,128)(2,1)S(1)}, bf16[16,64,128]{2,1,0:T(8,128)(2,1)}, u32[]{:S(2)}) copy-start(bf16[16,64,128]{2,1,0:T(8,128)(2,1)} %param.6) | copy-start | bytes 786436
  0.0 14.4 %copy-start.4 = (bf16[1,16,64,128]{3,2,1,0:T(8,128)(2,1)S(1)}, bf16[1,16,64,128]{3,2,1,0:T(8,128)(2,1)}, u32[]{:S(2)}) copy-start(bf16[1,16,64,128]{3,2,1,0:T(8,128)(2,1)} %param.7) | copy-start | bytes 786436
  0.0 14.4 %copy-start = (bf16[16,64,128]{2,1,0:T(8,128)(2,1)S(1)}, bf16[16,64,128]{2,1,0:T(8,128)(2,1)}, u32[]{:S(2)}) copy-start(bf16[16,64,128]{2,1,0:T(8,128)(2,1)} %param.8) | copy-start | bytes 786436
  0.0 14.4 %copy-start.2 = (bf16[16,64,128]{2,1,0:T(8,128)(2,1)S(1)}, bf16[16,64,128]{2,1,0:T(8,128)(2,1)}, u32[]{:S(2)}) copy-start(bf16[16,64,128]{2,1,0:T(8,128)(2,1)} %param.9) | copy-start | bytes 786436
  0.0 14.4 %collective-permute-start.2 = (bf16[16,64,128]{2,1,0:T(8,128)(2,1)}, bf16[16,64,128]{2,1,0:T(8,128)(2,1)S(1)}, u32[]{:S(2)}, u32[]{:S(2)}) collective-permute-start(bf16[16,64,128]{2,1,0:T(8,128)(2,1)} %bitcast.186), channel_id=1, source_target_pairs={{0,8},{8,16},{16,24},{24,32},{32,40},{40,48},{48,56},{56,64},{64,7... | collective-permute-start | bytes 786440 | tf_op jit(solution)/shard_map/ppermute | solution.py:23
  2.7 6.8 %collective-permute-start = (bf16[1,2,64,128]{3,2,1,0:T(8,128)(2,1)S(1)}, bf16[1,2,64,128]{3,2,1,0:T(8,128)(2,1)S(1)}, u32[]{:S(2)}, u32[]{:S(2)}) collective-permute-start(bf16[1,2,64,128]{3,2,1,0:T(8,128)(2,1)S(1)} %get-tuple-element.41), channel_id=1, source_target_pairs={{0,1},{1,2},{2,3},{3,4},{4,5},{5,6},{6,7},{8,9},{9,10},{10,11},{11... | collective-permute-start | bytes 98312 | tf_op jit(solution)/shard_map/ppermute | solution.py:31
  6.1 7.2 %collective-permute-start.1 = (bf16[1,2,64,128]{3,2,1,0:T(8,128)(2,1)S(1)}, bf16[1,2,64,128]{3,2,1,0:T(8,128)(2,1)S(1)}, u32[]{:S(2)}, u32[]{:S(2)}) collective-permute-start(bf16[1,2,64,128]{3,2,1,0:T(8,128)(2,1)S(1)} %get-tuple-element.42), channel_id=1, source_target_pairs={{1,0},{2,1},{3,2},{4,3},{5,4},{6,5},{7,6},{9,8},{10,9},{11,10},{12... | collective-permute-start | bytes 98312 | tf_op jit(solution)/shard_map/ppermute | solution.py:34
  20.2 21.7 %all-to-all-start.1 = ((bf16[16,2,1,16,256]{4,3,1,2,0:T(8,128)(2,1)}), bf16[16,2,1,16,256]{4,3,1,2,0:T(8,128)(2,1)S(1)}, u32[]{:S(2)}, u32[]{:S(2)}) async-start(bf16[16,2,1,16,256]{4,3,1,2,0:T(8,128)(2,1)} %copy.37), calls=%async_computation.1 | async-start | bytes 524288 | tf_op jit(solution)/shard_map/all_to_all | solution.py:55
  44.0 24.7 %all-to-all-start.2 = ((bf16[2,32,16,256]{3,2,0,1:T(8,128)(2,1)}), bf16[2,32,16,256]{3,2,0,1:T(8,128)(2,1)S(1)}, u32[]{:S(2)}, u32[]{:S(2)}) async-start(bf16[2,32,16,256]{3,2,0,1:T(8,128)(2,1)} %copy.40), calls=%async_computation.2 | async-start | bytes 1048576 | tf_op jit(solution)/shard_map/all_to_all | solution.py:185
  73.8 13.7 %collective-permute-start.5 = (f32[4,2,64,128]{3,2,1,0:T(8,128)S(1)}, f32[4,2,64,128]{3,2,1,0:T(8,128)S(1)}, u32[]{:S(2)}, u32[]{:S(2)}) collective-permute-start(f32[4,2,64,128]{3,2,1,0:T(8,128)S(1)} %get-tuple-element.26), channel_id=1, source_target_pairs={{0,1},{1,2},{2,3},{3,4},{4,5},{5,6},{6,7},{8,9},{9,10},{10,11},{11... | collective-permute-start | bytes 786440 | tf_op jit(solution)/shard_map/ppermute | solution.py:31
  77.6 13.7 %collective-permute-start.6 = (f32[4,2,64,128]{3,2,1,0:T(8,128)S(1)}, f32[4,2,64,128]{3,2,1,0:T(8,128)S(1)}, u32[]{:S(2)}, u32[]{:S(2)}) collective-permute-start(f32[4,2,64,128]{3,2,1,0:T(8,128)S(1)} %get-tuple-element.27), channel_id=1, source_target_pairs={{1,0},{2,1},{3,2},{4,3},{5,4},{6,5},{7,6},{9,8},{10,9},{11,10},{12... | collective-permute-start | bytes 786440 | tf_op jit(solution)/shard_map/ppermute | solution.py:34
  80.8 16.2 %collective-permute-start.3 = (f32[2,1,4,64,128]{4,3,2,1,0:T(8,128)S(1)}, f32[2,1,4,64,128]{4,3,2,1,0:T(8,128)S(1)}, u32[]{:S(2)}, u32[]{:S(2)}) collective-permute-start(f32[2,1,4,64,128]{4,3,2,1,0:T(8,128)S(1)} %get-tuple-element.32), channel_id=1, source_target_pairs={{0,1},{1,2},{2,3},{3,4},{4,5},{5,6},{6,7},{8,9},{9,10},{10,11},{11... | collective-permute-start | bytes 786440 | tf_op jit(solution)/shard_map/ppermute | solution.py:31
  83.7 16.3 %collective-permute-start.4 = (f32[2,1,4,64,128]{4,3,2,1,0:T(8,128)S(1)}, f32[2,1,4,64,128]{4,3,2,1,0:T(8,128)S(1)}, u32[]{:S(2)}, u32[]{:S(2)}) collective-permute-start(f32[2,1,4,64,128]{4,3,2,1,0:T(8,128)S(1)} %get-tuple-element.33), channel_id=1, source_target_pairs={{1,0},{2,1},{3,2},{4,3},{5,4},{6,5},{7,6},{9,8},{10,9},{11,10},{12... | collective-permute-start | bytes 786440 | tf_op jit(solution)/shard_map/ppermute | solution.py:34
  105.3 11.4 %collective-permute-start.7 = (f32[2,1,4,64,128]{4,3,2,1,0:T(8,128)S(1)}, f32[2,1,4,64,128]{4,3,2,1,0:T(8,128)S(1)}, u32[]{:S(2)}, u32[]{:S(2)}) collective-permute-start(f32[2,1,4,64,128]{4,3,2,1,0:T(8,128)S(1)} %get-tuple-element.30), channel_id=1, source_target_pairs={{0,1},{1,2},{2,3},{3,4},{4,5},{5,6},{6,7},{8,9},{9,10},{10,11},{11... | collective-permute-start | bytes 786440 | tf_op jit(solution)/shard_map/ppermute | solution.py:31
  107.5 10.7 %collective-permute-start.8 = (f32[2,1,4,64,128]{4,3,2,1,0:T(8,128)S(1)}, f32[2,1,4,64,128]{4,3,2,1,0:T(8,128)S(1)}, u32[]{:S(2)}, u32[]{:S(2)}) collective-permute-start(f32[2,1,4,64,128]{4,3,2,1,0:T(8,128)S(1)} %get-tuple-element.31), channel_id=1, source_target_pairs={{1,0},{2,1},{3,2},{4,3},{5,4},{6,5},{7,6},{9,8},{10,9},{11,10},{12... | collective-permute-start | bytes 786440 | tf_op jit(solution)/shard_map/ppermute | solution.py:34
  123.6 11.0 %collective-permute-start.10 = (f32[2,1,4,64,128]{4,3,2,1,0:T(8,128)S(1)}, f32[2,1,4,64,128]{4,3,2,1,0:T(8,128)S(1)}, u32[]{:S(2)}, u32[]{:S(2)}) collective-permute-start(f32[2,1,4,64,128]{4,3,2,1,0:T(8,128)S(1)} %get-tuple-element.29), channel_id=1, source_target_pairs={{1,0},{2,1},{3,2},{4,3},{5,4},{6,5},{7,6},{9,8},{10,9},{11,10},{12... | collective-permute-start | bytes 786440 | tf_op jit(solution)/shard_map/ppermute | solution.py:34
  128.1 10.6 %collective-permute-start.9 = (f32[2,1,4,64,128]{4,3,2,1,0:T(8,128)S(1)}, f32[2,1,4,64,128]{4,3,2,1,0:T(8,128)S(1)}, u32[]{:S(2)}, u32[]{:S(2)}) collective-permute-start(f32[2,1,4,64,128]{4,3,2,1,0:T(8,128)S(1)} %get-tuple-element.28), channel_id=1, source_target_pairs={{0,1},{1,2},{2,3},{3,4},{4,5},{5,6},{6,7},{8,9},{9,10},{10,11},{11... | collective-permute-start | bytes 786440 | tf_op jit(solution)/shard_map/ppermute | solution.py:31
  149.6 24.1 %all-to-all-start.4 = ((bf16[16,2,2,1,16,256]{5,4,1,2,3,0:T(8,128)(2,1)}), bf16[16,2,2,1,16,256]{5,4,1,2,3,0:T(8,128)(2,1)S(1)}, u32[]{:S(2)}, u32[]{:S(2)}) async-start(bf16[16,2,2,1,16,256]{5,4,1,2,3,0:T(8,128)(2,1)} %copy.46), calls=%async_computation.4 | async-start | bytes 1048576 | tf_op jit(solution)/shard_map/all_to_all | solution.py:55
  195.6 1.0 copy-start.1
where the time goes:
time: 199 us; the launch traced here: 197 us
  waiting for transfers between devices  79.3 us (40%)
  starting transfers between devices  56.8 us (29%)
  blocking collectives  28.6 us (14%)
  other arithmetic  19.9 us (10%)
  local copies, waits for them, and re-layouts  10 us (5%)
    all_to_all x2, waiting for transfers between devices, moved_by_axis(): result = lax.all_to_all(result, axes[k], k, k, tiled=True)  29.2 us
    all_to_all x4, blocking collectives, moved_by_axis(): result = lax.all_to_all(result, axes[k], k, k, tiled=True)  28.6 us
    all_to_all x1, waiting for transfers between devices, on_device(): lax.all_to_all(spectrum, TM, split_axis=1, concat_axis=3, tiled=True)  19.6 us
    ppermute x5, starting transfers between devices, with_halo(): lax.ppermute(lax.slice_in_dim(block, 0, width, axis=dim), axis, backward)  19.5 us
    all_to_all x2, starting transfers between devices, moved_by_axis(): result = lax.all_to_all(result, axes[k], k, k, tiled=True)  16.6 us
    ppermute x5, waiting for transfers between devices, with_halo(): lax.ppermute(lax.slice_in_dim(block, 0, width, axis=dim), axis, backward)  16.5 us
    ppermute x5, starting transfers between devices, with_halo(): lax.ppermute(lax.slice_in_dim(block, block.shape[dim] - width, None, axis...  14.1 us
    ppermute x5, waiting for transfers between devices, with_halo(): lax.ppermute(lax.slice_in_dim(block, block.shape[dim] - width, None, axis...  14 us
  transfers between devices with their start and end apart: 14, of which 11 were waited for; matrix products, arithmetic and copies ran while one was open for 1% of the time, Pallas kernels for 0%

commit v1 on v0

v1 whole, which is shorter than its diff:
```python
import functools
import math

import jax
import jax.numpy as jnp
from jax import lax
from jax.experimental import pallas as pl
from jax.experimental.pallas import tpu as pltpu
from jax.sharding import Mesh
from jax.sharding import PartitionSpec as P

SWEEPS = 6
HALF = SWEEPS // 2
TM = ("tm_0", "tm_1", "tm_2")
CHIPS = ("tm_0", "tm_1")
CORE_SPACE = ("tm_2", "space")

alpha_ratio = 0.25
near_weight = 0.5
far_weight = 1.0
centre_weight = 6.0 * (near_weight + far_weight)
VMEM = pl.BlockSpec(memory_space=pltpu.VMEM)
SMEM = pl.BlockSpec(memory_space=pltpu.SMEM)
PAD = 8


def sweep_weights():
    return [
        1.0 / (1.0 + 0.4 * math.cos(math.pi * (2 * k + 1) / (2 * SWEEPS))) for k in range(SWEEPS)
    ]


def rotated(re, im, c, s):
    if abs(s) < 1e-12:
        return re * c, im * c
    if abs(c) < 1e-12:
        return -im * s, re * s
    return re * c - im * s, re * s + im * c


def real_dft(x):
    n = len(x)
    if n == 2:
        return [(x[0] + x[1], None), (x[0] - x[1], None)]
    even, odd = real_dft(x[0::2]), real_dft(x[1::2])
    half = n // 2
    out = [None] * (half + 1)
    out[0] = (even[0][0] + odd[0][0], None)
    out[half] = (even[0][0] - odd[0][0], None)
    for k in range(1, n // 4):
        angle = -2.0 * math.pi * k / n
        re, im = rotated(odd[k][0], odd[k][1], math.cos(angle), math.sin(angle))
        out[k] = (even[k][0] + re, even[k][1] + im)
        out[half - k] = (even[k][0] - re, im - even[k][1])
    quarter = n // 4
    out[quarter] = (even[quarter][0], -odd[quarter][0])
    return out


def real_inverse(X):
    half = len(X) - 1
    n = 2 * half
    if n == 2:
        return [X[0][0] + X[1][0], X[0][0] - X[1][0]]
    quarter = n // 4
    even, odd = [None] * (quarter + 1), [None] * (quarter + 1)
    even[0] = (X[0][0] + X[half][0], None)
    odd[0] = (X[0][0] - X[half][0], None)
    for k in range(1, quarter):
        a, b = X[k], X[half - k]
        even[k] = (a[0] + b[0], a[1] - b[1])
        angle = 2.0 * math.pi * k / n
        odd[k] = rotated(a[0] - b[0], a[1] + b[1], math.cos(angle), math.sin(angle))
    even[quarter] = (2.0 * X[quarter][0], None)
    odd[quarter] = (-2.0 * X[quarter][1], None)
    out = [None] * n
    out[0::2] = real_inverse(even)
    out[1::2] = real_inverse(odd)
    return out


def lane_masks(shape):
    lane = lax.broadcasted_iota(jnp.int32, shape, len(shape) - 1)
    last = shape[-1] - 1
    return (
        (1, jnp.where(lane >= 1, near_weight, 0.0)),
        (last, jnp.where(lane <= last - 1, near_weight, 0.0)),
        (2, jnp.where(lane >= 2, far_weight, 0.0)),
        (last - 1, jnp.where(lane <= last - 2, far_weight, 0.0)),
    )


def neighbour_sum(ref, lead, plane, rows, masks):
    def at(dp, dr):
        return ref[(*lead, plane + dp, pl.ds(PAD + dr, rows), slice(None))]

    centre = at(0, 0)
    near = (at(1, 0) + at(-1, 0)) + (at(0, 1) + at(0, -1))
    far = (at(2, 0) + at(-2, 0)) + (at(0, 2) + at(0, -2))
    total = near_weight * near + far_weight * far
    for amount, mask in masks:
        total = total + pltpu.roll(centre, amount, 1) * mask
    return centre, total


def residual_kernel(
    flag, u, lo, hi, before, initial, forcing, kappa, reaction, out, ext
):
    planes, rows, lanes = u.shape
    share = out.shape[2]
    per_plane = rows // share
    half = planes // 2
    zero = jnp.zeros((planes + 4, PAD, lanes), jnp.float32)
    ext[:, :PAD] = zero
    ext[:, PAD + rows :] = zero
    ext[:2, PAD : PAD + rows] = lo[...].astype(jnp.float32)
    ext[planes + 2 :, PAD : PAD + rows] = hi[...].astype(jnp.float32)

    def fill(p, _):
        ext[p + 2, PAD : PAD + rows] = u[p].astype(jnp.float32)
        return 0

    lax.fori_loop(0, planes, fill, 0)
    masks = lane_masks((rows, lanes))
    first = flag[0] == 0

    def one(p, _):
        centre, total = neighbour_sum(ext, (), p + 2, rows, masks)
        prior = jnp.where(first, initial[p], before[p]).astype(jnp.float32)
        value = (
            forcing[p].astype(jnp.float32)
            - centre
            + prior
            - kappa[p].astype(jnp.float32) * (centre_weight * centre - total)
            - reaction[p].astype(jnp.float32) * centre * centre * centre
        ).astype(jnp.bfloat16)
        part, inner = p // half, p % half
        for piece in range(per_plane):
            out[per_plane * inner + piece, part] = value[piece * share : (piece + 1) * share]
        return 0

    lax.fori_loop(0, planes, one, 0)


def forward_kernel(r, out):
    steps, rows, lanes = r.shape
    for start in range(0, rows, 16):
        part = pl.ds(start, 16)
        scaled = [
            r[n, part].astype(jnp.float32) * (alpha_ratio ** (n / steps)) for n in range(steps)
        ]
        spectrum = real_dft(scaled)
        out[0, 0, part] = spectrum[0][0].astype(jnp.bfloat16)
        out[0, 1, part] = spectrum[steps // 2][0].astype(jnp.bfloat16)
        for j in range(1, steps // 2):
            out[j, 0, part] = spectrum[j][0].astype(jnp.bfloat16)
            out[j, 1, part] = spectrum[j][1].astype(jnp.bfloat16)


def inverse_kernel(s, out):
    steps, rows, lanes = out.shape
    for start in range(0, rows, 16):
        part = pl.ds(start, 16)
        spectrum = [(s[0, 0, part].astype(jnp.float32), None)]
        for j in range(1, steps // 2):
            spectrum.append((s[j, 0, part].astype(jnp.float32), s[j, 1, part].astype(jnp.float32)))
        spectrum.append((s[0, 1, part].astype(jnp.float32), None))
        values = real_inverse(spectrum)
        for n in range(steps):
            scale = 1.0 / (alpha_ratio ** (n / steps) * steps)
            out[n, part] = (values[n] * scale).astype(jnp.bfloat16)


def coefficient_kernel(core, shift, kappa, initial, reaction, halo, p0, p1, q, k):
    width = halo.shape[1]
    ext = p0.shape[0]
    inner = ext - width
    side = core[0]

    def put(e, kv, iv, rv):
        kv, iv, rv = (v.astype(jnp.float32) for v in (kv, iv, rv))
        base = kv * centre_weight + 3.0 * rv * iv * iv
        si = shift[2]
        d0, d1 = shift[0] + base, shift[1] + base
        inv0 = 1.0 / (d0 * d0 + si * si)
        inv1 = 1.0 / (d1 * d1 + si * si)
        p0[e] = d0 * inv0
        p1[e] = d1 * inv1
        q[e] = si * inv0
        k[e] = kv

    def own(i, _):
        src = i + side * (kappa.shape[0] - inner)
        put(i + (1 - side) * width, kappa[src], initial[src], reaction[src])
        return 0

    def outer(i, _):
        put(i + side * inner, halo[0, i], halo[1, i], halo[2, i])
        return 0

    lax.fori_loop(0, inner, own, 0)
    lax.fori_loop(0, width, outer, 0)


def sweeps_kernel(second, core, y, ya, yb, p0, p1, q, k, *rest):
    if second:
        x_in, xa, xb, out, x0, kp, x = rest
    else:
        x_out, send_a, send_b, x0, kp, x = rest
    ext, rows, lanes = p0.shape
    share = y.shape[2]
    per_plane = rows // share
    width = ya.shape[0] // per_plane
    own = ext - 2 * width
    side = core[0]
    start_a = side * (ext - width)
    start_b = (1 - side) * (ext - width)
    inside = pl.ds(PAD, rows)

    zero = jnp.zeros((PAD, lanes), jnp.float32)

    def clear(p, _):
        for b in range(2):
            for c in range(2):
                x[b, c, p, :PAD] = zero
                x[b, c, p, PAD + rows :] = zero
        return 0

    lax.fori_loop(0, ext, clear, 0)

    def begin(ref, i, e):
        def comp(c):
            return jnp.concatenate(
                [ref[per_plane * i + h, c].astype(jnp.float32) for h in range(per_plane)], axis=0
            )

        re, im = comp(0), comp(1)
        c0, c1, cq, ck = p0[e], p1[e], q[e], k[e]
        x0_re = re * c0 + im * cq
        x0_im = im * c1 - re * cq
        x0[0, e], x0[1, e] = x0_re, x0_im
        kp[0, e], kp[1, e], kp[2, e] = ck * c0, ck * c1, ck * cq
        if not second:
            x[0, 0, e, inside], x[0, 1, e, inside] = x0_re, x0_im

    def fill(ref, base):
        def body(i, _):
            begin(ref, i, base + i)
            return 0

        return body

    lax.fori_loop(0, own, fill(y, width), 0)
    lax.fori_loop(0, width, fill(ya, start_a), 0)
    lax.fori_loop(0, width, fill(yb, start_b), 0)
    if second:

        def take_own(i, _):
            for c in range(2):
                x[0, c, width + i, inside] = x_in[c, i]
            return 0

        def take(i, _):
            for c in range(2):
                x[0, c, start_a + i, inside] = xa[c, i]
                x[0, c, start_b + i, inside] = xb[c, i]
            return 0

        lax.fori_loop(0, own, take_own, 0)
        lax.fori_loop(0, width, take, 0)

    masks = lane_masks((rows, lanes))
    weights = sweep_weights()[HALF:] if second else sweep_weights()[:HALF]
    for step, weight in enumerate(weights):
        src, dst = step % 2, (step + 1) % 2
        margin = 2 * (step + 1)
        last = step == len(weights) - 1

        def sweep(e, _, src=src, dst=dst, weight=weight, last=last):
            re, sum_re = neighbour_sum(x, (src, 0), e, rows, masks)
            im, sum_im = neighbour_sum(x, (src, 1), e, rows, masks)
            k0, k1, kq = kp[0, e], kp[1, e], kp[2, e]
            new_re = (1.0 - weight) * re + weight * (x0[0, e] + k0 * sum_re + kq * sum_im)
            new_im = (1.0 - weight) * im + weight * (x0[1, e] + k1 * sum_im - kq * sum_re)
            if not last:
                x[dst, 0, e, inside], x[dst, 1, e, inside] = new_re, new_im
            elif second:
                i = e - width
                for c, value in ((0, new_re), (1, new_im)):
                    value = value.astype(jnp.bfloat16)
                    for h in range(per_plane):
                        out[per_plane * i + h, c] = value[h * share : (h + 1) * share]
            else:
                x_out[0, e - width], x_out[1, e - width] = new_re, new_im
            return 0

        lax.fori_loop(margin, ext - margin, sweep, 0)
    if not second:
        gap = own - width

        def send(i, _):
            for c in range(2):
                send_a[c, i] = x_out[c, i + side * gap]
                send_b[c, i] = x_out[c, i + (1 - side) * gap]
            return 0

        lax.fori_loop(0, width, send, 0)


def final_kernel(state, correction, out):
    planes, rows, lanes = state.shape
    share = correction.shape[2]
    per_plane = rows // share
    half = planes // 2

    def one(p, _):
        part, inner = p // half, p % half
        value = jnp.concatenate(
            [
                correction[per_plane * inner + h, part].astype(jnp.float32)
                for h in range(per_plane)
            ],
            axis=0,
        )
        out[p] = (state[p].astype(jnp.float32) + value).astype(jnp.bfloat16)
        return 0

    lax.fori_loop(0, planes, one, 0)


def call(kernel, shapes, inputs, scratch=(), scalars=0, name=None):
    outs = [jax.ShapeDtypeStruct(s, d) for s, d in shapes]
    return pl.pallas_call(
        kernel,
        out_shape=outs,
        in_specs=[SMEM] * scalars + [VMEM] * (len(inputs) - scalars),
        out_specs=[VMEM] * len(outs),
        scratch_shapes=list(scratch),
        name=name,
        compiler_params=pltpu.CompilerParams(vmem_limit_bytes=24 << 20),
    )(*inputs)


def on_device(state, initial, forcing, kappa, reaction):
    _, planes, rows, lanes = state.shape
    members = lax.axis_size(TM)
    slots = lax.axis_size(CHIPS)
    slabs = lax.axis_size("space")
    own = planes // 2
    share = own * rows // slots
    per_plane = rows // share
    width = 2 * HALF
    ext = own + 2 * width
    bf16, f32 = jnp.bfloat16, jnp.float32
    position = lax.axis_index(TM)
    core = lax.axis_index("tm_2")
    slot = lax.axis_index(CHIPS)
    u = state[0]
    core_arg = core.astype(jnp.int32).reshape(1)

    forward = [(i, i + 1) for i in range(slabs - 1)]
    backward = [(t, s) for s, t in forward]
    outer = []
    for s in range(slabs - 1):
        outer += [(slabs + s, s + 1), (s + 1, slabs + s)]
    lo = lax.ppermute(u[planes - 2 :], "space", forward)
    hi = lax.ppermute(u[:2], "space", backward)
    before = lax.ppermute(u, TM, [(i, i + 1) for i in range(members - 1)])
    coefs = jnp.stack([kappa, initial, reaction])
    rim = jnp.where(core == 0, coefs[:, :width], coefs[:, planes - width :])
    rim = lax.ppermute(rim, CORE_SPACE, outer)

    (residual,) = call(
        residual_kernel,
        [((slots, 2, share, lanes), bf16)],
        [
            position.astype(jnp.int32).reshape(1),
            u,
            lo,
            hi,
            before,
            initial,
            forcing[0],
            kappa,
            reaction,
        ],
        [pltpu.VMEM((planes + 4, rows + 2 * PAD, lanes), f32)],
        scalars=1,
        name="residual",
    )
    cells = lax.all_to_all(residual.reshape(members, share, lanes), TM, 0, 0, tiled=True)
    (spectrum,) = call(forward_kernel, [((slots, 2, share, lanes), bf16)], [cells], name="forward")
    y = lax.all_to_all(spectrum, CHIPS, 0, 0, tiled=True)

    factor = math.exp(math.log(alpha_ratio) / members)
    table = []
    for j in range(slots):
        phase = 2.0 * math.pi * j / members
        sr = 1.0 - factor * math.cos(phase)
        table.append([sr, 1.0 + factor if j == 0 else sr, factor * math.sin(phase)])
    shift = lax.dynamic_slice_in_dim(jnp.asarray(table, f32), slot, 1, axis=0)[0]
    fields = call(
        coefficient_kernel,
        [((ext, rows, lanes), f32)] * 4,
        [core_arg, shift, kappa, initial, reaction, rim],
        scalars=2,
        name="coefficients",
    )

    swap = [(i, slabs + i) for i in range(slabs)] + [(slabs + i, i) for i in range(slabs)]
    pieces = per_plane * width
    gap = per_plane * (own - width)
    ya = lax.ppermute(
        jnp.where(core == 0, y[:pieces], y[gap:]), CORE_SPACE, outer
    )
    yb = lax.ppermute(
        jnp.where(core == 0, y[gap:], y[:pieces]), CORE_SPACE, swap
    )
    scratch = [
        pltpu.VMEM((2, ext, rows, lanes), f32),
        pltpu.VMEM((3, ext, rows, lanes), f32),
        pltpu.VMEM((2, 2, ext, rows + 2 * PAD, lanes), f32),
    ]
    x, send_a, send_b = call(
        functools.partial(sweeps_kernel, False),
        [
            ((2, own, rows, lanes), f32),
            ((2, width, rows, lanes), f32),
            ((2, width, rows, lanes), f32),
        ],
        [core_arg, y, ya, yb, *fields],
        scratch,
        scalars=1,
        name="sweeps_a",
    )
    xa = lax.ppermute(send_a, CORE_SPACE, outer)
    xb = lax.ppermute(send_b, CORE_SPACE, swap)
    (solved,) = call(
        functools.partial(sweeps_kernel, True),
        [((slots, 2, share, lanes), bf16)],
        [core_arg, y, ya, yb, *fields, x, xa, xb],
        scratch,
        scalars=1,
        name="sweeps_b",
    )
    modes = lax.all_to_all(solved, CHIPS, 0, 0, tiled=True)
    (correction,) = call(inverse_kernel, [((members, share, lanes), bf16)], [modes], name="inverse")
    returned = lax.all_to_all(correction, TM, 0, 0, tiled=True)
    (updated,) = call(
        final_kernel,
        [((planes, rows, lanes), bf16)],
        [u, returned.reshape(slots, 2, share, lanes)],
        name="final",
    )
    return updated[None]


def solution(mesh):
    torus = Mesh(
        mesh.devices.reshape(2, 8, 2, mesh.shape["space"]), ("tm_0", "tm_1", "tm_2", "space")
    )
    in_specs = (
        P(TM, "space", None, None),
        P("space", None, None),
        P(TM, "space", None, None),
        P("space", None, None),
        P("space", None, None),
    )
    out_specs = P(TM, "space", None, None)
    return jax.shard_map(
        on_device, mesh=torus, in_specs=in_specs, out_specs=out_specs, check_vma=False
    )
```

time: 199 us -> 132 us (0.66)
  waiting for transfers between devices: 79.3 us -> 29.8 us
  starting transfers between devices: 56.8 us -> 17.3 us
  blocking collectives: 28.6 us -> 60.6 us
  other arithmetic: 19.9 us -> 0.09 us
  Pallas kernels: 0 us -> 16.8 us
  local copies, waits for them, and re-layouts: 10 us -> 6.25 us
    all_to_all x3 -> x1, waiting for transfers between devices: 48.8 us -> 8.91 us  [on_device(): y = lax.all_to_all(spectrum, CHIPS, 0, 0, tiled=True)]
    all_to_all x4 -> x3, blocking collectives: 28.6 us -> 60.6 us  [the longest x1 25.8 us: on_device(): lax.all_to_all(residual.reshape(members, share, lanes), TM, 0, 0, tiled=T...]
    ppermute x11 -> x8, starting transfers between devices: 35.5 us -> 13.7 us  [the longest x1 3.27 us: on_device(): hi = lax.ppermute(u[:2], 'space', backward)]
    all_to_all x3 -> x1, starting transfers between devices: 21.3 us -> 3.66 us  [on_device(): y = lax.all_to_all(spectrum, CHIPS, 0, 0, tiled=True)]
    pallas_call x0 -> x7, Pallas kernels: none -> 16.8 us  [call(): pl.pallas_call(kernel, out_shape=outs, in_specs=[SMEM] * scalars + [VMEM]...]
    ppermute x11 -> x8, waiting for transfers between devices: 30.5 us -> 20.9 us  [the longest x1 10.8 us: on_device(): xa = lax.ppermute(send_a, CORE_SPACE, outer)]
    sub x6 -> x0, other arithmetic: 9.09 us -> none  [update(): base_part * centre]
    another operation x15 -> x0, other arithmetic: 5.79 us -> none  [the longest x14 5.74 us: divided(): jnp.stack([(error_real * diag_real + error_imag * shift_imag) / magnitude...]
  transfers between devices with their start and end apart: 14 -> 9, of which waited for: 11 -> 4; matrix products, arithmetic and copies ran while one was open for 1% -> 1% of each run, Pallas kernels for 0% -> 1%
where the time goes in v1:
time: 132 us; the launch traced here: 131 us
  blocking collectives  60.6 us (46%)
  waiting for transfers between devices  29.8 us (23%)
  starting transfers between devices  17.3 us (13%)
  Pallas kernels  16.8 us (13%)
  local copies, waits for them, and re-layouts  6.25 us (5%)
    all_to_all x1, blocking collectives, on_device(): lax.all_to_all(residual.reshape(members, share, lanes), TM, 0, 0, tiled=T...  25.8 us
    all_to_all x1, blocking collectives, on_device(): returned = lax.all_to_all(correction, TM, 0, 0, tiled=True)  19.5 us
    pallas_call x7, Pallas kernels, call(): pl.pallas_call(kernel, out_shape=outs, in_specs=[SMEM] * scalars + [VMEM]...  16.8 us
    all_to_all x1, blocking collectives, on_device(): modes = lax.all_to_all(solved, CHIPS, 0, 0, tiled=True)  15.3 us
    ppermute x1, waiting for transfers between devices, on_device(): xa = lax.ppermute(send_a, CORE_SPACE, outer)  10.8 us
    all_to_all x1, waiting for transfers between devices, on_device(): y = lax.all_to_all(spectrum, CHIPS, 0, 0, tiled=True)  8.91 us
    ppermute x1, waiting for transfers between devices, on_device(): lax.ppermute(jnp.where(core == 0, y[:pieces], y[gap:]), CORE_SPACE, outer)  5.86 us
    unnamed x18, local copies, waits for them, and re-layouts  4.77 us
  transfers between devices with their start and end apart: 9, of which 4 were waited for; matrix products, arithmetic and copies ran while one was open for 1% of the time, Pallas kernels for 1%

profile of v1, /device:TPU:16, one launch (start us, length us, event | category | flops | bytes accessed | tf_op | source)
XLA Modules:
  0.0 131.1 jit_solution(2265150775068673707)
XLA Ops:
  0.0 1.7 %collective-permute-start.2 = (bf16[16,64,128]{2,1,0:T(8,128)(2,1)}, bf16[16,64,128]{2,1,0:T(8,128)(2,1)S(1)}, u32[]{:S(2)}, u32[]{:S(2)}) collective-permute-start(bf16[16,64,128]{2,1,0:T(8,128)(2,1)} %bitcast.19), channel_id=1, source_target_pairs={{0,8},{8,16},{16,24},{24,32},{32,40},{40,48},{48,56},{56,64},{64,7... | collective-permute-start | bytes 786440 | tf_op jit(solution)/shard_map/ppermute | solution.py:368
  1.8 0.8 slice_bitcast_fusion
  2.5 3.3 %collective-permute-start.1 = (bf16[2,64,128]{2,1,0:T(8,128)(2,1)S(1)}, bf16[2,64,128]{2,1,0:T(8,128)(2,1)S(1)}, u32[]{:S(2)}, u32[]{:S(2)}) collective-permute-start(bf16[2,64,128]{2,1,0:T(8,128)(2,1)S(1)} %get-tuple-element.21), channel_id=1, source_target_pairs={{1,0},{2,1},{3,2},{4,3},{5,4},{6,5},{7,6},{9,8},{10,9},{11,10},{12... | collective-permute-start | bytes 98312 | tf_op jit(solution)/shard_map/ppermute | solution.py:367
  5.8 2.6 %collective-permute-start = (bf16[2,64,128]{2,1,0:T(8,128)(2,1)S(1)}, bf16[2,64,128]{2,1,0:T(8,128)(2,1)S(1)}, u32[]{:S(2)}, u32[]{:S(2)}) collective-permute-start(bf16[2,64,128]{2,1,0:T(8,128)(2,1)S(1)} %get-tuple-element.22), channel_id=1, source_target_pairs={{0,1},{1,2},{2,3},{3,4},{4,5},{5,6},{6,7},{8,9},{9,10},{10,11},{11... | collective-permute-start | bytes 98312 | tf_op jit(solution)/shard_map/ppermute | solution.py:366
  8.4 0.0 collective-permute-done.1.hi
  8.4 4.2 %collective-permute-done.lo = bf16[2,64,128]{2,1,0:T(8,128)(2,1)S(1)} collective-permute-done((bf16[2,64,128]{2,1,0:T(8,128)(2,1)S(1)}, bf16[2,64,128]{2,1,0:T(8,128)(2,1)S(1)}, u32[]{:S(2)}, u32[]{:S(2)}) %collective-permute-start) | collective-permute-done | bytes 32800 | tf_op jit(solution)/shard_map/ppermute | solution.py:366
  12.6 0.0 collective-permute-done.2.before
  12.6 0.0 copy-start
  12.6 0.9 copy-done
  13.6 0.0 copy-start.2
  13.6 0.9 copy-done.2
  14.5 0.0 copy-start.4
  14.5 0.9 copy-done.4
  15.5 0.0 copy-start.6
  15.5 0.9 copy-done.6
  16.4 0.0 copy-start.8
  16.4 0.9 copy-done.8
  17.4 1.9 %residual.1 = bf16[16,2,32,128]{3,2,1,0:T(8,128)(2,1)S(1)} custom-call(s32[1]{0:T(128)} %bitcast.2.flag, bf16[16,64,128]{2,1,0:T(8,128)(2,1)S(1)} %bitcast.20, bf16[2,64,128]{2,1,0:T(8,128)(2,1)S(1)} %collective-permute-done.lo, bf16[2,64,128]{2,1,0:T(8,128)(2,1)S(1)} %collective-permute-done.1.hi, bf16[16,64,128]{2,1,0:T(8,128)(2,1)S(1)} %collective-permute-done.2.before, ...), custom_call_target="tpu_custom_call" | custom-call | tf_op jit(solution)/shard_map/residual/pallas_call | solution.py:333
  19.3 25.8 %all_to_all.20.r = bf16[32,32,128]{2,1,0:T(8,128)(2,1)S(1)} all-to-all(bf16[32,32,128]{2,1,0:T(8,128)(2,1)S(1)} %bitcast.23), channel_id=1, replica_groups=mesh['tm_0'=2,'tm_1'=8,'tm_2'=2,'space'=8] {'tm_0','tm_1','tm_2'}, dimensions={0} | all-to-all | bytes 524288 | tf_op jit(solution)/shard_map/all_to_all | solution.py:391
  45.1 0.0 copy-start.5
  45.1 0.9 forward.1
  46.0 0.0 copy-start.1
  46.0 0.0 copy-start.3
  46.0 3.7 %all-to-all-start.1 = ((bf16[16,2,32,128]{3,2,1,0:T(8,128)(2,1)}), bf16[16,2,32,128]{3,2,1,0:T(8,128)(2,1)S(1)}, u32[]{:S(2)}, u32[]{:S(2)}) async-start(bf16[16,2,32,128]{3,2,1,0:T(8,128)(2,1)} %forward.1), calls=%async_computation.1 | async-start | bytes 524288 | tf_op jit(solution)/shard_map/all_to_all | solution.py:393
  49.6 0.0 copy-done.5
  49.7 0.0 copy-done.1
  49.7 0.0 copy-done.3
  49.7 0.1 fusion
  49.7 1.9 %collective-permute-start.5 = (bf16[3,6,64,128]{3,2,1,0:T(8,128)(2,1)S(1)}, bf16[3,6,64,128]{3,2,1,0:T(8,128)(2,1)S(1)}, u32[]{:S(2)}, u32[]{:S(2)}) collective-permute-start(bf16[3,6,64,128]{3,2,1,0:T(8,128)(2,1)S(1)} %fusion), channel_id=1, source_target_pairs={{8,1},{1,8},{9,2},{2,9},{10,3},{3,10},{11,4},{4,11},{12,5},{5,12},... | collective-permute-start | bytes 884744 | tf_op jit(solution)/shard_map/ppermute | solution.py:371
  51.7 8.9 %all-to-all-done.1.y = bf16[16,2,32,128]{3,2,1,0:T(8,128)(2,1)S(1)} async-done(((bf16[16,2,32,128]{3,2,1,0:T(8,128)(2,1)}), bf16[16,2,32,128]{3,2,1,0:T(8,128)(2,1)S(1)}, u32[]{:S(2)}, u32[]{:S(2)}) %all-to-all-start.1) | async-done | bytes 262176 | tf_op jit(solution)/shard_map/all_to_all | solution.py:393
  60.6 0.1 collective-permute-start.4
  60.7 1.9 %collective-permute-start.3 = (bf16[12,2,32,128]{3,2,1,0:T(8,128)(2,1)S(1)}, bf16[12,2,32,128]{3,2,1,0:T(8,128)(2,1)S(1)}, u32[]{:S(2)}, u32[]{:S(2)}) collective-permute-start(bf16[12,2,32,128]{3,2,1,0:T(8,128)(2,1)S(1)} %get-tuple-element.20), channel_id=1, source_target_pairs={{8,1},{1,8},{9,2},{2,9},{10,3},{3,10},{11,4},{4,11},{12,5},{5,12},... | collective-permute-start | bytes 589832 | tf_op jit(solution)/shard_map/ppermute | solution.py:413
  62.7 0.7 dynamic-slice_bitcast_fusion.shift
  63.4 0.0 collective-permute-done.5.halo
  63.4 1.1 coefficients.1
  64.5 0.0 collective-permute-done.4.yb
  64.5 5.9 %collective-permute-done.3.ya = bf16[12,2,32,128]{3,2,1,0:T(8,128)(2,1)S(1)} collective-permute-done((bf16[12,2,32,128]{3,2,1,0:T(8,128)(2,1)S(1)}, bf16[12,2,32,128]{3,2,1,0:T(8,128)(2,1)S(1)}, u32[]{:S(2)}, u32[]{:S(2)}) %collective-permute-start.3) | collective-permute-done | bytes 196640 | tf_op jit(solution)/shard_map/ppermute | solution.py:413
  70.4 5.9 %sweeps_a.1 = (f32[2,8,64,128]{3,2,1,0:T(8,128)S(1)}, f32[2,6,64,128]{3,2,1,0:T(8,128)S(1)}, f32[2,6,64,128]{3,2,1,0:T(8,128)S(1)}) custom-call(s32[1]{0:T(128)} %bitcast.1.core, bf16[16,2,32,128]{3,2,1,0:T(8,128)(2,1)S(1)} %all-to-all-done.1.y, bf16[12,2,32,128]{3,2,1,0:T(8,128)(2,1)S(1)} %collective-permute-done.3.ya, ...), custom_call_target="tpu_custom_call" | custom-call | tf_op jit(solution)/shard_map/sweeps_a/pallas_call | solution.py:333
  76.2 2.1 %collective-permute-start.6 = (f32[2,6,64,128]{3,2,1,0:T(8,128)S(1)}, f32[2,6,64,128]{3,2,1,0:T(8,128)S(1)}, u32[]{:S(2)}, u32[]{:S(2)}) collective-permute-start(f32[2,6,64,128]{3,2,1,0:T(8,128)S(1)} %get-tuple-element.17), channel_id=1, source_target_pairs={{8,1},{1,8},{9,2},{2,9},{10,3},{3,10},{11,4},{4,11},{12,5},{5,12},... | collective-permute-start | bytes 1179656 | tf_op jit(solution)/shard_map/ppermute | solution.py:436
  78.3 0.1 collective-permute-start.7
  78.4 10.8 %collective-permute-done.6.rest_1_ = f32[2,6,64,128]{3,2,1,0:T(8,128)S(1)} collective-permute-done((f32[2,6,64,128]{3,2,1,0:T(8,128)S(1)}, f32[2,6,64,128]{3,2,1,0:T(8,128)S(1)}, u32[]{:S(2)}, u32[]{:S(2)}) %collective-permute-start.6) | collective-permute-done | bytes 393248 | tf_op jit(solution)/shard_map/ppermute | solution.py:436
  89.2 0.0 collective-permute-done.7.rest_2_
  89.2 5.9 %sweeps_b.1 = bf16[16,2,32,128]{3,2,1,0:T(8,128)(2,1)S(1)} custom-call(s32[1]{0:T(128)} %bitcast.1.core, bf16[16,2,32,128]{3,2,1,0:T(8,128)(2,1)S(1)} %all-to-all-done.1.y, bf16[12,2,32,128]{3,2,1,0:T(8,128)(2,1)S(1)} %collective-permute-done.3.ya, bf16[12,2,32,128]{3,2,1,0:T(8,128)(2,1)S(1)} %collective-permute-done.4.yb, ...), custom_call_target="tpu_custom_call" | custom-call | tf_op jit(solution)/shard_map/sweeps_b/pallas_call | solution.py:333
  95.1 15.3 %all_to_all.21.s = bf16[16,2,32,128]{3,2,1,0:T(8,128)(2,1)S(1)} all-to-all(bf16[16,2,32,128]{3,2,1,0:T(8,128)(2,1)S(1)} %sweeps_b.1), channel_id=1, replica_groups=mesh['tm_0'=2,'tm_1'=8,'tm_2'=2,'space'=8] {'tm_0','tm_1'}, dimensions={0} | all-to-all | bytes 524288 | tf_op jit(solution)/shard_map/all_to_all | solution.py:446
  110.4 0.2 inverse.1
  110.6 0.0 copy-start.7
  110.6 19.5 %all_to_all.22 = bf16[32,32,128]{2,1,0:T(8,128)(2,1)S(1)} all-to-all(bf16[32,32,128]{2,1,0:T(8,128)(2,1)S(1)} %inverse.1), channel_id=1, replica_groups=mesh['tm_0'=2,'tm_1'=8,'tm_2'=2,'space'=8] {'tm_0','tm_1','tm_2'}, dimensions={0} | all-to-all | bytes 524288 | tf_op jit(solution)/shard_map/all_to_all | solution.py:448
  130.1 0.0 copy-done.7
  130.1 0.9 final.1
  (1 shorter events, 0.0 us)
Async XLA Ops:
  0.0 12.6 %collective-permute-start.2 = (bf16[16,64,128]{2,1,0:T(8,128)(2,1)}, bf16[16,64,128]{2,1,0:T(8,128)(2,1)S(1)}, u32[]{:S(2)}, u32[]{:S(2)}) collective-permute-start(bf16[16,64,128]{2,1,0:T(8,128)(2,1)} %bitcast.19), channel_id=1, source_target_pairs={{0,8},{8,16},{16,24},{24,32},{32,40},{40,48},{48,56},{56,64},{64,7... | collective-permute-start | bytes 786440 | tf_op jit(solution)/shard_map/ppermute | solution.py:368
  2.5 5.9 %collective-permute-start.1 = (bf16[2,64,128]{2,1,0:T(8,128)(2,1)S(1)}, bf16[2,64,128]{2,1,0:T(8,128)(2,1)S(1)}, u32[]{:S(2)}, u32[]{:S(2)}) collective-permute-start(bf16[2,64,128]{2,1,0:T(8,128)(2,1)S(1)} %get-tuple-element.21), channel_id=1, source_target_pairs={{1,0},{2,1},{3,2},{4,3},{5,4},{6,5},{7,6},{9,8},{10,9},{11,10},{12... | collective-permute-start | bytes 98312 | tf_op jit(solution)/shard_map/ppermute | solution.py:367
  5.8 6.8 %collective-permute-start = (bf16[2,64,128]{2,1,0:T(8,128)(2,1)S(1)}, bf16[2,64,128]{2,1,0:T(8,128)(2,1)S(1)}, u32[]{:S(2)}, u32[]{:S(2)}) collective-permute-start(bf16[2,64,128]{2,1,0:T(8,128)(2,1)S(1)} %get-tuple-element.22), channel_id=1, source_target_pairs={{0,1},{1,2},{2,3},{3,4},{4,5},{5,6},{6,7},{8,9},{9,10},{10,11},{11... | collective-permute-start | bytes 98312 | tf_op jit(solution)/shard_map/ppermute | solution.py:366
  12.6 1.0 copy-start
  13.6 0.9 copy-start.2
  14.5 0.9 copy-start.4
  15.5 0.9 copy-start.6
  16.4 0.9 copy-start.8
  45.1 4.6 %copy-start.5 = (bf16[16,64,128]{2,1,0:T(8,128)(2,1)S(1)}, bf16[16,64,128]{2,1,0:T(8,128)(2,1)}, u32[]{:S(2)}) copy-start(bf16[16,64,128]{2,1,0:T(8,128)(2,1)} %reaction.3) | copy-start | bytes 786436
  46.0 3.7 %copy-start.1 = (bf16[16,64,128]{2,1,0:T(8,128)(2,1)S(1)}, bf16[16,64,128]{2,1,0:T(8,128)(2,1)}, u32[]{:S(2)}) copy-start(bf16[16,64,128]{2,1,0:T(8,128)(2,1)} %initial.3) | copy-start | bytes 786436
  46.0 3.7 %copy-start.3 = (bf16[16,64,128]{2,1,0:T(8,128)(2,1)S(1)}, bf16[16,64,128]{2,1,0:T(8,128)(2,1)}, u32[]{:S(2)}) copy-start(bf16[16,64,128]{2,1,0:T(8,128)(2,1)} %kappa.3) | copy-start | bytes 786436
  46.0 14.6 %all-to-all-start.1 = ((bf16[16,2,32,128]{3,2,1,0:T(8,128)(2,1)}), bf16[16,2,32,128]{3,2,1,0:T(8,128)(2,1)S(1)}, u32[]{:S(2)}, u32[]{:S(2)}) async-start(bf16[16,2,32,128]{3,2,1,0:T(8,128)(2,1)} %forward.1), calls=%async_computation.1 | async-start | bytes 524288 | tf_op jit(solution)/shard_map/all_to_all | solution.py:393
  49.7 13.6 %collective-permute-start.5 = (bf16[3,6,64,128]{3,2,1,0:T(8,128)(2,1)S(1)}, bf16[3,6,64,128]{3,2,1,0:T(8,128)(2,1)S(1)}, u32[]{:S(2)}, u32[]{:S(2)}) collective-permute-start(bf16[3,6,64,128]{3,2,1,0:T(8,128)(2,1)S(1)} %fusion), channel_id=1, source_target_pairs={{8,1},{1,8},{9,2},{2,9},{10,3},{3,10},{11,4},{4,11},{12,5},{5,12},... | collective-permute-start | bytes 884744 | tf_op jit(solution)/shard_map/ppermute | solution.py:371
  60.6 3.9 %collective-permute-start.4 = (bf16[12,2,32,128]{3,2,1,0:T(8,128)(2,1)S(1)}, bf16[12,2,32,128]{3,2,1,0:T(8,128)(2,1)S(1)}, u32[]{:S(2)}, u32[]{:S(2)}) collective-permute-start(bf16[12,2,32,128]{3,2,1,0:T(8,128)(2,1)S(1)} %get-tuple-element.19), channel_id=1, source_target_pairs={{0,8},{1,9},{2,10},{3,11},{4,12},{5,13},{6,14},{7,15},{8,0},{9,1},... | collective-permute-start | bytes 589832 | tf_op jit(solution)/shard_map/ppermute | solution.py:416
  60.7 9.6 %collective-permute-start.3 = (bf16[12,2,32,128]{3,2,1,0:T(8,128)(2,1)S(1)}, bf16[12,2,32,128]{3,2,1,0:T(8,128)(2,1)S(1)}, u32[]{:S(2)}, u32[]{:S(2)}) collective-permute-start(bf16[12,2,32,128]{3,2,1,0:T(8,128)(2,1)S(1)} %get-tuple-element.20), channel_id=1, source_target_pairs={{8,1},{1,8},{9,2},{2,9},{10,3},{3,10},{11,4},{4,11},{12,5},{5,12},... | collective-permute-start | bytes 589832 | tf_op jit(solution)/shard_map/ppermute | solution.py:413
  76.2 13.0 %collective-permute-start.6 = (f32[2,6,64,128]{3,2,1,0:T(8,128)S(1)}, f32[2,6,64,128]{3,2,1,0:T(8,128)S(1)}, u32[]{:S(2)}, u32[]{:S(2)}) collective-permute-start(f32[2,6,64,128]{3,2,1,0:T(8,128)S(1)} %get-tuple-element.17), channel_id=1, source_target_pairs={{8,1},{1,8},{9,2},{2,9},{10,3},{3,10},{11,4},{4,11},{12,5},{5,12},... | collective-permute-start | bytes 1179656 | tf_op jit(solution)/shard_map/ppermute | solution.py:436
  78.3 10.9 %collective-permute-start.7 = (f32[2,6,64,128]{3,2,1,0:T(8,128)S(1)}, f32[2,6,64,128]{3,2,1,0:T(8,128)S(1)}, u32[]{:S(2)}, u32[]{:S(2)}) collective-permute-start(f32[2,6,64,128]{3,2,1,0:T(8,128)S(1)} %get-tuple-element.18), channel_id=1, source_target_pairs={{0,8},{1,9},{2,10},{3,11},{4,12},{5,13},{6,14},{7,15},{8,0},{9,1},... | collective-permute-start | bytes 1179656 | tf_op jit(solution)/shard_map/ppermute | solution.py:437
  110.6 19.5 %copy-start.7 = (bf16[1,16,64,128]{3,2,1,0:T(8,128)(2,1)S(1)}, bf16[1,16,64,128]{3,2,1,0:T(8,128)(2,1)}, u32[]{:S(2)}) copy-start(bf16[1,16,64,128]{3,2,1,0:T(8,128)(2,1)} %param.6) | copy-start | bytes 786436

commit v2 on v1

v2 whole, which is shorter than its diff:
```python
import math

import jax
import jax.numpy as jnp
from jax import lax
from jax.experimental import pallas as pl
from jax.experimental.pallas import tpu as pltpu
from jax.sharding import Mesh
from jax.sharding import PartitionSpec as P

SWEEPS = 6
STEPS = 32
UNROLL = 2
TM = ("tm_0", "tm_1", "tm_2")
CHIPS = ("tm_0", "tm_1")
CORE_SPACE = ("tm_2", "space")

alpha_ratio = 0.25
near_weight = 0.5
far_weight = 1.0
centre_weight = 6.0 * (near_weight + far_weight)
VMEM = pl.BlockSpec(memory_space=pltpu.VMEM)
HBM = pl.BlockSpec(memory_space=pltpu.HBM)
SMEM = pl.BlockSpec(memory_space=pltpu.SMEM)
PAD = 8


def sweep_weights():
    return [
        1.0 / (1.0 + 0.4 * math.cos(math.pi * (2 * k + 1) / (2 * SWEEPS))) for k in range(SWEEPS)
    ]


def rotated(re, im, c, s):
    if abs(s) < 1e-12:
        return re * c, im * c
    if abs(c) < 1e-12:
        return -im * s, re * s
    return re * c - im * s, re * s + im * c


def real_dft(x):
    n = len(x)
    if n == 2:
        return [(x[0] + x[1], None), (x[0] - x[1], None)]
    even, odd = real_dft(x[0::2]), real_dft(x[1::2])
    half = n // 2
    out = [None] * (half + 1)
    out[0] = (even[0][0] + odd[0][0], None)
    out[half] = (even[0][0] - odd[0][0], None)
    for k in range(1, n // 4):
        angle = -2.0 * math.pi * k / n
        re, im = rotated(odd[k][0], odd[k][1], math.cos(angle), math.sin(angle))
        out[k] = (even[k][0] + re, even[k][1] + im)
        out[half - k] = (even[k][0] - re, im - even[k][1])
    quarter = n // 4
    out[quarter] = (even[quarter][0], -odd[quarter][0])
    return out


def real_inverse(X):
    half = len(X) - 1
    n = 2 * half
    if n == 2:
        return [X[0][0] + X[1][0], X[0][0] - X[1][0]]
    quarter = n // 4
    even, odd = [None] * (quarter + 1), [None] * (quarter + 1)
    even[0] = (X[0][0] + X[half][0], None)
    odd[0] = (X[0][0] - X[half][0], None)
    for k in range(1, quarter):
        a, b = X[k], X[half - k]
        even[k] = (a[0] + b[0], a[1] - b[1])
        angle = 2.0 * math.pi * k / n
        odd[k] = rotated(a[0] - b[0], a[1] + b[1], math.cos(angle), math.sin(angle))
    even[quarter] = (2.0 * X[quarter][0], None)
    odd[quarter] = (-2.0 * X[quarter][1], None)
    out = [None] * n
    out[0::2] = real_inverse(even)
    out[1::2] = real_inverse(odd)
    return out


def lane_masks(shape):
    lane = lax.broadcasted_iota(jnp.int32, shape, len(shape) - 1)
    last = shape[-1] - 1
    return (
        (1, jnp.where(lane >= 1, near_weight, 0.0)),
        (last, jnp.where(lane <= last - 1, near_weight, 0.0)),
        (2, jnp.where(lane >= 2, far_weight, 0.0)),
        (last - 1, jnp.where(lane <= last - 2, far_weight, 0.0)),
    )


def neighbour_sum(ref, lead, plane, rows, masks):
    def at(dp, dr):
        return ref[(*lead, plane + dp, pl.ds(PAD + dr, rows), slice(None))]

    centre = at(0, 0)
    near = (at(1, 0) + at(-1, 0)) + (at(0, 1) + at(0, -1))
    far = (at(2, 0) + at(-2, 0)) + (at(0, 2) + at(0, -2))
    total = near_weight * near + far_weight * far
    for amount, mask in masks:
        total = total + pltpu.roll(centre, amount, 1) * mask
    return centre, total


def local_kernel(flag, u_hbm, initial_hbm, forcing_hbm, kappa_hbm, reaction_hbm, part, rim, *rest):
    ext, u, initial, forcing, kappa, reaction, sems = rest
    planes, rows, lanes = u.shape
    pairs = ((u_hbm, u), (forcing_hbm, forcing), (kappa_hbm, kappa), (reaction_hbm, reaction))
    pairs += ((initial_hbm, initial),)
    copies = [pltpu.make_async_copy(src, dst, sems.at[i]) for i, (src, dst) in enumerate(pairs)]
    for copy in copies:
        copy.start()
    zero = jnp.zeros((PAD, lanes), jnp.float32)

    def clear(p, _):
        ext[p, :PAD] = zero
        ext[p, PAD + rows :] = zero
        return 0

    lax.fori_loop(0, planes + 4, clear, 0)
    blank = jnp.zeros((rows, lanes), jnp.float32)
    for p in (0, 1, planes + 2, planes + 3):
        ext[p, PAD : PAD + rows] = blank
    for copy in copies:
        copy.wait()

    def fill(p, _):
        ext[p + 2, PAD : PAD + rows] = u[p].astype(jnp.float32)
        return 0

    lax.fori_loop(0, planes, fill, 0)
    masks = lane_masks((rows, lanes))
    first = flag[0] == 0

    def one(p, _):
        centre, total = neighbour_sum(ext, (), p + 2, rows, masks)
        prior = jnp.where(first, initial[p].astype(jnp.float32), 0.0)
        part[p] = (
            forcing[p].astype(jnp.float32)
            - centre
            + prior
            - kappa[p].astype(jnp.float32) * (centre_weight * centre - total)
            - reaction[p].astype(jnp.float32) * centre * centre * centre
        )
        return 0

    lax.fori_loop(0, planes, one, 0)
    for i, p in enumerate((0, 1, planes - 2, planes - 1)):
        rim[i] = kappa[p].astype(jnp.float32)


def residual_kernel(part, rim, lo, hi, before, out):
    planes, rows, _ = part.shape
    share = out.shape[2]
    per_plane = rows // share
    half = planes // 2

    def put(p, value):
        value = value.astype(jnp.bfloat16)
        side, inner = p // half, p % half
        for piece in range(per_plane):
            out[per_plane * inner + piece, side] = value[piece * share : (piece + 1) * share]

    def one(p, _):
        put(p, part[p] + before[p].astype(jnp.float32))
        return 0

    lax.fori_loop(2, planes - 2, one, 0)
    l0, l1, h0, h1 = (v.astype(jnp.float32) for v in (lo[0], lo[1], hi[0], hi[1]))
    edges = (
        (0, near_weight * l1 + far_weight * l0),
        (1, far_weight * l1),
        (planes - 2, far_weight * h0),
        (planes - 1, near_weight * h0 + far_weight * h1),
    )
    for i, (p, total) in enumerate(edges):
        put(p, part[p] + rim[i] * total + before[p].astype(jnp.float32))


def forward_kernel(r, out):
    steps, rows, _ = r.shape
    for start in range(0, rows, 16):
        part = pl.ds(start, 16)
        scaled = [
            r[n, part].astype(jnp.float32) * (alpha_ratio ** (n / steps)) for n in range(steps)
        ]
        spectrum = real_dft(scaled)
        out[0, 0, part] = spectrum[0][0].astype(jnp.bfloat16)
        out[0, 1, part] = spectrum[steps // 2][0].astype(jnp.bfloat16)
        for j in range(1, steps // 2):
            out[j, 0, part] = spectrum[j][0].astype(jnp.bfloat16)
            out[j, 1, part] = spectrum[j][1].astype(jnp.bfloat16)


def inverse_kernel(s, out):
    steps, rows, _ = out.shape
    for start in range(0, rows, 16):
        part = pl.ds(start, 16)
        spectrum = [(s[0, 0, part].astype(jnp.float32), None)]
        for j in range(1, steps // 2):
            spectrum.append((s[j, 0, part].astype(jnp.float32), s[j, 1, part].astype(jnp.float32)))
        spectrum.append((s[0, 1, part].astype(jnp.float32), None))
        values = real_inverse(spectrum)
        for n in range(steps):
            scale = 1.0 / (alpha_ratio ** (n / steps) * steps)
            out[n, part] = (values[n] * scale).astype(jnp.bfloat16)


def coefficient_kernel(where, kappa, initial, reaction, outer, inner, p0, p1, q, k):
    planes = kappa.shape[0]
    wide, narrow = outer.shape[1], inner.shape[1]
    core, slot = where[0], where[1]
    members = STEPS
    factor = math.exp(math.log(alpha_ratio) / members)
    s0 = s1 = si = jnp.float32(0.0)
    for j in range(members // 2):
        phase = 2.0 * math.pi * j / members
        real, imag = 1.0 - factor * math.cos(phase), factor * math.sin(phase)
        hit = slot == j
        s0 = jnp.where(hit, jnp.float32(real), s0)
        s1 = jnp.where(hit, jnp.float32(real if j else 1.0 + factor), s1)
        si = jnp.where(hit, jnp.float32(imag if j else 0.0), si)

    def put(e, kv, iv, rv):
        kv, iv, rv = (v.astype(jnp.float32) for v in (kv, iv, rv))
        base = kv * centre_weight + 3.0 * rv * iv * iv
        d0, d1 = s0 + base, s1 + base
        inv0 = 1.0 / (d0 * d0 + si * si)
        inv1 = 1.0 / (d1 * d1 + si * si)
        p0[e] = d0 * inv0
        p1[e] = d1 * inv1
        q[e] = si * inv0
        k[e] = kv

    def own(i, _):
        put(i + jnp.where(core == 0, wide, narrow), kappa[i], initial[i], reaction[i])
        return 0

    def far(i, _):
        put(i + jnp.where(core == 0, 0, planes + narrow), outer[0, i], outer[1, i], outer[2, i])
        return 0

    def close(i, _):
        put(i + jnp.where(core == 0, planes + wide, 0), inner[0, i], inner[1, i], inner[2, i])
        return 0

    lax.fori_loop(0, planes, own, 0)
    lax.fori_loop(0, wide, far, 0)
    lax.fori_loop(0, narrow, close, 0)


def sweeps_kernel(where, y, ya, yb, yc, yd, p0, p1, q, k, out, x0, kp, xs, xt):
    ext, rows, lanes = p0.shape
    share = y.shape[2]
    per_plane = rows // share
    own = y.shape[0] // per_plane
    margin = (ext - own) // 2
    core = where[0]
    inside = pl.ds(PAD, rows)
    zero = jnp.zeros((PAD, lanes), jnp.float32)

    def clear(p, _):
        for x in (xs, xt):
            for c in range(2):
                x[c, p, :PAD] = zero
                x[c, p, PAD + rows :] = zero
        return 0

    lax.fori_loop(0, ext, clear, 0)

    def fill(ref, base):
        def body(i, _):
            e = base + i

            def comp(c):
                return jnp.concatenate(
                    [ref[per_plane * i + h, c].astype(jnp.float32) for h in range(per_plane)],
                    axis=0,
                )

            re, im = comp(0), comp(1)
            c0, c1, cq, ck = p0[e], p1[e], q[e], k[e]
            x0_re = re * c0 + im * cq
            x0_im = im * c1 - re * cq
            x0[0, e], x0[1, e] = x0_re, x0_im
            xs[0, e, inside], xs[1, e, inside] = x0_re, x0_im
            kp[0, e], kp[1, e], kp[2, e] = ck * c0, ck * c1, ck * cq
            return 0

        lax.fori_loop(0, ref.shape[0] // per_plane, body, 0)

    far = yc.shape[0] // per_plane
    fill(y, margin)
    fill(ya, jnp.where(core == 0, far, margin + own))
    fill(yb, jnp.where(core == 0, margin + own, far))
    fill(yc, jnp.where(core == 0, 0, ext - far))
    fill(yd, jnp.where(core == 0, ext - far, 0))

    masks = lane_masks((rows, lanes))
    weights = sweep_weights()
    for step, weight in enumerate(weights):
        src, dst = (xs, xt) if step % 2 == 0 else (xt, xs)
        edge = 2 * (step + 1)
        last = step == len(weights) - 1

        def value(e, src=src, weight=weight):
            re, sum_re = neighbour_sum(src, (0,), e, rows, masks)
            im, sum_im = neighbour_sum(src, (1,), e, rows, masks)
            k0, k1, kq = kp[0, e], kp[1, e], kp[2, e]
            new_re = (1.0 - weight) * re + weight * (x0[0, e] + k0 * sum_re + kq * sum_im)
            new_im = (1.0 - weight) * im + weight * (x0[1, e] + k1 * sum_im - kq * sum_re)
            return new_re, new_im

        def store(e, pair, dst=dst, last=last):
            for c in range(2):
                if not last:
                    dst[c, e, inside] = pair[c]
                    continue
                rounded = pair[c].astype(jnp.bfloat16)
                for h in range(per_plane):
                    out[per_plane * (e - margin) + h, c] = rounded[h * share : (h + 1) * share]

        def sweep(i, _, edge=edge, value=value, store=store):
            planes = [edge + UNROLL * i + r for r in range(UNROLL)]
            pairs = [value(e) for e in planes]
            for e, pair in zip(planes, pairs):
                store(e, pair)
            return 0

        lax.fori_loop(0, (ext - 2 * edge) // UNROLL, sweep, 0)


def final_kernel(state, correction, out):
    planes, rows, _ = state.shape
    share = correction.shape[2]
    per_plane = rows // share
    half = planes // 2

    def one(p, _):
        part, inner = p // half, p % half
        value = jnp.concatenate(
            [
                correction[per_plane * inner + h, part].astype(jnp.float32)
                for h in range(per_plane)
            ],
            axis=0,
        )
        out[p] = (state[p].astype(jnp.float32) + value).astype(jnp.bfloat16)
        return 0

    lax.fori_loop(0, planes, one, 0)


def call(kernel, shapes, inputs, scratch=(), scalars=0, anywhere=0, flops=None):
    outs = [jax.ShapeDtypeStruct(s, d) for s, d in shapes]
    cost = None
    if flops is not None:
        cost = pl.CostEstimate(flops=flops, transcendentals=0, bytes_accessed=flops // 8)
    rest = len(inputs) - scalars - anywhere
    return pl.pallas_call(
        kernel,
        out_shape=outs,
        in_specs=[SMEM] * scalars + [HBM] * anywhere + [VMEM] * rest,
        out_specs=[VMEM] * len(outs),
        scratch_shapes=list(scratch),
        cost_estimate=cost,
        compiler_params=pltpu.CompilerParams(vmem_limit_bytes=24 << 20),
    )(*inputs)


def iteration(state, initial, forcing, kappa, reaction):
    _, planes, rows, lanes = state.shape
    members = lax.axis_size(TM)
    slots = lax.axis_size(CHIPS)
    slabs = lax.axis_size("space")
    own = planes // 2
    share = own * rows // slots
    per_plane = rows // share
    wide = 2 * SWEEPS
    narrow = wide - own
    ext = own + 2 * wide
    bf16, f32, i32 = jnp.bfloat16, jnp.float32, jnp.int32
    position = lax.axis_index(TM).astype(i32).reshape(1)
    core = lax.axis_index("tm_2")
    slot = lax.axis_index(CHIPS)
    where = jnp.stack([core, slot]).astype(i32)
    u = state[0]

    forward = [(i, i + 1) for i in range(slabs - 1)]
    backward = [(t, s) for s, t in forward]
    outer = []
    for s in range(slabs - 1):
        outer += [(slabs + s, s + 1), (s + 1, slabs + s)]
    swap = [(i, slabs + i) for i in range(slabs)] + [(slabs + i, i) for i in range(slabs)]
    same = forward + [(slabs + s, slabs + t) for s, t in backward]
    lo = lax.ppermute(u[planes - 2 :], "space", forward)
    hi = lax.ppermute(u[:2], "space", backward)
    before = lax.ppermute(u, TM, [(i, i + 1) for i in range(members - 1)])
    coefs = jnp.stack([kappa, initial, reaction])
    rim = jnp.where(core == 0, coefs[:, :wide], coefs[:, planes - wide :])
    rim = lax.ppermute(rim, CORE_SPACE, outer)
    inner = jnp.where(core == 0, rim[:, wide - narrow :], rim[:, :narrow])
    inner = lax.ppermute(inner, CORE_SPACE, swap)

    block = ((planes, rows, lanes), bf16)
    part, edge = call(
        local_kernel,
        [((planes, rows, lanes), f32), ((4, rows, lanes), f32)],
        [position, u, initial, forcing[0], kappa, reaction],
        [pltpu.VMEM((planes + 4, rows + 2 * PAD, lanes), f32)]
        + [pltpu.VMEM(*block)] * 5
        + [pltpu.SemaphoreType.DMA((5,))],
        scalars=1,
        anywhere=5,
        flops=20_000_000,
    )
    (residual,) = call(
        residual_kernel, [((slots, 2, share, lanes), bf16)], [part, edge, lo, hi, before]
    )
    cells = lax.all_to_all(residual.reshape(members, share, lanes), TM, 0, 0, tiled=True)
    (spectrum,) = call(forward_kernel, [((slots, 2, share, lanes), bf16)], [cells])
    y = lax.all_to_all(spectrum, CHIPS, 0, 0, tiled=True)

    fields = call(
        coefficient_kernel,
        [((ext, rows, lanes), f32)] * 4,
        [where, kappa, initial, reaction, rim, inner],
        scalars=1,
    )
    n = per_plane * narrow
    first = core == 0
    ya = lax.ppermute(y, CORE_SPACE, outer)
    yc = lax.ppermute(jnp.where(first, y[-n:], y[:n]), CORE_SPACE, same)
    yb = lax.ppermute(y, CORE_SPACE, swap)
    yd = lax.ppermute(jnp.where(first, ya[-n:], ya[:n]), CORE_SPACE, swap)
    (solved,) = call(
        sweeps_kernel,
        [((slots, 2, share, lanes), bf16)],
        [where, y, ya, yb, yc, yd, *fields],
        [
            pltpu.VMEM((2, ext, rows, lanes), f32),
            pltpu.VMEM((3, ext, rows, lanes), f32),
            pltpu.VMEM((2, ext, rows + 2 * PAD, lanes), f32),
            pltpu.VMEM((2, ext, rows + 2 * PAD, lanes), f32),
        ],
        scalars=1,
    )
    modes = lax.all_to_all(solved, CHIPS, 0, 0, tiled=True)
    (correction,) = call(inverse_kernel, [((members, share, lanes), bf16)], [modes])
    returned = lax.all_to_all(correction, TM, 0, 0, tiled=True)
    (updated,) = call(
        final_kernel, [((planes, rows, lanes), bf16)], [u, returned.reshape(slots, 2, share, lanes)]
    )
    return updated[None]


def solution(mesh):
    torus = Mesh(
        mesh.devices.reshape(2, 8, 2, mesh.shape["space"]), ("tm_0", "tm_1", "tm_2", "space")
    )
    in_specs = (
        P(TM, "space", None, None),
        P("space", None, None),
        P(TM, "space", None, None),
        P("space", None, None),
        P("space", None, None),
    )
    out_specs = P(TM, "space", None, None)
    return jax.shard_map(
        iteration, mesh=torus, in_specs=in_specs, out_specs=out_specs, check_vma=False
    )
```

time: 132 us -> 121 us (0.917)
  waiting for transfers between devices: 29.8 us -> 15.4 us
  starting transfers between devices: 17.3 us -> 29.1 us
  blocking collectives: 60.6 us -> 50.8 us
  Pallas kernels: 16.8 us -> 18.7 us
    ppermute x8 -> x9, waiting for transfers between devices: 20.9 us -> 2.73 us  [the longest x1 2.04 us: iteration(): ya = lax.ppermute(y, CORE_SPACE, outer)]
    all_to_all x3, blocking collectives: 60.6 us -> 50.8 us  [the longest x1 19.5 us: iteration(): returned = lax.all_to_all(correction, TM, 0, 0, tiled=True)]
    all_to_all x1, starting transfers between devices: 3.66 us -> 11.8 us  [iteration(): lax.all_to_all(residual.reshape(members, share, lanes), TM, 0, 0, tiled=T...]
    all_to_all x1, waiting for transfers between devices: 8.91 us -> 12.6 us  [iteration(): lax.all_to_all(residual.reshape(members, share, lanes), TM, 0, 0, tiled=T...]
    ppermute x8 -> x9, starting transfers between devices: 13.7 us -> 17.3 us  [the longest x1 4.74 us: iteration(): yc = lax.ppermute(jnp.where(first, y[-n:], y[:n]), CORE_SPACE, same)]
    pallas_call x7, Pallas kernels: 16.8 us -> 18.7 us  [call(): pl.pallas_call(kernel, out_shape=outs, in_specs=[SMEM] * scalars + [HBM]...]
  transfers between devices with their start and end apart: 9 -> 10, of which waited for: 4 -> 3; matrix products, arithmetic and copies ran while one was open for 1% -> 1% of each run, Pallas kernels for 1% -> 3%
where the time goes in v2:
time: 121 us; the launch traced here: 120 us
  blocking collectives  50.8 us (42%)
  starting transfers between devices  29.1 us (24%)
  Pallas kernels  18.7 us (15%)
  waiting for transfers between devices  15.4 us (13%)
  local copies, waits for them, and re-layouts  5.55 us (5%)
    all_to_all x1, blocking collectives, iteration(): returned = lax.all_to_all(correction, TM, 0, 0, tiled=True)  19.5 us
    pallas_call x7, Pallas kernels, call(): pl.pallas_call(kernel, out_shape=outs, in_specs=[SMEM] * scalars + [HBM]...  18.7 us
    all_to_all x1, blocking collectives, iteration(): modes = lax.all_to_all(solved, CHIPS, 0, 0, tiled=True)  17.7 us
    all_to_all x1, blocking collectives, iteration(): y = lax.all_to_all(spectrum, CHIPS, 0, 0, tiled=True)  13.6 us
    all_to_all x1, waiting for transfers between devices, iteration(): lax.all_to_all(residual.reshape(members, share, lanes), TM, 0, 0, tiled=T...  12.6 us
    all_to_all x1, starting transfers between devices, iteration(): lax.all_to_all(residual.reshape(members, share, lanes), TM, 0, 0, tiled=T...  11.8 us
    unnamed x18, local copies, waits for them, and re-layouts  4.76 us
    ppermute x1, starting transfers between devices, iteration(): yc = lax.ppermute(jnp.where(first, y[-n:], y[:n]), CORE_SPACE, same)  4.74 us
  transfers between devices with their start and end apart: 10, of which 3 were waited for; matrix products, arithmetic and copies ran while one was open for 1% of the time, Pallas kernels for 3%

profile of v2, /device:TPU:16, one launch (start us, length us, event | category | flops | bytes accessed | tf_op | source)
XLA Modules:
  0.0 120.1 jit_solution(11708304288059155809)
XLA Ops:
  0.0 1.7 %collective-permute-start.2 = (bf16[16,64,128]{2,1,0:T(8,128)(2,1)}, bf16[16,64,128]{2,1,0:T(8,128)(2,1)S(1)}, u32[]{:S(2)}, u32[]{:S(2)}) collective-permute-start(bf16[16,64,128]{2,1,0:T(8,128)(2,1)} %bitcast.18), channel_id=1, source_target_pairs={{0,8},{8,16},{16,24},{24,32},{32,40},{40,48},{48,56},{56,64},{64,7... | collective-permute-start | bytes 786440 | tf_op jit(solution)/shard_map/ppermute | solution.py:400
  1.8 0.8 slice_bitcast_fusion
  2.5 3.4 %collective-permute-start = (bf16[2,64,128]{2,1,0:T(8,128)(2,1)S(1)}, bf16[2,64,128]{2,1,0:T(8,128)(2,1)S(1)}, u32[]{:S(2)}, u32[]{:S(2)}) collective-permute-start(bf16[2,64,128]{2,1,0:T(8,128)(2,1)S(1)} %get-tuple-element.18), channel_id=1, source_target_pairs={{0,1},{1,2},{2,3},{3,4},{4,5},{5,6},{6,7},{8,9},{9,10},{10,11},{11... | collective-permute-start | bytes 98312 | tf_op jit(solution)/shard_map/ppermute | solution.py:398
  5.9 3.3 %collective-permute-start.1 = (bf16[2,64,128]{2,1,0:T(8,128)(2,1)S(1)}, bf16[2,64,128]{2,1,0:T(8,128)(2,1)S(1)}, u32[]{:S(2)}, u32[]{:S(2)}) collective-permute-start(bf16[2,64,128]{2,1,0:T(8,128)(2,1)S(1)} %get-tuple-element.17), channel_id=1, source_target_pairs={{1,0},{2,1},{3,2},{4,3},{5,4},{6,5},{7,6},{9,8},{10,9},{11,10},{12... | collective-permute-start | bytes 98312 | tf_op jit(solution)/shard_map/ppermute | solution.py:399
  9.3 0.0 copy-start
  9.3 0.9 copy-done
  10.2 0.0 copy-start.2
  10.2 0.9 copy-done.2
  11.2 0.0 copy-start.4
  11.2 0.9 copy-done.4
  12.1 0.0 copy-start.6
  12.2 0.9 copy-done.6
  13.1 0.0 copy-start.8
  13.1 0.9 copy-done.8
  14.0 2.1 %shard_map.55 = (f32[16,64,128]{2,1,0:T(8,128)S(1)}, f32[4,64,128]{2,1,0:T(8,128)S(1)}) custom-call(s32[1]{0:T(128)} %bitcast.3.flag, bf16[16,64,128]{2,1,0:T(8,128)(2,1)S(1)} %bitcast.19, bf16[16,64,128]{2,1,0:T(8,128)(2,1)S(1)} %copy-done, bf16[16,64,128]{2,1,0:T(8,128)(2,1)S(1)} %bitcast.22, bf16[16,64,128]{2,1,0:T(8,128)(2,1)S(1)} %copy-done.2, ...), custom_call_target="tpu_custom_call" | custom-call | flops 20000000 | bytes 2500000 | tf_op jit(solution)/shard_map/pallas_call | solution.py:362
  16.1 0.0 collective-permute-done.lo
  16.1 0.0 collective-permute-done.1.hi
  16.1 0.0 collective-permute-done.2.before
  16.2 0.0 copy-start.5
  16.2 0.9 shard_map.56
  17.0 0.0 copy-start.1
  17.0 0.0 copy-start.3
  17.0 11.8 %all-to-all-start = ((bf16[32,32,128]{2,1,0:T(8,128)(2,1)}), bf16[32,32,128]{2,1,0:T(8,128)(2,1)S(1)}, u32[]{:S(2)}, u32[]{:S(2)}) async-start(bf16[32,32,128]{2,1,0:T(8,128)(2,1)} %bitcast.7), calls=%async_computation | async-start | bytes 524288 | tf_op jit(solution)/shard_map/all_to_all | solution.py:422
  28.9 0.0 copy-done.5
  28.9 0.0 copy-done.1
  28.9 0.0 copy-done.3
  28.9 0.1 pad_maximum_fusion
  29.0 1.9 %collective-permute-start.7 = (bf16[3,12,64,128]{3,2,1,0:T(8,128)(2,1)S(1)}, bf16[3,12,64,128]{3,2,1,0:T(8,128)(2,1)S(1)}, u32[]{:S(2)}, u32[]{:S(2)}) collective-permute-start(bf16[3,12,64,128]{3,2,1,0:T(8,128)(2,1)S(1)} %slice_select_fusion), channel_id=1, source_target_pairs={{8,1},{1,8},{9,2},{2,9},{10,3},{3,10},{11,4},{4,11},{12,5},{5,12},... | collective-permute-start | bytes 1769480 | tf_op jit(solution)/shard_map/ppermute | solution.py:403
  31.0 12.6 %all-to-all-done.r = bf16[32,32,128]{2,1,0:T(8,128)(2,1)S(1)} async-done(((bf16[32,32,128]{2,1,0:T(8,128)(2,1)}), bf16[32,32,128]{2,1,0:T(8,128)(2,1)S(1)}, u32[]{:S(2)}, u32[]{:S(2)}) %all-to-all-start) | async-done | bytes 262176 | tf_op jit(solution)/shard_map/all_to_all | solution.py:422
  43.6 0.2 shard_map.57
  43.8 13.6 %all_to_all.20.y = bf16[16,2,32,128]{3,2,1,0:T(8,128)(2,1)S(1)} all-to-all(bf16[16,2,32,128]{3,2,1,0:T(8,128)(2,1)S(1)} %shard_map.57), channel_id=1, replica_groups=mesh['tm_0'=2,'tm_1'=8,'tm_2'=2,'space'=8] {'tm_0','tm_1'}, dimensions={0} | all-to-all | bytes 524288 | tf_op jit(solution)/shard_map/all_to_all | solution.py:424
  57.4 1.9 %collective-permute-start.3 = (bf16[16,2,32,128]{3,2,1,0:T(8,128)(2,1)S(1)}, bf16[16,2,32,128]{3,2,1,0:T(8,128)(2,1)S(1)}, u32[]{:S(2)}, u32[]{:S(2)}) collective-permute-start(bf16[16,2,32,128]{3,2,1,0:T(8,128)(2,1)S(1)} %all_to_all.20.y), channel_id=1, source_target_pairs={{8,1},{1,8},{9,2},{2,9},{10,3},{3,10},{11,4},{4,11},{12,5},{5,12},... | collective-permute-start | bytes 786440 | tf_op jit(solution)/shard_map/ppermute | solution.py:434
  59.3 0.0 collective-permute-done.7.outer
  59.4 0.1 collective-permute-start.8
  59.5 4.7 %collective-permute-start.5 = (bf16[8,2,32,128]{3,2,1,0:T(8,128)(2,1)S(1)}, bf16[8,2,32,128]{3,2,1,0:T(8,128)(2,1)S(1)}, u32[]{:S(2)}, u32[]{:S(2)}) collective-permute-start(bf16[8,2,32,128]{3,2,1,0:T(8,128)(2,1)S(1)} %slice_select_fusion.3), channel_id=1, source_target_pairs={{0,1},{1,2},{2,3},{3,4},{4,5},{5,6},{6,7},{9,8},{10,9},{11,10},{12... | collective-permute-start | bytes 393224 | tf_op jit(solution)/shard_map/ppermute | solution.py:435
  64.2 0.1 collective-permute-start.4
  64.3 2.0 %collective-permute-done.3.ya = bf16[16,2,32,128]{3,2,1,0:T(8,128)(2,1)S(1)} collective-permute-done((bf16[16,2,32,128]{3,2,1,0:T(8,128)(2,1)S(1)}, bf16[16,2,32,128]{3,2,1,0:T(8,128)(2,1)S(1)}, u32[]{:S(2)}, u32[]{:S(2)}) %collective-permute-start.3) | collective-permute-done | bytes 262176 | tf_op jit(solution)/shard_map/ppermute | solution.py:434
  66.4 0.1 collective-permute-start.6
  66.5 0.1 pad_add_fusion.where
  66.6 0.0 collective-permute-done.8.inner
  66.6 1.5 %shard_map.58 = (f32[32,64,128]{2,1,0:T(8,128)S(1)}, f32[32,64,128]{2,1,0:T(8,128)S(1)}, f32[32,64,128]{2,1,0:T(8,128)S(1)}, f32[32,64,128]{2,1,0:T(8,128)S(1)}) custom-call(s32[2]{0:T(128)S(1)} %pad_add_fusion.where, bf16[16,64,128]{2,1,0:T(8,128)(2,1)S(1)} %copy-done.3, bf16[16,64,128]{2,1,0:T(8,128)(2,1)S(1)} %copy-done.1, ...), custom_call_target="tpu_custom_call" | custom-call | tf_op jit(solution)/shard_map/pallas_call | solution.py:362
  68.1 0.7 collective-permute-done.5.yc
  68.8 0.0 collective-permute-done.4.yb
  68.8 0.0 collective-permute-done.6.yd
  68.8 13.0 %shard_map.59 = bf16[16,2,32,128]{3,2,1,0:T(8,128)(2,1)S(1)} custom-call(s32[2]{0:T(128)S(1)} %pad_add_fusion.where, bf16[16,2,32,128]{3,2,1,0:T(8,128)(2,1)S(1)} %all_to_all.20.y, bf16[16,2,32,128]{3,2,1,0:T(8,128)(2,1)S(1)} %collective-permute-done.3.ya, bf16[16,2,32,128]{3,2,1,0:T(8,128)(2,1)S(1)} %collective-permute-done.4.yb, ...), custom_call_target="tpu_custom_call" | custom-call | tf_op jit(solution)/shard_map/pallas_call | solution.py:362
  81.8 17.7 %all_to_all.21.s = bf16[16,2,32,128]{3,2,1,0:T(8,128)(2,1)S(1)} all-to-all(bf16[16,2,32,128]{3,2,1,0:T(8,128)(2,1)S(1)} %shard_map.59), channel_id=1, replica_groups=mesh['tm_0'=2,'tm_1'=8,'tm_2'=2,'space'=8] {'tm_0','tm_1'}, dimensions={0} | all-to-all | bytes 524288 | tf_op jit(solution)/shard_map/all_to_all | solution.py:450
  99.4 0.2 shard_map.60
  99.7 0.0 copy-start.7
  99.7 19.5 %all_to_all.22 = bf16[32,32,128]{2,1,0:T(8,128)(2,1)S(1)} all-to-all(bf16[32,32,128]{2,1,0:T(8,128)(2,1)S(1)} %shard_map.60), channel_id=1, replica_groups=mesh['tm_0'=2,'tm_1'=8,'tm_2'=2,'space'=8] {'tm_0','tm_1','tm_2'}, dimensions={0} | all-to-all | bytes 524288 | tf_op jit(solution)/shard_map/all_to_all | solution.py:452
  119.2 0.0 copy-done.7
  119.2 0.9 shard_map.61
  (4 shorter events, 0.1 us)
Async XLA Ops:
  0.0 16.1 %collective-permute-start.2 = (bf16[16,64,128]{2,1,0:T(8,128)(2,1)}, bf16[16,64,128]{2,1,0:T(8,128)(2,1)S(1)}, u32[]{:S(2)}, u32[]{:S(2)}) collective-permute-start(bf16[16,64,128]{2,1,0:T(8,128)(2,1)} %bitcast.18), channel_id=1, source_target_pairs={{0,8},{8,16},{16,24},{24,32},{32,40},{40,48},{48,56},{56,64},{64,7... | collective-permute-start | bytes 786440 | tf_op jit(solution)/shard_map/ppermute | solution.py:400
  2.5 13.6 %collective-permute-start = (bf16[2,64,128]{2,1,0:T(8,128)(2,1)S(1)}, bf16[2,64,128]{2,1,0:T(8,128)(2,1)S(1)}, u32[]{:S(2)}, u32[]{:S(2)}) collective-permute-start(bf16[2,64,128]{2,1,0:T(8,128)(2,1)S(1)} %get-tuple-element.18), channel_id=1, source_target_pairs={{0,1},{1,2},{2,3},{3,4},{4,5},{5,6},{6,7},{8,9},{9,10},{10,11},{11... | collective-permute-start | bytes 98312 | tf_op jit(solution)/shard_map/ppermute | solution.py:398
  5.9 10.2 %collective-permute-start.1 = (bf16[2,64,128]{2,1,0:T(8,128)(2,1)S(1)}, bf16[2,64,128]{2,1,0:T(8,128)(2,1)S(1)}, u32[]{:S(2)}, u32[]{:S(2)}) collective-permute-start(bf16[2,64,128]{2,1,0:T(8,128)(2,1)S(1)} %get-tuple-element.17), channel_id=1, source_target_pairs={{1,0},{2,1},{3,2},{4,3},{5,4},{6,5},{7,6},{9,8},{10,9},{11,10},{12... | collective-permute-start | bytes 98312 | tf_op jit(solution)/shard_map/ppermute | solution.py:399
  9.3 1.0 copy-start
  10.2 0.9 copy-start.2
  11.2 0.9 copy-start.4
  12.1 0.9 copy-start.6
  13.1 0.9 copy-start.8
  16.2 12.7 %copy-start.5 = (bf16[16,64,128]{2,1,0:T(8,128)(2,1)S(1)}, bf16[16,64,128]{2,1,0:T(8,128)(2,1)}, u32[]{:S(2)}) copy-start(bf16[16,64,128]{2,1,0:T(8,128)(2,1)} %reaction.1) | copy-start | bytes 786436
  17.0 11.8 %copy-start.1 = (bf16[16,64,128]{2,1,0:T(8,128)(2,1)S(1)}, bf16[16,64,128]{2,1,0:T(8,128)(2,1)}, u32[]{:S(2)}) copy-start(bf16[16,64,128]{2,1,0:T(8,128)(2,1)} %initial.1) | copy-start | bytes 786436
  17.0 11.8 %copy-start.3 = (bf16[16,64,128]{2,1,0:T(8,128)(2,1)S(1)}, bf16[16,64,128]{2,1,0:T(8,128)(2,1)}, u32[]{:S(2)}) copy-start(bf16[16,64,128]{2,1,0:T(8,128)(2,1)} %kappa.1) | copy-start | bytes 786436
  17.0 26.6 %all-to-all-start = ((bf16[32,32,128]{2,1,0:T(8,128)(2,1)}), bf16[32,32,128]{2,1,0:T(8,128)(2,1)S(1)}, u32[]{:S(2)}, u32[]{:S(2)}) async-start(bf16[32,32,128]{2,1,0:T(8,128)(2,1)} %bitcast.7), calls=%async_computation | async-start | bytes 524288 | tf_op jit(solution)/shard_map/all_to_all | solution.py:422
  29.0 30.3 %collective-permute-start.7 = (bf16[3,12,64,128]{3,2,1,0:T(8,128)(2,1)S(1)}, bf16[3,12,64,128]{3,2,1,0:T(8,128)(2,1)S(1)}, u32[]{:S(2)}, u32[]{:S(2)}) collective-permute-start(bf16[3,12,64,128]{3,2,1,0:T(8,128)(2,1)S(1)} %slice_select_fusion), channel_id=1, source_target_pairs={{8,1},{1,8},{9,2},{2,9},{10,3},{3,10},{11,4},{4,11},{12,5},{5,12},... | collective-permute-start | bytes 1769480 | tf_op jit(solution)/shard_map/ppermute | solution.py:403
  57.4 9.0 %collective-permute-start.3 = (bf16[16,2,32,128]{3,2,1,0:T(8,128)(2,1)S(1)}, bf16[16,2,32,128]{3,2,1,0:T(8,128)(2,1)S(1)}, u32[]{:S(2)}, u32[]{:S(2)}) collective-permute-start(bf16[16,2,32,128]{3,2,1,0:T(8,128)(2,1)S(1)} %all_to_all.20.y), channel_id=1, source_target_pairs={{8,1},{1,8},{9,2},{2,9},{10,3},{3,10},{11,4},{4,11},{12,5},{5,12},... | collective-permute-start | bytes 786440 | tf_op jit(solution)/shard_map/ppermute | solution.py:434
  59.4 7.2 %collective-permute-start.8 = (bf16[3,4,64,128]{3,2,1,0:T(8,128)(2,1)S(1)}, bf16[3,4,64,128]{3,2,1,0:T(8,128)(2,1)S(1)}, u32[]{:S(2)}, u32[]{:S(2)}) collective-permute-start(bf16[3,4,64,128]{3,2,1,0:T(8,128)(2,1)S(1)} %slice_select_fusion.1), channel_id=1, source_target_pairs={{0,8},{1,9},{2,10},{3,11},{4,12},{5,13},{6,14},{7,15},{8,0},{9,1},... | collective-permute-start | bytes 589832 | tf_op jit(solution)/shard_map/ppermute | solution.py:405
  59.5 9.3 %collective-permute-start.5 = (bf16[8,2,32,128]{3,2,1,0:T(8,128)(2,1)S(1)}, bf16[8,2,32,128]{3,2,1,0:T(8,128)(2,1)S(1)}, u32[]{:S(2)}, u32[]{:S(2)}) collective-permute-start(bf16[8,2,32,128]{3,2,1,0:T(8,128)(2,1)S(1)} %slice_select_fusion.3), channel_id=1, source_target_pairs={{0,1},{1,2},{2,3},{3,4},{4,5},{5,6},{6,7},{9,8},{10,9},{11,10},{12... | collective-permute-start | bytes 393224 | tf_op jit(solution)/shard_map/ppermute | solution.py:435
  64.2 4.5 %collective-permute-start.4 = (bf16[16,2,32,128]{3,2,1,0:T(8,128)(2,1)S(1)}, bf16[16,2,32,128]{3,2,1,0:T(8,128)(2,1)S(1)}, u32[]{:S(2)}, u32[]{:S(2)}) collective-permute-start(bf16[16,2,32,128]{3,2,1,0:T(8,128)(2,1)S(1)} %all_to_all.20.y), channel_id=1, source_target_pairs={{0,8},{1,9},{2,10},{3,11},{4,12},{5,13},{6,14},{7,15},{8,0},{9,1},... | collective-permute-start | bytes 786440 | tf_op jit(solution)/shard_map/ppermute | solution.py:436
  66.4 2.4 %collective-permute-start.6 = (bf16[8,2,32,128]{3,2,1,0:T(8,128)(2,1)S(1)}, bf16[8,2,32,128]{3,2,1,0:T(8,128)(2,1)S(1)}, u32[]{:S(2)}, u32[]{:S(2)}) collective-permute-start(bf16[8,2,32,128]{3,2,1,0:T(8,128)(2,1)S(1)} %slice_select_fusion.2), channel_id=1, source_target_pairs={{0,8},{1,9},{2,10},{3,11},{4,12},{5,13},{6,14},{7,15},{8,0},{9,1},... | collective-permute-start | bytes 393224 | tf_op jit(solution)/shard_map/ppermute | solution.py:437
  99.7 19.5 %copy-start.7 = (bf16[1,16,64,128]{3,2,1,0:T(8,128)(2,1)S(1)}, bf16[1,16,64,128]{3,2,1,0:T(8,128)(2,1)}, u32[]{:S(2)}) copy-start(bf16[1,16,64,128]{3,2,1,0:T(8,128)(2,1)} %param.5) | copy-start | bytes 786436

commit v3 on v2

--- a/solution.py
+++ b/solution.py
@@ -11,6 +11,7 @@
 SWEEPS = 6
 STEPS = 32
 UNROLL = 2
+LARGE = 24 * 2**20
 TM = ("tm_0", "tm_1", "tm_2")
 CHIPS = ("tm_0", "tm_1")
 CORE_SPACE = ("tm_2", "space")
@@ -104,7 +105,9 @@
     return centre, total
 
 
-def local_kernel(flag, u_hbm, initial_hbm, forcing_hbm, kappa_hbm, reaction_hbm, part, rim, *rest):
+def local_kernel(
+    where, u_hbm, initial_hbm, forcing_hbm, kappa_hbm, reaction_hbm, part, rim, coefs, *rest
+):
     ext, u, initial, forcing, kappa, reaction, sems = rest
     planes, rows, lanes = u.shape
     pairs = ((u_hbm, u), (forcing_hbm, forcing), (kappa_hbm, kappa), (reaction_hbm, reaction))
@@ -132,7 +135,7 @@
 
     lax.fori_loop(0, planes, fill, 0)
     masks = lane_masks((rows, lanes))
-    first = flag[0] == 0
+    first = jnp.logical_and(where[0] == 0, where[1] == 0)
 
     def one(p, _):
         centre, total = neighbour_sum(ext, (), p + 2, rows, masks)
@@ -149,25 +152,36 @@
     lax.fori_loop(0, planes, one, 0)
     for i, p in enumerate((0, 1, planes - 2, planes - 1)):
         rim[i] = kappa[p].astype(jnp.float32)
-
-
-def residual_kernel(part, rim, lo, hi, before, out):
+    width = coefs.shape[1]
+    skip = where[0] * (planes - width)
+
+    def send(i, _):
+        for row, source in enumerate((kappa, initial, reaction)):
+            coefs[row, i] = source[i + skip]
+        return 0
+
+    lax.fori_loop(0, width, send, 0)
+
+
+def residual_kernel(where, part, rim, lo, hi, before, mine, theirs):
     planes, rows, _ = part.shape
-    share = out.shape[2]
+    share = mine.shape[1]
     per_plane = rows // share
     half = planes // 2
-
-    def put(p, value):
+    core = where[0]
+
+    def put(out, inner, value):
         value = value.astype(jnp.bfloat16)
-        side, inner = p // half, p % half
         for piece in range(per_plane):
-            out[per_plane * inner + piece, side] = value[piece * share : (piece + 1) * share]
-
-    def one(p, _):
-        put(p, part[p] + before[p].astype(jnp.float32))
-        return 0
-
-    lax.fori_loop(2, planes - 2, one, 0)
+            out[per_plane * inner + piece] = value[piece * share : (piece + 1) * share]
+
+    def one(i, _):
+        for out, side in ((mine, core), (theirs, 1 - core)):
+            p = side * half + i
+            put(out, i, part[p] + before[p].astype(jnp.float32))
+        return 0
+
+    lax.fori_loop(0, half, one, 0)
     l0, l1, h0, h1 = (v.astype(jnp.float32) for v in (lo[0], lo[1], hi[0], hi[1]))
     edges = (
         (0, near_weight * l1 + far_weight * l0),
@@ -175,17 +189,38 @@
         (planes - 2, far_weight * h0),
         (planes - 1, near_weight * h0 + far_weight * h1),
     )
-    for i, (p, total) in enumerate(edges):
-        put(p, part[p] + rim[i] * total + before[p].astype(jnp.float32))
-
-
-def forward_kernel(r, out):
-    steps, rows, _ = r.shape
+    values = [
+        part[p] + rim[i] * total + before[p].astype(jnp.float32)
+        for i, (p, total) in enumerate(edges)
+    ]
+
+    def lower(low, high):
+        for i, p in enumerate((0, 1)):
+            put(low, p, values[i])
+        for i, p in enumerate((half - 2, half - 1)):
+            put(high, p, values[2 + i])
+
+    @pl.when(core == 0)
+    def _():
+        lower(mine, theirs)
+
+    @pl.when(core != 0)
+    def _():
+        lower(theirs, mine)
+
+
+def forward_kernel(where, r, out):
+    chips, cores, rows, _ = r.shape
+    steps = chips * cores
+    core = where[0]
     for start in range(0, rows, 16):
         part = pl.ds(start, 16)
-        scaled = [
-            r[n, part].astype(jnp.float32) * (alpha_ratio ** (n / steps)) for n in range(steps)
-        ]
+        scaled = []
+        for n in range(steps):
+            turn = core if n % cores == 0 else 1 - core
+            scaled.append(
+                r[n // cores, turn, part].astype(jnp.float32) * (alpha_ratio ** (n / steps))
+            )
         spectrum = real_dft(scaled)
         out[0, 0, part] = spectrum[0][0].astype(jnp.bfloat16)
         out[0, 1, part] = spectrum[steps // 2][0].astype(jnp.bfloat16)
@@ -194,8 +229,10 @@
             out[j, 1, part] = spectrum[j][1].astype(jnp.bfloat16)
 
 
-def inverse_kernel(s, out):
-    steps, rows, _ = out.shape
+def inverse_kernel(where, s, out):
+    chips, cores, rows, _ = out.shape
+    steps = chips * cores
+    core = where[0]
     for start in range(0, rows, 16):
         part = pl.ds(start, 16)
         spectrum = [(s[0, 0, part].astype(jnp.float32), None)]
@@ -204,8 +241,9 @@
         spectrum.append((s[0, 1, part].astype(jnp.float32), None))
         values = real_inverse(spectrum)
         for n in range(steps):
+            turn = core if n % cores == 0 else 1 - core
             scale = 1.0 / (alpha_ratio ** (n / steps) * steps)
-            out[n, part] = (values[n] * scale).astype(jnp.bfloat16)
+            out[n // cores, turn, part] = (values[n] * scale).astype(jnp.bfloat16)
 
 
 def coefficient_kernel(where, kappa, initial, reaction, outer, inner, p0, p1, q, k):
@@ -332,28 +370,26 @@
         lax.fori_loop(0, (ext - 2 * edge) // UNROLL, sweep, 0)
 
 
-def final_kernel(state, correction, out):
+def final_kernel(where, state, mine, theirs, out):
     planes, rows, _ = state.shape
-    share = correction.shape[2]
+    share = theirs.shape[1]
     per_plane = rows // share
     half = planes // 2
-
-    def one(p, _):
-        part, inner = p // half, p % half
-        value = jnp.concatenate(
-            [
-                correction[per_plane * inner + h, part].astype(jnp.float32)
-                for h in range(per_plane)
-            ],
-            axis=0,
-        )
-        out[p] = (state[p].astype(jnp.float32) + value).astype(jnp.bfloat16)
-        return 0
-
-    lax.fori_loop(0, planes, one, 0)
-
-
-def call(kernel, shapes, inputs, scratch=(), scalars=0, anywhere=0, flops=None):
+    core = where[0]
+
+    def one(i, _):
+        pieces = [per_plane * i + h for h in range(per_plane)]
+        both = ((core, [mine[k, 0] for k in pieces]), (1 - core, [theirs[k] for k in pieces]))
+        for side, values in both:
+            p = side * half + i
+            value = jnp.concatenate([v.astype(jnp.float32) for v in values], axis=0)
+            out[p] = (state[p].astype(jnp.float32) + value).astype(jnp.bfloat16)
+        return 0
+
+    lax.fori_loop(0, half, one, 0)
+
+
+def call(kernel, shapes, inputs, scratch=(), scalars=0, anywhere=0, flops=None, vmem=24 << 20):
     outs = [jax.ShapeDtypeStruct(s, d) for s, d in shapes]
     cost = None
     if flops is not None:
@@ -366,7 +402,7 @@
         out_specs=[VMEM] * len(outs),
         scratch_shapes=list(scratch),
         cost_estimate=cost,
-        compiler_params=pltpu.CompilerParams(vmem_limit_bytes=24 << 20),
+        compiler_params=pltpu.CompilerParams(vmem_limit_bytes=vmem),
     )(*inputs)
 
 
@@ -382,7 +418,6 @@
     narrow = wide - own
     ext = own + 2 * wide
     bf16, f32, i32 = jnp.bfloat16, jnp.float32, jnp.int32
-    position = lax.axis_index(TM).astype(i32).reshape(1)
     core = lax.axis_index("tm_2")
     slot = lax.axis_index(CHIPS)
     where = jnp.stack([core, slot]).astype(i32)
@@ -398,29 +433,40 @@
     lo = lax.ppermute(u[planes - 2 :], "space", forward)
     hi = lax.ppermute(u[:2], "space", backward)
     before = lax.ppermute(u, TM, [(i, i + 1) for i in range(members - 1)])
-    coefs = jnp.stack([kappa, initial, reaction])
-    rim = jnp.where(core == 0, coefs[:, :wide], coefs[:, planes - wide :])
-    rim = lax.ppermute(rim, CORE_SPACE, outer)
-    inner = jnp.where(core == 0, rim[:, wide - narrow :], rim[:, :narrow])
-    inner = lax.ppermute(inner, CORE_SPACE, swap)
-
     block = ((planes, rows, lanes), bf16)
-    part, edge = call(
+    part, edge, coefs = call(
         local_kernel,
-        [((planes, rows, lanes), f32), ((4, rows, lanes), f32)],
-        [position, u, initial, forcing[0], kappa, reaction],
+        [
+            ((planes, rows, lanes), f32),
+            ((4, rows, lanes), f32),
+            ((3, wide, rows, lanes), bf16),
+        ],
+        [where]
+        + [
+            pltpu.with_memory_space_constraint(v, pltpu.HBM)
+            for v in (u, initial, forcing[0], kappa, reaction)
+        ],
         [pltpu.VMEM((planes + 4, rows + 2 * PAD, lanes), f32)]
         + [pltpu.VMEM(*block)] * 5
         + [pltpu.SemaphoreType.DMA((5,))],
         scalars=1,
         anywhere=5,
         flops=20_000_000,
-    )
-    (residual,) = call(
-        residual_kernel, [((slots, 2, share, lanes), bf16)], [part, edge, lo, hi, before]
-    )
-    cells = lax.all_to_all(residual.reshape(members, share, lanes), TM, 0, 0, tiled=True)
-    (spectrum,) = call(forward_kernel, [((slots, 2, share, lanes), bf16)], [cells])
+        vmem=LARGE,
+    )
+    rim = lax.ppermute(coefs, CORE_SPACE, outer)
+    inner = jnp.where(core == 0, rim[:, wide - narrow :], rim[:, :narrow])
+    inner = lax.ppermute(inner, CORE_SPACE, swap)
+
+    thin = ((slots, share, lanes), bf16)
+    pair = ((slots, 2, share, lanes), bf16)
+    mine, theirs = call(
+        residual_kernel, [thin, thin], [where, part, edge, lo, hi, before], scalars=1
+    )
+    theirs = lax.ppermute(theirs, CORE_SPACE, swap)
+    times = jnp.stack([mine, theirs], axis=1)
+    cells = lax.all_to_all(times, CHIPS, 0, 0, tiled=True)
+    (spectrum,) = call(forward_kernel, [pair], [where, cells], scalars=1)
     y = lax.all_to_all(spectrum, CHIPS, 0, 0, tiled=True)
 
     fields = call(
@@ -448,11 +494,10 @@
         scalars=1,
     )
     modes = lax.all_to_all(solved, CHIPS, 0, 0, tiled=True)
-    (correction,) = call(inverse_kernel, [((members, share, lanes), bf16)], [modes])
-    returned = lax.all_to_all(correction, TM, 0, 0, tiled=True)
-    (updated,) = call(
-        final_kernel, [((planes, rows, lanes), bf16)], [u, returned.reshape(slots, 2, share, lanes)]
-    )
+    (correction,) = call(inverse_kernel, [pair], [where, modes], scalars=1)
+    returned = lax.all_to_all(correction, CHIPS, 0, 0, tiled=True)
+    other = lax.ppermute(returned[:, 1], CORE_SPACE, swap)
+    (updated,) = call(final_kernel, [block], [where, u, returned, other], scalars=1)
     return updated[None]
 
 

time: 121 us -> 120 us (level)
  blocking collectives: 50.8 us -> 32.5 us
  waiting for transfers between devices: 15.4 us -> 27.5 us
  local copies, waits for them, and re-layouts: 5.55 us -> 0.81 us
  starting transfers between devices: 29.1 us -> 33.7 us
  Pallas kernels: 18.7 us -> 22.4 us
    all_to_all x2 -> x1, blocking collectives: 33.1 us -> 15.5 us  [iteration(): returned = lax.all_to_all(correction, CHIPS, 0, 0, tiled=True)]
    all_to_all x1 -> x2, waiting for transfers between devices: 12.6 us -> 20.5 us  [the longest x1 11.4 us: iteration(): y = lax.all_to_all(spectrum, CHIPS, 0, 0, tiled=True)]
    unnamed x18 -> x8, local copies, waits for them, and re-layouts: 4.76 us -> 0.02 us
    pallas_call x7, Pallas kernels: 18.7 us -> 22.4 us  [call(): pl.pallas_call(kernel, out_shape=outs, in_specs=[SMEM] * scalars + [HBM]...]
    all_to_all x1 -> x2, starting transfers between devices: 11.8 us -> 14.7 us  [the longest x1 10.2 us: iteration(): cells = lax.all_to_all(times, CHIPS, 0, 0, tiled=True)]
    ppermute x1 -> x3, starting transfers between devices: 1.92 us -> 4.39 us  [the longest x1 2.95 us: iteration(): rim = lax.ppermute(coefs, CORE_SPACE, outer)]
    ppermute x1 -> x3, waiting for transfers between devices: 0.01 us -> 2.32 us  [the longest x1 1.33 us: iteration(): other = lax.ppermute(returned[:, 1], CORE_SPACE, swap)]
    ppermute x1, starting transfers between devices: 0.09 us -> 1.75 us  [iteration(): inner = lax.ppermute(inner, CORE_SPACE, swap)]
  transfers between devices with their start and end apart: 10 -> 13, of which waited for: 3 -> 7; matrix products, arithmetic and copies ran while one was open for 1% -> 1% of each run, Pallas kernels for 3% -> 6%
where the time goes in v3:
time: 120 us; the launch traced here: 118 us
  starting transfers between devices  33.7 us (28%)
  blocking collectives  32.5 us (27%)
  waiting for transfers between devices  27.5 us (23%)
  Pallas kernels  22.4 us (19%)
    pallas_call x7, Pallas kernels, call(): pl.pallas_call(kernel, out_shape=outs, in_specs=[SMEM] * scalars + [HBM]...  22.4 us
    all_to_all x1, blocking collectives, iteration(): modes = lax.all_to_all(solved, CHIPS, 0, 0, tiled=True)  17 us
    all_to_all x1, blocking collectives, iteration(): returned = lax.all_to_all(correction, CHIPS, 0, 0, tiled=True)  15.5 us
    all_to_all x1, waiting for transfers between devices, iteration(): y = lax.all_to_all(spectrum, CHIPS, 0, 0, tiled=True)  11.4 us
    all_to_all x1, starting transfers between devices, iteration(): cells = lax.all_to_all(times, CHIPS, 0, 0, tiled=True)  10.2 us
    all_to_all x1, waiting for transfers between devices, iteration(): cells = lax.all_to_all(times, CHIPS, 0, 0, tiled=True)  9.16 us
    all_to_all x1, starting transfers between devices, iteration(): y = lax.all_to_all(spectrum, CHIPS, 0, 0, tiled=True)  4.51 us
    ppermute x1, waiting for transfers between devices, iteration(): ya = lax.ppermute(y, CORE_SPACE, outer)  3.66 us
  transfers between devices with their start and end apart: 13, of which 7 were waited for; matrix products, arithmetic and copies ran while one was open for 1% of the time, Pallas kernels for 6%

profile of v3, /device:TPU:16, one launch (start us, length us, event | category | flops | bytes accessed | tf_op | source)
XLA Modules:
  0.0 118.1 jit_solution(5544447264765822128)
XLA Ops:
  0.0 1.7 %collective-permute-start.2 = (bf16[16,64,128]{2,1,0:T(8,128)(2,1)}, bf16[16,64,128]{2,1,0:T(8,128)(2,1)S(1)}, u32[]{:S(2)}, u32[]{:S(2)}) collective-permute-start(bf16[16,64,128]{2,1,0:T(8,128)(2,1)} %bitcast.15), channel_id=1, source_target_pairs={{0,8},{8,16},{16,24},{24,32},{32,40},{40,48},{48,56},{56,64},{64,7... | collective-permute-start | bytes 786440 | tf_op jit(solution)/shard_map/ppermute | solution.py:435
  1.8 0.8 slice_bitcast_fusion.1
  2.5 3.3 %collective-permute-start.1 = (bf16[2,64,128]{2,1,0:T(8,128)(2,1)S(1)}, bf16[2,64,128]{2,1,0:T(8,128)(2,1)S(1)}, u32[]{:S(2)}, u32[]{:S(2)}) collective-permute-start(bf16[2,64,128]{2,1,0:T(8,128)(2,1)S(1)} %get-tuple-element.23), channel_id=1, source_target_pairs={{1,0},{2,1},{3,2},{4,3},{5,4},{6,5},{7,6},{9,8},{10,9},{11,10},{12... | collective-permute-start | bytes 98312 | tf_op jit(solution)/shard_map/ppermute | solution.py:434
  5.8 2.6 %collective-permute-start = (bf16[2,64,128]{2,1,0:T(8,128)(2,1)S(1)}, bf16[2,64,128]{2,1,0:T(8,128)(2,1)S(1)}, u32[]{:S(2)}, u32[]{:S(2)}) collective-permute-start(bf16[2,64,128]{2,1,0:T(8,128)(2,1)S(1)} %get-tuple-element.24), channel_id=1, source_target_pairs={{0,1},{1,2},{2,3},{3,4},{4,5},{5,6},{6,7},{8,9},{9,10},{10,11},{11... | collective-permute-start | bytes 98312 | tf_op jit(solution)/shard_map/ppermute | solution.py:433
  8.4 0.1 pad_add_fusion.where
  8.5 3.7 %shard_map.55 = (f32[16,64,128]{2,1,0:T(8,128)S(1)}, f32[4,64,128]{2,1,0:T(8,128)S(1)}, bf16[3,12,64,128]{3,2,1,0:T(8,128)(2,1)S(1)}) custom-call(s32[2]{0:T(128)S(1)} %pad_add_fusion.where, bf16[16,64,128]{2,1,0:T(8,128)(2,1)} %bitcast.16, bf16[16,64,128]{2,1,0:T(8,128)(2,1)} %initial.1, bf16[16,64,128]{2,1,0:T(8,128)(2,1)} %bitcast.19, ...), custom_call_target="tpu_custom_call" | custom-call | flops 20000000 | bytes 2500000 | tf_op jit(solution)/shard_map/pallas_call | solution.py:398
  12.2 0.0 collective-permute-done.1.hi
  12.2 0.4 collective-permute-done.lo
  12.6 0.0 collective-permute-done.2.before
  12.6 0.7 shard_map.56
  13.3 1.4 %collective-permute-start.3 = (bf16[16,32,128]{2,1,0:T(8,128)(2,1)S(1)}, bf16[16,32,128]{2,1,0:T(8,128)(2,1)S(1)}, u32[]{:S(2)}, u32[]{:S(2)}) collective-permute-start(bf16[16,32,128]{2,1,0:T(8,128)(2,1)S(1)} %get-tuple-element.17), channel_id=1, source_target_pairs={{0,8},{1,9},{2,10},{3,11},{4,12},{5,13},{6,14},{7,15},{8,0},{9,1},... | collective-permute-start | bytes 393224 | tf_op jit(solution)/shard_map/ppermute | solution.py:466
  14.7 1.0 collective-permute-done.3
  15.7 0.7 pad_maximum_fusion
  16.4 10.2 %all-to-all-start = ((bf16[16,2,32,128]{3,2,1,0:T(8,128)(2,1)}), bf16[16,2,32,128]{3,2,1,0:T(8,128)(2,1)S(1)}, u32[]{:S(2)}, u32[]{:S(2)}) async-start(bf16[16,2,32,128]{3,2,1,0:T(8,128)(2,1)} %pad_maximum_fusion), calls=%async_computation | async-start | bytes 524288 | tf_op jit(solution)/shard_map/all_to_all | solution.py:468
  26.5 3.0 %collective-permute-start.8 = (bf16[3,12,64,128]{3,2,1,0:T(8,128)(2,1)S(1)}, bf16[3,12,64,128]{3,2,1,0:T(8,128)(2,1)S(1)}, u32[]{:S(2)}, u32[]{:S(2)}) collective-permute-start(bf16[3,12,64,128]{3,2,1,0:T(8,128)(2,1)S(1)} %get-tuple-element.18), channel_id=1, source_target_pairs={{8,1},{1,8},{9,2},{2,9},{10,3},{3,10},{11,4},{4,11},{12,5},{5,12},... | collective-permute-start | bytes 1769480 | tf_op jit(solution)/shard_map/ppermute | solution.py:457
  29.5 9.2 %all-to-all-done.r = bf16[16,2,32,128]{3,2,1,0:T(8,128)(2,1)S(1)} async-done(((bf16[16,2,32,128]{3,2,1,0:T(8,128)(2,1)}), bf16[16,2,32,128]{3,2,1,0:T(8,128)(2,1)S(1)}, u32[]{:S(2)}, u32[]{:S(2)}) %all-to-all-start) | async-done | bytes 262176 | tf_op jit(solution)/shard_map/all_to_all | solution.py:468
  38.7 1.4 %shard_map.57 = bf16[16,2,32,128]{3,2,1,0:T(8,128)(2,1)} custom-call(s32[2]{0:T(128)S(1)} %pad_add_fusion.where, bf16[16,2,32,128]{3,2,1,0:T(8,128)(2,1)S(1)} %all-to-all-done.r), custom_call_target="tpu_custom_call" | custom-call | tf_op jit(solution)/shard_map/pallas_call | solution.py:398
  40.1 4.5 %all-to-all-start.1 = ((bf16[16,2,32,128]{3,2,1,0:T(8,128)(2,1)}), bf16[16,2,32,128]{3,2,1,0:T(8,128)(2,1)S(1)}, u32[]{:S(2)}, u32[]{:S(2)}) async-start(bf16[16,2,32,128]{3,2,1,0:T(8,128)(2,1)} %shard_map.57), calls=%async_computation.1 | async-start | bytes 524288 | tf_op jit(solution)/shard_map/all_to_all | solution.py:470
  44.6 11.4 %all-to-all-done.1.y = bf16[16,2,32,128]{3,2,1,0:T(8,128)(2,1)S(1)} async-done(((bf16[16,2,32,128]{3,2,1,0:T(8,128)(2,1)}), bf16[16,2,32,128]{3,2,1,0:T(8,128)(2,1)S(1)}, u32[]{:S(2)}, u32[]{:S(2)}) %all-to-all-start.1) | async-done | bytes 262176 | tf_op jit(solution)/shard_map/all_to_all | solution.py:470
  56.0 1.9 %collective-permute-start.4 = (bf16[16,2,32,128]{3,2,1,0:T(8,128)(2,1)S(1)}, bf16[16,2,32,128]{3,2,1,0:T(8,128)(2,1)S(1)}, u32[]{:S(2)}, u32[]{:S(2)}) collective-permute-start(bf16[16,2,32,128]{3,2,1,0:T(8,128)(2,1)S(1)} %all-to-all-done.1.y), channel_id=1, source_target_pairs={{8,1},{1,8},{9,2},{2,9},{10,3},{3,10},{11,4},{4,11},{12,5},{5,12},... | collective-permute-start | bytes 786440 | tf_op jit(solution)/shard_map/ppermute | solution.py:480
  57.9 0.0 collective-permute-done.8.outer
  57.9 1.8 %collective-permute-start.9 = (bf16[3,4,64,128]{3,2,1,0:T(8,128)(2,1)S(1)}, bf16[3,4,64,128]{3,2,1,0:T(8,128)(2,1)S(1)}, u32[]{:S(2)}, u32[]{:S(2)}) collective-permute-start(bf16[3,4,64,128]{3,2,1,0:T(8,128)(2,1)S(1)} %slice_select_fusion), channel_id=1, source_target_pairs={{0,8},{1,9},{2,10},{3,11},{4,12},{5,13},{6,14},{7,15},{8,0},{9,1},... | collective-permute-start | bytes 589832 | tf_op jit(solution)/shard_map/ppermute | solution.py:459
  59.7 0.0 copy-start.2
  59.7 0.0 copy-start.3
  59.7 0.0 copy-start.1
  59.7 3.2 %collective-permute-start.6 = (bf16[8,2,32,128]{3,2,1,0:T(8,128)(2,1)S(1)}, bf16[8,2,32,128]{3,2,1,0:T(8,128)(2,1)S(1)}, u32[]{:S(2)}, u32[]{:S(2)}) collective-permute-start(bf16[8,2,32,128]{3,2,1,0:T(8,128)(2,1)S(1)} %slice_select_fusion.2), channel_id=1, source_target_pairs={{0,1},{1,2},{2,3},{3,4},{4,5},{5,6},{6,7},{9,8},{10,9},{11,10},{12... | collective-permute-start | bytes 393224 | tf_op jit(solution)/shard_map/ppermute | solution.py:481
  63.0 0.1 collective-permute-start.5
  63.1 3.7 %collective-permute-done.4.ya = bf16[16,2,32,128]{3,2,1,0:T(8,128)(2,1)S(1)} collective-permute-done((bf16[16,2,32,128]{3,2,1,0:T(8,128)(2,1)S(1)}, bf16[16,2,32,128]{3,2,1,0:T(8,128)(2,1)S(1)}, u32[]{:S(2)}, u32[]{:S(2)}) %collective-permute-start.4) | collective-permute-done | bytes 262176 | tf_op jit(solution)/shard_map/ppermute | solution.py:480
  66.8 0.1 collective-permute-start.7
  66.9 0.0 collective-permute-done.9.inner
  66.9 0.0 copy-done.2
  66.9 0.0 copy-done.3
  66.9 0.0 copy-done.1
  66.9 1.5 %shard_map.58 = (f32[32,64,128]{2,1,0:T(8,128)S(1)}, f32[32,64,128]{2,1,0:T(8,128)S(1)}, f32[32,64,128]{2,1,0:T(8,128)S(1)}, f32[32,64,128]{2,1,0:T(8,128)S(1)}) custom-call(s32[2]{0:T(128)S(1)} %pad_add_fusion.where, bf16[16,64,128]{2,1,0:T(8,128)(2,1)S(1)} %copy-done.2, bf16[16,64,128]{2,1,0:T(8,128)(2,1)S(1)} %copy-done.1, ...), custom_call_target="tpu_custom_call" | custom-call | tf_op jit(solution)/shard_map/pallas_call | solution.py:398
  68.4 0.6 collective-permute-done.6.yc
  69.0 0.0 collective-permute-done.5.yb
  69.0 0.0 collective-permute-done.7.yd
  69.0 13.0 %shard_map.59 = bf16[16,2,32,128]{3,2,1,0:T(8,128)(2,1)S(1)} custom-call(s32[2]{0:T(128)S(1)} %pad_add_fusion.where, bf16[16,2,32,128]{3,2,1,0:T(8,128)(2,1)S(1)} %all-to-all-done.1.y, bf16[16,2,32,128]{3,2,1,0:T(8,128)(2,1)S(1)} %collective-permute-done.4.ya, bf16[16,2,32,128]{3,2,1,0:T(8,128)(2,1)S(1)} %collective-permute-done.5.yb, ...), custom_call_target="tpu_custom_call" | custom-call | tf_op jit(solution)/shard_map/pallas_call | solution.py:398
  82.0 17.0 %all_to_all.20.s = bf16[16,2,32,128]{3,2,1,0:T(8,128)(2,1)S(1)} all-to-all(bf16[16,2,32,128]{3,2,1,0:T(8,128)(2,1)S(1)} %shard_map.59), channel_id=1, replica_groups=mesh['tm_0'=2,'tm_1'=8,'tm_2'=2,'space'=8] {'tm_0','tm_1'}, dimensions={0} | all-to-all | bytes 524288 | tf_op jit(solution)/shard_map/all_to_all | solution.py:496
  99.0 0.7 shard_map.60
  99.8 15.5 %all_to_all.21.mine = bf16[16,2,32,128]{3,2,1,0:T(8,128)(2,1)S(1)} all-to-all(bf16[16,2,32,128]{3,2,1,0:T(8,128)(2,1)S(1)} %shard_map.60), channel_id=1, replica_groups=mesh['tm_0'=2,'tm_1'=8,'tm_2'=2,'space'=8] {'tm_0','tm_1'}, dimensions={0} | all-to-all | bytes 524288 | tf_op jit(solution)/shard_map/all_to_all | solution.py:498
  115.3 0.0 copy-start
  115.3 0.1 collective-permute-start.10
  115.4 1.3 %collective-permute-done.10.theirs = bf16[16,32,128]{2,1,0:T(8,128)(2,1)S(1)} collective-permute-done((bf16[16,32,128]{2,1,0:T(8,128)(2,1)S(1)}, bf16[16,32,128]{2,1,0:T(8,128)(2,1)S(1)}, u32[]{:S(2)}, u32[]{:S(2)}) %collective-permute-start.10) | collective-permute-done | bytes 131104 | tf_op jit(solution)/shard_map/ppermute | solution.py:499
  116.8 0.0 copy-done
  116.8 1.3 %shard_map.61 = bf16[16,64,128]{2,1,0:T(8,128)(2,1)} custom-call(s32[2]{0:T(128)S(1)} %pad_add_fusion.where, bf16[16,64,128]{2,1,0:T(8,128)(2,1)S(1)} %bitcast.17, bf16[16,2,32,128]{3,2,1,0:T(8,128)(2,1)S(1)} %all_to_all.21.mine, bf16[16,32,128]{2,1,0:T(8,128)(2,1)S(1)} %collective-permute-done.10.theirs), custom_call_target="tpu_custom_call" | custom-call | tf_op jit(solution)/shard_map/pallas_call | solution.py:398
  (4 shorter events, 0.1 us)
Async XLA Ops:
  0.0 12.6 %collective-permute-start.2 = (bf16[16,64,128]{2,1,0:T(8,128)(2,1)}, bf16[16,64,128]{2,1,0:T(8,128)(2,1)S(1)}, u32[]{:S(2)}, u32[]{:S(2)}) collective-permute-start(bf16[16,64,128]{2,1,0:T(8,128)(2,1)} %bitcast.15), channel_id=1, source_target_pairs={{0,8},{8,16},{16,24},{24,32},{32,40},{40,48},{48,56},{56,64},{64,7... | collective-permute-start | bytes 786440 | tf_op jit(solution)/shard_map/ppermute | solution.py:435
  2.5 9.7 %collective-permute-start.1 = (bf16[2,64,128]{2,1,0:T(8,128)(2,1)S(1)}, bf16[2,64,128]{2,1,0:T(8,128)(2,1)S(1)}, u32[]{:S(2)}, u32[]{:S(2)}) collective-permute-start(bf16[2,64,128]{2,1,0:T(8,128)(2,1)S(1)} %get-tuple-element.23), channel_id=1, source_target_pairs={{1,0},{2,1},{3,2},{4,3},{5,4},{6,5},{7,6},{9,8},{10,9},{11,10},{12... | collective-permute-start | bytes 98312 | tf_op jit(solution)/shard_map/ppermute | solution.py:434
  5.8 6.8 %collective-permute-start = (bf16[2,64,128]{2,1,0:T(8,128)(2,1)S(1)}, bf16[2,64,128]{2,1,0:T(8,128)(2,1)S(1)}, u32[]{:S(2)}, u32[]{:S(2)}) collective-permute-start(bf16[2,64,128]{2,1,0:T(8,128)(2,1)S(1)} %get-tuple-element.24), channel_id=1, source_target_pairs={{0,1},{1,2},{2,3},{3,4},{4,5},{5,6},{6,7},{8,9},{9,10},{10,11},{11... | collective-permute-start | bytes 98312 | tf_op jit(solution)/shard_map/ppermute | solution.py:433
  13.3 2.3 %collective-permute-start.3 = (bf16[16,32,128]{2,1,0:T(8,128)(2,1)S(1)}, bf16[16,32,128]{2,1,0:T(8,128)(2,1)S(1)}, u32[]{:S(2)}, u32[]{:S(2)}) collective-permute-start(bf16[16,32,128]{2,1,0:T(8,128)(2,1)S(1)} %get-tuple-element.17), channel_id=1, source_target_pairs={{0,8},{1,9},{2,10},{3,11},{4,12},{5,13},{6,14},{7,15},{8,0},{9,1},... | collective-permute-start | bytes 393224 | tf_op jit(solution)/shard_map/ppermute | solution.py:466
  16.4 22.3 %all-to-all-start = ((bf16[16,2,32,128]{3,2,1,0:T(8,128)(2,1)}), bf16[16,2,32,128]{3,2,1,0:T(8,128)(2,1)S(1)}, u32[]{:S(2)}, u32[]{:S(2)}) async-start(bf16[16,2,32,128]{3,2,1,0:T(8,128)(2,1)} %pad_maximum_fusion), calls=%async_computation | async-start | bytes 524288 | tf_op jit(solution)/shard_map/all_to_all | solution.py:468
  26.5 31.4 %collective-permute-start.8 = (bf16[3,12,64,128]{3,2,1,0:T(8,128)(2,1)S(1)}, bf16[3,12,64,128]{3,2,1,0:T(8,128)(2,1)S(1)}, u32[]{:S(2)}, u32[]{:S(2)}) collective-permute-start(bf16[3,12,64,128]{3,2,1,0:T(8,128)(2,1)S(1)} %get-tuple-element.18), channel_id=1, source_target_pairs={{8,1},{1,8},{9,2},{2,9},{10,3},{3,10},{11,4},{4,11},{12,5},{5,12},... | collective-permute-start | bytes 1769480 | tf_op jit(solution)/shard_map/ppermute | solution.py:457
  40.1 15.9 %all-to-all-start.1 = ((bf16[16,2,32,128]{3,2,1,0:T(8,128)(2,1)}), bf16[16,2,32,128]{3,2,1,0:T(8,128)(2,1)S(1)}, u32[]{:S(2)}, u32[]{:S(2)}) async-start(bf16[16,2,32,128]{3,2,1,0:T(8,128)(2,1)} %shard_map.57), calls=%async_computation.1 | async-start | bytes 524288 | tf_op jit(solution)/shard_map/all_to_all | solution.py:470
  56.0 10.8 %collective-permute-start.4 = (bf16[16,2,32,128]{3,2,1,0:T(8,128)(2,1)S(1)}, bf16[16,2,32,128]{3,2,1,0:T(8,128)(2,1)S(1)}, u32[]{:S(2)}, u32[]{:S(2)}) collective-permute-start(bf16[16,2,32,128]{3,2,1,0:T(8,128)(2,1)S(1)} %all-to-all-done.1.y), channel_id=1, source_target_pairs={{8,1},{1,8},{9,2},{2,9},{10,3},{3,10},{11,4},{4,11},{12,5},{5,12},... | collective-permute-start | bytes 786440 | tf_op jit(solution)/shard_map/ppermute | solution.py:480
  57.9 8.9 %collective-permute-start.9 = (bf16[3,4,64,128]{3,2,1,0:T(8,128)(2,1)S(1)}, bf16[3,4,64,128]{3,2,1,0:T(8,128)(2,1)S(1)}, u32[]{:S(2)}, u32[]{:S(2)}) collective-permute-start(bf16[3,4,64,128]{3,2,1,0:T(8,128)(2,1)S(1)} %slice_select_fusion), channel_id=1, source_target_pairs={{0,8},{1,9},{2,10},{3,11},{4,12},{5,13},{6,14},{7,15},{8,0},{9,1},... | collective-permute-start | bytes 589832 | tf_op jit(solution)/shard_map/ppermute | solution.py:459
  59.7 7.2 %copy-start.2 = (bf16[16,64,128]{2,1,0:T(8,128)(2,1)S(1)}, bf16[16,64,128]{2,1,0:T(8,128)(2,1)}, u32[]{:S(2)}) copy-start(bf16[16,64,128]{2,1,0:T(8,128)(2,1)} %kappa.1) | copy-start | bytes 786436
  59.7 7.2 %copy-start.3 = (bf16[16,64,128]{2,1,0:T(8,128)(2,1)S(1)}, bf16[16,64,128]{2,1,0:T(8,128)(2,1)}, u32[]{:S(2)}) copy-start(bf16[16,64,128]{2,1,0:T(8,128)(2,1)} %reaction.1) | copy-start | bytes 786436
  59.7 7.2 %copy-start.1 = (bf16[16,64,128]{2,1,0:T(8,128)(2,1)S(1)}, bf16[16,64,128]{2,1,0:T(8,128)(2,1)}, u32[]{:S(2)}) copy-start(bf16[16,64,128]{2,1,0:T(8,128)(2,1)} %initial.1) | copy-start | bytes 786436
  59.7 9.3 %collective-permute-start.6 = (bf16[8,2,32,128]{3,2,1,0:T(8,128)(2,1)S(1)}, bf16[8,2,32,128]{3,2,1,0:T(8,128)(2,1)S(1)}, u32[]{:S(2)}, u32[]{:S(2)}) collective-permute-start(bf16[8,2,32,128]{3,2,1,0:T(8,128)(2,1)S(1)} %slice_select_fusion.2), channel_id=1, source_target_pairs={{0,1},{1,2},{2,3},{3,4},{4,5},{5,6},{6,7},{9,8},{10,9},{11,10},{12... | collective-permute-start | bytes 393224 | tf_op jit(solution)/shard_map/ppermute | solution.py:481
  63.0 6.0 %collective-permute-start.5 = (bf16[16,2,32,128]{3,2,1,0:T(8,128)(2,1)S(1)}, bf16[16,2,32,128]{3,2,1,0:T(8,128)(2,1)S(1)}, u32[]{:S(2)}, u32[]{:S(2)}) collective-permute-start(bf16[16,2,32,128]{3,2,1,0:T(8,128)(2,1)S(1)} %all-to-all-done.1.y), channel_id=1, source_target_pairs={{0,8},{1,9},{2,10},{3,11},{4,12},{5,13},{6,14},{7,15},{8,0},{9,1},... | collective-permute-start | bytes 786440 | tf_op jit(solution)/shard_map/ppermute | solution.py:482
  66.8 2.3 %collective-permute-start.7 = (bf16[8,2,32,128]{3,2,1,0:T(8,128)(2,1)S(1)}, bf16[8,2,32,128]{3,2,1,0:T(8,128)(2,1)S(1)}, u32[]{:S(2)}, u32[]{:S(2)}) collective-permute-start(bf16[8,2,32,128]{3,2,1,0:T(8,128)(2,1)S(1)} %slice_select_fusion.1), channel_id=1, source_target_pairs={{0,8},{1,9},{2,10},{3,11},{4,12},{5,13},{6,14},{7,15},{8,0},{9,1},... | collective-permute-start | bytes 393224 | tf_op jit(solution)/shard_map/ppermute | solution.py:483
  115.3 1.5 %copy-start = (bf16[1,16,64,128]{3,2,1,0:T(8,128)(2,1)S(1)}, bf16[1,16,64,128]{3,2,1,0:T(8,128)(2,1)}, u32[]{:S(2)}) copy-start(bf16[1,16,64,128]{3,2,1,0:T(8,128)(2,1)} %param.5) | copy-start | bytes 786436
  115.3 1.4 %collective-permute-start.10 = (bf16[16,32,128]{2,1,0:T(8,128)(2,1)S(1)}, bf16[16,32,128]{2,1,0:T(8,128)(2,1)S(1)}, u32[]{:S(2)}, u32[]{:S(2)}) collective-permute-start(bf16[16,32,128]{2,1,0:T(8,128)(2,1)S(1)} %slice_bitcast_fusion), channel_id=1, source_target_pairs={{0,8},{1,9},{2,10},{3,11},{4,12},{5,13},{6,14},{7,15},{8,0},{9,1},... | collective-permute-start | bytes 393224 | tf_op jit(solution)/shard_map/ppermute | solution.py:499

commit v4 on v2

--- a/solution.py
+++ b/solution.py
@@ -10,7 +10,8 @@
 
 SWEEPS = 6
 STEPS = 32
-UNROLL = 2
+CHUNK = 16
+GROUPS = (14, 12, 10, 8, 12, 8)
 TM = ("tm_0", "tm_1", "tm_2")
 CHIPS = ("tm_0", "tm_1")
 CORE_SPACE = ("tm_2", "space")
@@ -208,7 +209,7 @@
             out[n, part] = (values[n] * scale).astype(jnp.bfloat16)
 
 
-def coefficient_kernel(where, kappa, initial, reaction, outer, inner, p0, p1, q, k):
+def coefficient_kernel(where, kappa, initial, reaction, outer, inner, inv, kinv):
     planes = kappa.shape[0]
     wide, narrow = outer.shape[1], inner.shape[1]
     core, slot = where[0], where[1]
@@ -229,10 +230,9 @@
         d0, d1 = s0 + base, s1 + base
         inv0 = 1.0 / (d0 * d0 + si * si)
         inv1 = 1.0 / (d1 * d1 + si * si)
-        p0[e] = d0 * inv0
-        p1[e] = d1 * inv1
-        q[e] = si * inv0
-        k[e] = kv
+        for c, value in enumerate((d0 * inv0, d1 * inv1, si * inv0)):
+            inv[e, c] = value
+            kinv[e, c] = kv * value
 
     def own(i, _):
         put(i + jnp.where(core == 0, wide, narrow), kappa[i], initial[i], reaction[i])
@@ -251,21 +251,26 @@
     lax.fori_loop(0, narrow, close, 0)
 
 
-def sweeps_kernel(where, y, ya, yb, yc, yd, p0, p1, q, k, out, x0, kp, xs, xt):
-    ext, rows, lanes = p0.shape
+def sweeps_kernel(where, y, ya, yb, yc, yd, inv, kinv, out, x0, xs, xt, band):
+    ext, _, rows, lanes = inv.shape
     share = y.shape[2]
     per_plane = rows // share
     own = y.shape[0] // per_plane
     margin = (ext - own) // 2
     core = where[0]
-    inside = pl.ds(PAD, rows)
+    starts = (PAD, 2 * PAD + rows)
     zero = jnp.zeros((PAD, lanes), jnp.float32)
-
-    def clear(p, _):
+    row = lax.broadcasted_iota(jnp.int32, (2 * lanes, lanes), 0)
+    row = jnp.where(row >= lanes, row - lanes, row)
+    gap = jnp.abs(row - lax.broadcasted_iota(jnp.int32, (2 * lanes, lanes), 1))
+    band[...] = jnp.where(gap == 1, near_weight, jnp.where(gap == 2, far_weight, 0.0)).astype(
+        jnp.bfloat16
+    )
+
+    def clear(e, _):
         for x in (xs, xt):
-            for c in range(2):
-                x[c, p, :PAD] = zero
-                x[c, p, PAD + rows :] = zero
+            for r in (0, PAD + rows, 2 * (PAD + rows)):
+                x[e, pl.ds(r, PAD)] = zero
         return 0
 
     lax.fori_loop(0, ext, clear, 0)
@@ -273,20 +278,13 @@
     def fill(ref, base):
         def body(i, _):
             e = base + i
-
-            def comp(c):
-                return jnp.concatenate(
-                    [ref[per_plane * i + h, c].astype(jnp.float32) for h in range(per_plane)],
-                    axis=0,
-                )
-
-            re, im = comp(0), comp(1)
-            c0, c1, cq, ck = p0[e], p1[e], q[e], k[e]
-            x0_re = re * c0 + im * cq
-            x0_im = im * c1 - re * cq
-            x0[0, e], x0[1, e] = x0_re, x0_im
-            xs[0, e, inside], xs[1, e, inside] = x0_re, x0_im
-            kp[0, e], kp[1, e], kp[2, e] = ck * c0, ck * c1, ck * cq
+            for h in range(per_plane):
+                part = pl.ds(h * share, share)
+                re, im = (ref[per_plane * i + h, c].astype(jnp.float32) for c in range(2))
+                i0, i1, iq = (inv[e, c, part] for c in range(3))
+                for c, value in enumerate((re * i0 + im * iq, im * i1 - re * iq)):
+                    x0[e, c, part] = value
+                    xs[e, pl.ds(starts[c] + h * share, share)] = value
             return 0
 
         lax.fori_loop(0, ref.shape[0] // per_plane, body, 0)
@@ -298,38 +296,59 @@
     fill(yc, jnp.where(core == 0, 0, ext - far))
     fill(yd, jnp.where(core == 0, ext - far, 0))
 
-    masks = lane_masks((rows, lanes))
-    weights = sweep_weights()
-    for step, weight in enumerate(weights):
+    for step, weight in enumerate(sweep_weights()):
         src, dst = (xs, xt) if step % 2 == 0 else (xt, xs)
         edge = 2 * (step + 1)
-        last = step == len(weights) - 1
-
-        def value(e, src=src, weight=weight):
-            re, sum_re = neighbour_sum(src, (0,), e, rows, masks)
-            im, sum_im = neighbour_sum(src, (1,), e, rows, masks)
-            k0, k1, kq = kp[0, e], kp[1, e], kp[2, e]
-            new_re = (1.0 - weight) * re + weight * (x0[0, e] + k0 * sum_re + kq * sum_im)
-            new_im = (1.0 - weight) * im + weight * (x0[1, e] + k1 * sum_im - kq * sum_re)
-            return new_re, new_im
-
-        def store(e, pair, dst=dst, last=last):
-            for c in range(2):
-                if not last:
-                    dst[c, e, inside] = pair[c]
-                    continue
-                rounded = pair[c].astype(jnp.bfloat16)
-                for h in range(per_plane):
-                    out[per_plane * (e - margin) + h, c] = rounded[h * share : (h + 1) * share]
-
-        def sweep(i, _, edge=edge, value=value, store=store):
-            planes = [edge + UNROLL * i + r for r in range(UNROLL)]
-            pairs = [value(e) for e in planes]
-            for e, pair in zip(planes, pairs):
-                store(e, pair)
+        last = step == SWEEPS - 1
+        group = GROUPS[step]
+
+        def sweep(i, _, src=src, dst=dst, edge=edge, last=last, group=group, weight=weight):
+            first = edge + group * i
+            parts = []
+            for u in range(group):
+                for start in starts:
+                    value = src[first + u, pl.ds(start, rows)]
+                    high = value.astype(jnp.bfloat16)
+                    low = (value - high.astype(jnp.float32)).astype(jnp.bfloat16)
+                    parts.append(jnp.concatenate([high, low], axis=1))
+            along = jnp.dot(
+                jnp.concatenate(parts, axis=0), band[...], preferred_element_type=jnp.float32
+            )
+            for r in range(0, rows, CHUNK):
+                columns = [
+                    [src[first + d, pl.ds(start + r, CHUNK)] for d in range(-2, group + 2)]
+                    for start in starts
+                ]
+                for u in range(group):
+                    e = first + u
+
+                    def total(c):
+                        x = columns[c]
+                        side = [src[e, pl.ds(starts[c] + r + d, CHUNK)] for d in (1, -1, 2, -2)]
+                        near = (x[u + 3] + x[u + 1]) + (side[0] + side[1])
+                        far = (x[u + 4] + x[u]) + (side[2] + side[3])
+                        k = (2 * u + c) * rows + r
+                        return near_weight * near + far_weight * far + along[k : k + CHUNK]
+
+                    re, im = columns[0][u + 2], columns[1][u + 2]
+                    sum_re, sum_im = total(0), total(1)
+                    part = pl.ds(r, CHUNK)
+                    k0, k1, kq = (kinv[e, c, part] for c in range(3))
+                    pair = (
+                        (1.0 - weight) * re
+                        + weight * (x0[e, 0, part] + k0 * sum_re + kq * sum_im),
+                        (1.0 - weight) * im
+                        + weight * (x0[e, 1, part] + k1 * sum_im - kq * sum_re),
+                    )
+                    for c, value in enumerate(pair):
+                        if last:
+                            k = per_plane * (e - margin) + r // share
+                            out[k, c, pl.ds(r % share, CHUNK)] = value.astype(jnp.bfloat16)
+                        else:
+                            dst[e, pl.ds(starts[c] + r, CHUNK)] = value
             return 0
 
-        lax.fori_loop(0, (ext - 2 * edge) // UNROLL, sweep, 0)
+        lax.fori_loop(0, (ext - 2 * edge) // group, sweep, 0)
 
 
 def final_kernel(state, correction, out):
@@ -408,7 +427,11 @@
     part, edge = call(
         local_kernel,
         [((planes, rows, lanes), f32), ((4, rows, lanes), f32)],
-        [position, u, initial, forcing[0], kappa, reaction],
+        [position]
+        + [
+            pltpu.with_memory_space_constraint(v, pltpu.HBM)
+            for v in (u, initial, forcing[0], kappa, reaction)
+        ],
         [pltpu.VMEM((planes + 4, rows + 2 * PAD, lanes), f32)]
         + [pltpu.VMEM(*block)] * 5
         + [pltpu.SemaphoreType.DMA((5,))],
@@ -425,7 +448,7 @@
 
     fields = call(
         coefficient_kernel,
-        [((ext, rows, lanes), f32)] * 4,
+        [((ext, 3, rows, lanes), f32)] * 2,
         [where, kappa, initial, reaction, rim, inner],
         scalars=1,
     )
@@ -440,10 +463,10 @@
         [((slots, 2, share, lanes), bf16)],
         [where, y, ya, yb, yc, yd, *fields],
         [
-            pltpu.VMEM((2, ext, rows, lanes), f32),
-            pltpu.VMEM((3, ext, rows, lanes), f32),
-            pltpu.VMEM((2, ext, rows + 2 * PAD, lanes), f32),
-            pltpu.VMEM((2, ext, rows + 2 * PAD, lanes), f32),
+            pltpu.VMEM((ext, 2, rows + PAD, lanes), f32),
+            pltpu.VMEM((ext, 2 * rows + 3 * PAD, lanes), f32),
+            pltpu.VMEM((ext, 2 * rows + 3 * PAD, lanes), f32),
+            pltpu.VMEM((2 * lanes, lanes), bf16),
         ],
         scalars=1,
     )

time: 121 us -> 113 us (0.934)
  local copies, waits for them, and re-layouts: 5.55 us -> 0.8 us
  Pallas kernels: 18.7 us -> 14.9 us
    unnamed x18 -> x8, local copies, waits for them, and re-layouts: 4.76 us -> 0.02 us
    pallas_call x7, Pallas kernels: 18.7 us -> 14.9 us  [call(): pl.pallas_call(kernel, out_shape=outs, in_specs=[SMEM] * scalars + [HBM]...]
    ppermute x1, waiting for transfers between devices: 2.04 us -> 3.9 us  [iteration(): ya = lax.ppermute(y, CORE_SPACE, outer)]
  transfers between devices with their start and end apart: 10 -> 10, of which waited for: 3 -> 3; matrix products, arithmetic and copies ran while one was open for 1% -> 1% of each run, Pallas kernels for 3% -> 4%
where the time goes in v4:
time: 113 us; the launch traced here: 112 us
  blocking collectives  50.1 us (44%)
  starting transfers between devices  29.4 us (26%)
  waiting for transfers between devices  16.4 us (15%)
  Pallas kernels  14.9 us (13%)
    all_to_all x1, blocking collectives, iteration(): returned = lax.all_to_all(correction, TM, 0, 0, tiled=True)  19.4 us
    all_to_all x1, blocking collectives, iteration(): modes = lax.all_to_all(solved, CHIPS, 0, 0, tiled=True)  17.1 us
    pallas_call x7, Pallas kernels, call(): pl.pallas_call(kernel, out_shape=outs, in_specs=[SMEM] * scalars + [HBM]...  14.9 us
    all_to_all x1, blocking collectives, iteration(): y = lax.all_to_all(spectrum, CHIPS, 0, 0, tiled=True)  13.6 us
    all_to_all x1, waiting for transfers between devices, iteration(): lax.all_to_all(residual.reshape(members, share, lanes), TM, 0, 0, tiled=T...  11.7 us
    all_to_all x1, starting transfers between devices, iteration(): lax.all_to_all(residual.reshape(members, share, lanes), TM, 0, 0, tiled=T...  11 us
    ppermute x1, waiting for transfers between devices, iteration(): ya = lax.ppermute(y, CORE_SPACE, outer)  3.9 us
    ppermute x1, starting transfers between devices, iteration(): yc = lax.ppermute(jnp.where(first, y[-n:], y[:n]), CORE_SPACE, same)  3.75 us
  transfers between devices with their start and end apart: 10, of which 3 were waited for; matrix products, arithmetic and copies ran while one was open for 1% of the time, Pallas kernels for 4%

profile of v4, /device:TPU:16, one launch (start us, length us, event | category | flops | bytes accessed | tf_op | source)
XLA Modules:
  0.0 112.1 jit_solution(4054777944382751128)
XLA Ops:
  0.0 0.0 copy-start
  0.0 0.0 copy-start.1
  0.0 0.0 copy-start.2
  0.0 1.9 %collective-permute-start.2 = (bf16[16,64,128]{2,1,0:T(8,128)(2,1)}, bf16[16,64,128]{2,1,0:T(8,128)(2,1)S(1)}, u32[]{:S(2)}, u32[]{:S(2)}) collective-permute-start(bf16[16,64,128]{2,1,0:T(8,128)(2,1)} %bitcast.18), channel_id=1, source_target_pairs={{0,8},{8,16},{16,24},{24,32},{32,40},{40,48},{48,56},{56,64},{64,7... | collective-permute-start | bytes 786440 | tf_op jit(solution)/shard_map/ppermute | solution.py:419
  1.9 0.8 slice_bitcast_fusion
  2.7 3.4 %collective-permute-start = (bf16[2,64,128]{2,1,0:T(8,128)(2,1)S(1)}, bf16[2,64,128]{2,1,0:T(8,128)(2,1)S(1)}, u32[]{:S(2)}, u32[]{:S(2)}) collective-permute-start(bf16[2,64,128]{2,1,0:T(8,128)(2,1)S(1)} %get-tuple-element.14), channel_id=1, source_target_pairs={{0,1},{1,2},{2,3},{3,4},{4,5},{5,6},{6,7},{8,9},{9,10},{10,11},{11... | collective-permute-start | bytes 98312 | tf_op jit(solution)/shard_map/ppermute | solution.py:417
  6.1 3.3 %collective-permute-start.1 = (bf16[2,64,128]{2,1,0:T(8,128)(2,1)S(1)}, bf16[2,64,128]{2,1,0:T(8,128)(2,1)S(1)}, u32[]{:S(2)}, u32[]{:S(2)}) collective-permute-start(bf16[2,64,128]{2,1,0:T(8,128)(2,1)S(1)} %get-tuple-element.13), channel_id=1, source_target_pairs={{1,0},{2,1},{3,2},{4,3},{5,4},{6,5},{7,6},{9,8},{10,9},{11,10},{12... | collective-permute-start | bytes 98312 | tf_op jit(solution)/shard_map/ppermute | solution.py:418
  9.4 3.1 %shard_map.55 = (f32[16,64,128]{2,1,0:T(8,128)S(1)}, f32[4,64,128]{2,1,0:T(8,128)S(1)}) custom-call(s32[1]{0:T(128)} %bitcast.3.flag, bf16[16,64,128]{2,1,0:T(8,128)(2,1)} %bitcast.19, bf16[16,64,128]{2,1,0:T(8,128)(2,1)} %initial.1, bf16[16,64,128]{2,1,0:T(8,128)(2,1)} %bitcast.22, bf16[16,64,128]{2,1,0:T(8,128)(2,1)} %kappa.1, bf16[16,64,128]{2,1,0:T(8,128)(2,1)} %reaction.1), custom_call_target="tpu_custom_call" | custom-call | flops 20000000 | bytes 2500000 | tf_op jit(solution)/shard_map/pallas_call | solution.py:381
  12.6 0.0 collective-permute-done.lo
  12.6 0.7 collective-permute-done.1.hi
  13.3 0.0 collective-permute-done.2.before
  13.3 0.9 shard_map.56
  14.2 11.0 %all-to-all-start = ((bf16[32,32,128]{2,1,0:T(8,128)(2,1)}), bf16[32,32,128]{2,1,0:T(8,128)(2,1)S(1)}, u32[]{:S(2)}, u32[]{:S(2)}) async-start(bf16[32,32,128]{2,1,0:T(8,128)(2,1)} %bitcast.7), calls=%async_computation | async-start | bytes 524288 | tf_op jit(solution)/shard_map/all_to_all | solution.py:445
  25.2 0.0 copy-done
  25.2 0.0 copy-done.1
  25.2 0.0 copy-done.2
  25.2 0.1 pad_maximum_fusion
  25.3 2.9 %collective-permute-start.7 = (bf16[3,12,64,128]{3,2,1,0:T(8,128)(2,1)S(1)}, bf16[3,12,64,128]{3,2,1,0:T(8,128)(2,1)S(1)}, u32[]{:S(2)}, u32[]{:S(2)}) collective-permute-start(bf16[3,12,64,128]{3,2,1,0:T(8,128)(2,1)S(1)} %slice_select_fusion), channel_id=1, source_target_pairs={{8,1},{1,8},{9,2},{2,9},{10,3},{3,10},{11,4},{4,11},{12,5},{5,12},... | collective-permute-start | bytes 1769480 | tf_op jit(solution)/shard_map/ppermute | solution.py:422
  28.2 11.7 %all-to-all-done.r = bf16[32,32,128]{2,1,0:T(8,128)(2,1)S(1)} async-done(((bf16[32,32,128]{2,1,0:T(8,128)(2,1)}), bf16[32,32,128]{2,1,0:T(8,128)(2,1)S(1)}, u32[]{:S(2)}, u32[]{:S(2)}) %all-to-all-start) | async-done | bytes 262176 | tf_op jit(solution)/shard_map/all_to_all | solution.py:445
  39.9 0.2 shard_map.57
  40.1 13.6 %all_to_all.20.y = bf16[16,2,32,128]{3,2,1,0:T(8,128)(2,1)S(1)} all-to-all(bf16[16,2,32,128]{3,2,1,0:T(8,128)(2,1)S(1)} %shard_map.57), channel_id=1, replica_groups=mesh['tm_0'=2,'tm_1'=8,'tm_2'=2,'space'=8] {'tm_0','tm_1'}, dimensions={0} | all-to-all | bytes 524288 | tf_op jit(solution)/shard_map/all_to_all | solution.py:447
  53.7 1.9 %collective-permute-start.3 = (bf16[16,2,32,128]{3,2,1,0:T(8,128)(2,1)S(1)}, bf16[16,2,32,128]{3,2,1,0:T(8,128)(2,1)S(1)}, u32[]{:S(2)}, u32[]{:S(2)}) collective-permute-start(bf16[16,2,32,128]{3,2,1,0:T(8,128)(2,1)S(1)} %all_to_all.20.y), channel_id=1, source_target_pairs={{8,1},{1,8},{9,2},{2,9},{10,3},{3,10},{11,4},{4,11},{12,5},{5,12},... | collective-permute-start | bytes 786440 | tf_op jit(solution)/shard_map/ppermute | solution.py:457
  55.6 0.0 collective-permute-done.7.outer
  55.7 1.1 collective-permute-start.8
  56.8 3.8 %collective-permute-start.5 = (bf16[8,2,32,128]{3,2,1,0:T(8,128)(2,1)S(1)}, bf16[8,2,32,128]{3,2,1,0:T(8,128)(2,1)S(1)}, u32[]{:S(2)}, u32[]{:S(2)}) collective-permute-start(bf16[8,2,32,128]{3,2,1,0:T(8,128)(2,1)S(1)} %slice_select_fusion.3), channel_id=1, source_target_pairs={{0,1},{1,2},{2,3},{3,4},{4,5},{5,6},{6,7},{9,8},{10,9},{11,10},{12... | collective-permute-start | bytes 393224 | tf_op jit(solution)/shard_map/ppermute | solution.py:458
  60.5 0.1 collective-permute-start.4
  60.6 3.9 %collective-permute-done.3.ya = bf16[16,2,32,128]{3,2,1,0:T(8,128)(2,1)S(1)} collective-permute-done((bf16[16,2,32,128]{3,2,1,0:T(8,128)(2,1)S(1)}, bf16[16,2,32,128]{3,2,1,0:T(8,128)(2,1)S(1)}, u32[]{:S(2)}, u32[]{:S(2)}) %collective-permute-start.3) | collective-permute-done | bytes 262176 | tf_op jit(solution)/shard_map/ppermute | solution.py:457
  64.6 0.1 collective-permute-start.6
  64.7 0.1 pad_add_fusion.where
  64.8 0.0 collective-permute-done.8.inner
  64.8 1.6 %shard_map.58 = (f32[32,3,64,128]{3,2,1,0:T(8,128)S(1)}, f32[32,3,64,128]{3,2,1,0:T(8,128)S(1)}) custom-call(s32[2]{0:T(128)S(1)} %pad_add_fusion.where, bf16[16,64,128]{2,1,0:T(8,128)(2,1)S(1)} %copy-done.1, bf16[16,64,128]{2,1,0:T(8,128)(2,1)S(1)} %copy-done, bf16[16,64,128]{2,1,0:T(8,128)(2,1)S(1)} %copy-done.2, ...), custom_call_target="tpu_custom_call" | custom-call | tf_op jit(solution)/shard_map/pallas_call | solution.py:381
  66.3 0.0 collective-permute-done.5.yc
  66.3 0.0 collective-permute-done.4.yb
  66.4 0.0 collective-permute-done.6.yd
  66.4 0.0 copy-start.3
  66.4 8.1 %shard_map.59 = bf16[16,2,32,128]{3,2,1,0:T(8,128)(2,1)S(1)} custom-call(s32[2]{0:T(128)S(1)} %pad_add_fusion.where, bf16[16,2,32,128]{3,2,1,0:T(8,128)(2,1)S(1)} %all_to_all.20.y, bf16[16,2,32,128]{3,2,1,0:T(8,128)(2,1)S(1)} %collective-permute-done.3.ya, bf16[16,2,32,128]{3,2,1,0:T(8,128)(2,1)S(1)} %collective-permute-done.4.yb, ...), custom_call_target="tpu_custom_call" | custom-call | tf_op jit(solution)/shard_map/pallas_call | solution.py:381
  74.5 17.1 %all_to_all.21.s = bf16[16,2,32,128]{3,2,1,0:T(8,128)(2,1)S(1)} all-to-all(bf16[16,2,32,128]{3,2,1,0:T(8,128)(2,1)S(1)} %shard_map.59), channel_id=1, replica_groups=mesh['tm_0'=2,'tm_1'=8,'tm_2'=2,'space'=8] {'tm_0','tm_1'}, dimensions={0} | all-to-all | bytes 524288 | tf_op jit(solution)/shard_map/all_to_all | solution.py:473
  91.6 0.2 shard_map.60
  91.8 19.4 %all_to_all.22 = bf16[32,32,128]{2,1,0:T(8,128)(2,1)S(1)} all-to-all(bf16[32,32,128]{2,1,0:T(8,128)(2,1)S(1)} %shard_map.60), channel_id=1, replica_groups=mesh['tm_0'=2,'tm_1'=8,'tm_2'=2,'space'=8] {'tm_0','tm_1','tm_2'}, dimensions={0} | all-to-all | bytes 524288 | tf_op jit(solution)/shard_map/all_to_all | solution.py:475
  111.2 0.0 copy-done.3
  111.2 0.9 shard_map.61
  (4 shorter events, 0.1 us)
Async XLA Ops:
  0.0 25.2 %copy-start = (bf16[16,64,128]{2,1,0:T(8,128)(2,1)S(1)}, bf16[16,64,128]{2,1,0:T(8,128)(2,1)}, u32[]{:S(2)}) copy-start(bf16[16,64,128]{2,1,0:T(8,128)(2,1)} %initial.1) | copy-start | bytes 786436
  0.0 25.2 %copy-start.1 = (bf16[16,64,128]{2,1,0:T(8,128)(2,1)S(1)}, bf16[16,64,128]{2,1,0:T(8,128)(2,1)}, u32[]{:S(2)}) copy-start(bf16[16,64,128]{2,1,0:T(8,128)(2,1)} %kappa.1) | copy-start | bytes 786436
  0.0 25.2 %copy-start.2 = (bf16[16,64,128]{2,1,0:T(8,128)(2,1)S(1)}, bf16[16,64,128]{2,1,0:T(8,128)(2,1)}, u32[]{:S(2)}) copy-start(bf16[16,64,128]{2,1,0:T(8,128)(2,1)} %reaction.1) | copy-start | bytes 786436
  0.0 13.3 %collective-permute-start.2 = (bf16[16,64,128]{2,1,0:T(8,128)(2,1)}, bf16[16,64,128]{2,1,0:T(8,128)(2,1)S(1)}, u32[]{:S(2)}, u32[]{:S(2)}) collective-permute-start(bf16[16,64,128]{2,1,0:T(8,128)(2,1)} %bitcast.18), channel_id=1, source_target_pairs={{0,8},{8,16},{16,24},{24,32},{32,40},{40,48},{48,56},{56,64},{64,7... | collective-permute-start | bytes 786440 | tf_op jit(solution)/shard_map/ppermute | solution.py:419
  2.7 9.9 %collective-permute-start = (bf16[2,64,128]{2,1,0:T(8,128)(2,1)S(1)}, bf16[2,64,128]{2,1,0:T(8,128)(2,1)S(1)}, u32[]{:S(2)}, u32[]{:S(2)}) collective-permute-start(bf16[2,64,128]{2,1,0:T(8,128)(2,1)S(1)} %get-tuple-element.14), channel_id=1, source_target_pairs={{0,1},{1,2},{2,3},{3,4},{4,5},{5,6},{6,7},{8,9},{9,10},{10,11},{11... | collective-permute-start | bytes 98312 | tf_op jit(solution)/shard_map/ppermute | solution.py:417
  6.1 7.2 %collective-permute-start.1 = (bf16[2,64,128]{2,1,0:T(8,128)(2,1)S(1)}, bf16[2,64,128]{2,1,0:T(8,128)(2,1)S(1)}, u32[]{:S(2)}, u32[]{:S(2)}) collective-permute-start(bf16[2,64,128]{2,1,0:T(8,128)(2,1)S(1)} %get-tuple-element.13), channel_id=1, source_target_pairs={{1,0},{2,1},{3,2},{4,3},{5,4},{6,5},{7,6},{9,8},{10,9},{11,10},{12... | collective-permute-start | bytes 98312 | tf_op jit(solution)/shard_map/ppermute | solution.py:418
  14.2 25.7 %all-to-all-start = ((bf16[32,32,128]{2,1,0:T(8,128)(2,1)}), bf16[32,32,128]{2,1,0:T(8,128)(2,1)S(1)}, u32[]{:S(2)}, u32[]{:S(2)}) async-start(bf16[32,32,128]{2,1,0:T(8,128)(2,1)} %bitcast.7), calls=%async_computation | async-start | bytes 524288 | tf_op jit(solution)/shard_map/all_to_all | solution.py:445
  25.3 30.3 %collective-permute-start.7 = (bf16[3,12,64,128]{3,2,1,0:T(8,128)(2,1)S(1)}, bf16[3,12,64,128]{3,2,1,0:T(8,128)(2,1)S(1)}, u32[]{:S(2)}, u32[]{:S(2)}) collective-permute-start(bf16[3,12,64,128]{3,2,1,0:T(8,128)(2,1)S(1)} %slice_select_fusion), channel_id=1, source_target_pairs={{8,1},{1,8},{9,2},{2,9},{10,3},{3,10},{11,4},{4,11},{12,5},{5,12},... | collective-permute-start | bytes 1769480 | tf_op jit(solution)/shard_map/ppermute | solution.py:422
  53.7 10.8 %collective-permute-start.3 = (bf16[16,2,32,128]{3,2,1,0:T(8,128)(2,1)S(1)}, bf16[16,2,32,128]{3,2,1,0:T(8,128)(2,1)S(1)}, u32[]{:S(2)}, u32[]{:S(2)}) collective-permute-start(bf16[16,2,32,128]{3,2,1,0:T(8,128)(2,1)S(1)} %all_to_all.20.y), channel_id=1, source_target_pairs={{8,1},{1,8},{9,2},{2,9},{10,3},{3,10},{11,4},{4,11},{12,5},{5,12},... | collective-permute-start | bytes 786440 | tf_op jit(solution)/shard_map/ppermute | solution.py:457
  55.7 9.1 %collective-permute-start.8 = (bf16[3,4,64,128]{3,2,1,0:T(8,128)(2,1)S(1)}, bf16[3,4,64,128]{3,2,1,0:T(8,128)(2,1)S(1)}, u32[]{:S(2)}, u32[]{:S(2)}) collective-permute-start(bf16[3,4,64,128]{3,2,1,0:T(8,128)(2,1)S(1)} %slice_select_fusion.1), channel_id=1, source_target_pairs={{0,8},{1,9},{2,10},{3,11},{4,12},{5,13},{6,14},{7,15},{8,0},{9,1},... | collective-permute-start | bytes 589832 | tf_op jit(solution)/shard_map/ppermute | solution.py:424
  56.8 9.6 %collective-permute-start.5 = (bf16[8,2,32,128]{3,2,1,0:T(8,128)(2,1)S(1)}, bf16[8,2,32,128]{3,2,1,0:T(8,128)(2,1)S(1)}, u32[]{:S(2)}, u32[]{:S(2)}) collective-permute-start(bf16[8,2,32,128]{3,2,1,0:T(8,128)(2,1)S(1)} %slice_select_fusion.3), channel_id=1, source_target_pairs={{0,1},{1,2},{2,3},{3,4},{4,5},{5,6},{6,7},{9,8},{10,9},{11,10},{12... | collective-permute-start | bytes 393224 | tf_op jit(solution)/shard_map/ppermute | solution.py:458
  60.5 5.8 %collective-permute-start.4 = (bf16[16,2,32,128]{3,2,1,0:T(8,128)(2,1)S(1)}, bf16[16,2,32,128]{3,2,1,0:T(8,128)(2,1)S(1)}, u32[]{:S(2)}, u32[]{:S(2)}) collective-permute-start(bf16[16,2,32,128]{3,2,1,0:T(8,128)(2,1)S(1)} %all_to_all.20.y), channel_id=1, source_target_pairs={{0,8},{1,9},{2,10},{3,11},{4,12},{5,13},{6,14},{7,15},{8,0},{9,1},... | collective-permute-start | bytes 786440 | tf_op jit(solution)/shard_map/ppermute | solution.py:459
  64.6 1.8 %collective-permute-start.6 = (bf16[8,2,32,128]{3,2,1,0:T(8,128)(2,1)S(1)}, bf16[8,2,32,128]{3,2,1,0:T(8,128)(2,1)S(1)}, u32[]{:S(2)}, u32[]{:S(2)}) collective-permute-start(bf16[8,2,32,128]{3,2,1,0:T(8,128)(2,1)S(1)} %slice_select_fusion.2), channel_id=1, source_target_pairs={{0,8},{1,9},{2,10},{3,11},{4,12},{5,13},{6,14},{7,15},{8,0},{9,1},... | collective-permute-start | bytes 393224 | tf_op jit(solution)/shard_map/ppermute | solution.py:460
  66.4 44.8 %copy-start.3 = (bf16[1,16,64,128]{3,2,1,0:T(8,128)(2,1)S(1)}, bf16[1,16,64,128]{3,2,1,0:T(8,128)(2,1)}, u32[]{:S(2)}) copy-start(bf16[1,16,64,128]{3,2,1,0:T(8,128)(2,1)} %param.5) | copy-start | bytes 786436

commit v5 on v4

--- a/solution.py
+++ b/solution.py
@@ -11,7 +11,6 @@
 SWEEPS = 6
 STEPS = 32
 CHUNK = 16
-GROUPS = (14, 12, 10, 8, 12, 8)
 TM = ("tm_0", "tm_1", "tm_2")
 CHIPS = ("tm_0", "tm_1")
 CORE_SPACE = ("tm_2", "space")
@@ -30,6 +29,15 @@
     return [
         1.0 / (1.0 + 0.4 * math.cos(math.pi * (2 * k + 1) / (2 * SWEEPS))) for k in range(SWEEPS)
     ]
+
+
+def in_groups(count, body, group=4):
+    def step(i, _):
+        for u in range(group):
+            body(group * i + u)
+        return 0
+
+    lax.fori_loop(0, count // group, step, 0)
 
 
 def rotated(re, im, c, s):
@@ -105,7 +113,7 @@
     return centre, total
 
 
-def local_kernel(flag, u_hbm, initial_hbm, forcing_hbm, kappa_hbm, reaction_hbm, part, rim, *rest):
+def local_kernel(where, u_hbm, initial_hbm, forcing_hbm, kappa_hbm, reaction_hbm, part, rim, *rest):
     ext, u, initial, forcing, kappa, reaction, sems = rest
     planes, rows, lanes = u.shape
     pairs = ((u_hbm, u), (forcing_hbm, forcing), (kappa_hbm, kappa), (reaction_hbm, reaction))
@@ -115,27 +123,26 @@
         copy.start()
     zero = jnp.zeros((PAD, lanes), jnp.float32)
 
-    def clear(p, _):
+    def clear(p):
         ext[p, :PAD] = zero
         ext[p, PAD + rows :] = zero
-        return 0
-
-    lax.fori_loop(0, planes + 4, clear, 0)
+
+    in_groups(planes + 4, clear)
     blank = jnp.zeros((rows, lanes), jnp.float32)
     for p in (0, 1, planes + 2, planes + 3):
         ext[p, PAD : PAD + rows] = blank
-    for copy in copies:
+    copies[0].wait()
+
+    def fill(p):
+        ext[p + 2, PAD : PAD + rows] = u[p].astype(jnp.float32)
+
+    in_groups(planes, fill)
+    for copy in copies[1:]:
         copy.wait()
-
-    def fill(p, _):
-        ext[p + 2, PAD : PAD + rows] = u[p].astype(jnp.float32)
-        return 0
-
-    lax.fori_loop(0, planes, fill, 0)
     masks = lane_masks((rows, lanes))
-    first = flag[0] == 0
-
-    def one(p, _):
+    first = jnp.logical_and(where[0] == 0, where[1] == 0)
+
+    def one(p):
         centre, total = neighbour_sum(ext, (), p + 2, rows, masks)
         prior = jnp.where(first, initial[p].astype(jnp.float32), 0.0)
         part[p] = (
@@ -145,14 +152,13 @@
             - kappa[p].astype(jnp.float32) * (centre_weight * centre - total)
             - reaction[p].astype(jnp.float32) * centre * centre * centre
         )
-        return 0
-
-    lax.fori_loop(0, planes, one, 0)
+
+    in_groups(planes, one)
     for i, p in enumerate((0, 1, planes - 2, planes - 1)):
         rim[i] = kappa[p].astype(jnp.float32)
 
 
-def residual_kernel(part, rim, lo, hi, before, out):
+def residual_kernel(odd, part, rim, even_pair, odd_pair, before, out):
     planes, rows, _ = part.shape
     share = out.shape[2]
     per_plane = rows // share
@@ -164,12 +170,15 @@
         for piece in range(per_plane):
             out[per_plane * inner + piece, side] = value[piece * share : (piece + 1) * share]
 
-    def one(p, _):
+    for p in range(2, planes - 2):
         put(p, part[p] + before[p].astype(jnp.float32))
-        return 0
-
-    lax.fori_loop(2, planes - 2, one, 0)
-    l0, l1, h0, h1 = (v.astype(jnp.float32) for v in (lo[0], lo[1], hi[0], hi[1]))
+    upper = odd[0] == 1
+
+    def chosen(a, b, i):
+        return jnp.where(upper, a[i].astype(jnp.float32), b[i].astype(jnp.float32))
+
+    l0, l1 = (chosen(even_pair, odd_pair, i) for i in range(2))
+    h0, h1 = (chosen(odd_pair, even_pair, i) for i in range(2))
     edges = (
         (0, near_weight * l1 + far_weight * l0),
         (1, far_weight * l1),
@@ -234,21 +243,18 @@
             inv[e, c] = value
             kinv[e, c] = kv * value
 
-    def own(i, _):
+    def own(i):
         put(i + jnp.where(core == 0, wide, narrow), kappa[i], initial[i], reaction[i])
-        return 0
-
-    def far(i, _):
+
+    def far(i):
         put(i + jnp.where(core == 0, 0, planes + narrow), outer[0, i], outer[1, i], outer[2, i])
-        return 0
-
-    def close(i, _):
+
+    def close(i):
         put(i + jnp.where(core == 0, planes + wide, 0), inner[0, i], inner[1, i], inner[2, i])
-        return 0
-
-    lax.fori_loop(0, planes, own, 0)
-    lax.fori_loop(0, wide, far, 0)
-    lax.fori_loop(0, narrow, close, 0)
+
+    in_groups(planes, own, 2)
+    in_groups(wide, far, 2)
+    in_groups(narrow, close, 2)
 
 
 def sweeps_kernel(where, y, ya, yb, yc, yd, inv, kinv, out, x0, xs, xt, band):
@@ -267,16 +273,15 @@
         jnp.bfloat16
     )
 
-    def clear(e, _):
+    def clear(e):
         for x in (xs, xt):
             for r in (0, PAD + rows, 2 * (PAD + rows)):
                 x[e, pl.ds(r, PAD)] = zero
-        return 0
-
-    lax.fori_loop(0, ext, clear, 0)
+
+    in_groups(ext, clear)
 
     def fill(ref, base):
-        def body(i, _):
+        def body(i):
             e = base + i
             for h in range(per_plane):
                 part = pl.ds(h * share, share)
@@ -285,9 +290,8 @@
                 for c, value in enumerate((re * i0 + im * iq, im * i1 - re * iq)):
                     x0[e, c, part] = value
                     xs[e, pl.ds(starts[c] + h * share, share)] = value
-            return 0
-
-        lax.fori_loop(0, ref.shape[0] // per_plane, body, 0)
+
+        in_groups(ref.shape[0] // per_plane, body)
 
     far = yc.shape[0] // per_plane
     fill(y, margin)
@@ -300,10 +304,9 @@
         src, dst = (xs, xt) if step % 2 == 0 else (xt, xs)
         edge = 2 * (step + 1)
         last = step == SWEEPS - 1
-        group = GROUPS[step]
-
-        def sweep(i, _, src=src, dst=dst, edge=edge, last=last, group=group, weight=weight):
-            first = edge + group * i
+        group = ext - 2 * edge
+
+        def sweep(src=src, dst=dst, first=edge, last=last, group=group, weight=weight):
             parts = []
             for u in range(group):
                 for start in starts:
@@ -346,9 +349,8 @@
                             out[k, c, pl.ds(r % share, CHUNK)] = value.astype(jnp.bfloat16)
                         else:
                             dst[e, pl.ds(starts[c] + r, CHUNK)] = value
-            return 0
-
-        lax.fori_loop(0, (ext - 2 * edge) // group, sweep, 0)
+
+        sweep()
 
 
 def final_kernel(state, correction, out):
@@ -357,7 +359,7 @@
     per_plane = rows // share
     half = planes // 2
 
-    def one(p, _):
+    for p in range(planes):
         part, inner = p // half, p % half
         value = jnp.concatenate(
             [
@@ -367,9 +369,6 @@
             axis=0,
         )
         out[p] = (state[p].astype(jnp.float32) + value).astype(jnp.bfloat16)
-        return 0
-
-    lax.fori_loop(0, planes, one, 0)
 
 
 def call(kernel, shapes, inputs, scratch=(), scalars=0, anywhere=0, flops=None):
@@ -401,7 +400,6 @@
     narrow = wide - own
     ext = own + 2 * wide
     bf16, f32, i32 = jnp.bfloat16, jnp.float32, jnp.int32
-    position = lax.axis_index(TM).astype(i32).reshape(1)
     core = lax.axis_index("tm_2")
     slot = lax.axis_index(CHIPS)
     where = jnp.stack([core, slot]).astype(i32)
@@ -414,8 +412,12 @@
         outer += [(slabs + s, s + 1), (s + 1, slabs + s)]
     swap = [(i, slabs + i) for i in range(slabs)] + [(slabs + i, i) for i in range(slabs)]
     same = forward + [(slabs + s, slabs + t) for s, t in backward]
-    lo = lax.ppermute(u[planes - 2 :], "space", forward)
-    hi = lax.ppermute(u[:2], "space", backward)
+    odd = lax.axis_index("space") % 2
+    even_first = [p for s in range(0, slabs - 1, 2) for p in ((s, s + 1), (s + 1, s))]
+    odd_first = [p for s in range(1, slabs - 1, 2) for p in ((s, s + 1), (s + 1, s))]
+    low, high = u[:2], u[planes - 2 :]
+    even_pair = lax.ppermute(jnp.where(odd == 1, low, high), "space", even_first)
+    odd_pair = lax.ppermute(jnp.where(odd == 1, high, low), "space", odd_first)
     before = lax.ppermute(u, TM, [(i, i + 1) for i in range(members - 1)])
     coefs = jnp.stack([kappa, initial, reaction])
     rim = jnp.where(core == 0, coefs[:, :wide], coefs[:, planes - wide :])
@@ -427,7 +429,7 @@
     part, edge = call(
         local_kernel,
         [((planes, rows, lanes), f32), ((4, rows, lanes), f32)],
-        [position]
+        [where]
         + [
             pltpu.with_memory_space_constraint(v, pltpu.HBM)
             for v in (u, initial, forcing[0], kappa, reaction)
@@ -440,7 +442,10 @@
         flops=20_000_000,
     )
     (residual,) = call(
-        residual_kernel, [((slots, 2, share, lanes), bf16)], [part, edge, lo, hi, before]
+        residual_kernel,
+        [((slots, 2, share, lanes), bf16)],
+        [odd.astype(i32).reshape(1), part, edge, even_pair, odd_pair, before],
+        scalars=1,
     )
     cells = lax.all_to_all(residual.reshape(members, share, lanes), TM, 0, 0, tiled=True)
     (spectrum,) = call(forward_kernel, [((slots, 2, share, lanes), bf16)], [cells])

time: 113 us -> 108 us (0.956)
  starting transfers between devices: 29.4 us -> 25 us
  Pallas kernels: 14.9 us -> 12.9 us
  waiting for transfers between devices: 16.4 us -> 18.4 us
    pallas_call x7, Pallas kernels: 14.9 us -> 12.9 us  [call(): pl.pallas_call(kernel, out_shape=outs, in_specs=[SMEM] * scalars + [HBM]...]
    ppermute x2, starting transfers between devices: 6.73 us -> 4.73 us  [the longest x1 3.28 us: iteration(): odd_pair = lax.ppermute(jnp.where(odd == 1, high, low), 'space', odd_first)]
    all_to_all x1, starting transfers between devices: 11 us -> 8.97 us  [iteration(): lax.all_to_all(residual.reshape(members, share, lanes), TM, 0, 0, tiled=T...]
    ppermute x2, waiting for transfers between devices: 0.75 us -> 2.72 us  [the longest x1 2.72 us: iteration(): lax.ppermute(jnp.where(odd == 1, low, high), 'space', even_first)]
where the time goes in v5:
time: 108 us
  blocking collectives  50.2 us (46%)
  starting transfers between devices  25 us (23%)
  waiting for transfers between devices  18.4 us (17%)
  Pallas kernels  12.9 us (12%)
    all_to_all x1, blocking collectives, iteration(): returned = lax.all_to_all(correction, TM, 0, 0, tiled=True)  19.4 us
    all_to_all x1, blocking collectives, iteration(): modes = lax.all_to_all(solved, CHIPS, 0, 0, tiled=True)  17.2 us
    all_to_all x1, blocking collectives, iteration(): y = lax.all_to_all(spectrum, CHIPS, 0, 0, tiled=True)  13.6 us
    pallas_call x7, Pallas kernels, call(): pl.pallas_call(kernel, out_shape=outs, in_specs=[SMEM] * scalars + [HBM]...  12.9 us
    all_to_all x1, waiting for transfers between devices, iteration(): lax.all_to_all(residual.reshape(members, share, lanes), TM, 0, 0, tiled=T...  12 us
    all_to_all x1, starting transfers between devices, iteration(): lax.all_to_all(residual.reshape(members, share, lanes), TM, 0, 0, tiled=T...  8.97 us
    ppermute x1, starting transfers between devices, iteration(): yc = lax.ppermute(jnp.where(first, y[-n:], y[:n]), CORE_SPACE, same)  3.89 us
    ppermute x1, waiting for transfers between devices, iteration(): ya = lax.ppermute(y, CORE_SPACE, outer)  3.64 us
  transfers between devices with their start and end apart: 10, of which 3 were waited for; matrix products, arithmetic and copies ran while one was open for 1% of the time, Pallas kernels for 4%

profile of v5, /device:TPU:16, one launch (start us, length us, event | category | flops | bytes accessed | tf_op | source)
XLA Modules:
  0.0 107.7 jit_solution(16163658625098427657)
XLA Ops:
  0.0 0.0 copy-start.2
  0.0 0.0 copy-start.1
  0.0 0.0 copy-start
  0.0 1.9 %collective-permute-start.2 = (bf16[16,64,128]{2,1,0:T(8,128)(2,1)}, bf16[16,64,128]{2,1,0:T(8,128)(2,1)S(1)}, u32[]{:S(2)}, u32[]{:S(2)}) collective-permute-start(bf16[16,64,128]{2,1,0:T(8,128)(2,1)} %bitcast.18), channel_id=1, source_target_pairs={{0,8},{8,16},{16,24},{24,32},{32,40},{40,48},{48,56},{56,64},{64,7... | collective-permute-start | bytes 786440 | tf_op jit(solution)/shard_map/ppermute | solution.py:421
  1.9 0.8 select_bitcast_fusion
  2.7 3.3 %collective-permute-start.1 = (bf16[2,64,128]{2,1,0:T(8,128)(2,1)S(1)}, bf16[2,64,128]{2,1,0:T(8,128)(2,1)S(1)}, u32[]{:S(2)}, u32[]{:S(2)}) collective-permute-start(bf16[2,64,128]{2,1,0:T(8,128)(2,1)S(1)} %get-tuple-element.13), channel_id=1, source_target_pairs={{1,2},{2,1},{3,4},{4,3},{5,6},{6,5},{9,10},{10,9},{11,12},{12,11},... | collective-permute-start | bytes 98312 | tf_op jit(solution)/shard_map/ppermute | solution.py:420
  6.0 1.5 %collective-permute-start = (bf16[2,64,128]{2,1,0:T(8,128)(2,1)S(1)}, bf16[2,64,128]{2,1,0:T(8,128)(2,1)S(1)}, u32[]{:S(2)}, u32[]{:S(2)}) collective-permute-start(bf16[2,64,128]{2,1,0:T(8,128)(2,1)S(1)} %get-tuple-element.14), channel_id=1, source_target_pairs={{0,1},{1,0},{2,3},{3,2},{4,5},{5,4},{6,7},{7,6},{8,9},{9,8},{10,11... | collective-permute-start | bytes 98312 | tf_op jit(solution)/shard_map/ppermute | solution.py:419
  7.4 0.1 pad_add_fusion.where
  7.5 2.7 %shard_map.55 = (f32[16,64,128]{2,1,0:T(8,128)S(1)}, f32[4,64,128]{2,1,0:T(8,128)S(1)}) custom-call(s32[2]{0:T(128)S(1)} %pad_add_fusion.where, bf16[16,64,128]{2,1,0:T(8,128)(2,1)} %bitcast.19, bf16[16,64,128]{2,1,0:T(8,128)(2,1)} %initial.1, bf16[16,64,128]{2,1,0:T(8,128)(2,1)} %bitcast.22, bf16[16,64,128]{2,1,0:T(8,128)(2,1)} %kappa.1, ...), custom_call_target="tpu_custom_call" | custom-call | flops 20000000 | bytes 2500000 | tf_op jit(solution)/shard_map/pallas_call | solution.py:380
  10.2 0.0 collective-permute-done.1.odd_pair
  10.2 2.7 %collective-permute-done.even_pair = bf16[2,64,128]{2,1,0:T(8,128)(2,1)S(1)} collective-permute-done((bf16[2,64,128]{2,1,0:T(8,128)(2,1)S(1)}, bf16[2,64,128]{2,1,0:T(8,128)(2,1)S(1)}, u32[]{:S(2)}, u32[]{:S(2)}) %collective-permute-start) | collective-permute-done | bytes 32800 | tf_op jit(solution)/shard_map/ppermute | solution.py:419
  13.0 0.0 collective-permute-done.2.before
  13.0 0.8 shard_map.56
  13.8 9.0 %all-to-all-start = ((bf16[32,32,128]{2,1,0:T(8,128)(2,1)}), bf16[32,32,128]{2,1,0:T(8,128)(2,1)S(1)}, u32[]{:S(2)}, u32[]{:S(2)}) async-start(bf16[32,32,128]{2,1,0:T(8,128)(2,1)} %bitcast.7), calls=%async_computation | async-start | bytes 524288 | tf_op jit(solution)/shard_map/all_to_all | solution.py:450
  22.7 0.0 copy-done.2
  22.8 0.0 copy-done.1
  22.8 0.0 copy-done
  22.8 0.1 pad_maximum_fusion
  22.9 2.5 %collective-permute-start.7 = (bf16[3,12,64,128]{3,2,1,0:T(8,128)(2,1)S(1)}, bf16[3,12,64,128]{3,2,1,0:T(8,128)(2,1)S(1)}, u32[]{:S(2)}, u32[]{:S(2)}) collective-permute-start(bf16[3,12,64,128]{3,2,1,0:T(8,128)(2,1)S(1)} %slice_select_fusion), channel_id=1, source_target_pairs={{8,1},{1,8},{9,2},{2,9},{10,3},{3,10},{11,4},{4,11},{12,5},{5,12},... | collective-permute-start | bytes 1769480 | tf_op jit(solution)/shard_map/ppermute | solution.py:424
  25.4 12.0 %all-to-all-done.r = bf16[32,32,128]{2,1,0:T(8,128)(2,1)S(1)} async-done(((bf16[32,32,128]{2,1,0:T(8,128)(2,1)}), bf16[32,32,128]{2,1,0:T(8,128)(2,1)S(1)}, u32[]{:S(2)}, u32[]{:S(2)}) %all-to-all-start) | async-done | bytes 262176 | tf_op jit(solution)/shard_map/all_to_all | solution.py:450
  37.5 0.2 shard_map.57
  37.7 13.6 %all_to_all.20.y = bf16[16,2,32,128]{3,2,1,0:T(8,128)(2,1)S(1)} all-to-all(bf16[16,2,32,128]{3,2,1,0:T(8,128)(2,1)S(1)} %shard_map.57), channel_id=1, replica_groups=mesh['tm_0'=2,'tm_1'=8,'tm_2'=2,'space'=8] {'tm_0','tm_1'}, dimensions={0} | all-to-all | bytes 524288 | tf_op jit(solution)/shard_map/all_to_all | solution.py:452
  51.3 1.9 %collective-permute-start.3 = (bf16[16,2,32,128]{3,2,1,0:T(8,128)(2,1)S(1)}, bf16[16,2,32,128]{3,2,1,0:T(8,128)(2,1)S(1)}, u32[]{:S(2)}, u32[]{:S(2)}) collective-permute-start(bf16[16,2,32,128]{3,2,1,0:T(8,128)(2,1)S(1)} %all_to_all.20.y), channel_id=1, source_target_pairs={{8,1},{1,8},{9,2},{2,9},{10,3},{3,10},{11,4},{4,11},{12,5},{5,12},... | collective-permute-start | bytes 786440 | tf_op jit(solution)/shard_map/ppermute | solution.py:462
  53.2 0.0 collective-permute-done.7.outer
  53.3 0.7 collective-permute-start.8
  54.0 3.9 %collective-permute-start.5 = (bf16[8,2,32,128]{3,2,1,0:T(8,128)(2,1)S(1)}, bf16[8,2,32,128]{3,2,1,0:T(8,128)(2,1)S(1)}, u32[]{:S(2)}, u32[]{:S(2)}) collective-permute-start(bf16[8,2,32,128]{3,2,1,0:T(8,128)(2,1)S(1)} %slice_select_fusion.3), channel_id=1, source_target_pairs={{0,1},{1,2},{2,3},{3,4},{4,5},{5,6},{6,7},{9,8},{10,9},{11,10},{12... | collective-permute-start | bytes 393224 | tf_op jit(solution)/shard_map/ppermute | solution.py:463
  57.9 0.2 collective-permute-start.4
  58.2 3.6 %collective-permute-done.3.ya = bf16[16,2,32,128]{3,2,1,0:T(8,128)(2,1)S(1)} collective-permute-done((bf16[16,2,32,128]{3,2,1,0:T(8,128)(2,1)S(1)}, bf16[16,2,32,128]{3,2,1,0:T(8,128)(2,1)S(1)}, u32[]{:S(2)}, u32[]{:S(2)}) %collective-permute-start.3) | collective-permute-done | bytes 262176 | tf_op jit(solution)/shard_map/ppermute | solution.py:462
  61.8 0.1 collective-permute-start.6
  61.9 0.0 collective-permute-done.8.inner
  61.9 1.4 %shard_map.58 = (f32[32,3,64,128]{3,2,1,0:T(8,128)S(1)}, f32[32,3,64,128]{3,2,1,0:T(8,128)S(1)}) custom-call(s32[2]{0:T(128)S(1)} %pad_add_fusion.where, bf16[16,64,128]{2,1,0:T(8,128)(2,1)S(1)} %copy-done.1, bf16[16,64,128]{2,1,0:T(8,128)(2,1)S(1)} %copy-done, bf16[16,64,128]{2,1,0:T(8,128)(2,1)S(1)} %copy-done.2, ...), custom_call_target="tpu_custom_call" | custom-call | tf_op jit(solution)/shard_map/pallas_call | solution.py:380
  63.4 0.0 collective-permute-done.5.yc
  63.4 0.0 collective-permute-done.4.yb
  63.4 0.0 collective-permute-done.6.yd
  63.4 0.0 copy-start.3
  63.4 6.8 %shard_map.59 = bf16[16,2,32,128]{3,2,1,0:T(8,128)(2,1)S(1)} custom-call(s32[2]{0:T(128)S(1)} %pad_add_fusion.where, bf16[16,2,32,128]{3,2,1,0:T(8,128)(2,1)S(1)} %all_to_all.20.y, bf16[16,2,32,128]{3,2,1,0:T(8,128)(2,1)S(1)} %collective-permute-done.3.ya, bf16[16,2,32,128]{3,2,1,0:T(8,128)(2,1)S(1)} %collective-permute-done.4.yb, ...), custom_call_target="tpu_custom_call" | custom-call | tf_op jit(solution)/shard_map/pallas_call | solution.py:380
  70.2 17.2 %all_to_all.21.s = bf16[16,2,32,128]{3,2,1,0:T(8,128)(2,1)S(1)} all-to-all(bf16[16,2,32,128]{3,2,1,0:T(8,128)(2,1)S(1)} %shard_map.59), channel_id=1, replica_groups=mesh['tm_0'=2,'tm_1'=8,'tm_2'=2,'space'=8] {'tm_0','tm_1'}, dimensions={0} | all-to-all | bytes 524288 | tf_op jit(solution)/shard_map/all_to_all | solution.py:478
  87.4 0.2 shard_map.60
  87.6 19.4 %all_to_all.22 = bf16[32,32,128]{2,1,0:T(8,128)(2,1)S(1)} all-to-all(bf16[32,32,128]{2,1,0:T(8,128)(2,1)S(1)} %shard_map.60), channel_id=1, replica_groups=mesh['tm_0'=2,'tm_1'=8,'tm_2'=2,'space'=8] {'tm_0','tm_1','tm_2'}, dimensions={0} | all-to-all | bytes 524288 | tf_op jit(solution)/shard_map/all_to_all | solution.py:480
  106.9 0.0 copy-done.3
  106.9 0.8 shard_map.61
  (4 shorter events, 0.1 us)
Async XLA Ops:
  0.0 22.7 %copy-start.2 = (bf16[16,64,128]{2,1,0:T(8,128)(2,1)S(1)}, bf16[16,64,128]{2,1,0:T(8,128)(2,1)}, u32[]{:S(2)}) copy-start(bf16[16,64,128]{2,1,0:T(8,128)(2,1)} %reaction.1) | copy-start | bytes 786436
  0.0 22.8 %copy-start.1 = (bf16[16,64,128]{2,1,0:T(8,128)(2,1)S(1)}, bf16[16,64,128]{2,1,0:T(8,128)(2,1)}, u32[]{:S(2)}) copy-start(bf16[16,64,128]{2,1,0:T(8,128)(2,1)} %kappa.1) | copy-start | bytes 786436
  0.0 22.8 %copy-start = (bf16[16,64,128]{2,1,0:T(8,128)(2,1)S(1)}, bf16[16,64,128]{2,1,0:T(8,128)(2,1)}, u32[]{:S(2)}) copy-start(bf16[16,64,128]{2,1,0:T(8,128)(2,1)} %initial.1) | copy-start | bytes 786436
  0.0 13.0 %collective-permute-start.2 = (bf16[16,64,128]{2,1,0:T(8,128)(2,1)}, bf16[16,64,128]{2,1,0:T(8,128)(2,1)S(1)}, u32[]{:S(2)}, u32[]{:S(2)}) collective-permute-start(bf16[16,64,128]{2,1,0:T(8,128)(2,1)} %bitcast.18), channel_id=1, source_target_pairs={{0,8},{8,16},{16,24},{24,32},{32,40},{40,48},{48,56},{56,64},{64,7... | collective-permute-start | bytes 786440 | tf_op jit(solution)/shard_map/ppermute | solution.py:421
  2.7 7.5 %collective-permute-start.1 = (bf16[2,64,128]{2,1,0:T(8,128)(2,1)S(1)}, bf16[2,64,128]{2,1,0:T(8,128)(2,1)S(1)}, u32[]{:S(2)}, u32[]{:S(2)}) collective-permute-start(bf16[2,64,128]{2,1,0:T(8,128)(2,1)S(1)} %get-tuple-element.13), channel_id=1, source_target_pairs={{1,2},{2,1},{3,4},{4,3},{5,6},{6,5},{9,10},{10,9},{11,12},{12,11},... | collective-permute-start | bytes 98312 | tf_op jit(solution)/shard_map/ppermute | solution.py:420
  6.0 7.0 %collective-permute-start = (bf16[2,64,128]{2,1,0:T(8,128)(2,1)S(1)}, bf16[2,64,128]{2,1,0:T(8,128)(2,1)S(1)}, u32[]{:S(2)}, u32[]{:S(2)}) collective-permute-start(bf16[2,64,128]{2,1,0:T(8,128)(2,1)S(1)} %get-tuple-element.14), channel_id=1, source_target_pairs={{0,1},{1,0},{2,3},{3,2},{4,5},{5,4},{6,7},{7,6},{8,9},{9,8},{10,11... | collective-permute-start | bytes 98312 | tf_op jit(solution)/shard_map/ppermute | solution.py:419
  13.8 23.7 %all-to-all-start = ((bf16[32,32,128]{2,1,0:T(8,128)(2,1)}), bf16[32,32,128]{2,1,0:T(8,128)(2,1)S(1)}, u32[]{:S(2)}, u32[]{:S(2)}) async-start(bf16[32,32,128]{2,1,0:T(8,128)(2,1)} %bitcast.7), calls=%async_computation | async-start | bytes 524288 | tf_op jit(solution)/shard_map/all_to_all | solution.py:450
  22.9 30.3 %collective-permute-start.7 = (bf16[3,12,64,128]{3,2,1,0:T(8,128)(2,1)S(1)}, bf16[3,12,64,128]{3,2,1,0:T(8,128)(2,1)S(1)}, u32[]{:S(2)}, u32[]{:S(2)}) collective-permute-start(bf16[3,12,64,128]{3,2,1,0:T(8,128)(2,1)S(1)} %slice_select_fusion), channel_id=1, source_target_pairs={{8,1},{1,8},{9,2},{2,9},{10,3},{3,10},{11,4},{4,11},{12,5},{5,12},... | collective-permute-start | bytes 1769480 | tf_op jit(solution)/shard_map/ppermute | solution.py:424
  51.3 10.5 %collective-permute-start.3 = (bf16[16,2,32,128]{3,2,1,0:T(8,128)(2,1)S(1)}, bf16[16,2,32,128]{3,2,1,0:T(8,128)(2,1)S(1)}, u32[]{:S(2)}, u32[]{:S(2)}) collective-permute-start(bf16[16,2,32,128]{3,2,1,0:T(8,128)(2,1)S(1)} %all_to_all.20.y), channel_id=1, source_target_pairs={{8,1},{1,8},{9,2},{2,9},{10,3},{3,10},{11,4},{4,11},{12,5},{5,12},... | collective-permute-start | bytes 786440 | tf_op jit(solution)/shard_map/ppermute | solution.py:462
  53.3 8.6 %collective-permute-start.8 = (bf16[3,4,64,128]{3,2,1,0:T(8,128)(2,1)S(1)}, bf16[3,4,64,128]{3,2,1,0:T(8,128)(2,1)S(1)}, u32[]{:S(2)}, u32[]{:S(2)}) collective-permute-start(bf16[3,4,64,128]{3,2,1,0:T(8,128)(2,1)S(1)} %slice_select_fusion.1), channel_id=1, source_target_pairs={{0,8},{1,9},{2,10},{3,11},{4,12},{5,13},{6,14},{7,15},{8,0},{9,1},... | collective-permute-start | bytes 589832 | tf_op jit(solution)/shard_map/ppermute | solution.py:426
  54.0 9.3 %collective-permute-start.5 = (bf16[8,2,32,128]{3,2,1,0:T(8,128)(2,1)S(1)}, bf16[8,2,32,128]{3,2,1,0:T(8,128)(2,1)S(1)}, u32[]{:S(2)}, u32[]{:S(2)}) collective-permute-start(bf16[8,2,32,128]{3,2,1,0:T(8,128)(2,1)S(1)} %slice_select_fusion.3), channel_id=1, source_target_pairs={{0,1},{1,2},{2,3},{3,4},{4,5},{5,6},{6,7},{9,8},{10,9},{11,10},{12... | collective-permute-start | bytes 393224 | tf_op jit(solution)/shard_map/ppermute | solution.py:463
  57.9 5.4 %collective-permute-start.4 = (bf16[16,2,32,128]{3,2,1,0:T(8,128)(2,1)S(1)}, bf16[16,2,32,128]{3,2,1,0:T(8,128)(2,1)S(1)}, u32[]{:S(2)}, u32[]{:S(2)}) collective-permute-start(bf16[16,2,32,128]{3,2,1,0:T(8,128)(2,1)S(1)} %all_to_all.20.y), channel_id=1, source_target_pairs={{0,8},{1,9},{2,10},{3,11},{4,12},{5,13},{6,14},{7,15},{8,0},{9,1},... | collective-permute-start | bytes 786440 | tf_op jit(solution)/shard_map/ppermute | solution.py:464
  61.8 1.6 %collective-permute-start.6 = (bf16[8,2,32,128]{3,2,1,0:T(8,128)(2,1)S(1)}, bf16[8,2,32,128]{3,2,1,0:T(8,128)(2,1)S(1)}, u32[]{:S(2)}, u32[]{:S(2)}) collective-permute-start(bf16[8,2,32,128]{3,2,1,0:T(8,128)(2,1)S(1)} %slice_select_fusion.2), channel_id=1, source_target_pairs={{0,8},{1,9},{2,10},{3,11},{4,12},{5,13},{6,14},{7,15},{8,0},{9,1},... | collective-permute-start | bytes 393224 | tf_op jit(solution)/shard_map/ppermute | solution.py:465
  63.4 43.5 %copy-start.3 = (bf16[1,16,64,128]{3,2,1,0:T(8,128)(2,1)S(1)}, bf16[1,16,64,128]{3,2,1,0:T(8,128)(2,1)}, u32[]{:S(2)}) copy-start(bf16[1,16,64,128]{3,2,1,0:T(8,128)(2,1)} %param.5) | copy-start | bytes 786436

commit v6 on v5

--- a/solution.py
+++ b/solution.py
@@ -11,6 +11,7 @@
 SWEEPS = 6
 STEPS = 32
 CHUNK = 16
+EARLY = 3
 TM = ("tm_0", "tm_1", "tm_2")
 CHIPS = ("tm_0", "tm_1")
 CORE_SPACE = ("tm_2", "space")
@@ -218,6 +219,10 @@
             out[n, part] = (values[n] * scale).astype(jnp.bfloat16)
 
 
+def mirrored(core, i, count):
+    return jnp.where(core == 0, i, count - 1 - i)
+
+
 def coefficient_kernel(where, kappa, initial, reaction, outer, inner, inv, kinv):
     planes = kappa.shape[0]
     wide, narrow = outer.shape[1], inner.shape[1]
@@ -244,113 +249,141 @@
             kinv[e, c] = kv * value
 
     def own(i):
-        put(i + jnp.where(core == 0, wide, narrow), kappa[i], initial[i], reaction[i])
+        put(wide + mirrored(core, i, planes), kappa[i], initial[i], reaction[i])
 
     def far(i):
-        put(i + jnp.where(core == 0, 0, planes + narrow), outer[0, i], outer[1, i], outer[2, i])
+        put(mirrored(core, i, wide), outer[0, i], outer[1, i], outer[2, i])
 
     def close(i):
-        put(i + jnp.where(core == 0, planes + wide, 0), inner[0, i], inner[1, i], inner[2, i])
+        put(wide + planes + mirrored(core, i, narrow), inner[0, i], inner[1, i], inner[2, i])
 
     in_groups(planes, own, 2)
     in_groups(wide, far, 2)
     in_groups(narrow, close, 2)
 
 
-def sweeps_kernel(where, y, ya, yb, yc, yd, inv, kinv, out, x0, xs, xt, band):
-    ext, _, rows, lanes = inv.shape
-    share = y.shape[2]
+def row_starts(rows):
+    return (PAD, 2 * PAD + rows)
+
+
+def write_band(band):
+    double, lanes = band.shape
+    row = lax.broadcasted_iota(jnp.int32, (double, lanes), 0)
+    row = jnp.where(row >= lanes, row - lanes, row)
+    gap = jnp.abs(row - lax.broadcasted_iota(jnp.int32, (double, lanes), 1))
+    weights = jnp.where(gap == 1, near_weight, jnp.where(gap == 2, far_weight, 0.0))
+    band[...] = weights.astype(jnp.bfloat16)
+
+
+def fill(core, ref, base, inv, x0, x):
+    share, rows = ref.shape[2], inv.shape[2]
     per_plane = rows // share
-    own = y.shape[0] // per_plane
-    margin = (ext - own) // 2
+    count = ref.shape[0] // per_plane
+    starts = row_starts(rows)
+
+    def body(i):
+        e = base + mirrored(core, i, count)
+        for h in range(per_plane):
+            part = pl.ds(h * share, share)
+            re, im = (ref[per_plane * i + h, c].astype(jnp.float32) for c in range(2))
+            i0, i1, iq = (inv[e, c, part] for c in range(3))
+            for c, value in enumerate((re * i0 + im * iq, im * i1 - re * iq)):
+                x0[e, c, part] = value
+                x[e, pl.ds(starts[c] + h * share, share)] = value
+
+    in_groups(count, body)
+
+
+def sweep(step, first, stop, x0, kinv, band, buffers, emit=None):
+    rows = kinv.shape[2]
+    starts = row_starts(rows)
+    src, dst = buffers[step % 2], buffers[(step + 1) % 2]
+    weight = sweep_weights()[step]
+    group = stop - first
+    parts = []
+    for u in range(group):
+        for start in starts:
+            value = src[first + u, pl.ds(start, rows)]
+            high = value.astype(jnp.bfloat16)
+            low = (value - high.astype(jnp.float32)).astype(jnp.bfloat16)
+            parts.append(jnp.concatenate([high, low], axis=1))
+    along = jnp.dot(jnp.concatenate(parts, axis=0), band[...], preferred_element_type=jnp.float32)
+    for r in range(0, rows, CHUNK):
+        columns = [
+            [src[first + d, pl.ds(start + r, CHUNK)] for d in range(-2, group + 2)]
+            for start in starts
+        ]
+        for u in range(group):
+            e = first + u
+
+            def total(c):
+                x = columns[c]
+                side = [src[e, pl.ds(starts[c] + r + d, CHUNK)] for d in (1, -1, 2, -2)]
+                near = (x[u + 3] + x[u + 1]) + (side[0] + side[1])
+                far = (x[u + 4] + x[u]) + (side[2] + side[3])
+                k = (2 * u + c) * rows + r
+                return near_weight * near + far_weight * far + along[k : k + CHUNK]
+
+            re, im = columns[0][u + 2], columns[1][u + 2]
+            sum_re, sum_im = total(0), total(1)
+            part = pl.ds(r, CHUNK)
+            k0, k1, kq = (kinv[e, c, part] for c in range(3))
+            pair = (
+                (1.0 - weight) * re + weight * (x0[e, 0, part] + k0 * sum_re + kq * sum_im),
+                (1.0 - weight) * im + weight * (x0[e, 1, part] + k1 * sum_im - kq * sum_re),
+            )
+            for c, value in enumerate(pair):
+                if emit is None:
+                    dst[e, pl.ds(starts[c] + r, CHUNK)] = value
+                else:
+                    emit(e, r, c, value)
+
+
+def inside_kernel(where, y, yb, inv, kinv, x0, xs, xt, band):
+    rows, lanes = inv.shape[2:]
+    own = y.shape[0] * y.shape[2] // rows
     core = where[0]
-    starts = (PAD, 2 * PAD + rows)
+    base = (inv.shape[0] - own) // 2
+    write_band(band)
     zero = jnp.zeros((PAD, lanes), jnp.float32)
-    row = lax.broadcasted_iota(jnp.int32, (2 * lanes, lanes), 0)
-    row = jnp.where(row >= lanes, row - lanes, row)
-    gap = jnp.abs(row - lax.broadcasted_iota(jnp.int32, (2 * lanes, lanes), 1))
-    band[...] = jnp.where(gap == 1, near_weight, jnp.where(gap == 2, far_weight, 0.0)).astype(
-        jnp.bfloat16
-    )
 
     def clear(e):
         for x in (xs, xt):
             for r in (0, PAD + rows, 2 * (PAD + rows)):
                 x[e, pl.ds(r, PAD)] = zero
 
-    in_groups(ext, clear)
-
-    def fill(ref, base):
-        def body(i):
-            e = base + i
-            for h in range(per_plane):
-                part = pl.ds(h * share, share)
-                re, im = (ref[per_plane * i + h, c].astype(jnp.float32) for c in range(2))
-                i0, i1, iq = (inv[e, c, part] for c in range(3))
-                for c, value in enumerate((re * i0 + im * iq, im * i1 - re * iq)):
-                    x0[e, c, part] = value
-                    xs[e, pl.ds(starts[c] + h * share, share)] = value
-
-        in_groups(ref.shape[0] // per_plane, body)
-
-    far = yc.shape[0] // per_plane
-    fill(y, margin)
-    fill(ya, jnp.where(core == 0, far, margin + own))
-    fill(yb, jnp.where(core == 0, margin + own, far))
-    fill(yc, jnp.where(core == 0, 0, ext - far))
-    fill(yd, jnp.where(core == 0, ext - far, 0))
-
-    for step, weight in enumerate(sweep_weights()):
-        src, dst = (xs, xt) if step % 2 == 0 else (xt, xs)
+    in_groups(inv.shape[0], clear)
+    fill(core, y, base, inv, x0, xs)
+    fill(core, yb, base + own, inv, x0, xs)
+    for step in range(EARLY):
         edge = 2 * (step + 1)
-        last = step == SWEEPS - 1
-        group = ext - 2 * edge
-
-        def sweep(src=src, dst=dst, first=edge, last=last, group=group, weight=weight):
-            parts = []
-            for u in range(group):
-                for start in starts:
-                    value = src[first + u, pl.ds(start, rows)]
-                    high = value.astype(jnp.bfloat16)
-                    low = (value - high.astype(jnp.float32)).astype(jnp.bfloat16)
-                    parts.append(jnp.concatenate([high, low], axis=1))
-            along = jnp.dot(
-                jnp.concatenate(parts, axis=0), band[...], preferred_element_type=jnp.float32
-            )
-            for r in range(0, rows, CHUNK):
-                columns = [
-                    [src[first + d, pl.ds(start + r, CHUNK)] for d in range(-2, group + 2)]
-                    for start in starts
-                ]
-                for u in range(group):
-                    e = first + u
-
-                    def total(c):
-                        x = columns[c]
-                        side = [src[e, pl.ds(starts[c] + r + d, CHUNK)] for d in (1, -1, 2, -2)]
-                        near = (x[u + 3] + x[u + 1]) + (side[0] + side[1])
-                        far = (x[u + 4] + x[u]) + (side[2] + side[3])
-                        k = (2 * u + c) * rows + r
-                        return near_weight * near + far_weight * far + along[k : k + CHUNK]
-
-                    re, im = columns[0][u + 2], columns[1][u + 2]
-                    sum_re, sum_im = total(0), total(1)
-                    part = pl.ds(r, CHUNK)
-                    k0, k1, kq = (kinv[e, c, part] for c in range(3))
-                    pair = (
-                        (1.0 - weight) * re
-                        + weight * (x0[e, 0, part] + k0 * sum_re + kq * sum_im),
-                        (1.0 - weight) * im
-                        + weight * (x0[e, 1, part] + k1 * sum_im - kq * sum_re),
-                    )
-                    for c, value in enumerate(pair):
-                        if last:
-                            k = per_plane * (e - margin) + r // share
-                            out[k, c, pl.ds(r % share, CHUNK)] = value.astype(jnp.bfloat16)
-                        else:
-                            dst[e, pl.ds(starts[c] + r, CHUNK)] = value
-
-        sweep()
+        sweep(step, base + edge, base + 2 * own - edge, x0, kinv, band, (xs, xt))
+
+
+def sweeps_kernel(where, y_a, yc, yd, inv, kinv, _x0, _xs, _xt, out, x0, xs, xt, band):
+    ext, _, rows, _ = inv.shape
+    share = y_a.shape[2]
+    per_plane = rows // share
+    own = y_a.shape[0] // per_plane
+    core = where[0]
+    base = (ext - own) // 2
+    write_band(band)
+    fill(core, y_a, base - own, inv, x0, xs)
+    fill(core, yc, 0, inv, x0, xs)
+    fill(core, yd, base + 2 * own, inv, x0, xs)
+
+    def emit(e, r, c, value):
+        i = mirrored(core, e - base, own)
+        out[per_plane * i + r // share, c, pl.ds(r % share, CHUNK)] = value.astype(jnp.bfloat16)
+
+    for step in range(SWEEPS):
+        edge = 2 * (step + 1)
+        if step < EARLY:
+            sweep(step, edge, base + edge, x0, kinv, band, (xs, xt))
+            sweep(step, base + 2 * own - edge, ext - edge, x0, kinv, band, (xs, xt))
+        else:
+            last = step == SWEEPS - 1
+            sweep(step, edge, ext - edge, x0, kinv, band, (xs, xt), emit if last else None)
 
 
 def final_kernel(state, correction, out):
@@ -371,7 +404,7 @@
         out[p] = (state[p].astype(jnp.float32) + value).astype(jnp.bfloat16)
 
 
-def call(kernel, shapes, inputs, scratch=(), scalars=0, anywhere=0, flops=None):
+def call(kernel, shapes, inputs, scratch=(), scalars=0, anywhere=0, flops=None, aliases=None):
     outs = [jax.ShapeDtypeStruct(s, d) for s, d in shapes]
     cost = None
     if flops is not None:
@@ -384,6 +417,7 @@
         out_specs=[VMEM] * len(outs),
         scratch_shapes=list(scratch),
         cost_estimate=cost,
+        input_output_aliases=aliases or {},
         compiler_params=pltpu.CompilerParams(vmem_limit_bytes=24 << 20),
     )(*inputs)
 
@@ -463,18 +497,18 @@
     yc = lax.ppermute(jnp.where(first, y[-n:], y[:n]), CORE_SPACE, same)
     yb = lax.ppermute(y, CORE_SPACE, swap)
     yd = lax.ppermute(jnp.where(first, ya[-n:], ya[:n]), CORE_SPACE, swap)
-    (solved,) = call(
+    tall = 2 * rows + 3 * PAD
+    buffers = [((ext, 2, rows + PAD, lanes), f32), ((ext, tall, lanes), f32), ((ext, tall, lanes), f32)]
+    band = [pltpu.VMEM((2 * lanes, lanes), bf16)]
+    state_arrays = call(inside_kernel, buffers, [where, y, yb, *fields], band, scalars=1)
+    solved = call(
         sweeps_kernel,
-        [((slots, 2, share, lanes), bf16)],
-        [where, y, ya, yb, yc, yd, *fields],
-        [
-            pltpu.VMEM((ext, 2, rows + PAD, lanes), f32),
-            pltpu.VMEM((ext, 2 * rows + 3 * PAD, lanes), f32),
-            pltpu.VMEM((ext, 2 * rows + 3 * PAD, lanes), f32),
-            pltpu.VMEM((2 * lanes, lanes), bf16),
-        ],
+        [((slots, 2, share, lanes), bf16), *buffers],
+        [where, ya, yc, yd, *fields, *state_arrays],
+        band,
         scalars=1,
-    )
+        aliases={6: 1, 7: 2, 8: 3},
+    )[0]
     modes = lax.all_to_all(solved, CHIPS, 0, 0, tiled=True)
     (correction,) = call(inverse_kernel, [((members, share, lanes), bf16)], [modes])
     returned = lax.all_to_all(correction, TM, 0, 0, tiled=True)

time: 108 us -> 109 us (level)
    pallas_call x7 -> x8, Pallas kernels: 12.9 us -> 13.8 us  [call(): pl.pallas_call(kernel, out_shape=outs, in_specs=[SMEM] * scalars + [HBM]...]
  transfers between devices with their start and end apart: 10 -> 10, of which waited for: 3 -> 3; matrix products, arithmetic and copies ran while one was open for 1% -> 1% of each run, Pallas kernels for 4% -> 6%
where the time goes in v6:
time: 109 us
  blocking collectives  50.2 us (46%)
  starting transfers between devices  25 us (23%)
  waiting for transfers between devices  18.4 us (17%)
  Pallas kernels  13.8 us (13%)
    all_to_all x1, blocking collectives, iteration(): returned = lax.all_to_all(correction, TM, 0, 0, tiled=True)  19.4 us
    all_to_all x1, blocking collectives, iteration(): modes = lax.all_to_all(solved, CHIPS, 0, 0, tiled=True)  17.2 us
    pallas_call x8, Pallas kernels, call(): pl.pallas_call(kernel, out_shape=outs, in_specs=[SMEM] * scalars + [HBM]...  13.8 us
    all_to_all x1, blocking collectives, iteration(): y = lax.all_to_all(spectrum, CHIPS, 0, 0, tiled=True)  13.6 us
    all_to_all x1, waiting for transfers between devices, iteration(): lax.all_to_all(residual.reshape(members, share, lanes), TM, 0, 0, tiled=T...  12 us
    all_to_all x1, starting transfers between devices, iteration(): lax.all_to_all(residual.reshape(members, share, lanes), TM, 0, 0, tiled=T...  8.97 us
    ppermute x1, starting transfers between devices, iteration(): yc = lax.ppermute(jnp.where(first, y[-n:], y[:n]), CORE_SPACE, same)  3.89 us
    ppermute x1, waiting for transfers between devices, iteration(): ya = lax.ppermute(y, CORE_SPACE, outer)  3.64 us
  transfers between devices with their start and end apart: 10, of which 3 were waited for; matrix products, arithmetic and copies ran while one was open for 1% of the time, Pallas kernels for 6%

profile of v6, /device:TPU:16, one launch (start us, length us, event | category | flops | bytes accessed | tf_op | source)
XLA Modules:
  0.0 108.7 jit_solution(12095025612427236044)
XLA Ops:
  0.0 0.0 copy-start.2
  0.0 0.0 copy-start.1
  0.0 0.0 copy-start
  0.0 1.9 %collective-permute-start.2 = (bf16[16,64,128]{2,1,0:T(8,128)(2,1)}, bf16[16,64,128]{2,1,0:T(8,128)(2,1)S(1)}, u32[]{:S(2)}, u32[]{:S(2)}) collective-permute-start(bf16[16,64,128]{2,1,0:T(8,128)(2,1)} %bitcast.18), channel_id=1, source_target_pairs={{0,8},{8,16},{16,24},{24,32},{32,40},{40,48},{48,56},{56,64},{64,7... | collective-permute-start | bytes 786440 | tf_op jit(solution)/shard_map/ppermute | solution.py:455
  1.9 0.8 select_bitcast_fusion
  2.7 3.3 %collective-permute-start.1 = (bf16[2,64,128]{2,1,0:T(8,128)(2,1)S(1)}, bf16[2,64,128]{2,1,0:T(8,128)(2,1)S(1)}, u32[]{:S(2)}, u32[]{:S(2)}) collective-permute-start(bf16[2,64,128]{2,1,0:T(8,128)(2,1)S(1)} %get-tuple-element.21), channel_id=1, source_target_pairs={{1,2},{2,1},{3,4},{4,3},{5,6},{6,5},{9,10},{10,9},{11,12},{12,11},... | collective-permute-start | bytes 98312 | tf_op jit(solution)/shard_map/ppermute | solution.py:454
  6.0 1.5 %collective-permute-start = (bf16[2,64,128]{2,1,0:T(8,128)(2,1)S(1)}, bf16[2,64,128]{2,1,0:T(8,128)(2,1)S(1)}, u32[]{:S(2)}, u32[]{:S(2)}) collective-permute-start(bf16[2,64,128]{2,1,0:T(8,128)(2,1)S(1)} %get-tuple-element.22), channel_id=1, source_target_pairs={{0,1},{1,0},{2,3},{3,2},{4,5},{5,4},{6,7},{7,6},{8,9},{9,8},{10,11... | collective-permute-start | bytes 98312 | tf_op jit(solution)/shard_map/ppermute | solution.py:453
  7.4 0.1 pad_add_fusion.where
  7.5 2.7 %shard_map.55 = (f32[16,64,128]{2,1,0:T(8,128)S(1)}, f32[4,64,128]{2,1,0:T(8,128)S(1)}) custom-call(s32[2]{0:T(128)S(1)} %pad_add_fusion.where, bf16[16,64,128]{2,1,0:T(8,128)(2,1)} %bitcast.19, bf16[16,64,128]{2,1,0:T(8,128)(2,1)} %initial.1, bf16[16,64,128]{2,1,0:T(8,128)(2,1)} %bitcast.22, bf16[16,64,128]{2,1,0:T(8,128)(2,1)} %kappa.1, ...), custom_call_target="tpu_custom_call" | custom-call | flops 20000000 | bytes 2500000 | tf_op jit(solution)/shard_map/pallas_call | solution.py:413
  10.2 0.0 collective-permute-done.1.odd_pair
  10.2 2.7 %collective-permute-done.even_pair = bf16[2,64,128]{2,1,0:T(8,128)(2,1)S(1)} collective-permute-done((bf16[2,64,128]{2,1,0:T(8,128)(2,1)S(1)}, bf16[2,64,128]{2,1,0:T(8,128)(2,1)S(1)}, u32[]{:S(2)}, u32[]{:S(2)}) %collective-permute-start) | collective-permute-done | bytes 32800 | tf_op jit(solution)/shard_map/ppermute | solution.py:453
  13.0 0.0 collective-permute-done.2.before
  13.0 0.8 shard_map.56
  13.8 9.0 %all-to-all-start = ((bf16[32,32,128]{2,1,0:T(8,128)(2,1)}), bf16[32,32,128]{2,1,0:T(8,128)(2,1)S(1)}, u32[]{:S(2)}, u32[]{:S(2)}) async-start(bf16[32,32,128]{2,1,0:T(8,128)(2,1)} %bitcast.7), calls=%async_computation | async-start | bytes 524288 | tf_op jit(solution)/shard_map/all_to_all | solution.py:484
  22.7 0.0 copy-done.2
  22.8 0.0 copy-done.1
  22.8 0.0 copy-done
  22.8 0.1 pad_maximum_fusion
  22.9 2.5 %collective-permute-start.6 = (bf16[3,12,64,128]{3,2,1,0:T(8,128)(2,1)S(1)}, bf16[3,12,64,128]{3,2,1,0:T(8,128)(2,1)S(1)}, u32[]{:S(2)}, u32[]{:S(2)}) collective-permute-start(bf16[3,12,64,128]{3,2,1,0:T(8,128)(2,1)S(1)} %slice_select_fusion), channel_id=1, source_target_pairs={{8,1},{1,8},{9,2},{2,9},{10,3},{3,10},{11,4},{4,11},{12,5},{5,12},... | collective-permute-start | bytes 1769480 | tf_op jit(solution)/shard_map/ppermute | solution.py:458
  25.4 12.0 %all-to-all-done.r = bf16[32,32,128]{2,1,0:T(8,128)(2,1)S(1)} async-done(((bf16[32,32,128]{2,1,0:T(8,128)(2,1)}), bf16[32,32,128]{2,1,0:T(8,128)(2,1)S(1)}, u32[]{:S(2)}, u32[]{:S(2)}) %all-to-all-start) | async-done | bytes 262176 | tf_op jit(solution)/shard_map/all_to_all | solution.py:484
  37.5 0.2 shard_map.57
  37.7 13.6 %all_to_all.20.y = bf16[16,2,32,128]{3,2,1,0:T(8,128)(2,1)S(1)} all-to-all(bf16[16,2,32,128]{3,2,1,0:T(8,128)(2,1)S(1)} %shard_map.57), channel_id=1, replica_groups=mesh['tm_0'=2,'tm_1'=8,'tm_2'=2,'space'=8] {'tm_0','tm_1'}, dimensions={0} | all-to-all | bytes 524288 | tf_op jit(solution)/shard_map/all_to_all | solution.py:486
  51.3 1.9 %collective-permute-start.3 = (bf16[16,2,32,128]{3,2,1,0:T(8,128)(2,1)S(1)}, bf16[16,2,32,128]{3,2,1,0:T(8,128)(2,1)S(1)}, u32[]{:S(2)}, u32[]{:S(2)}) collective-permute-start(bf16[16,2,32,128]{3,2,1,0:T(8,128)(2,1)S(1)} %all_to_all.20.y), channel_id=1, source_target_pairs={{8,1},{1,8},{9,2},{2,9},{10,3},{3,10},{11,4},{4,11},{12,5},{5,12},... | collective-permute-start | bytes 786440 | tf_op jit(solution)/shard_map/ppermute | solution.py:496
  53.2 0.0 collective-permute-done.6.outer
  53.3 0.7 collective-permute-start.7
  54.0 3.9 %collective-permute-start.4 = (bf16[8,2,32,128]{3,2,1,0:T(8,128)(2,1)S(1)}, bf16[8,2,32,128]{3,2,1,0:T(8,128)(2,1)S(1)}, u32[]{:S(2)}, u32[]{:S(2)}) collective-permute-start(bf16[8,2,32,128]{3,2,1,0:T(8,128)(2,1)S(1)} %slice_select_fusion.3), channel_id=1, source_target_pairs={{0,1},{1,2},{2,3},{3,4},{4,5},{5,6},{6,7},{9,8},{10,9},{11,10},{12... | collective-permute-start | bytes 393224 | tf_op jit(solution)/shard_map/ppermute | solution.py:497
  57.9 0.2 collective-permute-start.8
  58.2 3.6 %collective-permute-done.3.y_a = bf16[16,2,32,128]{3,2,1,0:T(8,128)(2,1)S(1)} collective-permute-done((bf16[16,2,32,128]{3,2,1,0:T(8,128)(2,1)S(1)}, bf16[16,2,32,128]{3,2,1,0:T(8,128)(2,1)S(1)}, u32[]{:S(2)}, u32[]{:S(2)}) %collective-permute-start.3) | collective-permute-done | bytes 262176 | tf_op jit(solution)/shard_map/ppermute | solution.py:496
  61.8 0.1 collective-permute-start.5
  61.9 0.0 collective-permute-done.7.inner
  61.9 1.6 %shard_map.58 = (f32[32,3,64,128]{3,2,1,0:T(8,128)S(1)}, f32[32,3,64,128]{3,2,1,0:T(8,128)S(1)}) custom-call(s32[2]{0:T(128)S(1)} %pad_add_fusion.where, bf16[16,64,128]{2,1,0:T(8,128)(2,1)S(1)} %copy-done.1, bf16[16,64,128]{2,1,0:T(8,128)(2,1)S(1)} %copy-done, bf16[16,64,128]{2,1,0:T(8,128)(2,1)S(1)} %copy-done.2, ...), custom_call_target="tpu_custom_call" | custom-call | tf_op jit(solution)/shard_map/pallas_call | solution.py:413
  63.5 0.0 collective-permute-done.8.yb
  63.5 2.2 %shard_map.59 = (f32[32,2,72,128]{3,2,1,0:T(8,128)S(1)}, f32[32,152,128]{2,1,0:T(8,128)S(1)}, f32[32,152,128]{2,1,0:T(8,128)S(1)}) custom-call(s32[2]{0:T(128)S(1)} %pad_add_fusion.where, bf16[16,2,32,128]{3,2,1,0:T(8,128)(2,1)S(1)} %all_to_all.20.y, bf16[16,2,32,128]{3,2,1,0:T(8,128)(2,1)S(1)} %collective-permute-done.8.yb, ...), custom_call_target="tpu_custom_call" | custom-call | tf_op jit(solution)/shard_map/pallas_call | solution.py:413
  65.8 0.0 collective-permute-done.4.yc
  65.8 0.0 collective-permute-done.5.yd
  65.8 0.0 copy-start.3
  65.8 5.3 %shard_map.60 = (bf16[16,2,32,128]{3,2,1,0:T(8,128)(2,1)S(1)}, f32[32,2,72,128]{3,2,1,0:T(8,128)S(1)}, f32[32,152,128]{2,1,0:T(8,128)S(1)}, f32[32,152,128]{2,1,0:T(8,128)S(1)}) custom-call(s32[2]{0:T(128)S(1)} %pad_add_fusion.where, ...), custom_call_target="tpu_custom_call", output_to_operand_aliasing={{1}: (6, {}), {2}: (7, {}), {3}: (8, {})} | custom-call | tf_op jit(solution)/shard_map/pallas_call | solution.py:413
  71.2 17.2 %all_to_all.21.s = bf16[16,2,32,128]{3,2,1,0:T(8,128)(2,1)S(1)} all-to-all(bf16[16,2,32,128]{3,2,1,0:T(8,128)(2,1)S(1)} %get-tuple-element.20), channel_id=1, replica_groups=mesh['tm_0'=2,'tm_1'=8,'tm_2'=2,'space'=8] {'tm_0','tm_1'}, dimensions={0} | all-to-all | bytes 524288 | tf_op jit(solution)/shard_map/all_to_all | solution.py:512
  88.3 0.2 shard_map.61
  88.5 19.4 %all_to_all.22 = bf16[32,32,128]{2,1,0:T(8,128)(2,1)S(1)} all-to-all(bf16[32,32,128]{2,1,0:T(8,128)(2,1)S(1)} %shard_map.61), channel_id=1, replica_groups=mesh['tm_0'=2,'tm_1'=8,'tm_2'=2,'space'=8] {'tm_0','tm_1','tm_2'}, dimensions={0} | all-to-all | bytes 524288 | tf_op jit(solution)/shard_map/all_to_all | solution.py:514
  107.9 0.0 copy-done.3
  107.9 0.8 shard_map.62
  (4 shorter events, 0.1 us)
Async XLA Ops:
  0.0 22.7 %copy-start.2 = (bf16[16,64,128]{2,1,0:T(8,128)(2,1)S(1)}, bf16[16,64,128]{2,1,0:T(8,128)(2,1)}, u32[]{:S(2)}) copy-start(bf16[16,64,128]{2,1,0:T(8,128)(2,1)} %reaction.1) | copy-start | bytes 786436
  0.0 22.8 %copy-start.1 = (bf16[16,64,128]{2,1,0:T(8,128)(2,1)S(1)}, bf16[16,64,128]{2,1,0:T(8,128)(2,1)}, u32[]{:S(2)}) copy-start(bf16[16,64,128]{2,1,0:T(8,128)(2,1)} %kappa.1) | copy-start | bytes 786436
  0.0 22.8 %copy-start = (bf16[16,64,128]{2,1,0:T(8,128)(2,1)S(1)}, bf16[16,64,128]{2,1,0:T(8,128)(2,1)}, u32[]{:S(2)}) copy-start(bf16[16,64,128]{2,1,0:T(8,128)(2,1)} %initial.1) | copy-start | bytes 786436
  0.0 13.0 %collective-permute-start.2 = (bf16[16,64,128]{2,1,0:T(8,128)(2,1)}, bf16[16,64,128]{2,1,0:T(8,128)(2,1)S(1)}, u32[]{:S(2)}, u32[]{:S(2)}) collective-permute-start(bf16[16,64,128]{2,1,0:T(8,128)(2,1)} %bitcast.18), channel_id=1, source_target_pairs={{0,8},{8,16},{16,24},{24,32},{32,40},{40,48},{48,56},{56,64},{64,7... | collective-permute-start | bytes 786440 | tf_op jit(solution)/shard_map/ppermute | solution.py:455
  2.7 7.5 %collective-permute-start.1 = (bf16[2,64,128]{2,1,0:T(8,128)(2,1)S(1)}, bf16[2,64,128]{2,1,0:T(8,128)(2,1)S(1)}, u32[]{:S(2)}, u32[]{:S(2)}) collective-permute-start(bf16[2,64,128]{2,1,0:T(8,128)(2,1)S(1)} %get-tuple-element.21), channel_id=1, source_target_pairs={{1,2},{2,1},{3,4},{4,3},{5,6},{6,5},{9,10},{10,9},{11,12},{12,11},... | collective-permute-start | bytes 98312 | tf_op jit(solution)/shard_map/ppermute | solution.py:454
  6.0 7.0 %collective-permute-start = (bf16[2,64,128]{2,1,0:T(8,128)(2,1)S(1)}, bf16[2,64,128]{2,1,0:T(8,128)(2,1)S(1)}, u32[]{:S(2)}, u32[]{:S(2)}) collective-permute-start(bf16[2,64,128]{2,1,0:T(8,128)(2,1)S(1)} %get-tuple-element.22), channel_id=1, source_target_pairs={{0,1},{1,0},{2,3},{3,2},{4,5},{5,4},{6,7},{7,6},{8,9},{9,8},{10,11... | collective-permute-start | bytes 98312 | tf_op jit(solution)/shard_map/ppermute | solution.py:453
  13.8 23.7 %all-to-all-start = ((bf16[32,32,128]{2,1,0:T(8,128)(2,1)}), bf16[32,32,128]{2,1,0:T(8,128)(2,1)S(1)}, u32[]{:S(2)}, u32[]{:S(2)}) async-start(bf16[32,32,128]{2,1,0:T(8,128)(2,1)} %bitcast.7), calls=%async_computation | async-start | bytes 524288 | tf_op jit(solution)/shard_map/all_to_all | solution.py:484
  22.9 30.3 %collective-permute-start.6 = (bf16[3,12,64,128]{3,2,1,0:T(8,128)(2,1)S(1)}, bf16[3,12,64,128]{3,2,1,0:T(8,128)(2,1)S(1)}, u32[]{:S(2)}, u32[]{:S(2)}) collective-permute-start(bf16[3,12,64,128]{3,2,1,0:T(8,128)(2,1)S(1)} %slice_select_fusion), channel_id=1, source_target_pairs={{8,1},{1,8},{9,2},{2,9},{10,3},{3,10},{11,4},{4,11},{12,5},{5,12},... | collective-permute-start | bytes 1769480 | tf_op jit(solution)/shard_map/ppermute | solution.py:458
  51.3 10.5 %collective-permute-start.3 = (bf16[16,2,32,128]{3,2,1,0:T(8,128)(2,1)S(1)}, bf16[16,2,32,128]{3,2,1,0:T(8,128)(2,1)S(1)}, u32[]{:S(2)}, u32[]{:S(2)}) collective-permute-start(bf16[16,2,32,128]{3,2,1,0:T(8,128)(2,1)S(1)} %all_to_all.20.y), channel_id=1, source_target_pairs={{8,1},{1,8},{9,2},{2,9},{10,3},{3,10},{11,4},{4,11},{12,5},{5,12},... | collective-permute-start | bytes 786440 | tf_op jit(solution)/shard_map/ppermute | solution.py:496
  53.3 8.6 %collective-permute-start.7 = (bf16[3,4,64,128]{3,2,1,0:T(8,128)(2,1)S(1)}, bf16[3,4,64,128]{3,2,1,0:T(8,128)(2,1)S(1)}, u32[]{:S(2)}, u32[]{:S(2)}) collective-permute-start(bf16[3,4,64,128]{3,2,1,0:T(8,128)(2,1)S(1)} %slice_select_fusion.1), channel_id=1, source_target_pairs={{0,8},{1,9},{2,10},{3,11},{4,12},{5,13},{6,14},{7,15},{8,0},{9,1},... | collective-permute-start | bytes 589832 | tf_op jit(solution)/shard_map/ppermute | solution.py:460
  54.0 11.7 %collective-permute-start.4 = (bf16[8,2,32,128]{3,2,1,0:T(8,128)(2,1)S(1)}, bf16[8,2,32,128]{3,2,1,0:T(8,128)(2,1)S(1)}, u32[]{:S(2)}, u32[]{:S(2)}) collective-permute-start(bf16[8,2,32,128]{3,2,1,0:T(8,128)(2,1)S(1)} %slice_select_fusion.3), channel_id=1, source_target_pairs={{0,1},{1,2},{2,3},{3,4},{4,5},{5,6},{6,7},{9,8},{10,9},{11,10},{12... | collective-permute-start | bytes 393224 | tf_op jit(solution)/shard_map/ppermute | solution.py:497
  57.9 5.6 %collective-permute-start.8 = (bf16[16,2,32,128]{3,2,1,0:T(8,128)(2,1)S(1)}, bf16[16,2,32,128]{3,2,1,0:T(8,128)(2,1)S(1)}, u32[]{:S(2)}, u32[]{:S(2)}) collective-permute-start(bf16[16,2,32,128]{3,2,1,0:T(8,128)(2,1)S(1)} %all_to_all.20.y), channel_id=1, source_target_pairs={{0,8},{1,9},{2,10},{3,11},{4,12},{5,13},{6,14},{7,15},{8,0},{9,1},... | collective-permute-start | bytes 786440 | tf_op jit(solution)/shard_map/ppermute | solution.py:498
  61.8 4.0 %collective-permute-start.5 = (bf16[8,2,32,128]{3,2,1,0:T(8,128)(2,1)S(1)}, bf16[8,2,32,128]{3,2,1,0:T(8,128)(2,1)S(1)}, u32[]{:S(2)}, u32[]{:S(2)}) collective-permute-start(bf16[8,2,32,128]{3,2,1,0:T(8,128)(2,1)S(1)} %slice_select_fusion.2), channel_id=1, source_target_pairs={{0,8},{1,9},{2,10},{3,11},{4,12},{5,13},{6,14},{7,15},{8,0},{9,1},... | collective-permute-start | bytes 393224 | tf_op jit(solution)/shard_map/ppermute | solution.py:499
  65.8 42.1 %copy-start.3 = (bf16[1,16,64,128]{3,2,1,0:T(8,128)(2,1)S(1)}, bf16[1,16,64,128]{3,2,1,0:T(8,128)(2,1)}, u32[]{:S(2)}) copy-start(bf16[1,16,64,128]{3,2,1,0:T(8,128)(2,1)} %param.5) | copy-start | bytes 786436

commit v7 on v6

--- a/solution.py
+++ b/solution.py
@@ -15,6 +15,7 @@
 TM = ("tm_0", "tm_1", "tm_2")
 CHIPS = ("tm_0", "tm_1")
 CORE_SPACE = ("tm_2", "space")
+SIDE_CORE_SPACE = ("tm_0", "tm_2", "space")
 
 alpha_ratio = 0.25
 near_weight = 0.5
@@ -141,7 +142,7 @@
     for copy in copies[1:]:
         copy.wait()
     masks = lane_masks((rows, lanes))
-    first = jnp.logical_and(where[0] == 0, where[1] == 0)
+    first = where[3] == 0
 
     def one(p):
         centre, total = neighbour_sum(ext, (), p + 2, rows, masks)
@@ -190,29 +191,40 @@
         put(p, part[p] + rim[i] * total + before[p].astype(jnp.float32))
 
 
-def forward_kernel(r, out):
+def slot_place(where, j, slots):
+    return jnp.where(where[2] == 0, j, (j + slots // 2) % slots)
+
+
+def forward_kernel(where, r, out):
     steps, rows, _ = r.shape
+    slots = steps // 2
+    places = [slot_place(where, j, slots) for j in range(slots)]
     for start in range(0, rows, 16):
         part = pl.ds(start, 16)
         scaled = [
             r[n, part].astype(jnp.float32) * (alpha_ratio ** (n / steps)) for n in range(steps)
         ]
         spectrum = real_dft(scaled)
-        out[0, 0, part] = spectrum[0][0].astype(jnp.bfloat16)
-        out[0, 1, part] = spectrum[steps // 2][0].astype(jnp.bfloat16)
-        for j in range(1, steps // 2):
-            out[j, 0, part] = spectrum[j][0].astype(jnp.bfloat16)
-            out[j, 1, part] = spectrum[j][1].astype(jnp.bfloat16)
-
-
-def inverse_kernel(s, out):
+        out[places[0], 0, part] = spectrum[0][0].astype(jnp.bfloat16)
+        out[places[0], 1, part] = spectrum[slots][0].astype(jnp.bfloat16)
+        for j in range(1, slots):
+            out[places[j], 0, part] = spectrum[j][0].astype(jnp.bfloat16)
+            out[places[j], 1, part] = spectrum[j][1].astype(jnp.bfloat16)
+
+
+def inverse_kernel(where, s, out):
     steps, rows, _ = out.shape
+    slots = steps // 2
+    places = [slot_place(where, j, slots) for j in range(slots)]
     for start in range(0, rows, 16):
         part = pl.ds(start, 16)
-        spectrum = [(s[0, 0, part].astype(jnp.float32), None)]
-        for j in range(1, steps // 2):
-            spectrum.append((s[j, 0, part].astype(jnp.float32), s[j, 1, part].astype(jnp.float32)))
-        spectrum.append((s[0, 1, part].astype(jnp.float32), None))
+
+        def given(j, c):
+            return s[places[j], c, part].astype(jnp.float32)
+
+        spectrum = [(given(0, 0), None)]
+        spectrum += [(given(j, 0), given(j, 1)) for j in range(1, slots)]
+        spectrum.append((given(0, 1), None))
         values = real_inverse(spectrum)
         for n in range(steps):
             scale = 1.0 / (alpha_ratio ** (n / steps) * steps)
@@ -435,17 +447,21 @@
     ext = own + 2 * wide
     bf16, f32, i32 = jnp.bfloat16, jnp.float32, jnp.int32
     core = lax.axis_index("tm_2")
+    flip = lax.axis_index("space") // 2 % 2
+    half_slots = slots // 2
     slot = lax.axis_index(CHIPS)
-    where = jnp.stack([core, slot]).astype(i32)
+    slot = jnp.where(flip == 0, slot, (slot + half_slots) % slots)
+    where = jnp.stack([core, slot, flip, lax.axis_index(TM)]).astype(i32)
     u = state[0]
 
-    forward = [(i, i + 1) for i in range(slabs - 1)]
-    backward = [(t, s) for s, t in forward]
-    outer = []
-    for s in range(slabs - 1):
-        outer += [(slabs + s, s + 1), (s + 1, slabs + s)]
+    outer, same = [], []
+    for side in range(2):
+        for t in range(slabs - 1):
+            near, beside = side * 2 * slabs, (side ^ (t % 2)) * 2 * slabs
+            low, high = near + slabs + t, beside + t + 1
+            outer += [(low, high), (high, low)]
+            same += [(near + t, beside + t + 1), (beside + slabs + t + 1, near + slabs + t)]
     swap = [(i, slabs + i) for i in range(slabs)] + [(slabs + i, i) for i in range(slabs)]
-    same = forward + [(slabs + s, slabs + t) for s, t in backward]
     odd = lax.axis_index("space") % 2
     even_first = [p for s in range(0, slabs - 1, 2) for p in ((s, s + 1), (s + 1, s))]
     odd_first = [p for s in range(1, slabs - 1, 2) for p in ((s, s + 1), (s + 1, s))]
@@ -455,7 +471,7 @@
     before = lax.ppermute(u, TM, [(i, i + 1) for i in range(members - 1)])
     coefs = jnp.stack([kappa, initial, reaction])
     rim = jnp.where(core == 0, coefs[:, :wide], coefs[:, planes - wide :])
-    rim = lax.ppermute(rim, CORE_SPACE, outer)
+    rim = lax.ppermute(rim, SIDE_CORE_SPACE, outer)
     inner = jnp.where(core == 0, rim[:, wide - narrow :], rim[:, :narrow])
     inner = lax.ppermute(inner, CORE_SPACE, swap)
 
@@ -482,7 +498,9 @@
         scalars=1,
     )
     cells = lax.all_to_all(residual.reshape(members, share, lanes), TM, 0, 0, tiled=True)
-    (spectrum,) = call(forward_kernel, [((slots, 2, share, lanes), bf16)], [cells])
+    (spectrum,) = call(
+        forward_kernel, [((slots, 2, share, lanes), bf16)], [where, cells], scalars=1
+    )
     y = lax.all_to_all(spectrum, CHIPS, 0, 0, tiled=True)
 
     fields = call(
@@ -493,8 +511,8 @@
     )
     n = per_plane * narrow
     first = core == 0
-    ya = lax.ppermute(y, CORE_SPACE, outer)
-    yc = lax.ppermute(jnp.where(first, y[-n:], y[:n]), CORE_SPACE, same)
+    ya = lax.ppermute(y, SIDE_CORE_SPACE, outer)
+    yc = lax.ppermute(jnp.where(first, y[-n:], y[:n]), SIDE_CORE_SPACE, same)
     yb = lax.ppermute(y, CORE_SPACE, swap)
     yd = lax.ppermute(jnp.where(first, ya[-n:], ya[:n]), CORE_SPACE, swap)
     tall = 2 * rows + 3 * PAD
@@ -510,7 +528,9 @@
         aliases={6: 1, 7: 2, 8: 3},
     )[0]
     modes = lax.all_to_all(solved, CHIPS, 0, 0, tiled=True)
-    (correction,) = call(inverse_kernel, [((members, share, lanes), bf16)], [modes])
+    (correction,) = call(
+        inverse_kernel, [((members, share, lanes), bf16)], [where, modes], scalars=1
+    )
     returned = lax.all_to_all(correction, TM, 0, 0, tiled=True)
     (updated,) = call(
         final_kernel, [((planes, rows, lanes), bf16)], [u, returned.reshape(slots, 2, share, lanes)]

time: 109 us -> 109 us (level)
  waiting for transfers between devices: 18.4 us -> 14.3 us
  starting transfers between devices: 25 us -> 28.4 us
  Pallas kernels: 13.8 us -> 14.9 us
    all_to_all x1, waiting for transfers between devices: 12 us -> 9.77 us  [iteration(): lax.all_to_all(residual.reshape(members, share, lanes), TM, 0, 0, tiled=T...]
    ppermute x3, waiting for transfers between devices: 3.65 us -> 1.75 us  [the longest x1 1.74 us: iteration(): ya = lax.ppermute(y, SIDE_CORE_SPACE, outer)]
    ppermute x1, starting transfers between devices: 0.22 us -> 2.09 us  [iteration(): yb = lax.ppermute(y, CORE_SPACE, swap)]
    ppermute x3, starting transfers between devices: 8.31 us -> 9.94 us  [the longest x1 4.8 us: iteration(): rim = lax.ppermute(rim, SIDE_CORE_SPACE, outer)]
    pallas_call x8, Pallas kernels: 13.8 us -> 14.9 us  [call(): pl.pallas_call(kernel, out_shape=outs, in_specs=[SMEM] * scalars + [HBM]...]
  transfers between devices with their start and end apart: 10 -> 10, of which waited for: 3 -> 3; matrix products, arithmetic and copies ran while one was open for 1% -> 1% of each run, Pallas kernels for 6% -> 7%
where the time goes in v7:
time: 109 us; the launch traced here: 108 us
  blocking collectives  49.4 us (45%)
  starting transfers between devices  28.4 us (26%)
  Pallas kernels  14.9 us (14%)
  waiting for transfers between devices  14.3 us (13%)
    all_to_all x1, blocking collectives, iteration(): returned = lax.all_to_all(correction, TM, 0, 0, tiled=True)  19.4 us
    all_to_all x1, blocking collectives, iteration(): modes = lax.all_to_all(solved, CHIPS, 0, 0, tiled=True)  16.4 us
    pallas_call x8, Pallas kernels, call(): pl.pallas_call(kernel, out_shape=outs, in_specs=[SMEM] * scalars + [HBM]...  14.9 us
    all_to_all x1, blocking collectives, iteration(): y = lax.all_to_all(spectrum, CHIPS, 0, 0, tiled=True)  13.6 us
    all_to_all x1, waiting for transfers between devices, iteration(): lax.all_to_all(residual.reshape(members, share, lanes), TM, 0, 0, tiled=T...  9.77 us
    all_to_all x1, starting transfers between devices, iteration(): lax.all_to_all(residual.reshape(members, share, lanes), TM, 0, 0, tiled=T...  8.97 us
    ppermute x1, starting transfers between devices, iteration(): rim = lax.ppermute(rim, SIDE_CORE_SPACE, outer)  4.8 us
    ppermute x1, starting transfers between devices, iteration(): odd_pair = lax.ppermute(jnp.where(odd == 1, high, low), 'space', odd_first)  3.28 us
  transfers between devices with their start and end apart: 10, of which 3 were waited for; matrix products, arithmetic and copies ran while one was open for 1% of the time, Pallas kernels for 7%

profile of v7, /device:TPU:16, one launch (start us, length us, event | category | flops | bytes accessed | tf_op | source)
XLA Modules:
  0.0 108.3 jit_solution(13486422822091579995)
XLA Ops:
  0.0 0.0 copy-start.2
  0.0 0.0 copy-start.1
  0.0 0.0 copy-start
  0.0 1.9 %collective-permute-start.2 = (bf16[16,64,128]{2,1,0:T(8,128)(2,1)}, bf16[16,64,128]{2,1,0:T(8,128)(2,1)S(1)}, u32[]{:S(2)}, u32[]{:S(2)}) collective-permute-start(bf16[16,64,128]{2,1,0:T(8,128)(2,1)} %bitcast.20), channel_id=1, source_target_pairs={{0,8},{8,16},{16,24},{24,32},{32,40},{40,48},{48,56},{56,64},{64,7... | collective-permute-start | bytes 786440 | tf_op jit(solution)/shard_map/ppermute | solution.py:471
  1.9 0.8 select_bitcast_fusion
  2.7 3.3 %collective-permute-start.1 = (bf16[2,64,128]{2,1,0:T(8,128)(2,1)S(1)}, bf16[2,64,128]{2,1,0:T(8,128)(2,1)S(1)}, u32[]{:S(2)}, u32[]{:S(2)}) collective-permute-start(bf16[2,64,128]{2,1,0:T(8,128)(2,1)S(1)} %get-tuple-element.21), channel_id=1, source_target_pairs={{1,2},{2,1},{3,4},{4,3},{5,6},{6,5},{9,10},{10,9},{11,12},{12,11},... | collective-permute-start | bytes 98312 | tf_op jit(solution)/shard_map/ppermute | solution.py:470
  6.0 1.5 %collective-permute-start = (bf16[2,64,128]{2,1,0:T(8,128)(2,1)S(1)}, bf16[2,64,128]{2,1,0:T(8,128)(2,1)S(1)}, u32[]{:S(2)}, u32[]{:S(2)}) collective-permute-start(bf16[2,64,128]{2,1,0:T(8,128)(2,1)S(1)} %get-tuple-element.22), channel_id=1, source_target_pairs={{0,1},{1,0},{2,3},{3,2},{4,5},{5,4},{6,7},{7,6},{8,9},{9,8},{10,11... | collective-permute-start | bytes 98312 | tf_op jit(solution)/shard_map/ppermute | solution.py:469
  7.4 0.1 pad_add_fusion.where
  7.5 2.7 %shard_map.55 = (f32[16,64,128]{2,1,0:T(8,128)S(1)}, f32[4,64,128]{2,1,0:T(8,128)S(1)}) custom-call(s32[4]{0:T(128)S(1)} %pad_add_fusion.where, bf16[16,64,128]{2,1,0:T(8,128)(2,1)} %bitcast.21, bf16[16,64,128]{2,1,0:T(8,128)(2,1)} %initial.1, bf16[16,64,128]{2,1,0:T(8,128)(2,1)} %bitcast.24, bf16[16,64,128]{2,1,0:T(8,128)(2,1)} %kappa.1, ...), custom_call_target="tpu_custom_call" | custom-call | flops 20000000 | bytes 2500000 | tf_op jit(solution)/shard_map/pallas_call | solution.py:425
  10.2 0.0 collective-permute-done.1.odd_pair
  10.2 2.7 %collective-permute-done.even_pair = bf16[2,64,128]{2,1,0:T(8,128)(2,1)S(1)} collective-permute-done((bf16[2,64,128]{2,1,0:T(8,128)(2,1)S(1)}, bf16[2,64,128]{2,1,0:T(8,128)(2,1)S(1)}, u32[]{:S(2)}, u32[]{:S(2)}) %collective-permute-start) | collective-permute-done | bytes 32800 | tf_op jit(solution)/shard_map/ppermute | solution.py:469
  13.0 0.0 collective-permute-done.2.before
  13.0 0.8 shard_map.56
  13.8 9.0 %all-to-all-start = ((bf16[32,32,128]{2,1,0:T(8,128)(2,1)}), bf16[32,32,128]{2,1,0:T(8,128)(2,1)S(1)}, u32[]{:S(2)}, u32[]{:S(2)}) async-start(bf16[32,32,128]{2,1,0:T(8,128)(2,1)} %bitcast.9), calls=%async_computation | async-start | bytes 524288 | tf_op jit(solution)/shard_map/all_to_all | solution.py:500
  22.7 0.0 copy-done.2
  22.8 0.0 copy-done.1
  22.8 0.0 copy-done
  22.8 0.1 pad_maximum_fusion
  22.9 4.8 %collective-permute-start.6 = (bf16[3,12,64,128]{3,2,1,0:T(8,128)(2,1)S(1)}, bf16[3,12,64,128]{3,2,1,0:T(8,128)(2,1)S(1)}, u32[]{:S(2)}, u32[]{:S(2)}) collective-permute-start(bf16[3,12,64,128]{3,2,1,0:T(8,128)(2,1)S(1)} %slice_select_fusion), channel_id=1, source_target_pairs={{8,1},{1,8},{9,130},{130,9},{10,3},{3,10},{11,132},{132,11},{12,5}... | collective-permute-start | bytes 1769480 | tf_op jit(solution)/shard_map/ppermute | solution.py:474
  27.7 9.8 %all-to-all-done.r = bf16[32,32,128]{2,1,0:T(8,128)(2,1)S(1)} async-done(((bf16[32,32,128]{2,1,0:T(8,128)(2,1)}), bf16[32,32,128]{2,1,0:T(8,128)(2,1)S(1)}, u32[]{:S(2)}, u32[]{:S(2)}) %all-to-all-start) | async-done | bytes 262176 | tf_op jit(solution)/shard_map/all_to_all | solution.py:500
  37.5 0.7 shard_map.57
  38.2 13.6 %all_to_all.20.y = bf16[16,2,32,128]{3,2,1,0:T(8,128)(2,1)S(1)} all-to-all(bf16[16,2,32,128]{3,2,1,0:T(8,128)(2,1)S(1)} %shard_map.57), channel_id=1, replica_groups=mesh['tm_0'=2,'tm_1'=8,'tm_2'=2,'space'=8] {'tm_0','tm_1'}, dimensions={0} | all-to-all | bytes 524288 | tf_op jit(solution)/shard_map/all_to_all | solution.py:504
  51.9 1.9 %collective-permute-start.3 = (bf16[16,2,32,128]{3,2,1,0:T(8,128)(2,1)S(1)}, bf16[16,2,32,128]{3,2,1,0:T(8,128)(2,1)S(1)}, u32[]{:S(2)}, u32[]{:S(2)}) collective-permute-start(bf16[16,2,32,128]{3,2,1,0:T(8,128)(2,1)S(1)} %all_to_all.20.y), channel_id=1, source_target_pairs={{8,1},{1,8},{9,130},{130,9},{10,3},{3,10},{11,132},{132,11},{12,5}... | collective-permute-start | bytes 786440 | tf_op jit(solution)/shard_map/ppermute | solution.py:514
  53.8 0.0 collective-permute-done.6.outer
  53.8 0.7 collective-permute-start.7
  54.6 3.2 %collective-permute-start.4 = (bf16[8,2,32,128]{3,2,1,0:T(8,128)(2,1)S(1)}, bf16[8,2,32,128]{3,2,1,0:T(8,128)(2,1)S(1)}, u32[]{:S(2)}, u32[]{:S(2)}) collective-permute-start(bf16[8,2,32,128]{3,2,1,0:T(8,128)(2,1)S(1)} %slice_select_fusion.3), channel_id=1, source_target_pairs={{0,1},{9,8},{1,130},{138,9},{2,3},{11,10},{3,132},{140,11},{4,5},{... | collective-permute-start | bytes 393224 | tf_op jit(solution)/shard_map/ppermute | solution.py:515
  57.8 2.1 %collective-permute-start.8 = (bf16[16,2,32,128]{3,2,1,0:T(8,128)(2,1)S(1)}, bf16[16,2,32,128]{3,2,1,0:T(8,128)(2,1)S(1)}, u32[]{:S(2)}, u32[]{:S(2)}) collective-permute-start(bf16[16,2,32,128]{3,2,1,0:T(8,128)(2,1)S(1)} %all_to_all.20.y), channel_id=1, source_target_pairs={{0,8},{1,9},{2,10},{3,11},{4,12},{5,13},{6,14},{7,15},{8,0},{9,1},... | collective-permute-start | bytes 786440 | tf_op jit(solution)/shard_map/ppermute | solution.py:516
  59.9 1.7 %collective-permute-done.3.y_a = bf16[16,2,32,128]{3,2,1,0:T(8,128)(2,1)S(1)} collective-permute-done((bf16[16,2,32,128]{3,2,1,0:T(8,128)(2,1)S(1)}, bf16[16,2,32,128]{3,2,1,0:T(8,128)(2,1)S(1)}, u32[]{:S(2)}, u32[]{:S(2)}) %collective-permute-start.3) | collective-permute-done | bytes 262176 | tf_op jit(solution)/shard_map/ppermute | solution.py:514
  61.7 0.1 collective-permute-start.5
  61.8 0.0 collective-permute-done.7.inner
  61.8 1.6 %shard_map.58 = (f32[32,3,64,128]{3,2,1,0:T(8,128)S(1)}, f32[32,3,64,128]{3,2,1,0:T(8,128)S(1)}) custom-call(s32[4]{0:T(128)S(1)} %pad_add_fusion.where, bf16[16,64,128]{2,1,0:T(8,128)(2,1)S(1)} %copy-done.1, bf16[16,64,128]{2,1,0:T(8,128)(2,1)S(1)} %copy-done, bf16[16,64,128]{2,1,0:T(8,128)(2,1)S(1)} %copy-done.2, ...), custom_call_target="tpu_custom_call" | custom-call | tf_op jit(solution)/shard_map/pallas_call | solution.py:425
  63.4 0.0 collective-permute-done.8.yb
  63.4 2.2 %shard_map.59 = (f32[32,2,72,128]{3,2,1,0:T(8,128)S(1)}, f32[32,152,128]{2,1,0:T(8,128)S(1)}, f32[32,152,128]{2,1,0:T(8,128)S(1)}) custom-call(s32[4]{0:T(128)S(1)} %pad_add_fusion.where, bf16[16,2,32,128]{3,2,1,0:T(8,128)(2,1)S(1)} %all_to_all.20.y, bf16[16,2,32,128]{3,2,1,0:T(8,128)(2,1)S(1)} %collective-permute-done.8.yb, ...), custom_call_target="tpu_custom_call" | custom-call | tf_op jit(solution)/shard_map/pallas_call | solution.py:425
  65.7 0.0 collective-permute-done.4.yc
  65.7 0.0 collective-permute-done.5.yd
  65.7 0.0 copy-start.3
  65.7 5.3 %shard_map.60 = (bf16[16,2,32,128]{3,2,1,0:T(8,128)(2,1)S(1)}, f32[32,2,72,128]{3,2,1,0:T(8,128)S(1)}, f32[32,152,128]{2,1,0:T(8,128)S(1)}, f32[32,152,128]{2,1,0:T(8,128)S(1)}) custom-call(s32[4]{0:T(128)S(1)} %pad_add_fusion.where, ...), custom_call_target="tpu_custom_call", output_to_operand_aliasing={{1}: (6, {}), {2}: (7, {}), {3}: (8, {})} | custom-call | tf_op jit(solution)/shard_map/pallas_call | solution.py:425
  71.0 16.4 %all_to_all.21.s = bf16[16,2,32,128]{3,2,1,0:T(8,128)(2,1)S(1)} all-to-all(bf16[16,2,32,128]{3,2,1,0:T(8,128)(2,1)S(1)} %get-tuple-element.20), channel_id=1, replica_groups=mesh['tm_0'=2,'tm_1'=8,'tm_2'=2,'space'=8] {'tm_0','tm_1'}, dimensions={0} | all-to-all | bytes 524288 | tf_op jit(solution)/shard_map/all_to_all | solution.py:530
  87.4 0.8 shard_map.61
  88.2 19.4 %all_to_all.22 = bf16[32,32,128]{2,1,0:T(8,128)(2,1)S(1)} all-to-all(bf16[32,32,128]{2,1,0:T(8,128)(2,1)S(1)} %shard_map.61), channel_id=1, replica_groups=mesh['tm_0'=2,'tm_1'=8,'tm_2'=2,'space'=8] {'tm_0','tm_1','tm_2'}, dimensions={0} | all-to-all | bytes 524288 | tf_op jit(solution)/shard_map/all_to_all | solution.py:534
  107.5 0.0 copy-done.3
  107.5 0.8 shard_map.62
  (4 shorter events, 0.1 us)
Async XLA Ops:
  0.0 22.8 %copy-start.2 = (bf16[16,64,128]{2,1,0:T(8,128)(2,1)S(1)}, bf16[16,64,128]{2,1,0:T(8,128)(2,1)}, u32[]{:S(2)}) copy-start(bf16[16,64,128]{2,1,0:T(8,128)(2,1)} %reaction.1) | copy-start | bytes 786436
  0.0 22.8 %copy-start.1 = (bf16[16,64,128]{2,1,0:T(8,128)(2,1)S(1)}, bf16[16,64,128]{2,1,0:T(8,128)(2,1)}, u32[]{:S(2)}) copy-start(bf16[16,64,128]{2,1,0:T(8,128)(2,1)} %kappa.1) | copy-start | bytes 786436
  0.0 22.8 %copy-start = (bf16[16,64,128]{2,1,0:T(8,128)(2,1)S(1)}, bf16[16,64,128]{2,1,0:T(8,128)(2,1)}, u32[]{:S(2)}) copy-start(bf16[16,64,128]{2,1,0:T(8,128)(2,1)} %initial.1) | copy-start | bytes 786436
  0.0 13.0 %collective-permute-start.2 = (bf16[16,64,128]{2,1,0:T(8,128)(2,1)}, bf16[16,64,128]{2,1,0:T(8,128)(2,1)S(1)}, u32[]{:S(2)}, u32[]{:S(2)}) collective-permute-start(bf16[16,64,128]{2,1,0:T(8,128)(2,1)} %bitcast.20), channel_id=1, source_target_pairs={{0,8},{8,16},{16,24},{24,32},{32,40},{40,48},{48,56},{56,64},{64,7... | collective-permute-start | bytes 786440 | tf_op jit(solution)/shard_map/ppermute | solution.py:471
  2.7 7.5 %collective-permute-start.1 = (bf16[2,64,128]{2,1,0:T(8,128)(2,1)S(1)}, bf16[2,64,128]{2,1,0:T(8,128)(2,1)S(1)}, u32[]{:S(2)}, u32[]{:S(2)}) collective-permute-start(bf16[2,64,128]{2,1,0:T(8,128)(2,1)S(1)} %get-tuple-element.21), channel_id=1, source_target_pairs={{1,2},{2,1},{3,4},{4,3},{5,6},{6,5},{9,10},{10,9},{11,12},{12,11},... | collective-permute-start | bytes 98312 | tf_op jit(solution)/shard_map/ppermute | solution.py:470
  6.0 7.0 %collective-permute-start = (bf16[2,64,128]{2,1,0:T(8,128)(2,1)S(1)}, bf16[2,64,128]{2,1,0:T(8,128)(2,1)S(1)}, u32[]{:S(2)}, u32[]{:S(2)}) collective-permute-start(bf16[2,64,128]{2,1,0:T(8,128)(2,1)S(1)} %get-tuple-element.22), channel_id=1, source_target_pairs={{0,1},{1,0},{2,3},{3,2},{4,5},{5,4},{6,7},{7,6},{8,9},{9,8},{10,11... | collective-permute-start | bytes 98312 | tf_op jit(solution)/shard_map/ppermute | solution.py:469
  13.8 23.7 %all-to-all-start = ((bf16[32,32,128]{2,1,0:T(8,128)(2,1)}), bf16[32,32,128]{2,1,0:T(8,128)(2,1)S(1)}, u32[]{:S(2)}, u32[]{:S(2)}) async-start(bf16[32,32,128]{2,1,0:T(8,128)(2,1)} %bitcast.9), calls=%async_computation | async-start | bytes 524288 | tf_op jit(solution)/shard_map/all_to_all | solution.py:500
  22.9 30.9 %collective-permute-start.6 = (bf16[3,12,64,128]{3,2,1,0:T(8,128)(2,1)S(1)}, bf16[3,12,64,128]{3,2,1,0:T(8,128)(2,1)S(1)}, u32[]{:S(2)}, u32[]{:S(2)}) collective-permute-start(bf16[3,12,64,128]{3,2,1,0:T(8,128)(2,1)S(1)} %slice_select_fusion), channel_id=1, source_target_pairs={{8,1},{1,8},{9,130},{130,9},{10,3},{3,10},{11,132},{132,11},{12,5}... | collective-permute-start | bytes 1769480 | tf_op jit(solution)/shard_map/ppermute | solution.py:474
  51.9 9.8 %collective-permute-start.3 = (bf16[16,2,32,128]{3,2,1,0:T(8,128)(2,1)S(1)}, bf16[16,2,32,128]{3,2,1,0:T(8,128)(2,1)S(1)}, u32[]{:S(2)}, u32[]{:S(2)}) collective-permute-start(bf16[16,2,32,128]{3,2,1,0:T(8,128)(2,1)S(1)} %all_to_all.20.y), channel_id=1, source_target_pairs={{8,1},{1,8},{9,130},{130,9},{10,3},{3,10},{11,132},{132,11},{12,5}... | collective-permute-start | bytes 786440 | tf_op jit(solution)/shard_map/ppermute | solution.py:514
  53.8 8.0 %collective-permute-start.7 = (bf16[3,4,64,128]{3,2,1,0:T(8,128)(2,1)S(1)}, bf16[3,4,64,128]{3,2,1,0:T(8,128)(2,1)S(1)}, u32[]{:S(2)}, u32[]{:S(2)}) collective-permute-start(bf16[3,4,64,128]{3,2,1,0:T(8,128)(2,1)S(1)} %slice_select_fusion.1), channel_id=1, source_target_pairs={{0,8},{1,9},{2,10},{3,11},{4,12},{5,13},{6,14},{7,15},{8,0},{9,1},... | collective-permute-start | bytes 589832 | tf_op jit(solution)/shard_map/ppermute | solution.py:476
  54.6 11.1 %collective-permute-start.4 = (bf16[8,2,32,128]{3,2,1,0:T(8,128)(2,1)S(1)}, bf16[8,2,32,128]{3,2,1,0:T(8,128)(2,1)S(1)}, u32[]{:S(2)}, u32[]{:S(2)}) collective-permute-start(bf16[8,2,32,128]{3,2,1,0:T(8,128)(2,1)S(1)} %slice_select_fusion.3), channel_id=1, source_target_pairs={{0,1},{9,8},{1,130},{138,9},{2,3},{11,10},{3,132},{140,11},{4,5},{... | collective-permute-start | bytes 393224 | tf_op jit(solution)/shard_map/ppermute | solution.py:515
  57.8 5.6 %collective-permute-start.8 = (bf16[16,2,32,128]{3,2,1,0:T(8,128)(2,1)S(1)}, bf16[16,2,32,128]{3,2,1,0:T(8,128)(2,1)S(1)}, u32[]{:S(2)}, u32[]{:S(2)}) collective-permute-start(bf16[16,2,32,128]{3,2,1,0:T(8,128)(2,1)S(1)} %all_to_all.20.y), channel_id=1, source_target_pairs={{0,8},{1,9},{2,10},{3,11},{4,12},{5,13},{6,14},{7,15},{8,0},{9,1},... | collective-permute-start | bytes 786440 | tf_op jit(solution)/shard_map/ppermute | solution.py:516
  61.7 4.0 %collective-permute-start.5 = (bf16[8,2,32,128]{3,2,1,0:T(8,128)(2,1)S(1)}, bf16[8,2,32,128]{3,2,1,0:T(8,128)(2,1)S(1)}, u32[]{:S(2)}, u32[]{:S(2)}) collective-permute-start(bf16[8,2,32,128]{3,2,1,0:T(8,128)(2,1)S(1)} %slice_select_fusion.2), channel_id=1, source_target_pairs={{0,8},{1,9},{2,10},{3,11},{4,12},{5,13},{6,14},{7,15},{8,0},{9,1},... | collective-permute-start | bytes 393224 | tf_op jit(solution)/shard_map/ppermute | solution.py:517
  65.7 41.9 %copy-start.3 = (bf16[1,16,64,128]{3,2,1,0:T(8,128)(2,1)S(1)}, bf16[1,16,64,128]{3,2,1,0:T(8,128)(2,1)}, u32[]{:S(2)}) copy-start(bf16[1,16,64,128]{3,2,1,0:T(8,128)(2,1)} %param.5) | copy-start | bytes 786436

commit v8 on v7

--- a/solution.py
+++ b/solution.py
@@ -11,7 +11,7 @@
 SWEEPS = 6
 STEPS = 32
 CHUNK = 16
-EARLY = 3
+EARLY = 1
 TM = ("tm_0", "tm_1", "tm_2")
 CHIPS = ("tm_0", "tm_1")
 CORE_SPACE = ("tm_2", "space")
@@ -191,44 +191,56 @@
         put(p, part[p] + rim[i] * total + before[p].astype(jnp.float32))
 
 
-def slot_place(where, j, slots):
-    return jnp.where(where[2] == 0, j, (j + slots // 2) % slots)
+def either_order(where, body, slots):
+    @pl.when(where[2] == 0)
+    def _():
+        body(list(range(slots)))
+
+    @pl.when(where[2] != 0)
+    def _():
+        body([(j + slots // 2) % slots for j in range(slots)])
 
 
 def forward_kernel(where, r, out):
     steps, rows, _ = r.shape
     slots = steps // 2
-    places = [slot_place(where, j, slots) for j in range(slots)]
-    for start in range(0, rows, 16):
-        part = pl.ds(start, 16)
-        scaled = [
-            r[n, part].astype(jnp.float32) * (alpha_ratio ** (n / steps)) for n in range(steps)
-        ]
-        spectrum = real_dft(scaled)
-        out[places[0], 0, part] = spectrum[0][0].astype(jnp.bfloat16)
-        out[places[0], 1, part] = spectrum[slots][0].astype(jnp.bfloat16)
-        for j in range(1, slots):
-            out[places[j], 0, part] = spectrum[j][0].astype(jnp.bfloat16)
-            out[places[j], 1, part] = spectrum[j][1].astype(jnp.bfloat16)
+
+    def body(places):
+        for start in range(0, rows, 16):
+            part = pl.ds(start, 16)
+            scaled = [
+                r[n, part].astype(jnp.float32) * (alpha_ratio ** (n / steps)) for n in range(steps)
+            ]
+            spectrum = real_dft(scaled)
+            out[places[0], 0, part] = spectrum[0][0].astype(jnp.bfloat16)
+            out[places[0], 1, part] = spectrum[slots][0].astype(jnp.bfloat16)
+            for j in range(1, slots):
+                out[places[j], 0, part] = spectrum[j][0].astype(jnp.bfloat16)
+                out[places[j], 1, part] = spectrum[j][1].astype(jnp.bfloat16)
+
+    either_order(where, body, slots)
 
 
 def inverse_kernel(where, s, out):
     steps, rows, _ = out.shape
     slots = steps // 2
-    places = [slot_place(where, j, slots) for j in range(slots)]
-    for start in range(0, rows, 16):
-        part = pl.ds(start, 16)
-
-        def given(j, c):
-            return s[places[j], c, part].astype(jnp.float32)
-
-        spectrum = [(given(0, 0), None)]
-        spectrum += [(given(j, 0), given(j, 1)) for j in range(1, slots)]
-        spectrum.append((given(0, 1), None))
-        values = real_inverse(spectrum)
-        for n in range(steps):
-            scale = 1.0 / (alpha_ratio ** (n / steps) * steps)
-            out[n, part] = (values[n] * scale).astype(jnp.bfloat16)
+
+    def body(places):
+        for start in range(0, rows, 16):
+            part = pl.ds(start, 16)
+
+            def given(j, c):
+                return s[places[j], c, part].astype(jnp.float32)
+
+            spectrum = [(given(0, 0), None)]
+            spectrum += [(given(j, 0), given(j, 1)) for j in range(1, slots)]
+            spectrum.append((given(0, 1), None))
+            values = real_inverse(spectrum)
+            for n in range(steps):
+                scale = 1.0 / (alpha_ratio ** (n / steps) * steps)
+                out[n, part] = (values[n] * scale).astype(jnp.bfloat16)
+
+    either_order(where, body, slots)
 
 
 def mirrored(core, i, count):
@@ -254,8 +266,9 @@
         kv, iv, rv = (v.astype(jnp.float32) for v in (kv, iv, rv))
         base = kv * centre_weight + 3.0 * rv * iv * iv
         d0, d1 = s0 + base, s1 + base
-        inv0 = 1.0 / (d0 * d0 + si * si)
-        inv1 = 1.0 / (d1 * d1 + si * si)
+        m0, m1 = d0 * d0 + si * si, d1 * d1 + si * si
+        both = 1.0 / (m0 * m1)
+        inv0, inv1 = m1 * both, m0 * both
         for c, value in enumerate((d0 * inv0, d1 * inv1, si * inv0)):
             inv[e, c] = value
             kinv[e, c] = kv * value
@@ -269,9 +282,9 @@
     def close(i):
         put(wide + planes + mirrored(core, i, narrow), inner[0, i], inner[1, i], inner[2, i])
 
-    in_groups(planes, own, 2)
-    in_groups(wide, far, 2)
-    in_groups(narrow, close, 2)
+    in_groups(planes, own)
+    in_groups(wide, far)
+    in_groups(narrow, close)
 
 
 def row_starts(rows):

time: 109 us -> 109 us (level)
  transfers between devices with their start and end apart: 10 -> 10, of which waited for: 3 -> 3; matrix products, arithmetic and copies ran while one was open for 1% -> 1% of each run, Pallas kernels for 7% -> 6%
where the time goes in v8:
time: 109 us; the launch traced here: 108 us
  blocking collectives  49.4 us (45%)
  starting transfers between devices  28.4 us (26%)
  Pallas kernels  15.1 us (14%)
  waiting for transfers between devices  14.3 us (13%)
    all_to_all x1, blocking collectives, iteration(): returned = lax.all_to_all(correction, TM, 0, 0, tiled=True)  19.4 us
    all_to_all x1, blocking collectives, iteration(): modes = lax.all_to_all(solved, CHIPS, 0, 0, tiled=True)  16.4 us
    pallas_call x8, Pallas kernels, call(): pl.pallas_call(kernel, out_shape=outs, in_specs=[SMEM] * scalars + [HBM]...  15.1 us
    all_to_all x1, blocking collectives, iteration(): y = lax.all_to_all(spectrum, CHIPS, 0, 0, tiled=True)  13.6 us
    all_to_all x1, waiting for transfers between devices, iteration(): lax.all_to_all(residual.reshape(members, share, lanes), TM, 0, 0, tiled=T...  9.77 us
    all_to_all x1, starting transfers between devices, iteration(): lax.all_to_all(residual.reshape(members, share, lanes), TM, 0, 0, tiled=T...  8.97 us
    ppermute x1, starting transfers between devices, iteration(): rim = lax.ppermute(rim, SIDE_CORE_SPACE, outer)  4.8 us
    ppermute x1, starting transfers between devices, iteration(): odd_pair = lax.ppermute(jnp.where(odd == 1, high, low), 'space', odd_first)  3.28 us
  transfers between devices with their start and end apart: 10, of which 3 were waited for; matrix products, arithmetic and copies ran while one was open for 1% of the time, Pallas kernels for 6%

profile of v8, /device:TPU:16, one launch (start us, length us, event | category | flops | bytes accessed | tf_op | source)
XLA Modules:
  0.0 108.5 jit_solution(15794757552681317453)
XLA Ops:
  0.0 0.0 copy-start.2
  0.0 0.0 copy-start.1
  0.0 0.0 copy-start
  0.0 1.9 %collective-permute-start.2 = (bf16[16,64,128]{2,1,0:T(8,128)(2,1)}, bf16[16,64,128]{2,1,0:T(8,128)(2,1)S(1)}, u32[]{:S(2)}, u32[]{:S(2)}) collective-permute-start(bf16[16,64,128]{2,1,0:T(8,128)(2,1)} %bitcast.20), channel_id=1, source_target_pairs={{0,8},{8,16},{16,24},{24,32},{32,40},{40,48},{48,56},{56,64},{64,7... | collective-permute-start | bytes 786440 | tf_op jit(solution)/shard_map/ppermute | solution.py:484
  1.9 0.8 select_bitcast_fusion
  2.7 3.3 %collective-permute-start.1 = (bf16[2,64,128]{2,1,0:T(8,128)(2,1)S(1)}, bf16[2,64,128]{2,1,0:T(8,128)(2,1)S(1)}, u32[]{:S(2)}, u32[]{:S(2)}) collective-permute-start(bf16[2,64,128]{2,1,0:T(8,128)(2,1)S(1)} %get-tuple-element.21), channel_id=1, source_target_pairs={{1,2},{2,1},{3,4},{4,3},{5,6},{6,5},{9,10},{10,9},{11,12},{12,11},... | collective-permute-start | bytes 98312 | tf_op jit(solution)/shard_map/ppermute | solution.py:483
  6.0 1.5 %collective-permute-start = (bf16[2,64,128]{2,1,0:T(8,128)(2,1)S(1)}, bf16[2,64,128]{2,1,0:T(8,128)(2,1)S(1)}, u32[]{:S(2)}, u32[]{:S(2)}) collective-permute-start(bf16[2,64,128]{2,1,0:T(8,128)(2,1)S(1)} %get-tuple-element.22), channel_id=1, source_target_pairs={{0,1},{1,0},{2,3},{3,2},{4,5},{5,4},{6,7},{7,6},{8,9},{9,8},{10,11... | collective-permute-start | bytes 98312 | tf_op jit(solution)/shard_map/ppermute | solution.py:482
  7.4 0.1 pad_add_fusion.where
  7.5 2.7 %shard_map.55 = (f32[16,64,128]{2,1,0:T(8,128)S(1)}, f32[4,64,128]{2,1,0:T(8,128)S(1)}) custom-call(s32[4]{0:T(128)S(1)} %pad_add_fusion.where, bf16[16,64,128]{2,1,0:T(8,128)(2,1)} %bitcast.21, bf16[16,64,128]{2,1,0:T(8,128)(2,1)} %initial.1, bf16[16,64,128]{2,1,0:T(8,128)(2,1)} %bitcast.24, bf16[16,64,128]{2,1,0:T(8,128)(2,1)} %kappa.1, ...), custom_call_target="tpu_custom_call" | custom-call | flops 20000000 | bytes 2500000 | tf_op jit(solution)/shard_map/pallas_call | solution.py:438
  10.2 0.0 collective-permute-done.1.odd_pair
  10.2 2.7 %collective-permute-done.even_pair = bf16[2,64,128]{2,1,0:T(8,128)(2,1)S(1)} collective-permute-done((bf16[2,64,128]{2,1,0:T(8,128)(2,1)S(1)}, bf16[2,64,128]{2,1,0:T(8,128)(2,1)S(1)}, u32[]{:S(2)}, u32[]{:S(2)}) %collective-permute-start) | collective-permute-done | bytes 32800 | tf_op jit(solution)/shard_map/ppermute | solution.py:482
  13.0 0.0 collective-permute-done.2.before
  13.0 0.8 shard_map.56
  13.8 9.0 %all-to-all-start = ((bf16[32,32,128]{2,1,0:T(8,128)(2,1)}), bf16[32,32,128]{2,1,0:T(8,128)(2,1)S(1)}, u32[]{:S(2)}, u32[]{:S(2)}) async-start(bf16[32,32,128]{2,1,0:T(8,128)(2,1)} %bitcast.9), calls=%async_computation | async-start | bytes 524288 | tf_op jit(solution)/shard_map/all_to_all | solution.py:513
  22.7 0.0 copy-done.2
  22.8 0.0 copy-done.1
  22.8 0.0 copy-done
  22.8 0.1 pad_maximum_fusion
  22.9 4.8 %collective-permute-start.6 = (bf16[3,12,64,128]{3,2,1,0:T(8,128)(2,1)S(1)}, bf16[3,12,64,128]{3,2,1,0:T(8,128)(2,1)S(1)}, u32[]{:S(2)}, u32[]{:S(2)}) collective-permute-start(bf16[3,12,64,128]{3,2,1,0:T(8,128)(2,1)S(1)} %slice_select_fusion), channel_id=1, source_target_pairs={{8,1},{1,8},{9,130},{130,9},{10,3},{3,10},{11,132},{132,11},{12,5}... | collective-permute-start | bytes 1769480 | tf_op jit(solution)/shard_map/ppermute | solution.py:487
  27.7 9.8 %all-to-all-done.r = bf16[32,32,128]{2,1,0:T(8,128)(2,1)S(1)} async-done(((bf16[32,32,128]{2,1,0:T(8,128)(2,1)}), bf16[32,32,128]{2,1,0:T(8,128)(2,1)S(1)}, u32[]{:S(2)}, u32[]{:S(2)}) %all-to-all-start) | async-done | bytes 262176 | tf_op jit(solution)/shard_map/all_to_all | solution.py:513
  37.5 0.7 shard_map.57
  38.2 13.6 %all_to_all.20.y = bf16[16,2,32,128]{3,2,1,0:T(8,128)(2,1)S(1)} all-to-all(bf16[16,2,32,128]{3,2,1,0:T(8,128)(2,1)S(1)} %shard_map.57), channel_id=1, replica_groups=mesh['tm_0'=2,'tm_1'=8,'tm_2'=2,'space'=8] {'tm_0','tm_1'}, dimensions={0} | all-to-all | bytes 524288 | tf_op jit(solution)/shard_map/all_to_all | solution.py:517
  51.9 1.9 %collective-permute-start.3 = (bf16[16,2,32,128]{3,2,1,0:T(8,128)(2,1)S(1)}, bf16[16,2,32,128]{3,2,1,0:T(8,128)(2,1)S(1)}, u32[]{:S(2)}, u32[]{:S(2)}) collective-permute-start(bf16[16,2,32,128]{3,2,1,0:T(8,128)(2,1)S(1)} %all_to_all.20.y), channel_id=1, source_target_pairs={{8,1},{1,8},{9,130},{130,9},{10,3},{3,10},{11,132},{132,11},{12,5}... | collective-permute-start | bytes 786440 | tf_op jit(solution)/shard_map/ppermute | solution.py:527
  53.8 0.0 collective-permute-done.6.outer
  53.8 0.7 collective-permute-start.7
  54.6 3.2 %collective-permute-start.4 = (bf16[8,2,32,128]{3,2,1,0:T(8,128)(2,1)S(1)}, bf16[8,2,32,128]{3,2,1,0:T(8,128)(2,1)S(1)}, u32[]{:S(2)}, u32[]{:S(2)}) collective-permute-start(bf16[8,2,32,128]{3,2,1,0:T(8,128)(2,1)S(1)} %slice_select_fusion.3), channel_id=1, source_target_pairs={{0,1},{9,8},{1,130},{138,9},{2,3},{11,10},{3,132},{140,11},{4,5},{... | collective-permute-start | bytes 393224 | tf_op jit(solution)/shard_map/ppermute | solution.py:528
  57.8 2.1 %collective-permute-start.8 = (bf16[16,2,32,128]{3,2,1,0:T(8,128)(2,1)S(1)}, bf16[16,2,32,128]{3,2,1,0:T(8,128)(2,1)S(1)}, u32[]{:S(2)}, u32[]{:S(2)}) collective-permute-start(bf16[16,2,32,128]{3,2,1,0:T(8,128)(2,1)S(1)} %all_to_all.20.y), channel_id=1, source_target_pairs={{0,8},{1,9},{2,10},{3,11},{4,12},{5,13},{6,14},{7,15},{8,0},{9,1},... | collective-permute-start | bytes 786440 | tf_op jit(solution)/shard_map/ppermute | solution.py:529
  59.9 1.7 %collective-permute-done.3.y_a = bf16[16,2,32,128]{3,2,1,0:T(8,128)(2,1)S(1)} collective-permute-done((bf16[16,2,32,128]{3,2,1,0:T(8,128)(2,1)S(1)}, bf16[16,2,32,128]{3,2,1,0:T(8,128)(2,1)S(1)}, u32[]{:S(2)}, u32[]{:S(2)}) %collective-permute-start.3) | collective-permute-done | bytes 262176 | tf_op jit(solution)/shard_map/ppermute | solution.py:527
  61.7 0.1 collective-permute-start.5
  61.8 0.0 collective-permute-done.7.inner
  61.8 1.7 %shard_map.58 = (f32[32,3,64,128]{3,2,1,0:T(8,128)S(1)}, f32[32,3,64,128]{3,2,1,0:T(8,128)S(1)}) custom-call(s32[4]{0:T(128)S(1)} %pad_add_fusion.where, bf16[16,64,128]{2,1,0:T(8,128)(2,1)S(1)} %copy-done.1, bf16[16,64,128]{2,1,0:T(8,128)(2,1)S(1)} %copy-done, bf16[16,64,128]{2,1,0:T(8,128)(2,1)S(1)} %copy-done.2, ...), custom_call_target="tpu_custom_call" | custom-call | tf_op jit(solution)/shard_map/pallas_call | solution.py:438
  63.5 0.0 collective-permute-done.8.yb
  63.5 1.6 %shard_map.59 = (f32[32,2,72,128]{3,2,1,0:T(8,128)S(1)}, f32[32,152,128]{2,1,0:T(8,128)S(1)}, f32[32,152,128]{2,1,0:T(8,128)S(1)}) custom-call(s32[4]{0:T(128)S(1)} %pad_add_fusion.where, bf16[16,2,32,128]{3,2,1,0:T(8,128)(2,1)S(1)} %all_to_all.20.y, bf16[16,2,32,128]{3,2,1,0:T(8,128)(2,1)S(1)} %collective-permute-done.8.yb, ...), custom_call_target="tpu_custom_call" | custom-call | tf_op jit(solution)/shard_map/pallas_call | solution.py:438
  65.1 0.0 collective-permute-done.4.yc
  65.1 0.0 collective-permute-done.5.yd
  65.2 0.0 copy-start.3
  65.2 6.0 %shard_map.60 = (bf16[16,2,32,128]{3,2,1,0:T(8,128)(2,1)S(1)}, f32[32,2,72,128]{3,2,1,0:T(8,128)S(1)}, f32[32,152,128]{2,1,0:T(8,128)S(1)}, f32[32,152,128]{2,1,0:T(8,128)S(1)}) custom-call(s32[4]{0:T(128)S(1)} %pad_add_fusion.where, ...), custom_call_target="tpu_custom_call", output_to_operand_aliasing={{1}: (6, {}), {2}: (7, {}), {3}: (8, {})} | custom-call | tf_op jit(solution)/shard_map/pallas_call | solution.py:438
  71.2 16.4 %all_to_all.21.s = bf16[16,2,32,128]{3,2,1,0:T(8,128)(2,1)S(1)} all-to-all(bf16[16,2,32,128]{3,2,1,0:T(8,128)(2,1)S(1)} %get-tuple-element.20), channel_id=1, replica_groups=mesh['tm_0'=2,'tm_1'=8,'tm_2'=2,'space'=8] {'tm_0','tm_1'}, dimensions={0} | all-to-all | bytes 524288 | tf_op jit(solution)/shard_map/all_to_all | solution.py:543
  87.6 0.8 shard_map.61
  88.3 19.4 %all_to_all.22 = bf16[32,32,128]{2,1,0:T(8,128)(2,1)S(1)} all-to-all(bf16[32,32,128]{2,1,0:T(8,128)(2,1)S(1)} %shard_map.61), channel_id=1, replica_groups=mesh['tm_0'=2,'tm_1'=8,'tm_2'=2,'space'=8] {'tm_0','tm_1','tm_2'}, dimensions={0} | all-to-all | bytes 524288 | tf_op jit(solution)/shard_map/all_to_all | solution.py:547
  107.7 0.0 copy-done.3
  107.7 0.8 shard_map.62
  (4 shorter events, 0.1 us)
Async XLA Ops:
  0.0 22.8 %copy-start.2 = (bf16[16,64,128]{2,1,0:T(8,128)(2,1)S(1)}, bf16[16,64,128]{2,1,0:T(8,128)(2,1)}, u32[]{:S(2)}) copy-start(bf16[16,64,128]{2,1,0:T(8,128)(2,1)} %reaction.1) | copy-start | bytes 786436
  0.0 22.8 %copy-start.1 = (bf16[16,64,128]{2,1,0:T(8,128)(2,1)S(1)}, bf16[16,64,128]{2,1,0:T(8,128)(2,1)}, u32[]{:S(2)}) copy-start(bf16[16,64,128]{2,1,0:T(8,128)(2,1)} %kappa.1) | copy-start | bytes 786436
  0.0 22.8 %copy-start = (bf16[16,64,128]{2,1,0:T(8,128)(2,1)S(1)}, bf16[16,64,128]{2,1,0:T(8,128)(2,1)}, u32[]{:S(2)}) copy-start(bf16[16,64,128]{2,1,0:T(8,128)(2,1)} %initial.1) | copy-start | bytes 786436
  0.0 13.0 %collective-permute-start.2 = (bf16[16,64,128]{2,1,0:T(8,128)(2,1)}, bf16[16,64,128]{2,1,0:T(8,128)(2,1)S(1)}, u32[]{:S(2)}, u32[]{:S(2)}) collective-permute-start(bf16[16,64,128]{2,1,0:T(8,128)(2,1)} %bitcast.20), channel_id=1, source_target_pairs={{0,8},{8,16},{16,24},{24,32},{32,40},{40,48},{48,56},{56,64},{64,7... | collective-permute-start | bytes 786440 | tf_op jit(solution)/shard_map/ppermute | solution.py:484
  2.7 7.5 %collective-permute-start.1 = (bf16[2,64,128]{2,1,0:T(8,128)(2,1)S(1)}, bf16[2,64,128]{2,1,0:T(8,128)(2,1)S(1)}, u32[]{:S(2)}, u32[]{:S(2)}) collective-permute-start(bf16[2,64,128]{2,1,0:T(8,128)(2,1)S(1)} %get-tuple-element.21), channel_id=1, source_target_pairs={{1,2},{2,1},{3,4},{4,3},{5,6},{6,5},{9,10},{10,9},{11,12},{12,11},... | collective-permute-start | bytes 98312 | tf_op jit(solution)/shard_map/ppermute | solution.py:483
  6.0 7.0 %collective-permute-start = (bf16[2,64,128]{2,1,0:T(8,128)(2,1)S(1)}, bf16[2,64,128]{2,1,0:T(8,128)(2,1)S(1)}, u32[]{:S(2)}, u32[]{:S(2)}) collective-permute-start(bf16[2,64,128]{2,1,0:T(8,128)(2,1)S(1)} %get-tuple-element.22), channel_id=1, source_target_pairs={{0,1},{1,0},{2,3},{3,2},{4,5},{5,4},{6,7},{7,6},{8,9},{9,8},{10,11... | collective-permute-start | bytes 98312 | tf_op jit(solution)/shard_map/ppermute | solution.py:482
  13.8 23.7 %all-to-all-start = ((bf16[32,32,128]{2,1,0:T(8,128)(2,1)}), bf16[32,32,128]{2,1,0:T(8,128)(2,1)S(1)}, u32[]{:S(2)}, u32[]{:S(2)}) async-start(bf16[32,32,128]{2,1,0:T(8,128)(2,1)} %bitcast.9), calls=%async_computation | async-start | bytes 524288 | tf_op jit(solution)/shard_map/all_to_all | solution.py:513
  22.9 30.9 %collective-permute-start.6 = (bf16[3,12,64,128]{3,2,1,0:T(8,128)(2,1)S(1)}, bf16[3,12,64,128]{3,2,1,0:T(8,128)(2,1)S(1)}, u32[]{:S(2)}, u32[]{:S(2)}) collective-permute-start(bf16[3,12,64,128]{3,2,1,0:T(8,128)(2,1)S(1)} %slice_select_fusion), channel_id=1, source_target_pairs={{8,1},{1,8},{9,130},{130,9},{10,3},{3,10},{11,132},{132,11},{12,5}... | collective-permute-start | bytes 1769480 | tf_op jit(solution)/shard_map/ppermute | solution.py:487
  51.9 9.8 %collective-permute-start.3 = (bf16[16,2,32,128]{3,2,1,0:T(8,128)(2,1)S(1)}, bf16[16,2,32,128]{3,2,1,0:T(8,128)(2,1)S(1)}, u32[]{:S(2)}, u32[]{:S(2)}) collective-permute-start(bf16[16,2,32,128]{3,2,1,0:T(8,128)(2,1)S(1)} %all_to_all.20.y), channel_id=1, source_target_pairs={{8,1},{1,8},{9,130},{130,9},{10,3},{3,10},{11,132},{132,11},{12,5}... | collective-permute-start | bytes 786440 | tf_op jit(solution)/shard_map/ppermute | solution.py:527
  53.8 8.0 %collective-permute-start.7 = (bf16[3,4,64,128]{3,2,1,0:T(8,128)(2,1)S(1)}, bf16[3,4,64,128]{3,2,1,0:T(8,128)(2,1)S(1)}, u32[]{:S(2)}, u32[]{:S(2)}) collective-permute-start(bf16[3,4,64,128]{3,2,1,0:T(8,128)(2,1)S(1)} %slice_select_fusion.1), channel_id=1, source_target_pairs={{0,8},{1,9},{2,10},{3,11},{4,12},{5,13},{6,14},{7,15},{8,0},{9,1},... | collective-permute-start | bytes 589832 | tf_op jit(solution)/shard_map/ppermute | solution.py:489
  54.6 10.5 %collective-permute-start.4 = (bf16[8,2,32,128]{3,2,1,0:T(8,128)(2,1)S(1)}, bf16[8,2,32,128]{3,2,1,0:T(8,128)(2,1)S(1)}, u32[]{:S(2)}, u32[]{:S(2)}) collective-permute-start(bf16[8,2,32,128]{3,2,1,0:T(8,128)(2,1)S(1)} %slice_select_fusion.3), channel_id=1, source_target_pairs={{0,1},{9,8},{1,130},{138,9},{2,3},{11,10},{3,132},{140,11},{4,5},{... | collective-permute-start | bytes 393224 | tf_op jit(solution)/shard_map/ppermute | solution.py:528
  57.8 5.6 %collective-permute-start.8 = (bf16[16,2,32,128]{3,2,1,0:T(8,128)(2,1)S(1)}, bf16[16,2,32,128]{3,2,1,0:T(8,128)(2,1)S(1)}, u32[]{:S(2)}, u32[]{:S(2)}) collective-permute-start(bf16[16,2,32,128]{3,2,1,0:T(8,128)(2,1)S(1)} %all_to_all.20.y), channel_id=1, source_target_pairs={{0,8},{1,9},{2,10},{3,11},{4,12},{5,13},{6,14},{7,15},{8,0},{9,1},... | collective-permute-start | bytes 786440 | tf_op jit(solution)/shard_map/ppermute | solution.py:529
  61.7 3.5 %collective-permute-start.5 = (bf16[8,2,32,128]{3,2,1,0:T(8,128)(2,1)S(1)}, bf16[8,2,32,128]{3,2,1,0:T(8,128)(2,1)S(1)}, u32[]{:S(2)}, u32[]{:S(2)}) collective-permute-start(bf16[8,2,32,128]{3,2,1,0:T(8,128)(2,1)S(1)} %slice_select_fusion.2), channel_id=1, source_target_pairs={{0,8},{1,9},{2,10},{3,11},{4,12},{5,13},{6,14},{7,15},{8,0},{9,1},... | collective-permute-start | bytes 393224 | tf_op jit(solution)/shard_map/ppermute | solution.py:530
  65.2 42.6 %copy-start.3 = (bf16[1,16,64,128]{3,2,1,0:T(8,128)(2,1)S(1)}, bf16[1,16,64,128]{3,2,1,0:T(8,128)(2,1)}, u32[]{:S(2)}) copy-start(bf16[1,16,64,128]{3,2,1,0:T(8,128)(2,1)} %param.5) | copy-start | bytes 786436

commit v9 on v8

--- a/solution.py
+++ b/solution.py
@@ -23,7 +23,6 @@
 centre_weight = 6.0 * (near_weight + far_weight)
 VMEM = pl.BlockSpec(memory_space=pltpu.VMEM)
 HBM = pl.BlockSpec(memory_space=pltpu.HBM)
-SMEM = pl.BlockSpec(memory_space=pltpu.SMEM)
 PAD = 8
 
 
@@ -160,7 +159,7 @@
         rim[i] = kappa[p].astype(jnp.float32)
 
 
-def residual_kernel(odd, part, rim, even_pair, odd_pair, before, out):
+def residual_kernel(where, part, rim, even_pair, odd_pair, before, out):
     planes, rows, _ = part.shape
     share = out.shape[2]
     per_plane = rows // share
@@ -174,7 +173,7 @@
 
     for p in range(2, planes - 2):
         put(p, part[p] + before[p].astype(jnp.float32))
-    upper = odd[0] == 1
+    upper = where[4] == 1
 
     def chosen(a, b, i):
         return jnp.where(upper, a[i].astype(jnp.float32), b[i].astype(jnp.float32))
@@ -429,16 +428,31 @@
         out[p] = (state[p].astype(jnp.float32) + value).astype(jnp.bfloat16)
 
 
-def call(kernel, shapes, inputs, scratch=(), scalars=0, anywhere=0, flops=None, aliases=None):
+def place():
+    slots = lax.axis_size(CHIPS)
+    side, chip, core = (lax.axis_index(a) for a in TM)
+    slab = lax.axis_index("space")
+    per_side = lax.axis_size("tm_1")
+    flip = slab // 2 % 2
+    slot = (side * per_side + chip + flip * (slots // 2)) % slots
+    timestep = (side * per_side + chip) * lax.axis_size("tm_2") + core
+    return core, slot, flip, timestep, slab % 2
+
+
+def placed(kernel):
+    return lambda *refs: kernel(place(), *refs)
+
+
+def call(kernel, shapes, inputs, scratch=(), anywhere=0, flops=None, aliases=None):
     outs = [jax.ShapeDtypeStruct(s, d) for s, d in shapes]
     cost = None
     if flops is not None:
         cost = pl.CostEstimate(flops=flops, transcendentals=0, bytes_accessed=flops // 8)
-    rest = len(inputs) - scalars - anywhere
+    rest = len(inputs) - anywhere
     return pl.pallas_call(
         kernel,
         out_shape=outs,
-        in_specs=[SMEM] * scalars + [HBM] * anywhere + [VMEM] * rest,
+        in_specs=[HBM] * anywhere + [VMEM] * rest,
         out_specs=[VMEM] * len(outs),
         scratch_shapes=list(scratch),
         cost_estimate=cost,
@@ -458,13 +472,8 @@
     wide = 2 * SWEEPS
     narrow = wide - own
     ext = own + 2 * wide
-    bf16, f32, i32 = jnp.bfloat16, jnp.float32, jnp.int32
+    bf16, f32 = jnp.bfloat16, jnp.float32
     core = lax.axis_index("tm_2")
-    flip = lax.axis_index("space") // 2 % 2
-    half_slots = slots // 2
-    slot = lax.axis_index(CHIPS)
-    slot = jnp.where(flip == 0, slot, (slot + half_slots) % slots)
-    where = jnp.stack([core, slot, flip, lax.axis_index(TM)]).astype(i32)
     u = state[0]
 
     outer, same = [], []
@@ -490,37 +499,31 @@
 
     block = ((planes, rows, lanes), bf16)
     part, edge = call(
-        local_kernel,
+        placed(local_kernel),
         [((planes, rows, lanes), f32), ((4, rows, lanes), f32)],
-        [where]
-        + [
+        [
             pltpu.with_memory_space_constraint(v, pltpu.HBM)
             for v in (u, initial, forcing[0], kappa, reaction)
         ],
         [pltpu.VMEM((planes + 4, rows + 2 * PAD, lanes), f32)]
         + [pltpu.VMEM(*block)] * 5
         + [pltpu.SemaphoreType.DMA((5,))],
-        scalars=1,
         anywhere=5,
         flops=20_000_000,
     )
     (residual,) = call(
-        residual_kernel,
+        placed(residual_kernel),
         [((slots, 2, share, lanes), bf16)],
-        [odd.astype(i32).reshape(1), part, edge, even_pair, odd_pair, before],
-        scalars=1,
+        [part, edge, even_pair, odd_pair, before],
     )
     cells = lax.all_to_all(residual.reshape(members, share, lanes), TM, 0, 0, tiled=True)
-    (spectrum,) = call(
-        forward_kernel, [((slots, 2, share, lanes), bf16)], [where, cells], scalars=1
-    )
+    (spectrum,) = call(placed(forward_kernel), [((slots, 2, share, lanes), bf16)], [cells])
     y = lax.all_to_all(spectrum, CHIPS, 0, 0, tiled=True)
 
     fields = call(
-        coefficient_kernel,
+        placed(coefficient_kernel),
         [((ext, 3, rows, lanes), f32)] * 2,
-        [where, kappa, initial, reaction, rim, inner],
-        scalars=1,
+        [kappa, initial, reaction, rim, inner],
     )
     n = per_plane * narrow
     first = core == 0
@@ -531,19 +534,16 @@
     tall = 2 * rows + 3 * PAD
     buffers = [((ext, 2, rows + PAD, lanes), f32), ((ext, tall, lanes), f32), ((ext, tall, lanes), f32)]
     band = [pltpu.VMEM((2 * lanes, lanes), bf16)]
-    state_arrays = call(inside_kernel, buffers, [where, y, yb, *fields], band, scalars=1)
+    state_arrays = call(placed(inside_kernel), buffers, [y, yb, *fields], band)
     solved = call(
-        sweeps_kernel,
+        placed(sweeps_kernel),
         [((slots, 2, share, lanes), bf16), *buffers],
-        [where, ya, yc, yd, *fields, *state_arrays],
+        [ya, yc, yd, *fields, *state_arrays],
         band,
-        scalars=1,
-        aliases={6: 1, 7: 2, 8: 3},
+        aliases={5: 1, 6: 2, 7: 3},
     )[0]
     modes = lax.all_to_all(solved, CHIPS, 0, 0, tiled=True)
-    (correction,) = call(
-        inverse_kernel, [((members, share, lanes), bf16)], [where, modes], scalars=1
-    )
+    (correction,) = call(placed(inverse_kernel), [((members, share, lanes), bf16)], [modes])
     returned = lax.all_to_all(correction, TM, 0, 0, tiled=True)
     (updated,) = call(
         final_kernel, [((planes, rows, lanes), bf16)], [u, returned.reshape(slots, 2, share, lanes)]

time: 109 us -> 106 us (0.972)
  Pallas kernels: 15.1 us -> 11.2 us
    pallas_call x8, Pallas kernels: 15.1 us -> 11.2 us  [call(): pl.pallas_call(kernel, out_shape=outs, in_specs=[HBM] * anywhere + [VMEM]...]
  transfers between devices with their start and end apart: 10 -> 10, of which waited for: 3 -> 3; matrix products, arithmetic and copies ran while one was open for 1% -> 1% of each run, Pallas kernels for 6% -> 4%
where the time goes in v9:
time: 106 us; the launch traced here: 105 us
  blocking collectives  49.3 us (47%)
  starting transfers between devices  28.5 us (27%)
  waiting for transfers between devices  14.5 us (14%)
  Pallas kernels  11.2 us (11%)
    all_to_all x1, blocking collectives, iteration(): returned = lax.all_to_all(correction, TM, 0, 0, tiled=True)  19.3 us
    all_to_all x1, blocking collectives, iteration(): modes = lax.all_to_all(solved, CHIPS, 0, 0, tiled=True)  16.4 us
    all_to_all x1, blocking collectives, iteration(): y = lax.all_to_all(spectrum, CHIPS, 0, 0, tiled=True)  13.6 us
    pallas_call x8, Pallas kernels, call(): pl.pallas_call(kernel, out_shape=outs, in_specs=[HBM] * anywhere + [VMEM]...  11.2 us
    all_to_all x1, waiting for transfers between devices, iteration(): lax.all_to_all(residual.reshape(members, share, lanes), TM, 0, 0, tiled=T...  9.39 us
    all_to_all x1, starting transfers between devices, iteration(): lax.all_to_all(residual.reshape(members, share, lanes), TM, 0, 0, tiled=T...  8.61 us
    ppermute x1, starting transfers between devices, iteration(): rim = lax.ppermute(rim, SIDE_CORE_SPACE, outer)  5.16 us
    ppermute x1, waiting for transfers between devices, iteration(): lax.ppermute(jnp.where(odd == 1, low, high), 'space', even_first)  3.34 us
  transfers between devices with their start and end apart: 10, of which 3 were waited for; matrix products, arithmetic and copies ran while one was open for 1% of the time, Pallas kernels for 4%

profile of v9, /device:TPU:16, one launch (start us, length us, event | category | flops | bytes accessed | tf_op | source)
XLA Modules:
  0.0 104.8 jit_solution(16814053854130452569)
XLA Ops:
  0.0 0.0 copy-start.2
  0.0 0.0 copy-start.1
  0.0 0.0 copy-start
  0.0 1.9 %collective-permute-start.2 = (bf16[16,64,128]{2,1,0:T(8,128)(2,1)}, bf16[16,64,128]{2,1,0:T(8,128)(2,1)S(1)}, u32[]{:S(2)}, u32[]{:S(2)}) collective-permute-start(bf16[16,64,128]{2,1,0:T(8,128)(2,1)} %bitcast.15), channel_id=1, source_target_pairs={{0,8},{8,16},{16,24},{24,32},{32,40},{40,48},{48,56},{56,64},{64,7... | collective-permute-start | bytes 786440 | tf_op jit(solution)/shard_map/ppermute | solution.py:493
  1.9 0.8 select_bitcast_fusion
  2.7 3.3 %collective-permute-start.1 = (bf16[2,64,128]{2,1,0:T(8,128)(2,1)S(1)}, bf16[2,64,128]{2,1,0:T(8,128)(2,1)S(1)}, u32[]{:S(2)}, u32[]{:S(2)}) collective-permute-start(bf16[2,64,128]{2,1,0:T(8,128)(2,1)S(1)} %get-tuple-element.21), channel_id=1, source_target_pairs={{1,2},{2,1},{3,4},{4,3},{5,6},{6,5},{9,10},{10,9},{11,12},{12,11},... | collective-permute-start | bytes 98312 | tf_op jit(solution)/shard_map/ppermute | solution.py:492
  6.0 1.5 %collective-permute-start = (bf16[2,64,128]{2,1,0:T(8,128)(2,1)S(1)}, bf16[2,64,128]{2,1,0:T(8,128)(2,1)S(1)}, u32[]{:S(2)}, u32[]{:S(2)}) collective-permute-start(bf16[2,64,128]{2,1,0:T(8,128)(2,1)S(1)} %get-tuple-element.22), channel_id=1, source_target_pairs={{0,1},{1,0},{2,3},{3,2},{4,5},{5,4},{6,7},{7,6},{8,9},{9,8},{10,11... | collective-permute-start | bytes 98312 | tf_op jit(solution)/shard_map/ppermute | solution.py:491
  7.4 2.2 %shard_map.55 = (f32[16,64,128]{2,1,0:T(8,128)S(1)}, f32[4,64,128]{2,1,0:T(8,128)S(1)}) custom-call(bf16[16,64,128]{2,1,0:T(8,128)(2,1)} %bitcast.16, bf16[16,64,128]{2,1,0:T(8,128)(2,1)} %refs_1_.3, bf16[16,64,128]{2,1,0:T(8,128)(2,1)} %bitcast.19, bf16[16,64,128]{2,1,0:T(8,128)(2,1)} %refs_0_.1, bf16[16,64,128]{2,1,0:T(8,128)(2,1)} %refs_2_.1), custom_call_target="tpu_custom_call" | custom-call | flops 20000000 | bytes 2500000 | tf_op jit(solution)/shard_map/pallas_call | solution.py:452
  9.6 0.0 collective-permute-done.1.refs_3_
  9.6 3.3 %collective-permute-done.refs_2_ = bf16[2,64,128]{2,1,0:T(8,128)(2,1)S(1)} collective-permute-done((bf16[2,64,128]{2,1,0:T(8,128)(2,1)S(1)}, bf16[2,64,128]{2,1,0:T(8,128)(2,1)S(1)}, u32[]{:S(2)}, u32[]{:S(2)}) %collective-permute-start) | collective-permute-done | bytes 32800 | tf_op jit(solution)/shard_map/ppermute | solution.py:491
  13.0 0.0 collective-permute-done.2.refs_4_
  13.0 0.8 shard_map.56
  13.7 8.6 %all-to-all-start = ((bf16[32,32,128]{2,1,0:T(8,128)(2,1)}), bf16[32,32,128]{2,1,0:T(8,128)(2,1)S(1)}, u32[]{:S(2)}, u32[]{:S(2)}) async-start(bf16[32,32,128]{2,1,0:T(8,128)(2,1)} %bitcast.4), calls=%async_computation | async-start | bytes 524288 | tf_op jit(solution)/shard_map/all_to_all | solution.py:519
  22.4 0.0 copy-done.2
  22.4 0.0 copy-done.1
  22.4 0.0 copy-done
  22.4 0.1 pad_maximum_fusion
  22.6 5.2 %collective-permute-start.6 = (bf16[3,12,64,128]{3,2,1,0:T(8,128)(2,1)S(1)}, bf16[3,12,64,128]{3,2,1,0:T(8,128)(2,1)S(1)}, u32[]{:S(2)}, u32[]{:S(2)}) collective-permute-start(bf16[3,12,64,128]{3,2,1,0:T(8,128)(2,1)S(1)} %slice_select_fusion), channel_id=1, source_target_pairs={{8,1},{1,8},{9,130},{130,9},{10,3},{3,10},{11,132},{132,11},{12,5}... | collective-permute-start | bytes 1769480 | tf_op jit(solution)/shard_map/ppermute | solution.py:496
  27.7 9.4 %all-to-all-done.refs_0_ = bf16[32,32,128]{2,1,0:T(8,128)(2,1)S(1)} async-done(((bf16[32,32,128]{2,1,0:T(8,128)(2,1)}), bf16[32,32,128]{2,1,0:T(8,128)(2,1)S(1)}, u32[]{:S(2)}, u32[]{:S(2)}) %all-to-all-start) | async-done | bytes 262176 | tf_op jit(solution)/shard_map/all_to_all | solution.py:519
  37.1 0.2 shard_map.57
  37.3 13.6 %all_to_all.20.refs_0_ = bf16[16,2,32,128]{3,2,1,0:T(8,128)(2,1)S(1)} all-to-all(bf16[16,2,32,128]{3,2,1,0:T(8,128)(2,1)S(1)} %shard_map.57), channel_id=1, replica_groups=mesh['tm_0'=2,'tm_1'=8,'tm_2'=2,'space'=8] {'tm_0','tm_1'}, dimensions={0} | all-to-all | bytes 524288 | tf_op jit(solution)/shard_map/all_to_all | solution.py:521
  50.9 1.9 %collective-permute-start.3 = (bf16[16,2,32,128]{3,2,1,0:T(8,128)(2,1)S(1)}, bf16[16,2,32,128]{3,2,1,0:T(8,128)(2,1)S(1)}, u32[]{:S(2)}, u32[]{:S(2)}) collective-permute-start(bf16[16,2,32,128]{3,2,1,0:T(8,128)(2,1)S(1)} %all_to_all.20.refs_0_), channel_id=1, source_target_pairs={{8,1},{1,8},{9,130},{130,9},{10,3},{3,10},{11,132},{132,11},{12,5}... | collective-permute-start | bytes 786440 | tf_op jit(solution)/shard_map/ppermute | solution.py:530
  52.9 0.0 collective-permute-done.6.refs_3_
  52.9 1.1 %collective-permute-start.7 = (bf16[3,4,64,128]{3,2,1,0:T(8,128)(2,1)S(1)}, bf16[3,4,64,128]{3,2,1,0:T(8,128)(2,1)S(1)}, u32[]{:S(2)}, u32[]{:S(2)}) collective-permute-start(bf16[3,4,64,128]{3,2,1,0:T(8,128)(2,1)S(1)} %slice_select_fusion.1), channel_id=1, source_target_pairs={{0,8},{1,9},{2,10},{3,11},{4,12},{5,13},{6,14},{7,15},{8,0},{9,1},... | collective-permute-start | bytes 589832 | tf_op jit(solution)/shard_map/ppermute | solution.py:498
  54.0 3.2 %collective-permute-start.4 = (bf16[8,2,32,128]{3,2,1,0:T(8,128)(2,1)S(1)}, bf16[8,2,32,128]{3,2,1,0:T(8,128)(2,1)S(1)}, u32[]{:S(2)}, u32[]{:S(2)}) collective-permute-start(bf16[8,2,32,128]{3,2,1,0:T(8,128)(2,1)S(1)} %slice_select_fusion.3), channel_id=1, source_target_pairs={{0,1},{9,8},{1,130},{138,9},{2,3},{11,10},{3,132},{140,11},{4,5},{... | collective-permute-start | bytes 393224 | tf_op jit(solution)/shard_map/ppermute | solution.py:531
  57.3 1.7 %collective-permute-start.8 = (bf16[16,2,32,128]{3,2,1,0:T(8,128)(2,1)S(1)}, bf16[16,2,32,128]{3,2,1,0:T(8,128)(2,1)S(1)}, u32[]{:S(2)}, u32[]{:S(2)}) collective-permute-start(bf16[16,2,32,128]{3,2,1,0:T(8,128)(2,1)S(1)} %all_to_all.20.refs_0_), channel_id=1, source_target_pairs={{0,8},{1,9},{2,10},{3,11},{4,12},{5,13},{6,14},{7,15},{8,0},{9,1},... | collective-permute-start | bytes 786440 | tf_op jit(solution)/shard_map/ppermute | solution.py:532
  59.0 1.7 %collective-permute-done.3.refs_0_ = bf16[16,2,32,128]{3,2,1,0:T(8,128)(2,1)S(1)} collective-permute-done((bf16[16,2,32,128]{3,2,1,0:T(8,128)(2,1)S(1)}, bf16[16,2,32,128]{3,2,1,0:T(8,128)(2,1)S(1)}, u32[]{:S(2)}, u32[]{:S(2)}) %collective-permute-start.3) | collective-permute-done | bytes 262176 | tf_op jit(solution)/shard_map/ppermute | solution.py:530
  60.7 0.1 collective-permute-start.5
  60.8 0.0 collective-permute-done.7.refs_4_
  60.9 1.1 %shard_map.58 = (f32[32,3,64,128]{3,2,1,0:T(8,128)S(1)}, f32[32,3,64,128]{3,2,1,0:T(8,128)S(1)}) custom-call(bf16[16,64,128]{2,1,0:T(8,128)(2,1)S(1)} %copy-done.1, bf16[16,64,128]{2,1,0:T(8,128)(2,1)S(1)} %copy-done, bf16[16,64,128]{2,1,0:T(8,128)(2,1)S(1)} %copy-done.2, bf16[3,12,64,128]{3,2,1,0:T(8,128)(2,1)S(1)} %collective-permute-done.6.refs_3_, ...), custom_call_target="tpu_custom_call" | custom-call | tf_op jit(solution)/shard_map/pallas_call | solution.py:452
  62.0 0.0 collective-permute-done.8.refs_1_
  62.0 1.0 shard_map.59
  63.0 0.0 collective-permute-done.4.refs_1_
  63.0 0.0 collective-permute-done.5.refs_2_
  63.0 0.0 copy-start.3
  63.1 5.0 %shard_map.60 = (bf16[16,2,32,128]{3,2,1,0:T(8,128)(2,1)S(1)}, f32[32,2,72,128]{3,2,1,0:T(8,128)S(1)}, f32[32,152,128]{2,1,0:T(8,128)S(1)}, f32[32,152,128]{2,1,0:T(8,128)S(1)}) custom-call(bf16[16,2,32,128]{3,2,1,0:T(8,128)(2,1)S(1)} %collective-permute-done.3.refs_0_, ...), custom_call_target="tpu_custom_call", output_to_operand_aliasing={{1}: (5, {}), {2}: (6, {}), {3}: (7, {})} | custom-call | tf_op jit(solution)/shard_map/pallas_call | solution.py:452
  68.0 16.4 %all_to_all.21.refs_0_ = bf16[16,2,32,128]{3,2,1,0:T(8,128)(2,1)S(1)} all-to-all(bf16[16,2,32,128]{3,2,1,0:T(8,128)(2,1)S(1)} %get-tuple-element.20), channel_id=1, replica_groups=mesh['tm_0'=2,'tm_1'=8,'tm_2'=2,'space'=8] {'tm_0','tm_1'}, dimensions={0} | all-to-all | bytes 524288 | tf_op jit(solution)/shard_map/all_to_all | solution.py:545
  84.4 0.2 shard_map.61
  84.7 19.3 %all_to_all.22 = bf16[32,32,128]{2,1,0:T(8,128)(2,1)S(1)} all-to-all(bf16[32,32,128]{2,1,0:T(8,128)(2,1)S(1)} %shard_map.61), channel_id=1, replica_groups=mesh['tm_0'=2,'tm_1'=8,'tm_2'=2,'space'=8] {'tm_0','tm_1','tm_2'}, dimensions={0} | all-to-all | bytes 524288 | tf_op jit(solution)/shard_map/all_to_all | solution.py:547
  104.0 0.0 copy-done.3
  104.0 0.8 shard_map.62
  (4 shorter events, 0.1 us)
Async XLA Ops:
  0.0 22.4 %copy-start.2 = (bf16[16,64,128]{2,1,0:T(8,128)(2,1)S(1)}, bf16[16,64,128]{2,1,0:T(8,128)(2,1)}, u32[]{:S(2)}) copy-start(bf16[16,64,128]{2,1,0:T(8,128)(2,1)} %refs_2_.1) | copy-start | bytes 786436
  0.0 22.4 %copy-start.1 = (bf16[16,64,128]{2,1,0:T(8,128)(2,1)S(1)}, bf16[16,64,128]{2,1,0:T(8,128)(2,1)}, u32[]{:S(2)}) copy-start(bf16[16,64,128]{2,1,0:T(8,128)(2,1)} %refs_0_.1) | copy-start | bytes 786436
  0.0 22.4 %copy-start = (bf16[16,64,128]{2,1,0:T(8,128)(2,1)S(1)}, bf16[16,64,128]{2,1,0:T(8,128)(2,1)}, u32[]{:S(2)}) copy-start(bf16[16,64,128]{2,1,0:T(8,128)(2,1)} %refs_1_.3) | copy-start | bytes 786436
  0.0 13.0 %collective-permute-start.2 = (bf16[16,64,128]{2,1,0:T(8,128)(2,1)}, bf16[16,64,128]{2,1,0:T(8,128)(2,1)S(1)}, u32[]{:S(2)}, u32[]{:S(2)}) collective-permute-start(bf16[16,64,128]{2,1,0:T(8,128)(2,1)} %bitcast.15), channel_id=1, source_target_pairs={{0,8},{8,16},{16,24},{24,32},{32,40},{40,48},{48,56},{56,64},{64,7... | collective-permute-start | bytes 786440 | tf_op jit(solution)/shard_map/ppermute | solution.py:493
  2.7 6.9 %collective-permute-start.1 = (bf16[2,64,128]{2,1,0:T(8,128)(2,1)S(1)}, bf16[2,64,128]{2,1,0:T(8,128)(2,1)S(1)}, u32[]{:S(2)}, u32[]{:S(2)}) collective-permute-start(bf16[2,64,128]{2,1,0:T(8,128)(2,1)S(1)} %get-tuple-element.21), channel_id=1, source_target_pairs={{1,2},{2,1},{3,4},{4,3},{5,6},{6,5},{9,10},{10,9},{11,12},{12,11},... | collective-permute-start | bytes 98312 | tf_op jit(solution)/shard_map/ppermute | solution.py:492
  6.0 7.0 %collective-permute-start = (bf16[2,64,128]{2,1,0:T(8,128)(2,1)S(1)}, bf16[2,64,128]{2,1,0:T(8,128)(2,1)S(1)}, u32[]{:S(2)}, u32[]{:S(2)}) collective-permute-start(bf16[2,64,128]{2,1,0:T(8,128)(2,1)S(1)} %get-tuple-element.22), channel_id=1, source_target_pairs={{0,1},{1,0},{2,3},{3,2},{4,5},{5,4},{6,7},{7,6},{8,9},{9,8},{10,11... | collective-permute-start | bytes 98312 | tf_op jit(solution)/shard_map/ppermute | solution.py:491
  13.7 23.4 %all-to-all-start = ((bf16[32,32,128]{2,1,0:T(8,128)(2,1)}), bf16[32,32,128]{2,1,0:T(8,128)(2,1)S(1)}, u32[]{:S(2)}, u32[]{:S(2)}) async-start(bf16[32,32,128]{2,1,0:T(8,128)(2,1)} %bitcast.4), calls=%async_computation | async-start | bytes 524288 | tf_op jit(solution)/shard_map/all_to_all | solution.py:519
  22.6 30.3 %collective-permute-start.6 = (bf16[3,12,64,128]{3,2,1,0:T(8,128)(2,1)S(1)}, bf16[3,12,64,128]{3,2,1,0:T(8,128)(2,1)S(1)}, u32[]{:S(2)}, u32[]{:S(2)}) collective-permute-start(bf16[3,12,64,128]{3,2,1,0:T(8,128)(2,1)S(1)} %slice_select_fusion), channel_id=1, source_target_pairs={{8,1},{1,8},{9,130},{130,9},{10,3},{3,10},{11,132},{132,11},{12,5}... | collective-permute-start | bytes 1769480 | tf_op jit(solution)/shard_map/ppermute | solution.py:496
  50.9 9.8 %collective-permute-start.3 = (bf16[16,2,32,128]{3,2,1,0:T(8,128)(2,1)S(1)}, bf16[16,2,32,128]{3,2,1,0:T(8,128)(2,1)S(1)}, u32[]{:S(2)}, u32[]{:S(2)}) collective-permute-start(bf16[16,2,32,128]{3,2,1,0:T(8,128)(2,1)S(1)} %all_to_all.20.refs_0_), channel_id=1, source_target_pairs={{8,1},{1,8},{9,130},{130,9},{10,3},{3,10},{11,132},{132,11},{12,5}... | collective-permute-start | bytes 786440 | tf_op jit(solution)/shard_map/ppermute | solution.py:530
  52.9 8.0 %collective-permute-start.7 = (bf16[3,4,64,128]{3,2,1,0:T(8,128)(2,1)S(1)}, bf16[3,4,64,128]{3,2,1,0:T(8,128)(2,1)S(1)}, u32[]{:S(2)}, u32[]{:S(2)}) collective-permute-start(bf16[3,4,64,128]{3,2,1,0:T(8,128)(2,1)S(1)} %slice_select_fusion.1), channel_id=1, source_target_pairs={{0,8},{1,9},{2,10},{3,11},{4,12},{5,13},{6,14},{7,15},{8,0},{9,1},... | collective-permute-start | bytes 589832 | tf_op jit(solution)/shard_map/ppermute | solution.py:498
  54.0 9.0 %collective-permute-start.4 = (bf16[8,2,32,128]{3,2,1,0:T(8,128)(2,1)S(1)}, bf16[8,2,32,128]{3,2,1,0:T(8,128)(2,1)S(1)}, u32[]{:S(2)}, u32[]{:S(2)}) collective-permute-start(bf16[8,2,32,128]{3,2,1,0:T(8,128)(2,1)S(1)} %slice_select_fusion.3), channel_id=1, source_target_pairs={{0,1},{9,8},{1,130},{138,9},{2,3},{11,10},{3,132},{140,11},{4,5},{... | collective-permute-start | bytes 393224 | tf_op jit(solution)/shard_map/ppermute | solution.py:531
  57.3 4.7 %collective-permute-start.8 = (bf16[16,2,32,128]{3,2,1,0:T(8,128)(2,1)S(1)}, bf16[16,2,32,128]{3,2,1,0:T(8,128)(2,1)S(1)}, u32[]{:S(2)}, u32[]{:S(2)}) collective-permute-start(bf16[16,2,32,128]{3,2,1,0:T(8,128)(2,1)S(1)} %all_to_all.20.refs_0_), channel_id=1, source_target_pairs={{0,8},{1,9},{2,10},{3,11},{4,12},{5,13},{6,14},{7,15},{8,0},{9,1},... | collective-permute-start | bytes 786440 | tf_op jit(solution)/shard_map/ppermute | solution.py:532
  60.7 2.3 %collective-permute-start.5 = (bf16[8,2,32,128]{3,2,1,0:T(8,128)(2,1)S(1)}, bf16[8,2,32,128]{3,2,1,0:T(8,128)(2,1)S(1)}, u32[]{:S(2)}, u32[]{:S(2)}) collective-permute-start(bf16[8,2,32,128]{3,2,1,0:T(8,128)(2,1)S(1)} %slice_select_fusion.2), channel_id=1, source_target_pairs={{0,8},{1,9},{2,10},{3,11},{4,12},{5,13},{6,14},{7,15},{8,0},{9,1},... | collective-permute-start | bytes 393224 | tf_op jit(solution)/shard_map/ppermute | solution.py:533
  63.0 41.0 %copy-start.3 = (bf16[1,16,64,128]{3,2,1,0:T(8,128)(2,1)S(1)}, bf16[1,16,64,128]{3,2,1,0:T(8,128)(2,1)}, u32[]{:S(2)}) copy-start(bf16[1,16,64,128]{3,2,1,0:T(8,128)(2,1)} %param.5) | copy-start | bytes 786436

commit v10 on v9

--- a/solution.py
+++ b/solution.py
@@ -11,7 +11,7 @@
 SWEEPS = 6
 STEPS = 32
 CHUNK = 16
-EARLY = 1
+EARLY = 2
 TM = ("tm_0", "tm_1", "tm_2")
 CHIPS = ("tm_0", "tm_1")
 CORE_SPACE = ("tm_2", "space")
@@ -246,15 +246,12 @@
     return jnp.where(core == 0, i, count - 1 - i)
 
 
-def coefficient_kernel(where, kappa, initial, reaction, outer, inner, inv, kinv):
-    planes = kappa.shape[0]
-    wide, narrow = outer.shape[1], inner.shape[1]
-    core, slot = where[0], where[1]
-    members = STEPS
-    factor = math.exp(math.log(alpha_ratio) / members)
+def coefficients(where, inv, kinv):
+    slot = where[1]
+    factor = math.exp(math.log(alpha_ratio) / STEPS)
     s0 = s1 = si = jnp.float32(0.0)
-    for j in range(members // 2):
-        phase = 2.0 * math.pi * j / members
+    for j in range(STEPS // 2):
+        phase = 2.0 * math.pi * j / STEPS
         real, imag = 1.0 - factor * math.cos(phase), factor * math.sin(phase)
         hit = slot == j
         s0 = jnp.where(hit, jnp.float32(real), s0)
@@ -272,16 +269,30 @@
             inv[e, c] = value
             kinv[e, c] = kv * value
 
+    return put
+
+
+def slab_kernel(where, kappa, initial, reaction, inv, kinv):
+    planes = kappa.shape[0]
+    put = coefficients(where, inv, kinv)
+
     def own(i):
-        put(wide + mirrored(core, i, planes), kappa[i], initial[i], reaction[i])
+        put(mirrored(where[0], i, planes), kappa[i], initial[i], reaction[i])
+
+    in_groups(planes, own)
+
+
+def rim_kernel(where, outer, inner, inv, kinv):
+    wide, narrow = outer.shape[1], inner.shape[1]
+    core = where[0]
+    put = coefficients(where, inv, kinv)
 
     def far(i):
         put(mirrored(core, i, wide), outer[0, i], outer[1, i], outer[2, i])
 
     def close(i):
-        put(wide + planes + mirrored(core, i, narrow), inner[0, i], inner[1, i], inner[2, i])
-
-    in_groups(planes, own)
+        put(wide + mirrored(core, i, narrow), inner[0, i], inner[1, i], inner[2, i])
+
     in_groups(wide, far)
     in_groups(narrow, close)
 
@@ -299,18 +310,19 @@
     band[...] = weights.astype(jnp.bfloat16)
 
 
-def fill(core, ref, base, inv, x0, x):
+def fill(core, ref, base, inv, first, x0, x):
     share, rows = ref.shape[2], inv.shape[2]
     per_plane = rows // share
     count = ref.shape[0] // per_plane
     starts = row_starts(rows)
 
     def body(i):
-        e = base + mirrored(core, i, count)
+        place_in = mirrored(core, i, count)
+        e = base + place_in
         for h in range(per_plane):
             part = pl.ds(h * share, share)
             re, im = (ref[per_plane * i + h, c].astype(jnp.float32) for c in range(2))
-            i0, i1, iq = (inv[e, c, part] for c in range(3))
+            i0, i1, iq = (inv[first + place_in, c, part] for c in range(3))
             for c, value in enumerate((re * i0 + im * iq, im * i1 - re * iq)):
                 x0[e, c, part] = value
                 x[e, pl.ds(starts[c] + h * share, share)] = value
@@ -318,8 +330,10 @@
     in_groups(count, body)
 
 
-def sweep(step, first, stop, x0, kinv, band, buffers, emit=None):
-    rows = kinv.shape[2]
+def sweep(step, first, stop, x0, kinvs, band, buffers, emit=None):
+    slab, rims = kinvs
+    rows = slab.shape[2]
+    wide = (x0.shape[0] - slab.shape[0] // 2) // 2
     starts = row_starts(rows)
     src, dst = buffers[step % 2], buffers[(step + 1) % 2]
     weight = sweep_weights()[step]
@@ -351,7 +365,11 @@
             re, im = columns[0][u + 2], columns[1][u + 2]
             sum_re, sum_im = total(0), total(1)
             part = pl.ds(r, CHUNK)
-            k0, k1, kq = (kinv[e, c, part] for c in range(3))
+            if wide <= e < wide + slab.shape[0]:
+                k0, k1, kq = (slab[e - wide, c, part] for c in range(3))
+            else:
+                k_e = e if e < wide else e - slab.shape[0]
+                k0, k1, kq = (rims[k_e, c, part] for c in range(3))
             pair = (
                 (1.0 - weight) * re + weight * (x0[e, 0, part] + k0 * sum_re + kq * sum_im),
                 (1.0 - weight) * im + weight * (x0[e, 1, part] + k1 * sum_im - kq * sum_re),
@@ -367,7 +385,7 @@
     rows, lanes = inv.shape[2:]
     own = y.shape[0] * y.shape[2] // rows
     core = where[0]
-    base = (inv.shape[0] - own) // 2
+    base = (x0.shape[0] - own) // 2
     write_band(band)
     zero = jnp.zeros((PAD, lanes), jnp.float32)
 
@@ -376,25 +394,27 @@
             for r in (0, PAD + rows, 2 * (PAD + rows)):
                 x[e, pl.ds(r, PAD)] = zero
 
-    in_groups(inv.shape[0], clear)
-    fill(core, y, base, inv, x0, xs)
-    fill(core, yb, base + own, inv, x0, xs)
+    in_groups(x0.shape[0], clear)
+    fill(core, y, base, inv, 0, x0, xs)
+    fill(core, yb, base + own, inv, own, x0, xs)
     for step in range(EARLY):
         edge = 2 * (step + 1)
-        sweep(step, base + edge, base + 2 * own - edge, x0, kinv, band, (xs, xt))
-
-
-def sweeps_kernel(where, y_a, yc, yd, inv, kinv, _x0, _xs, _xt, out, x0, xs, xt, band):
-    ext, _, rows, _ = inv.shape
+        sweep(step, base + edge, base + 2 * own - edge, x0, (kinv, None), band, (xs, xt))
+
+
+def sweeps_kernel(where, y_a, yc, yd, kslab, inv, krim, _x0, _xs, _xt, out, x0, xs, xt, band):
+    rows, _ = inv.shape[2:]
+    ext = x0.shape[0]
     share = y_a.shape[2]
     per_plane = rows // share
     own = y_a.shape[0] // per_plane
     core = where[0]
     base = (ext - own) // 2
+    kinv = (kslab, krim)
     write_band(band)
-    fill(core, y_a, base - own, inv, x0, xs)
-    fill(core, yc, 0, inv, x0, xs)
-    fill(core, yd, base + 2 * own, inv, x0, xs)
+    fill(core, y_a, base - own, inv, base - own, x0, xs)
+    fill(core, yc, 0, inv, 0, x0, xs)
+    fill(core, yd, base + 2 * own, inv, base, x0, xs)
 
     def emit(e, r, c, value):
         i = mirrored(core, e - base, own)
@@ -520,11 +540,10 @@
     (spectrum,) = call(placed(forward_kernel), [((slots, 2, share, lanes), bf16)], [cells])
     y = lax.all_to_all(spectrum, CHIPS, 0, 0, tiled=True)
 
-    fields = call(
-        placed(coefficient_kernel),
-        [((ext, 3, rows, lanes), f32)] * 2,
-        [kappa, initial, reaction, rim, inner],
-    )
+    table = [((planes, 3, rows, lanes), f32)] * 2
+    inv_slab, kinv_slab = call(placed(slab_kernel), table, [kappa, initial, reaction])
+    table = [((wide + narrow, 3, rows, lanes), f32)] * 2
+    inv_rim, kinv_rim = call(placed(rim_kernel), table, [rim, inner])
     n = per_plane * narrow
     first = core == 0
     ya = lax.ppermute(y, SIDE_CORE_SPACE, outer)
@@ -534,13 +553,13 @@
     tall = 2 * rows + 3 * PAD
     buffers = [((ext, 2, rows + PAD, lanes), f32), ((ext, tall, lanes), f32), ((ext, tall, lanes), f32)]
     band = [pltpu.VMEM((2 * lanes, lanes), bf16)]
-    state_arrays = call(placed(inside_kernel), buffers, [y, yb, *fields], band)
+    state_arrays = call(placed(inside_kernel), buffers, [y, yb, inv_slab, kinv_slab], band)
     solved = call(
         placed(sweeps_kernel),
         [((slots, 2, share, lanes), bf16), *buffers],
-        [ya, yc, yd, *fields, *state_arrays],
+        [ya, yc, yd, kinv_slab, inv_rim, kinv_rim, *state_arrays],
         band,
-        aliases={5: 1, 6: 2, 7: 3},
+        aliases={6: 1, 7: 2, 8: 3},
     )[0]
     modes = lax.all_to_all(solved, CHIPS, 0, 0, tiled=True)
     (correction,) = call(placed(inverse_kernel), [((members, share, lanes), bf16)], [modes])

time: 106 us -> 106 us (level)
    pallas_call x8 -> x9, Pallas kernels: 11.2 us -> 11.1 us  [call(): pl.pallas_call(kernel, out_shape=outs, in_specs=[HBM] * anywhere + [VMEM]...]
  transfers between devices with their start and end apart: 10 -> 10, of which waited for: 3 -> 3; matrix products, arithmetic and copies ran while one was open for 1% -> 1% of each run, Pallas kernels for 4% -> 5%
where the time goes in v10:
time: 106 us; the launch traced here: 105 us
  blocking collectives  49.4 us (47%)
  starting transfers between devices  28.5 us (27%)
  waiting for transfers between devices  14.5 us (14%)
  Pallas kernels  11.1 us (10%)
    all_to_all x1, blocking collectives, iteration(): returned = lax.all_to_all(correction, TM, 0, 0, tiled=True)  19.3 us
    all_to_all x1, blocking collectives, iteration(): modes = lax.all_to_all(solved, CHIPS, 0, 0, tiled=True)  16.4 us
    all_to_all x1, blocking collectives, iteration(): y = lax.all_to_all(spectrum, CHIPS, 0, 0, tiled=True)  13.6 us
    pallas_call x9, Pallas kernels, call(): pl.pallas_call(kernel, out_shape=outs, in_specs=[HBM] * anywhere + [VMEM]...  11.1 us
    all_to_all x1, waiting for transfers between devices, iteration(): lax.all_to_all(residual.reshape(members, share, lanes), TM, 0, 0, tiled=T...  9.39 us
    all_to_all x1, starting transfers between devices, iteration(): lax.all_to_all(residual.reshape(members, share, lanes), TM, 0, 0, tiled=T...  8.61 us
    ppermute x1, starting transfers between devices, iteration(): rim = lax.ppermute(rim, SIDE_CORE_SPACE, outer)  5.16 us
    ppermute x1, waiting for transfers between devices, iteration(): lax.ppermute(jnp.where(odd == 1, low, high), 'space', even_first)  3.34 us
  transfers between devices with their start and end apart: 10, of which 3 were waited for; matrix products, arithmetic and copies ran while one was open for 1% of the time, Pallas kernels for 5%

profile of v10, /device:TPU:16, one launch (start us, length us, event | category | flops | bytes accessed | tf_op | source)
XLA Modules:
  0.0 104.7 jit_solution(13077282071742314311)
XLA Ops:
  0.0 0.0 copy-start.2
  0.0 0.0 copy-start.1
  0.0 0.0 copy-start
  0.0 1.9 %collective-permute-start.2 = (bf16[16,64,128]{2,1,0:T(8,128)(2,1)}, bf16[16,64,128]{2,1,0:T(8,128)(2,1)S(1)}, u32[]{:S(2)}, u32[]{:S(2)}) collective-permute-start(bf16[16,64,128]{2,1,0:T(8,128)(2,1)} %bitcast.15), channel_id=1, source_target_pairs={{0,8},{8,16},{16,24},{24,32},{32,40},{40,48},{48,56},{56,64},{64,7... | collective-permute-start | bytes 786440 | tf_op jit(solution)/shard_map/ppermute | solution.py:513
  1.9 0.8 select_bitcast_fusion
  2.7 3.3 %collective-permute-start.1 = (bf16[2,64,128]{2,1,0:T(8,128)(2,1)S(1)}, bf16[2,64,128]{2,1,0:T(8,128)(2,1)S(1)}, u32[]{:S(2)}, u32[]{:S(2)}) collective-permute-start(bf16[2,64,128]{2,1,0:T(8,128)(2,1)S(1)} %get-tuple-element.25), channel_id=1, source_target_pairs={{1,2},{2,1},{3,4},{4,3},{5,6},{6,5},{9,10},{10,9},{11,12},{12,11},... | collective-permute-start | bytes 98312 | tf_op jit(solution)/shard_map/ppermute | solution.py:512
  6.0 1.5 %collective-permute-start = (bf16[2,64,128]{2,1,0:T(8,128)(2,1)S(1)}, bf16[2,64,128]{2,1,0:T(8,128)(2,1)S(1)}, u32[]{:S(2)}, u32[]{:S(2)}) collective-permute-start(bf16[2,64,128]{2,1,0:T(8,128)(2,1)S(1)} %get-tuple-element.26), channel_id=1, source_target_pairs={{0,1},{1,0},{2,3},{3,2},{4,5},{5,4},{6,7},{7,6},{8,9},{9,8},{10,11... | collective-permute-start | bytes 98312 | tf_op jit(solution)/shard_map/ppermute | solution.py:511
  7.4 2.2 %shard_map.55 = (f32[16,64,128]{2,1,0:T(8,128)S(1)}, f32[4,64,128]{2,1,0:T(8,128)S(1)}) custom-call(bf16[16,64,128]{2,1,0:T(8,128)(2,1)} %bitcast.16, bf16[16,64,128]{2,1,0:T(8,128)(2,1)} %refs_1_.3, bf16[16,64,128]{2,1,0:T(8,128)(2,1)} %bitcast.19, bf16[16,64,128]{2,1,0:T(8,128)(2,1)} %refs_0_.1, bf16[16,64,128]{2,1,0:T(8,128)(2,1)} %refs_2_.1), custom_call_target="tpu_custom_call" | custom-call | flops 20000000 | bytes 2500000 | tf_op jit(solution)/shard_map/pallas_call | solution.py:472
  9.6 0.0 collective-permute-done.1.refs_3_
  9.6 3.3 %collective-permute-done.refs_2_ = bf16[2,64,128]{2,1,0:T(8,128)(2,1)S(1)} collective-permute-done((bf16[2,64,128]{2,1,0:T(8,128)(2,1)S(1)}, bf16[2,64,128]{2,1,0:T(8,128)(2,1)S(1)}, u32[]{:S(2)}, u32[]{:S(2)}) %collective-permute-start) | collective-permute-done | bytes 32800 | tf_op jit(solution)/shard_map/ppermute | solution.py:511
  13.0 0.0 collective-permute-done.2.refs_4_
  13.0 0.8 shard_map.56
  13.7 8.6 %all-to-all-start = ((bf16[32,32,128]{2,1,0:T(8,128)(2,1)}), bf16[32,32,128]{2,1,0:T(8,128)(2,1)S(1)}, u32[]{:S(2)}, u32[]{:S(2)}) async-start(bf16[32,32,128]{2,1,0:T(8,128)(2,1)} %bitcast.4), calls=%async_computation | async-start | bytes 524288 | tf_op jit(solution)/shard_map/all_to_all | solution.py:539
  22.4 0.0 copy-done.2
  22.4 0.0 copy-done.1
  22.4 0.0 copy-done
  22.4 0.1 pad_maximum_fusion
  22.6 5.2 %collective-permute-start.6 = (bf16[3,12,64,128]{3,2,1,0:T(8,128)(2,1)S(1)}, bf16[3,12,64,128]{3,2,1,0:T(8,128)(2,1)S(1)}, u32[]{:S(2)}, u32[]{:S(2)}) collective-permute-start(bf16[3,12,64,128]{3,2,1,0:T(8,128)(2,1)S(1)} %slice_select_fusion), channel_id=1, source_target_pairs={{8,1},{1,8},{9,130},{130,9},{10,3},{3,10},{11,132},{132,11},{12,5}... | collective-permute-start | bytes 1769480 | tf_op jit(solution)/shard_map/ppermute | solution.py:516
  27.7 9.4 %all-to-all-done.refs_0_ = bf16[32,32,128]{2,1,0:T(8,128)(2,1)S(1)} async-done(((bf16[32,32,128]{2,1,0:T(8,128)(2,1)}), bf16[32,32,128]{2,1,0:T(8,128)(2,1)S(1)}, u32[]{:S(2)}, u32[]{:S(2)}) %all-to-all-start) | async-done | bytes 262176 | tf_op jit(solution)/shard_map/all_to_all | solution.py:539
  37.1 0.2 shard_map.57
  37.3 13.6 %all_to_all.20.refs_0_ = bf16[16,2,32,128]{3,2,1,0:T(8,128)(2,1)S(1)} all-to-all(bf16[16,2,32,128]{3,2,1,0:T(8,128)(2,1)S(1)} %shard_map.57), channel_id=1, replica_groups=mesh['tm_0'=2,'tm_1'=8,'tm_2'=2,'space'=8] {'tm_0','tm_1'}, dimensions={0} | all-to-all | bytes 524288 | tf_op jit(solution)/shard_map/all_to_all | solution.py:541
  50.9 1.9 %collective-permute-start.3 = (bf16[16,2,32,128]{3,2,1,0:T(8,128)(2,1)S(1)}, bf16[16,2,32,128]{3,2,1,0:T(8,128)(2,1)S(1)}, u32[]{:S(2)}, u32[]{:S(2)}) collective-permute-start(bf16[16,2,32,128]{3,2,1,0:T(8,128)(2,1)S(1)} %all_to_all.20.refs_0_), channel_id=1, source_target_pairs={{8,1},{1,8},{9,130},{130,9},{10,3},{3,10},{11,132},{132,11},{12,5}... | collective-permute-start | bytes 786440 | tf_op jit(solution)/shard_map/ppermute | solution.py:549
  52.9 0.0 collective-permute-done.6.refs_0_
  52.9 1.1 %collective-permute-start.7 = (bf16[3,4,64,128]{3,2,1,0:T(8,128)(2,1)S(1)}, bf16[3,4,64,128]{3,2,1,0:T(8,128)(2,1)S(1)}, u32[]{:S(2)}, u32[]{:S(2)}) collective-permute-start(bf16[3,4,64,128]{3,2,1,0:T(8,128)(2,1)S(1)} %slice_select_fusion.1), channel_id=1, source_target_pairs={{0,8},{1,9},{2,10},{3,11},{4,12},{5,13},{6,14},{7,15},{8,0},{9,1},... | collective-permute-start | bytes 589832 | tf_op jit(solution)/shard_map/ppermute | solution.py:518
  54.0 3.2 %collective-permute-start.4 = (bf16[8,2,32,128]{3,2,1,0:T(8,128)(2,1)S(1)}, bf16[8,2,32,128]{3,2,1,0:T(8,128)(2,1)S(1)}, u32[]{:S(2)}, u32[]{:S(2)}) collective-permute-start(bf16[8,2,32,128]{3,2,1,0:T(8,128)(2,1)S(1)} %slice_select_fusion.3), channel_id=1, source_target_pairs={{0,1},{9,8},{1,130},{138,9},{2,3},{11,10},{3,132},{140,11},{4,5},{... | collective-permute-start | bytes 393224 | tf_op jit(solution)/shard_map/ppermute | solution.py:550
  57.3 1.7 %collective-permute-start.8 = (bf16[16,2,32,128]{3,2,1,0:T(8,128)(2,1)S(1)}, bf16[16,2,32,128]{3,2,1,0:T(8,128)(2,1)S(1)}, u32[]{:S(2)}, u32[]{:S(2)}) collective-permute-start(bf16[16,2,32,128]{3,2,1,0:T(8,128)(2,1)S(1)} %all_to_all.20.refs_0_), channel_id=1, source_target_pairs={{0,8},{1,9},{2,10},{3,11},{4,12},{5,13},{6,14},{7,15},{8,0},{9,1},... | collective-permute-start | bytes 786440 | tf_op jit(solution)/shard_map/ppermute | solution.py:551
  59.0 1.7 %collective-permute-done.3.refs_0_ = bf16[16,2,32,128]{3,2,1,0:T(8,128)(2,1)S(1)} collective-permute-done((bf16[16,2,32,128]{3,2,1,0:T(8,128)(2,1)S(1)}, bf16[16,2,32,128]{3,2,1,0:T(8,128)(2,1)S(1)}, u32[]{:S(2)}, u32[]{:S(2)}) %collective-permute-start.3) | collective-permute-done | bytes 262176 | tf_op jit(solution)/shard_map/ppermute | solution.py:549
  60.7 0.1 collective-permute-start.5
  60.8 0.7 shard_map.58
  61.6 0.0 collective-permute-done.7.refs_1_
  61.6 0.5 shard_map.59
  62.1 0.0 collective-permute-done.8.refs_1_
  62.1 1.3 %shard_map.60 = (f32[32,2,72,128]{3,2,1,0:T(8,128)S(1)}, f32[32,152,128]{2,1,0:T(8,128)S(1)}, f32[32,152,128]{2,1,0:T(8,128)S(1)}) custom-call(bf16[16,2,32,128]{3,2,1,0:T(8,128)(2,1)S(1)} %all_to_all.20.refs_0_, bf16[16,2,32,128]{3,2,1,0:T(8,128)(2,1)S(1)} %collective-permute-done.8.refs_1_, f32[16,3,64,128]{3,2,1,0:T(8,128)S(1)} %get-tuple-element.20.refs_2_, ...), custom_call_target="tpu_custom_call" | custom-call | tf_op jit(solution)/shard_map/pallas_call | solution.py:472
  63.4 0.0 collective-permute-done.4.refs_1_
  63.4 0.0 collective-permute-done.5.refs_2_
  63.4 0.0 copy-start.3
  63.5 4.5 %shard_map.61 = (bf16[16,2,32,128]{3,2,1,0:T(8,128)(2,1)S(1)}, f32[32,2,72,128]{3,2,1,0:T(8,128)S(1)}, f32[32,152,128]{2,1,0:T(8,128)S(1)}, f32[32,152,128]{2,1,0:T(8,128)S(1)}) custom-call(bf16[16,2,32,128]{3,2,1,0:T(8,128)(2,1)S(1)} %collective-permute-done.3.refs_0_, ...), custom_call_target="tpu_custom_call", output_to_operand_aliasing={{1}: (6, {}), {2}: (7, {}), {3}: (8, {})} | custom-call | tf_op jit(solution)/shard_map/pallas_call | solution.py:472
  68.0 16.4 %all_to_all.21.refs_0_ = bf16[16,2,32,128]{3,2,1,0:T(8,128)(2,1)S(1)} all-to-all(bf16[16,2,32,128]{3,2,1,0:T(8,128)(2,1)S(1)} %get-tuple-element.24), channel_id=1, replica_groups=mesh['tm_0'=2,'tm_1'=8,'tm_2'=2,'space'=8] {'tm_0','tm_1'}, dimensions={0} | all-to-all | bytes 524288 | tf_op jit(solution)/shard_map/all_to_all | solution.py:564
  84.4 0.2 shard_map.62
  84.6 19.3 %all_to_all.22 = bf16[32,32,128]{2,1,0:T(8,128)(2,1)S(1)} all-to-all(bf16[32,32,128]{2,1,0:T(8,128)(2,1)S(1)} %shard_map.62), channel_id=1, replica_groups=mesh['tm_0'=2,'tm_1'=8,'tm_2'=2,'space'=8] {'tm_0','tm_1','tm_2'}, dimensions={0} | all-to-all | bytes 524288 | tf_op jit(solution)/shard_map/all_to_all | solution.py:566
  103.9 0.0 copy-done.3
  103.9 0.8 shard_map.63
  (4 shorter events, 0.1 us)
Async XLA Ops:
  0.0 22.4 %copy-start.2 = (bf16[16,64,128]{2,1,0:T(8,128)(2,1)S(1)}, bf16[16,64,128]{2,1,0:T(8,128)(2,1)}, u32[]{:S(2)}) copy-start(bf16[16,64,128]{2,1,0:T(8,128)(2,1)} %refs_2_.1) | copy-start | bytes 786436
  0.0 22.4 %copy-start.1 = (bf16[16,64,128]{2,1,0:T(8,128)(2,1)S(1)}, bf16[16,64,128]{2,1,0:T(8,128)(2,1)}, u32[]{:S(2)}) copy-start(bf16[16,64,128]{2,1,0:T(8,128)(2,1)} %refs_0_.1) | copy-start | bytes 786436
  0.0 22.4 %copy-start = (bf16[16,64,128]{2,1,0:T(8,128)(2,1)S(1)}, bf16[16,64,128]{2,1,0:T(8,128)(2,1)}, u32[]{:S(2)}) copy-start(bf16[16,64,128]{2,1,0:T(8,128)(2,1)} %refs_1_.3) | copy-start | bytes 786436
  0.0 13.0 %collective-permute-start.2 = (bf16[16,64,128]{2,1,0:T(8,128)(2,1)}, bf16[16,64,128]{2,1,0:T(8,128)(2,1)S(1)}, u32[]{:S(2)}, u32[]{:S(2)}) collective-permute-start(bf16[16,64,128]{2,1,0:T(8,128)(2,1)} %bitcast.15), channel_id=1, source_target_pairs={{0,8},{8,16},{16,24},{24,32},{32,40},{40,48},{48,56},{56,64},{64,7... | collective-permute-start | bytes 786440 | tf_op jit(solution)/shard_map/ppermute | solution.py:513
  2.7 6.9 %collective-permute-start.1 = (bf16[2,64,128]{2,1,0:T(8,128)(2,1)S(1)}, bf16[2,64,128]{2,1,0:T(8,128)(2,1)S(1)}, u32[]{:S(2)}, u32[]{:S(2)}) collective-permute-start(bf16[2,64,128]{2,1,0:T(8,128)(2,1)S(1)} %get-tuple-element.25), channel_id=1, source_target_pairs={{1,2},{2,1},{3,4},{4,3},{5,6},{6,5},{9,10},{10,9},{11,12},{12,11},... | collective-permute-start | bytes 98312 | tf_op jit(solution)/shard_map/ppermute | solution.py:512
  6.0 7.0 %collective-permute-start = (bf16[2,64,128]{2,1,0:T(8,128)(2,1)S(1)}, bf16[2,64,128]{2,1,0:T(8,128)(2,1)S(1)}, u32[]{:S(2)}, u32[]{:S(2)}) collective-permute-start(bf16[2,64,128]{2,1,0:T(8,128)(2,1)S(1)} %get-tuple-element.26), channel_id=1, source_target_pairs={{0,1},{1,0},{2,3},{3,2},{4,5},{5,4},{6,7},{7,6},{8,9},{9,8},{10,11... | collective-permute-start | bytes 98312 | tf_op jit(solution)/shard_map/ppermute | solution.py:511
  13.7 23.4 %all-to-all-start = ((bf16[32,32,128]{2,1,0:T(8,128)(2,1)}), bf16[32,32,128]{2,1,0:T(8,128)(2,1)S(1)}, u32[]{:S(2)}, u32[]{:S(2)}) async-start(bf16[32,32,128]{2,1,0:T(8,128)(2,1)} %bitcast.4), calls=%async_computation | async-start | bytes 524288 | tf_op jit(solution)/shard_map/all_to_all | solution.py:539
  22.6 30.3 %collective-permute-start.6 = (bf16[3,12,64,128]{3,2,1,0:T(8,128)(2,1)S(1)}, bf16[3,12,64,128]{3,2,1,0:T(8,128)(2,1)S(1)}, u32[]{:S(2)}, u32[]{:S(2)}) collective-permute-start(bf16[3,12,64,128]{3,2,1,0:T(8,128)(2,1)S(1)} %slice_select_fusion), channel_id=1, source_target_pairs={{8,1},{1,8},{9,130},{130,9},{10,3},{3,10},{11,132},{132,11},{12,5}... | collective-permute-start | bytes 1769480 | tf_op jit(solution)/shard_map/ppermute | solution.py:516
  50.9 9.8 %collective-permute-start.3 = (bf16[16,2,32,128]{3,2,1,0:T(8,128)(2,1)S(1)}, bf16[16,2,32,128]{3,2,1,0:T(8,128)(2,1)S(1)}, u32[]{:S(2)}, u32[]{:S(2)}) collective-permute-start(bf16[16,2,32,128]{3,2,1,0:T(8,128)(2,1)S(1)} %all_to_all.20.refs_0_), channel_id=1, source_target_pairs={{8,1},{1,8},{9,130},{130,9},{10,3},{3,10},{11,132},{132,11},{12,5}... | collective-permute-start | bytes 786440 | tf_op jit(solution)/shard_map/ppermute | solution.py:549
  52.9 8.7 %collective-permute-start.7 = (bf16[3,4,64,128]{3,2,1,0:T(8,128)(2,1)S(1)}, bf16[3,4,64,128]{3,2,1,0:T(8,128)(2,1)S(1)}, u32[]{:S(2)}, u32[]{:S(2)}) collective-permute-start(bf16[3,4,64,128]{3,2,1,0:T(8,128)(2,1)S(1)} %slice_select_fusion.1), channel_id=1, source_target_pairs={{0,8},{1,9},{2,10},{3,11},{4,12},{5,13},{6,14},{7,15},{8,0},{9,1},... | collective-permute-start | bytes 589832 | tf_op jit(solution)/shard_map/ppermute | solution.py:518
  54.0 9.4 %collective-permute-start.4 = (bf16[8,2,32,128]{3,2,1,0:T(8,128)(2,1)S(1)}, bf16[8,2,32,128]{3,2,1,0:T(8,128)(2,1)S(1)}, u32[]{:S(2)}, u32[]{:S(2)}) collective-permute-start(bf16[8,2,32,128]{3,2,1,0:T(8,128)(2,1)S(1)} %slice_select_fusion.3), channel_id=1, source_target_pairs={{0,1},{9,8},{1,130},{138,9},{2,3},{11,10},{3,132},{140,11},{4,5},{... | collective-permute-start | bytes 393224 | tf_op jit(solution)/shard_map/ppermute | solution.py:550
  57.3 4.8 %collective-permute-start.8 = (bf16[16,2,32,128]{3,2,1,0:T(8,128)(2,1)S(1)}, bf16[16,2,32,128]{3,2,1,0:T(8,128)(2,1)S(1)}, u32[]{:S(2)}, u32[]{:S(2)}) collective-permute-start(bf16[16,2,32,128]{3,2,1,0:T(8,128)(2,1)S(1)} %all_to_all.20.refs_0_), channel_id=1, source_target_pairs={{0,8},{1,9},{2,10},{3,11},{4,12},{5,13},{6,14},{7,15},{8,0},{9,1},... | collective-permute-start | bytes 786440 | tf_op jit(solution)/shard_map/ppermute | solution.py:551
  60.7 2.7 %collective-permute-start.5 = (bf16[8,2,32,128]{3,2,1,0:T(8,128)(2,1)S(1)}, bf16[8,2,32,128]{3,2,1,0:T(8,128)(2,1)S(1)}, u32[]{:S(2)}, u32[]{:S(2)}) collective-permute-start(bf16[8,2,32,128]{3,2,1,0:T(8,128)(2,1)S(1)} %slice_select_fusion.2), channel_id=1, source_target_pairs={{0,8},{1,9},{2,10},{3,11},{4,12},{5,13},{6,14},{7,15},{8,0},{9,1},... | collective-permute-start | bytes 393224 | tf_op jit(solution)/shard_map/ppermute | solution.py:552
  63.4 40.5 %copy-start.3 = (bf16[1,16,64,128]{3,2,1,0:T(8,128)(2,1)S(1)}, bf16[1,16,64,128]{3,2,1,0:T(8,128)(2,1)}, u32[]{:S(2)}) copy-start(bf16[1,16,64,128]{3,2,1,0:T(8,128)(2,1)} %param.5) | copy-start | bytes 786436

commit v11 on v10

--- a/solution.py
+++ b/solution.py
@@ -11,7 +11,7 @@
 SWEEPS = 6
 STEPS = 32
 CHUNK = 16
-EARLY = 2
+EARLY = 3
 TM = ("tm_0", "tm_1", "tm_2")
 CHIPS = ("tm_0", "tm_1")
 CORE_SPACE = ("tm_2", "space")
@@ -30,6 +30,10 @@
     return [
         1.0 / (1.0 + 0.4 * math.cos(math.pi * (2 * k + 1) / (2 * SWEEPS))) for k in range(SWEEPS)
     ]
+
+
+def scaled(weight, value):
+    return value if weight == 1.0 else weight * value
 
 
 def in_groups(count, body, group=4):
@@ -108,7 +112,7 @@
     centre = at(0, 0)
     near = (at(1, 0) + at(-1, 0)) + (at(0, 1) + at(0, -1))
     far = (at(2, 0) + at(-2, 0)) + (at(0, 2) + at(0, -2))
-    total = near_weight * near + far_weight * far
+    total = scaled(near_weight, near) + scaled(far_weight, far)
     for amount, mask in masks:
         total = total + pltpu.roll(centre, amount, 1) * mask
     return centre, total
@@ -279,7 +283,7 @@
     def own(i):
         put(mirrored(where[0], i, planes), kappa[i], initial[i], reaction[i])
 
-    in_groups(planes, own)
+    in_groups(planes, own, 8)
 
 
 def rim_kernel(where, outer, inner, inv, kinv):
@@ -327,7 +331,7 @@
                 x0[e, c, part] = value
                 x[e, pl.ds(starts[c] + h * share, share)] = value
 
-    in_groups(count, body)
+    in_groups(count, body, count)
 
 
 def sweep(step, first, stop, x0, kinvs, band, buffers, emit=None):
@@ -360,7 +364,7 @@
                 near = (x[u + 3] + x[u + 1]) + (side[0] + side[1])
                 far = (x[u + 4] + x[u]) + (side[2] + side[3])
                 k = (2 * u + c) * rows + r
-                return near_weight * near + far_weight * far + along[k : k + CHUNK]
+                return scaled(near_weight, near) + scaled(far_weight, far) + along[k : k + CHUNK]
 
             re, im = columns[0][u + 2], columns[1][u + 2]
             sum_re, sum_im = total(0), total(1)

time: 106 us -> 106 us (level)
  no operation moved by 1% of the time
where the time goes in v11:
time: 106 us; the launch traced here: 105 us
  blocking collectives  49.4 us (47%)
  starting transfers between devices  28.5 us (27%)
  waiting for transfers between devices  14.5 us (14%)
  Pallas kernels  11.3 us (11%)
    all_to_all x1, blocking collectives, iteration(): returned = lax.all_to_all(correction, TM, 0, 0, tiled=True)  19.3 us
    all_to_all x1, blocking collectives, iteration(): modes = lax.all_to_all(solved, CHIPS, 0, 0, tiled=True)  16.4 us
    all_to_all x1, blocking collectives, iteration(): y = lax.all_to_all(spectrum, CHIPS, 0, 0, tiled=True)  13.6 us
    pallas_call x9, Pallas kernels, call(): pl.pallas_call(kernel, out_shape=outs, in_specs=[HBM] * anywhere + [VMEM]...  11.3 us
    all_to_all x1, waiting for transfers between devices, iteration(): lax.all_to_all(residual.reshape(members, share, lanes), TM, 0, 0, tiled=T...  9.39 us
    all_to_all x1, starting transfers between devices, iteration(): lax.all_to_all(residual.reshape(members, share, lanes), TM, 0, 0, tiled=T...  8.61 us
    ppermute x1, starting transfers between devices, iteration(): rim = lax.ppermute(rim, SIDE_CORE_SPACE, outer)  5.16 us
    ppermute x1, waiting for transfers between devices, iteration(): lax.ppermute(jnp.where(odd == 1, low, high), 'space', even_first)  3.34 us
  transfers between devices with their start and end apart: 10, of which 3 were waited for; matrix products, arithmetic and copies ran while one was open for 1% of the time, Pallas kernels for 5%

profile of v11, /device:TPU:16, one launch (start us, length us, event | category | flops | bytes accessed | tf_op | source)
XLA Modules:
  0.0 104.9 jit_solution(499989909614486196)
XLA Ops:
  0.0 0.0 copy-start.2
  0.0 0.0 copy-start.1
  0.0 0.0 copy-start
  0.0 1.9 %collective-permute-start.2 = (bf16[16,64,128]{2,1,0:T(8,128)(2,1)}, bf16[16,64,128]{2,1,0:T(8,128)(2,1)S(1)}, u32[]{:S(2)}, u32[]{:S(2)}) collective-permute-start(bf16[16,64,128]{2,1,0:T(8,128)(2,1)} %bitcast.15), channel_id=1, source_target_pairs={{0,8},{8,16},{16,24},{24,32},{32,40},{40,48},{48,56},{56,64},{64,7... | collective-permute-start | bytes 786440 | tf_op jit(solution)/shard_map/ppermute | solution.py:517
  1.9 0.8 select_bitcast_fusion
  2.7 3.3 %collective-permute-start.1 = (bf16[2,64,128]{2,1,0:T(8,128)(2,1)S(1)}, bf16[2,64,128]{2,1,0:T(8,128)(2,1)S(1)}, u32[]{:S(2)}, u32[]{:S(2)}) collective-permute-start(bf16[2,64,128]{2,1,0:T(8,128)(2,1)S(1)} %get-tuple-element.25), channel_id=1, source_target_pairs={{1,2},{2,1},{3,4},{4,3},{5,6},{6,5},{9,10},{10,9},{11,12},{12,11},... | collective-permute-start | bytes 98312 | tf_op jit(solution)/shard_map/ppermute | solution.py:516
  6.0 1.5 %collective-permute-start = (bf16[2,64,128]{2,1,0:T(8,128)(2,1)S(1)}, bf16[2,64,128]{2,1,0:T(8,128)(2,1)S(1)}, u32[]{:S(2)}, u32[]{:S(2)}) collective-permute-start(bf16[2,64,128]{2,1,0:T(8,128)(2,1)S(1)} %get-tuple-element.26), channel_id=1, source_target_pairs={{0,1},{1,0},{2,3},{3,2},{4,5},{5,4},{6,7},{7,6},{8,9},{9,8},{10,11... | collective-permute-start | bytes 98312 | tf_op jit(solution)/shard_map/ppermute | solution.py:515
  7.4 2.2 %shard_map.55 = (f32[16,64,128]{2,1,0:T(8,128)S(1)}, f32[4,64,128]{2,1,0:T(8,128)S(1)}) custom-call(bf16[16,64,128]{2,1,0:T(8,128)(2,1)} %bitcast.16, bf16[16,64,128]{2,1,0:T(8,128)(2,1)} %refs_1_.3, bf16[16,64,128]{2,1,0:T(8,128)(2,1)} %bitcast.19, bf16[16,64,128]{2,1,0:T(8,128)(2,1)} %refs_0_.1, bf16[16,64,128]{2,1,0:T(8,128)(2,1)} %refs_2_.1), custom_call_target="tpu_custom_call" | custom-call | flops 20000000 | bytes 2500000 | tf_op jit(solution)/shard_map/pallas_call | solution.py:476
  9.6 0.0 collective-permute-done.1.refs_3_
  9.6 3.3 %collective-permute-done.refs_2_ = bf16[2,64,128]{2,1,0:T(8,128)(2,1)S(1)} collective-permute-done((bf16[2,64,128]{2,1,0:T(8,128)(2,1)S(1)}, bf16[2,64,128]{2,1,0:T(8,128)(2,1)S(1)}, u32[]{:S(2)}, u32[]{:S(2)}) %collective-permute-start) | collective-permute-done | bytes 32800 | tf_op jit(solution)/shard_map/ppermute | solution.py:515
  13.0 0.0 collective-permute-done.2.refs_4_
  13.0 0.8 shard_map.56
  13.7 8.6 %all-to-all-start = ((bf16[32,32,128]{2,1,0:T(8,128)(2,1)}), bf16[32,32,128]{2,1,0:T(8,128)(2,1)S(1)}, u32[]{:S(2)}, u32[]{:S(2)}) async-start(bf16[32,32,128]{2,1,0:T(8,128)(2,1)} %bitcast.4), calls=%async_computation | async-start | bytes 524288 | tf_op jit(solution)/shard_map/all_to_all | solution.py:543
  22.4 0.0 copy-done.2
  22.4 0.0 copy-done.1
  22.4 0.0 copy-done
  22.4 0.1 pad_maximum_fusion
  22.6 5.2 %collective-permute-start.6 = (bf16[3,12,64,128]{3,2,1,0:T(8,128)(2,1)S(1)}, bf16[3,12,64,128]{3,2,1,0:T(8,128)(2,1)S(1)}, u32[]{:S(2)}, u32[]{:S(2)}) collective-permute-start(bf16[3,12,64,128]{3,2,1,0:T(8,128)(2,1)S(1)} %slice_select_fusion), channel_id=1, source_target_pairs={{8,1},{1,8},{9,130},{130,9},{10,3},{3,10},{11,132},{132,11},{12,5}... | collective-permute-start | bytes 1769480 | tf_op jit(solution)/shard_map/ppermute | solution.py:520
  27.7 9.4 %all-to-all-done.refs_0_ = bf16[32,32,128]{2,1,0:T(8,128)(2,1)S(1)} async-done(((bf16[32,32,128]{2,1,0:T(8,128)(2,1)}), bf16[32,32,128]{2,1,0:T(8,128)(2,1)S(1)}, u32[]{:S(2)}, u32[]{:S(2)}) %all-to-all-start) | async-done | bytes 262176 | tf_op jit(solution)/shard_map/all_to_all | solution.py:543
  37.1 0.2 shard_map.57
  37.3 13.6 %all_to_all.20.refs_0_ = bf16[16,2,32,128]{3,2,1,0:T(8,128)(2,1)S(1)} all-to-all(bf16[16,2,32,128]{3,2,1,0:T(8,128)(2,1)S(1)} %shard_map.57), channel_id=1, replica_groups=mesh['tm_0'=2,'tm_1'=8,'tm_2'=2,'space'=8] {'tm_0','tm_1'}, dimensions={0} | all-to-all | bytes 524288 | tf_op jit(solution)/shard_map/all_to_all | solution.py:545
  50.9 1.9 %collective-permute-start.3 = (bf16[16,2,32,128]{3,2,1,0:T(8,128)(2,1)S(1)}, bf16[16,2,32,128]{3,2,1,0:T(8,128)(2,1)S(1)}, u32[]{:S(2)}, u32[]{:S(2)}) collective-permute-start(bf16[16,2,32,128]{3,2,1,0:T(8,128)(2,1)S(1)} %all_to_all.20.refs_0_), channel_id=1, source_target_pairs={{8,1},{1,8},{9,130},{130,9},{10,3},{3,10},{11,132},{132,11},{12,5}... | collective-permute-start | bytes 786440 | tf_op jit(solution)/shard_map/ppermute | solution.py:553
  52.9 0.0 collective-permute-done.6.refs_0_
  52.9 1.1 %collective-permute-start.7 = (bf16[3,4,64,128]{3,2,1,0:T(8,128)(2,1)S(1)}, bf16[3,4,64,128]{3,2,1,0:T(8,128)(2,1)S(1)}, u32[]{:S(2)}, u32[]{:S(2)}) collective-permute-start(bf16[3,4,64,128]{3,2,1,0:T(8,128)(2,1)S(1)} %slice_select_fusion.1), channel_id=1, source_target_pairs={{0,8},{1,9},{2,10},{3,11},{4,12},{5,13},{6,14},{7,15},{8,0},{9,1},... | collective-permute-start | bytes 589832 | tf_op jit(solution)/shard_map/ppermute | solution.py:522
  54.0 3.2 %collective-permute-start.4 = (bf16[8,2,32,128]{3,2,1,0:T(8,128)(2,1)S(1)}, bf16[8,2,32,128]{3,2,1,0:T(8,128)(2,1)S(1)}, u32[]{:S(2)}, u32[]{:S(2)}) collective-permute-start(bf16[8,2,32,128]{3,2,1,0:T(8,128)(2,1)S(1)} %slice_select_fusion.3), channel_id=1, source_target_pairs={{0,1},{9,8},{1,130},{138,9},{2,3},{11,10},{3,132},{140,11},{4,5},{... | collective-permute-start | bytes 393224 | tf_op jit(solution)/shard_map/ppermute | solution.py:554
  57.3 1.7 %collective-permute-start.8 = (bf16[16,2,32,128]{3,2,1,0:T(8,128)(2,1)S(1)}, bf16[16,2,32,128]{3,2,1,0:T(8,128)(2,1)S(1)}, u32[]{:S(2)}, u32[]{:S(2)}) collective-permute-start(bf16[16,2,32,128]{3,2,1,0:T(8,128)(2,1)S(1)} %all_to_all.20.refs_0_), channel_id=1, source_target_pairs={{0,8},{1,9},{2,10},{3,11},{4,12},{5,13},{6,14},{7,15},{8,0},{9,1},... | collective-permute-start | bytes 786440 | tf_op jit(solution)/shard_map/ppermute | solution.py:555
  59.0 1.7 %collective-permute-done.3.refs_0_ = bf16[16,2,32,128]{3,2,1,0:T(8,128)(2,1)S(1)} collective-permute-done((bf16[16,2,32,128]{3,2,1,0:T(8,128)(2,1)S(1)}, bf16[16,2,32,128]{3,2,1,0:T(8,128)(2,1)S(1)}, u32[]{:S(2)}, u32[]{:S(2)}) %collective-permute-start.3) | collective-permute-done | bytes 262176 | tf_op jit(solution)/shard_map/ppermute | solution.py:553
  60.7 0.1 collective-permute-start.5
  60.8 0.5 shard_map.58
  61.3 0.0 collective-permute-done.7.refs_1_
  61.3 0.5 shard_map.59
  61.8 0.0 collective-permute-done.8.refs_1_
  61.8 1.8 %shard_map.60 = (f32[32,2,72,128]{3,2,1,0:T(8,128)S(1)}, f32[32,152,128]{2,1,0:T(8,128)S(1)}, f32[32,152,128]{2,1,0:T(8,128)S(1)}) custom-call(bf16[16,2,32,128]{3,2,1,0:T(8,128)(2,1)S(1)} %all_to_all.20.refs_0_, bf16[16,2,32,128]{3,2,1,0:T(8,128)(2,1)S(1)} %collective-permute-done.8.refs_1_, f32[16,3,64,128]{3,2,1,0:T(8,128)S(1)} %get-tuple-element.20.refs_2_, ...), custom_call_target="tpu_custom_call" | custom-call | tf_op jit(solution)/shard_map/pallas_call | solution.py:476
  63.6 0.0 collective-permute-done.4.refs_1_
  63.6 0.0 collective-permute-done.5.refs_2_
  63.6 0.0 copy-start.3
  63.6 4.5 %shard_map.61 = (bf16[16,2,32,128]{3,2,1,0:T(8,128)(2,1)S(1)}, f32[32,2,72,128]{3,2,1,0:T(8,128)S(1)}, f32[32,152,128]{2,1,0:T(8,128)S(1)}, f32[32,152,128]{2,1,0:T(8,128)S(1)}) custom-call(bf16[16,2,32,128]{3,2,1,0:T(8,128)(2,1)S(1)} %collective-permute-done.3.refs_0_, ...), custom_call_target="tpu_custom_call", output_to_operand_aliasing={{1}: (6, {}), {2}: (7, {}), {3}: (8, {})} | custom-call | tf_op jit(solution)/shard_map/pallas_call | solution.py:476
  68.1 16.4 %all_to_all.21.refs_0_ = bf16[16,2,32,128]{3,2,1,0:T(8,128)(2,1)S(1)} all-to-all(bf16[16,2,32,128]{3,2,1,0:T(8,128)(2,1)S(1)} %get-tuple-element.24), channel_id=1, replica_groups=mesh['tm_0'=2,'tm_1'=8,'tm_2'=2,'space'=8] {'tm_0','tm_1'}, dimensions={0} | all-to-all | bytes 524288 | tf_op jit(solution)/shard_map/all_to_all | solution.py:568
  84.5 0.2 shard_map.62
  84.8 19.3 %all_to_all.22 = bf16[32,32,128]{2,1,0:T(8,128)(2,1)S(1)} all-to-all(bf16[32,32,128]{2,1,0:T(8,128)(2,1)S(1)} %shard_map.62), channel_id=1, replica_groups=mesh['tm_0'=2,'tm_1'=8,'tm_2'=2,'space'=8] {'tm_0','tm_1','tm_2'}, dimensions={0} | all-to-all | bytes 524288 | tf_op jit(solution)/shard_map/all_to_all | solution.py:570
  104.1 0.0 copy-done.3
  104.1 0.8 shard_map.63
  (4 shorter events, 0.1 us)
Async XLA Ops:
  0.0 22.4 %copy-start.2 = (bf16[16,64,128]{2,1,0:T(8,128)(2,1)S(1)}, bf16[16,64,128]{2,1,0:T(8,128)(2,1)}, u32[]{:S(2)}) copy-start(bf16[16,64,128]{2,1,0:T(8,128)(2,1)} %refs_2_.1) | copy-start | bytes 786436
  0.0 22.4 %copy-start.1 = (bf16[16,64,128]{2,1,0:T(8,128)(2,1)S(1)}, bf16[16,64,128]{2,1,0:T(8,128)(2,1)}, u32[]{:S(2)}) copy-start(bf16[16,64,128]{2,1,0:T(8,128)(2,1)} %refs_0_.1) | copy-start | bytes 786436
  0.0 22.4 %copy-start = (bf16[16,64,128]{2,1,0:T(8,128)(2,1)S(1)}, bf16[16,64,128]{2,1,0:T(8,128)(2,1)}, u32[]{:S(2)}) copy-start(bf16[16,64,128]{2,1,0:T(8,128)(2,1)} %refs_1_.3) | copy-start | bytes 786436
  0.0 13.0 %collective-permute-start.2 = (bf16[16,64,128]{2,1,0:T(8,128)(2,1)}, bf16[16,64,128]{2,1,0:T(8,128)(2,1)S(1)}, u32[]{:S(2)}, u32[]{:S(2)}) collective-permute-start(bf16[16,64,128]{2,1,0:T(8,128)(2,1)} %bitcast.15), channel_id=1, source_target_pairs={{0,8},{8,16},{16,24},{24,32},{32,40},{40,48},{48,56},{56,64},{64,7... | collective-permute-start | bytes 786440 | tf_op jit(solution)/shard_map/ppermute | solution.py:517
  2.7 6.9 %collective-permute-start.1 = (bf16[2,64,128]{2,1,0:T(8,128)(2,1)S(1)}, bf16[2,64,128]{2,1,0:T(8,128)(2,1)S(1)}, u32[]{:S(2)}, u32[]{:S(2)}) collective-permute-start(bf16[2,64,128]{2,1,0:T(8,128)(2,1)S(1)} %get-tuple-element.25), channel_id=1, source_target_pairs={{1,2},{2,1},{3,4},{4,3},{5,6},{6,5},{9,10},{10,9},{11,12},{12,11},... | collective-permute-start | bytes 98312 | tf_op jit(solution)/shard_map/ppermute | solution.py:516
  6.0 7.0 %collective-permute-start = (bf16[2,64,128]{2,1,0:T(8,128)(2,1)S(1)}, bf16[2,64,128]{2,1,0:T(8,128)(2,1)S(1)}, u32[]{:S(2)}, u32[]{:S(2)}) collective-permute-start(bf16[2,64,128]{2,1,0:T(8,128)(2,1)S(1)} %get-tuple-element.26), channel_id=1, source_target_pairs={{0,1},{1,0},{2,3},{3,2},{4,5},{5,4},{6,7},{7,6},{8,9},{9,8},{10,11... | collective-permute-start | bytes 98312 | tf_op jit(solution)/shard_map/ppermute | solution.py:515
  13.7 23.4 %all-to-all-start = ((bf16[32,32,128]{2,1,0:T(8,128)(2,1)}), bf16[32,32,128]{2,1,0:T(8,128)(2,1)S(1)}, u32[]{:S(2)}, u32[]{:S(2)}) async-start(bf16[32,32,128]{2,1,0:T(8,128)(2,1)} %bitcast.4), calls=%async_computation | async-start | bytes 524288 | tf_op jit(solution)/shard_map/all_to_all | solution.py:543
  22.6 30.3 %collective-permute-start.6 = (bf16[3,12,64,128]{3,2,1,0:T(8,128)(2,1)S(1)}, bf16[3,12,64,128]{3,2,1,0:T(8,128)(2,1)S(1)}, u32[]{:S(2)}, u32[]{:S(2)}) collective-permute-start(bf16[3,12,64,128]{3,2,1,0:T(8,128)(2,1)S(1)} %slice_select_fusion), channel_id=1, source_target_pairs={{8,1},{1,8},{9,130},{130,9},{10,3},{3,10},{11,132},{132,11},{12,5}... | collective-permute-start | bytes 1769480 | tf_op jit(solution)/shard_map/ppermute | solution.py:520
  50.9 9.8 %collective-permute-start.3 = (bf16[16,2,32,128]{3,2,1,0:T(8,128)(2,1)S(1)}, bf16[16,2,32,128]{3,2,1,0:T(8,128)(2,1)S(1)}, u32[]{:S(2)}, u32[]{:S(2)}) collective-permute-start(bf16[16,2,32,128]{3,2,1,0:T(8,128)(2,1)S(1)} %all_to_all.20.refs_0_), channel_id=1, source_target_pairs={{8,1},{1,8},{9,130},{130,9},{10,3},{3,10},{11,132},{132,11},{12,5}... | collective-permute-start | bytes 786440 | tf_op jit(solution)/shard_map/ppermute | solution.py:553
  52.9 8.4 %collective-permute-start.7 = (bf16[3,4,64,128]{3,2,1,0:T(8,128)(2,1)S(1)}, bf16[3,4,64,128]{3,2,1,0:T(8,128)(2,1)S(1)}, u32[]{:S(2)}, u32[]{:S(2)}) collective-permute-start(bf16[3,4,64,128]{3,2,1,0:T(8,128)(2,1)S(1)} %slice_select_fusion.1), channel_id=1, source_target_pairs={{0,8},{1,9},{2,10},{3,11},{4,12},{5,13},{6,14},{7,15},{8,0},{9,1},... | collective-permute-start | bytes 589832 | tf_op jit(solution)/shard_map/ppermute | solution.py:522
  54.0 9.6 %collective-permute-start.4 = (bf16[8,2,32,128]{3,2,1,0:T(8,128)(2,1)S(1)}, bf16[8,2,32,128]{3,2,1,0:T(8,128)(2,1)S(1)}, u32[]{:S(2)}, u32[]{:S(2)}) collective-permute-start(bf16[8,2,32,128]{3,2,1,0:T(8,128)(2,1)S(1)} %slice_select_fusion.3), channel_id=1, source_target_pairs={{0,1},{9,8},{1,130},{138,9},{2,3},{11,10},{3,132},{140,11},{4,5},{... | collective-permute-start | bytes 393224 | tf_op jit(solution)/shard_map/ppermute | solution.py:554
  57.3 4.6 %collective-permute-start.8 = (bf16[16,2,32,128]{3,2,1,0:T(8,128)(2,1)S(1)}, bf16[16,2,32,128]{3,2,1,0:T(8,128)(2,1)S(1)}, u32[]{:S(2)}, u32[]{:S(2)}) collective-permute-start(bf16[16,2,32,128]{3,2,1,0:T(8,128)(2,1)S(1)} %all_to_all.20.refs_0_), channel_id=1, source_target_pairs={{0,8},{1,9},{2,10},{3,11},{4,12},{5,13},{6,14},{7,15},{8,0},{9,1},... | collective-permute-start | bytes 786440 | tf_op jit(solution)/shard_map/ppermute | solution.py:555
  60.7 2.9 %collective-permute-start.5 = (bf16[8,2,32,128]{3,2,1,0:T(8,128)(2,1)S(1)}, bf16[8,2,32,128]{3,2,1,0:T(8,128)(2,1)S(1)}, u32[]{:S(2)}, u32[]{:S(2)}) collective-permute-start(bf16[8,2,32,128]{3,2,1,0:T(8,128)(2,1)S(1)} %slice_select_fusion.2), channel_id=1, source_target_pairs={{0,8},{1,9},{2,10},{3,11},{4,12},{5,13},{6,14},{7,15},{8,0},{9,1},... | collective-permute-start | bytes 393224 | tf_op jit(solution)/shard_map/ppermute | solution.py:556
  63.6 40.5 %copy-start.3 = (bf16[1,16,64,128]{3,2,1,0:T(8,128)(2,1)S(1)}, bf16[1,16,64,128]{3,2,1,0:T(8,128)(2,1)}, u32[]{:S(2)}) copy-start(bf16[1,16,64,128]{3,2,1,0:T(8,128)(2,1)} %param.5) | copy-start | bytes 786436
